TPU v7x, 32 devices: a whole 2x2x4 slice. The times are simulated.
32 devices in a mesh: grp: 2 (over y), dec: 4 (over z), stg: 2 (over x), tp: 2 (over core).
Axes of the slice: x: 2, y: 2, z: 4, core: 2. Of those that a mesh axis runs over, the one named last changes fastest.
Arguments:
- hidden_x: bfloat16 [3072, 7168], P(('grp', 'dec'), ('stg', 'tp')), parts along dimension 0, may hold values from -8 to 8
- proj_weight: bfloat16 [7168, 2112], P(('stg', 'tp'), 'dec'), may hold values from -0.0625 to 0.0625
- q_gain: float32 [1536], replicated, may hold values from 0.25 to 1.75
- kv_gain: float32 [512], replicated, may hold values from 0.25 to 1.75
- old_cache: bfloat16 [256, 32, 576], P(('grp', 'dec')), parts along dimension 0, may hold values from -6 to 6
- page_plan: int32 [96, 2], P(('grp', 'dec')), parts along dimension 0, may hold values from 0 to 31, as said below
- block_table: int32 [8, 4, 8], P(('grp', 'dec')), parts along dimension 0, may hold values from 0 to 31, as said below
- split_lens: int32 [8, 4], P('grp', 'dec'), parts along dimension 0, may hold values from 2 to 256, as said below
- dec_query: bfloat16 [8, 128, 576], P('grp', ('stg', 'tp')), parts along dimension 0, may hold values from -66 to 66
- new_key: bfloat16 [8, 576], P('grp'), parts along dimension 0, may hold values from -12 to 12
Outputs:
- q_latent: bfloat16 [3072, 1536], P(('grp', 'dec'), ('stg', 'tp')), parts along dimension 0
- attn_latent: bfloat16 [8, 128, 512], P('grp', ('stg', 'tp')), parts along dimension 0
There are 2 independent parts, one for each index of `grp`. A program takes and returns all parts, laid end to end along the dimension named above; an argument that names none is the same for every part. Nothing has to cross between parts.
Inputs may be any that keep to these rules, and one draw needn't show every extreme that they name: `page_plan`: column 0 is the owner of prefill page g, column 1 its slot among the owner's 32; no two pages share owner and slot; in each aligned block of 12 rows (one index of dec) no owner appears more than 3 times and some owner exactly 3 times; no page goes to a slot block_table[o, r, 0]. `block_table`: for each owner the 4 x 8 entries are its 32 slots, each once. `split_lens`: each request has exactly 256 tokens on at least one owner.
All inputs are finite; a program needn't handle non-finite values.
Results may differ from a plain program's by a relative error of at most 0.0054.
Values may be sent and summed in bfloat16 or wider, within the bound.
No kernel may reach another device: no remote copies, remote signals or barrier semaphores. Data moves between devices by JAX's collectives and lax.ppermute only.
A program may use at most 64 MiB of HBM per device.

v0:
```python
import functools

import jax
import jax.numpy as jnp
from jax import lax
from jax.experimental import pallas as pl
from jax.experimental.pallas import tpu as pltpu
from jax.sharding import PartitionSpec as P


QL = 1536
KVL = 512
ROPE = 64
PAGE = 32
KVW = KVL + ROPE
MASKED = -1e30

softmax_scale = 192.0 ** (-0.5)
norm_eps = 1e-06


def combined_all(part, axis, combine):
    gathered = jax.tree.map(lambda a: lax.all_gather(a, axis), part)

    def take(source):
        return jax.tree.map(lambda a: lax.dynamic_index_in_dim(a, source, 0, False), gathered)

    return lax.fori_loop(
        1, lax.axis_size(axis), lambda source, state: combine(state, take(source)), take(0)
    )


def rope_rotate(matrix, col_start, positions):
    col_count = matrix.shape[1]
    columns = col_start + jnp.arange(col_count, dtype=jnp.int32)
    is_rope = columns >= KVL
    pair_index = jnp.maximum(columns - KVL, 0) // 2
    frequency = jnp.power(jnp.float32(10000.0), -(2 * pair_index).astype(jnp.float32) / ROPE)
    angles = positions[:, None] * frequency[None, :]
    cosine = jnp.where(is_rope[None, :], jnp.cos(angles), 1.0)
    sine_part = jnp.where(is_rope[None, :], jnp.sin(angles), 0.0)
    paired = matrix.reshape(matrix.shape[0], col_count // 2, 2)
    partner = jnp.stack([-paired[:, :, 1], paired[:, :, 0]], axis=2).reshape(matrix.shape)
    return matrix * cosine + partner * sine_part


def kv_finish(matrix, col_start, latent_sq, kv_gain, positions):
    col_count = matrix.shape[1]
    columns = col_start + jnp.arange(col_count, dtype=jnp.int32)
    gain_full = jnp.concatenate([kv_gain, jnp.ones((ROPE,), jnp.float32)])
    gain_cols = lax.dynamic_slice_in_dim(gain_full, col_start, col_count)
    inverse = lax.rsqrt(latent_sq / KVL + norm_eps)
    row_scale = jnp.where(columns[None, :] < KVL, inverse[:, None] * gain_cols[None, :], 1.0)
    return rope_rotate(matrix * row_scale, col_start, positions).astype(jnp.bfloat16)


def pack_pages(kv_pages, page_table, owner_count, capacity):
    owners = page_table[:, 0]
    slot_ids = page_table[:, 1]
    page_ids = jnp.arange(kv_pages.shape[0], dtype=jnp.int32)
    earlier = (owners[:, None] == owners[None, :]) & (page_ids[None, :] < page_ids[:, None])
    ranking = jnp.sum(earlier.astype(jnp.int32), axis=1)
    targets = owners * capacity + ranking
    places = jnp.arange(owner_count * capacity, dtype=jnp.int32)
    matches = targets[None, :] == places[:, None]
    source_ids = jnp.sum(jnp.where(matches, page_ids[None, :], 0), axis=1)
    filled = jnp.any(matches, axis=1)
    chosen = jnp.where(
        filled[:, None, None], jnp.take(kv_pages, source_ids, axis=0), jnp.zeros((), kv_pages.dtype)
    )
    labels = jnp.where(filled, jnp.take(slot_ids, source_ids), -1).astype(jnp.bfloat16)
    return (
        chosen.reshape(owner_count, capacity, kv_pages.shape[1], kv_pages.shape[2]),
        labels.reshape(owner_count, capacity),
    )


def place_pages(old_cache, got_pages, got_labels):
    flat_pages = got_pages.reshape(-1, old_cache.shape[1], old_cache.shape[2])
    label_ids = got_labels.reshape(-1).astype(jnp.int32)
    slot_ids = jnp.arange(old_cache.shape[0], dtype=jnp.int32)
    arrival_ids = jnp.arange(label_ids.shape[0], dtype=jnp.int32)
    matches = label_ids[None, :] == slot_ids[:, None]
    source_ids = jnp.sum(jnp.where(matches, arrival_ids[None, :], 0), axis=1)
    arrived = jnp.any(matches, axis=1)
    return jnp.where(arrived[:, None, None], jnp.take(flat_pages, source_ids, axis=0), old_cache)


def combine_parts(former, latter):
    overall = jnp.maximum(former[0], latter[0])
    front_scale = jnp.exp(former[0] - overall)
    back_scale = jnp.exp(latter[0] - overall)
    return (
        overall,
        former[1] * front_scale + latter[1] * back_scale,
        former[2] * front_scale[:, :, None] + latter[2] * back_scale[:, :, None],
    )


def body_general(
    hidden_x,
    proj_weight,
    q_gain,
    kv_gain,
    old_cache,
    page_plan,
    block_table,
    split_lens,
    dec_query,
    new_key,
):
    projected = jnp.dot(
        hidden_x,
        lax.all_gather(proj_weight, "dec", axis=1, tiled=True),
        preferred_element_type=jnp.float32,
    )
    query_part = projected[:, :QL]
    kv_part = projected[:, QL:]
    tokens_here = hidden_x.shape[0]
    positions = (
        lax.axis_index("dec") * tokens_here + jnp.arange(tokens_here, dtype=jnp.int32)
    ).astype(jnp.float32)
    lane_count = lax.axis_size(("stg", "tp"))
    lane_index = lax.axis_index(("stg", "tp"))
    owner_count = lax.axis_size("dec")
    page_count = page_plan.shape[0]
    capacity = max(2, -(-page_count // owner_count))
    query_width = QL // lane_count
    query_cols, kv_cols = (
        lax.psum_scatter(query_part, ("stg", "tp"), scatter_dimension=1, tiled=True),
        lax.psum_scatter(kv_part, ("stg", "tp"), scatter_dimension=1, tiled=True),
    )
    kv_width = kv_cols.shape[1]
    col_start = lane_index * kv_width
    columns = col_start + jnp.arange(kv_width, dtype=jnp.int32)
    latent_part_sq = jnp.sum(jnp.where(columns[None, :] < KVL, kv_cols * kv_cols, 0.0), axis=1)
    query_sq, latent_sq = lax.psum(
        (jnp.sum(query_cols * query_cols, axis=1), latent_part_sq), ("stg", "tp")
    )
    kv_rows = kv_finish(kv_cols, col_start, latent_sq, kv_gain, positions)
    kv_pages = kv_rows.reshape(page_count, PAGE, kv_width)
    send_pages, send_labels = pack_pages(kv_pages, page_plan, owner_count, capacity)
    got_slices, got_labels = (
        lax.all_to_all(send_pages, "dec", split_axis=0, concat_axis=0, tiled=True),
        lax.all_to_all(send_labels, "dec", split_axis=0, concat_axis=0, tiled=True),
    )
    got_pages = lax.all_gather(got_slices, ("stg", "tp"), axis=3, tiled=True)
    query_gain = lax.dynamic_slice_in_dim(q_gain, lane_index * query_width, query_width)
    q_latent = (
        query_cols * lax.rsqrt(query_sq / QL + norm_eps)[:, None] * query_gain[None, :]
    ).astype(jnp.bfloat16)
    cache = place_pages(old_cache, got_pages, got_labels)
    slot_table = block_table[0]
    request_count = slot_table.shape[0]
    key_rows = jnp.take(cache, slot_table.reshape(-1), axis=0).reshape(
        request_count, -1, cache.shape[2]
    )
    scores = (
        jnp.einsum("rhc,rlc->rhl", dec_query, key_rows, preferred_element_type=jnp.float32)
        * softmax_scale
    )
    live_mask = jnp.arange(key_rows.shape[1], dtype=jnp.int32)[None, :] < split_lens[:, 0][:, None]
    scores = jnp.where(live_mask[:, None, :], scores, -1e30)
    row_peak = jnp.max(scores, axis=2)
    weights = jnp.where(live_mask[:, None, :], jnp.exp(scores - row_peak[:, :, None]), 0.0)
    row_total = jnp.sum(weights, axis=2)
    rounded = weights.astype(jnp.bfloat16)
    partial_out = jnp.einsum(
        "rhl,rlc->rhc", rounded, key_rows[:, :, :KVL], preferred_element_type=jnp.float32
    )
    peak_all, total_all, output_all = combined_all(
        (row_peak, row_total, partial_out), "dec", combine_parts
    )
    self_score = (
        jnp.einsum("rhc,rc->rh", dec_query, new_key, preferred_element_type=jnp.float32)
        * softmax_scale
    )
    overall = jnp.maximum(peak_all, self_score)
    carried = jnp.exp(peak_all - overall)
    self_weight = jnp.exp(self_score - overall)
    denom = total_all * carried + self_weight
    numer = output_all * carried[:, :, None] + self_weight[:, :, None] * new_key[
        :, None, :KVL
    ].astype(jnp.float32)
    attn_latent = (numer / denom[:, :, None]).astype(jnp.bfloat16)
    return (q_latent, attn_latent)


VMEM = pl.BlockSpec(memory_space=pltpu.VMEM)
SMEM = pl.BlockSpec(memory_space=pltpu.SMEM)
VMEM_GRANT = 16 * 2**20
F32 = jnp.float32
BF16 = jnp.bfloat16


def swap(a, axis):
    return lax.ppermute(a, axis, [(0, 1), (1, 0)])


def dot_t(a, b, **kw):
    return lax.dot_general(a, b, (((1,), (1,)), ((), ())), preferred_element_type=F32, **kw)


def dot_n(a, b, **kw):
    return lax.dot_general(a, b, (((1,), (0,)), ((), ())), preferred_element_type=F32, **kw)


def matmul_kernel(blocks, ids, *refs):
    group, core = ids[0], ids[1]
    xs, (head_z, tail_z, head_y, tail_y), outs = refs[:blocks], refs[blocks : blocks + 4], refs[blocks + 4 :]
    half = head_z.shape[1]
    split = head_z.shape[0]
    here = pl.ds(pl.multiple_of(group * half, 128), half)
    there = pl.ds(pl.multiple_of((1 - group) * half, 128), half)
    for i, x_ref in enumerate(xs):
        send, keep = outs[2 * i], outs[2 * i + 1]
        rows = send.shape[0]
        near, far = x_ref[:, here], x_ref[:, there]
        for z, y, at in ((head_z, head_y, slice(0, split)), (tail_z, tail_y, slice(split, None))):
            out = dot_t(near, z[...]) + dot_t(far, y[...])
            top, bottom = out[:rows], out[rows:]
            send[:, at] = jnp.where(core == 0, bottom, top)
            keep[:, at] = jnp.where(core == 0, top, bottom)


def matmul(ids, xs, weights):
    rows, feats = xs[0].shape
    cols = weights[0].shape[0] + weights[1].shape[0]
    blocks = len(xs)
    return pl.pallas_call(
        functools.partial(matmul_kernel, blocks),
        in_specs=[SMEM] + [VMEM] * (blocks + 4),
        out_specs=[VMEM] * (2 * blocks),
        out_shape=[jax.ShapeDtypeStruct((rows // 2, cols), F32)] * (2 * blocks),
        cost_estimate=pl.CostEstimate(
            flops=2 * rows * feats * cols * blocks,
            bytes_accessed=8 * rows * cols * blocks,
            transcendentals=0,
        ),
        compiler_params=pltpu.CompilerParams(vmem_limit_bytes=VMEM_GRANT),
        name="project",
    )(ids, *xs, *weights)


def old_kernel(n, pages, ids, tab_ref, query_ref, rows_ref, own_ref, peak_ref, total_ref, out_ref, bias_ref):
    index, core = ids[2], ids[1]
    query = query_ref[...]
    keys = rows_ref.shape[0]
    requests = own_ref.shape[0] // 4
    heads = query.shape[0] // requests
    base = 2 * pages
    slots = keys // PAGE
    per = slots // requests

    def iota(rows, cols, axis):
        return lax.broadcasted_iota(jnp.int32, (rows, cols), axis)

    size = tab_ref.shape[1]
    diagonal = iota(size, size, 0) == iota(size, size, 1)
    columns = [
        jnp.sum(jnp.where(diagonal, tab_ref[s : s + 1, :], 0), axis=1, keepdims=True)
        for s in range(n)
    ]
    entry = iota(slots, 1, 0)
    readers = entry // per

    def limits(column):
        lengths = jnp.zeros((slots, 1), jnp.int32)
        for r in range(requests):
            at = base + slots + r
            lengths = jnp.where(readers == r, column[at : at + 1, :], lengths)
        return lengths - PAGE * (entry % per)

    def lookup(hit, values):
        return jnp.sum(jnp.where(hit, values, 0), axis=0, keepdims=True)

    page = iota(1, keys, 1) // PAGE
    hit = columns[0][base : base + slots, :] == page
    limit = lookup(hit, limits(columns[0]))
    reader = lookup(hit, readers)
    is_slot = iota(base, 1, 0) % 2 == 1
    taken = jnp.zeros((1, keys), jnp.int32)
    odd_row = iota(base, base, 0)
    follows = (iota(base, base, 1) == odd_row - 1) & (odd_row % 2 == 1)
    for s in range(n):
        plan = columns[s][:base, :]
        owners = jnp.sum(jnp.where(follows, tab_ref[s : s + 1, :base], 0), axis=1, keepdims=True)
        here = is_slot & (owners == index)
        taken = taken + jnp.sum(jnp.where(here & (plan == page), 1, 0), axis=0, keepdims=True)
    limit = jnp.where(taken > 0, 0, limit)
    live = (iota(1, keys, 1) % PAGE) < limit
    bias = jnp.where(live & (reader == iota(8, keys, 0)), 0.0, MASKED)
    wide = jnp.concatenate(
        [jnp.broadcast_to(bias[r : r + 1], (heads, keys)) for r in range(requests)], axis=0
    )
    scores = dot_t(query, rows_ref[...]) * softmax_scale + wide
    own = dot_t(query, own_ref[...]) * softmax_scale
    mine = iota(*own.shape, 0) // heads == iota(*own.shape, 1)
    own = jnp.sum(jnp.where(mine, own, 0.0), axis=1, keepdims=True)
    own = jnp.where(index == 0, own, MASKED)
    peak = jnp.maximum(jnp.max(scores, axis=1, keepdims=True), own)
    weights = jnp.where(wide < 0.0, 0.0, jnp.exp(scores - peak))
    own_weight = jnp.where(index == 0, jnp.exp(own - peak), 0.0)
    peak_ref[...] = peak
    total_ref[...] = jnp.sum(weights, axis=1, keepdims=True) + own_weight
    out = dot_n(weights.astype(BF16), rows_ref[:, :KVL])
    own_rows = own_ref[:, :KVL].astype(F32)
    latent = jnp.concatenate(
        [jnp.broadcast_to(own_rows[r : r + 1], (heads, KVL)) for r in range(requests)], axis=0
    )
    out_ref[...] = out + own_weight * latent

    width = bias_ref.shape[1]
    half = pages // 2
    spot = iota(1, width, 1) // PAGE
    which = jnp.where(spot // pages == 1, 1 - core, core) * half + spot % half
    partner = (spot % pages) // half == 1
    line = iota(base, width, 0)
    plan = jnp.where(partner, columns[n - 1][:base, :], columns[0][:base, :])
    plan = jnp.where(line % 2 == 1, plan, plan * (2 * slots))
    code = jnp.sum(jnp.where(line // 2 == which, plan, 0), axis=0, keepdims=True)
    limit = jnp.zeros((1, width), jnp.int32)
    reader = jnp.zeros((1, width), jnp.int32)
    for s in range(n):
        owner = (index + s) % n
        hit = columns[s][base : base + slots, :] + owner * (2 * slots) == code
        limit = limit + lookup(hit, limits(columns[s]))
        reader = reader + lookup(hit, readers)
    limit = jnp.where(index % 2 == 1, limit, 0)
    live = (iota(1, width, 1) % PAGE) < limit
    bias_ref[...] = jnp.where(live & (reader == iota(8, width, 0)), 0.0, MASKED)


def middle_kernel(ids, *refs):
    (ak, ar, bk, br, pak, par, pbk, pbr, kv_send, kv_keep, q_send, q_keep) = refs
    first, stage = ids[2] < 2, ids[3]
    rows, cols = ak.shape
    cut = QL - 2 * cols
    quarter = rows // 2
    for i, (a0, a1, b0, b1) in enumerate(((ak, ar, bk, br), (pak, par, pbk, pbr))):
        a = a0[...] + a1[...]
        b = b0[...] + b1[...]
        low, high = jnp.where(first, b, a), jnp.where(first, a, b)
        tail = jnp.concatenate([low[:, cut:], high], axis=1)
        at = slice(i * rows, (i + 1) * rows)
        kv_keep[at, :] = tail
        kv_send[at, :] = tail.astype(BF16)
        top, bottom = low[:quarter, :cut], low[quarter:, :cut]
        at = slice(i * quarter, (i + 1) * quarter)
        q_keep[at, :] = jnp.where(stage == 0, top, bottom)
        q_send[at, :] = jnp.where(stage == 0, bottom, top).astype(BF16)


def keys_kernel(keep, got, cos, sin, turn, gain, out):
    raw = keep[...] + got[...].astype(F32)
    latent = raw[:, :KVL]
    inverse = lax.rsqrt(jnp.sum(latent * latent, axis=1, keepdims=True) / KVL + norm_eps)
    out[:, :KVL] = (latent * inverse * gain[...]).astype(BF16)
    rope = raw[:, KVL:]
    partner = dot_n(rope, turn[...], precision=lax.Precision.HIGHEST)
    out[:, KVL:] = (rope * cos[...] + partner * sin[...]).astype(BF16)


def attend_kernel(query_ref, k0_ref, k1_ref, bias_ref, peak_ref, total_ref, out_ref, packed_ref):
    query = query_ref[...]
    keys = k0_ref.shape[0]
    rows = query.shape[0]
    requests = bias_ref.shape[0] // 2
    heads = rows // requests
    bias = bias_ref[...]
    wide = jnp.concatenate(
        [jnp.broadcast_to(bias[r : r + 1], (heads, 2 * keys)) for r in range(requests)], axis=0
    )
    scores = jnp.concatenate([dot_t(query, k0_ref[...]), dot_t(query, k1_ref[...])], axis=1)
    scores = scores * softmax_scale + wide
    old_peak = peak_ref[...]
    peak = jnp.maximum(old_peak, jnp.max(scores, axis=1, keepdims=True))
    weights = jnp.where(wide < 0.0, 0.0, jnp.exp(scores - peak))
    carried = jnp.exp(old_peak - peak)
    total = jnp.sum(weights, axis=1, keepdims=True) + total_ref[...] * carried
    rounded = weights.astype(BF16)
    out = dot_n(rounded[:, :keys], k0_ref[:, :KVL]) + dot_n(rounded[:, keys:], k1_ref[:, :KVL])
    out = (out + out_ref[...] * carried) / total
    level = peak + jnp.log(total)
    packed_ref[:, :KVL] = out.astype(BF16)
    lead = level.astype(BF16).astype(F32)
    rest = (level - lead).astype(BF16).astype(F32)
    last = level - lead - rest
    lane = lax.broadcasted_iota(jnp.int32, (rows, 128), 1)
    tail = jnp.where(lane == 0, lead, jnp.where(lane == 1, rest, jnp.where(lane == 2, last, 0.0)))
    packed_ref[:, KVL:] = tail.astype(BF16)


def combine_kernel(*refs):
    parts, out = refs[:-1], refs[-1]
    levels = [jnp.sum(p[:, KVL:].astype(F32), axis=1, keepdims=True) for p in parts]
    top = functools.reduce(jnp.maximum, levels)
    shares = [jnp.exp(level - top) for level in levels]
    numer = sum(s * p[:, :KVL].astype(F32) for s, p in zip(shares, parts))
    out[...] = (numer / sum(shares)).astype(BF16)


def return_kernel(ids, kv_keep, kv_got, q_keep, q_got, low, high, send):
    stage = ids[3]
    rows = kv_keep.shape[0] // 2
    quarter = rows // 2
    start = pl.multiple_of(stage * quarter, 32)
    for i in range(2):
        at = pl.ds(i * rows + start, quarter)
        wide = kv_keep[at, :] + kv_got[at, :].astype(F32)
        near = slice(i * quarter, (i + 1) * quarter)
        short = q_keep[near, :] + q_got[near, :].astype(F32)
        if i == 0:
            low[...] = short
            high[...] = wide
        else:
            send[:, : short.shape[1]] = short.astype(BF16)
            send[:, short.shape[1] :] = wide.astype(BF16)


def query_kernel(ids, low, high, got, gain, *refs):
    sends, scratch = refs[:-1], refs[-1]
    odd = ids[2] % 2 == 1
    cut = low.shape[1]
    got_low, got_high = got[:, :cut].astype(F32), got[:, cut:].astype(F32)
    first = jnp.where(odd, got_low, low[...])
    second = jnp.where(odd, got_high, high[...])
    third = jnp.where(odd, low[...], got_low)
    rows = jnp.concatenate([first, second, third], axis=1)
    inverse = lax.rsqrt(jnp.sum(rows * rows, axis=1, keepdims=True) / QL + norm_eps)
    rows = (rows * inverse * gain[...]).astype(BF16)
    scratch[...] = rows
    width = QL // len(sends)
    lane = 2 * ids[3] + ids[1]
    for k, send in enumerate(sends):
        target = jnp.bitwise_xor(lane, k)
        send[...] = scratch[:, pl.ds(pl.multiple_of(target * width, 128), width)]


def place_kernel(ids, *refs):
    gots, out = refs[:-1], refs[-1]
    rows = gots[0].shape[0]
    lane = 2 * ids[3] + ids[1]
    for k, got in enumerate(gots):
        source = jnp.bitwise_xor(lane, k)
        order = 2 * (source % 2) + source // 2
        out[pl.ds(pl.multiple_of(order * rows, 32), rows), :] = got[...]


def call(kernel, shapes, specs, args, scratch=()):
    return pl.pallas_call(
        kernel,
        scratch_shapes=scratch,
        out_shape=shapes,
        in_specs=specs,
        out_specs=[VMEM] * len(shapes) if isinstance(shapes, list) else VMEM,
        cost_estimate=pl.CostEstimate(flops=20_000_000, bytes_accessed=2_000_000, transcendentals=0),
        compiler_params=pltpu.CompilerParams(vmem_limit_bytes=VMEM_GRANT),
    )(*args)


def shaped(*dims, kind=F32):
    return jax.ShapeDtypeStruct(dims, kind)


def body_pairs(*args):
    return pairs_step(*args)


def pairs_step(
    hidden_x,
    proj_weight,
    q_gain,
    kv_gain,
    old_cache,
    page_plan,
    block_table,
    split_lens,
    dec_query,
    new_key,
):
    n = lax.axis_size("dec")
    group, index = lax.axis_index("grp"), lax.axis_index("dec")
    stage, core = lax.axis_index("stg"), lax.axis_index("tp")
    ids = jnp.stack([group, core, index, stage]).astype(jnp.int32)
    tokens, feats = hidden_x.shape
    cols = proj_weight.shape[1]
    cut = QL - 2 * cols
    half = feats // 2
    pages = page_plan.shape[0]
    requests, heads, _ = dec_query.shape
    queries = requests * heads

    weight = lax.dynamic_slice_in_dim(proj_weight.T, group * half, half, axis=1)
    split = cols // 2 // 128 * 128
    pieces = {"head": weight[:split], "tail": weight[split:]}
    a_pairs = [(0, 2), (3, 1), (1, 0), (2, 3)]
    b_pairs = [(0, 0), (1, 2), (2, 1), (3, 3)]
    a_z, a_y, b_z, b_y = {}, {}, {}, {}
    for name in ("tail", "head"):
        a_z[name] = lax.ppermute(pieces[name], "dec", a_pairs)
    x_far = lax.ppermute(hidden_x, "dec", [(0, 1), (1, 0), (2, 3), (3, 2)])
    packed = jnp.concatenate(
        [page_plan.reshape(-1), block_table.reshape(-1), split_lens.reshape(-1)]
    ).reshape(1, -1)
    tables = [packed]
    for s in range(1, n):
        tables.append(lax.ppermute(packed, "dec", [((i + s) % n, i) for i in range(n)]))
    tables = jnp.pad(
        jnp.concatenate(tables, axis=0), ((0, 8 - n), (0, -packed.shape[1] % 128))
    )
    held, held_tail, held_head = pieces, *lax.optimization_barrier(
        (pieces["tail"], pieces["head"], a_z["head"])
    )[:2]
    held = {"tail": held_tail, "head": held_head}
    for name in ("tail", "head"):
        a_y[name] = swap(a_z[name], "grp")
        b_z[name] = lax.ppermute(held[name], "dec", b_pairs)
    for name in ("tail", "head"):
        b_y[name] = swap(b_z[name], "grp")
    a_weights = (a_z["head"], a_z["tail"], a_y["head"], a_y["tail"])
    b_weights = (b_z["head"], b_z["tail"], b_y["head"], b_y["tail"])

    query = dec_query.reshape(queries, KVW)
    padded_key = jnp.pad(new_key, ((0, 3 * requests), (0, 0)))
    peak, total, out, bias = call(
        functools.partial(old_kernel, n, pages),
        [shaped(queries, 1), shaped(queries, 1), shaped(queries, KVL), shaped(8, 2 * tokens)],
        [SMEM, VMEM, VMEM, VMEM, VMEM],
        (ids, tables, query, old_cache.reshape(-1, KVW), padded_key),
    )

    rows = tokens // 2
    partner = index + 1 - 2 * (index % 2)
    place = core * rows + jnp.arange(rows, dtype=jnp.int32)
    positions = jnp.concatenate([index * tokens + place, partner * tokens + place]).astype(F32)
    pair = jnp.arange(ROPE, dtype=jnp.int32) // 2
    frequency = jnp.power(F32(10000.0), -(2 * pair).astype(F32) / ROPE)
    angles = positions[:, None] * frequency[None, :]
    source = jnp.arange(ROPE, dtype=jnp.int32)[:, None]
    target = jnp.arange(ROPE, dtype=jnp.int32)[None, :]
    turn = jnp.where(
        source == target + 1,
        jnp.where(target % 2 == 0, -1.0, 0.0),
        jnp.where((source + 1 == target) & (target % 2 == 1), 1.0, 0.0),
    )
    early_ids, cos, sin, turn, kv_scale, q_scale = lax.optimization_barrier(
        (ids, jnp.cos(angles), jnp.sin(angles), turn, kv_gain.reshape(1, -1), q_gain.reshape(1, -1))
    )
    a_near = matmul(early_ids, (hidden_x,), a_weights)
    a_far = matmul(ids, (x_far,), a_weights)
    b_both = matmul(ids, (hidden_x, x_far), b_weights)
    sums = []
    for (send, keep) in (a_near, b_both[:2], a_far, b_both[2:]):
        sums += [keep, swap(send, "tp")]
    rows = tokens // 2
    quarter = rows // 2
    kv_send, kv_keep, q_send, q_keep = call(
        middle_kernel,
        [
            shaped(2 * rows, KVW, kind=BF16),
            shaped(2 * rows, KVW),
            shaped(rows, cut, kind=BF16),
            shaped(rows, cut),
        ],
        [SMEM] + [VMEM] * 8,
        (ids, *sums),
    )
    kv_got = swap(kv_send, "stg")
    q_got = swap(q_send, "stg")

    key_rows = call(
        keys_kernel,
        shaped(2 * rows, KVW, kind=BF16),
        [VMEM] * 6,
        (kv_keep, kv_got, cos, sin, turn, kv_scale),
    )
    far_keys = swap(key_rows, "tp")
    part_out = call(
        attend_kernel,
        shaped(queries, KVL + 128, kind=BF16),
        [VMEM] * 7,
        (query, key_rows, far_keys, bias, peak, total, out),
    )
    parts = [part_out]
    for s in range(1, n):
        parts.append(
            lax.ppermute(part_out, "dec", [((i + s) % n, i) for i in range(n)])
        )
    attn = call(combine_kernel, shaped(queries, KVL, kind=BF16), [VMEM] * n, tuple(parts))

    low, high, back = call(
        return_kernel,
        [shaped(quarter, cut), shaped(quarter, KVW), shaped(quarter, cut + KVW, kind=BF16)],
        [SMEM] + [VMEM] * 4,
        (ids, kv_keep, kv_got, q_keep, q_got),
    )
    back = lax.ppermute(back, "dec", [(0, 1), (1, 0), (2, 3), (3, 2)])
    lanes = 4
    width = QL // lanes
    tile = shaped(quarter, width, kind=BF16)
    blocks = call(
        query_kernel,
        [tile] * lanes,
        [SMEM] + [VMEM] * 4,
        (ids, low, high, back, q_scale),
        scratch=[pltpu.VMEM((quarter, QL), BF16)],
    )
    gots = [blocks[0]]
    for k in range(1, lanes):
        gots.append(
            lax.ppermute(blocks[k], ("stg", "tp"), [(i, i ^ k) for i in range(lanes)])
        )
    q_latent = call(
        place_kernel, shaped(tokens, width, kind=BF16), [SMEM] + [VMEM] * lanes, (ids, *gots)
    )
    return (q_latent, attn.reshape(requests, heads, KVL))


def solution(mesh):
    sizes = dict(mesh.shape)
    pairs = sizes["dec"] == 4 and sizes["grp"] == sizes["stg"] == sizes["tp"] == 2
    return jax.shard_map(
        body_pairs if pairs else body_general,
        mesh=mesh,
        in_specs=(
            P(("grp", "dec"), ("stg", "tp")),
            P(("stg", "tp"), "dec"),
            P(),
            P(),
            P(("grp", "dec"), None, None),
            P(("grp", "dec"), None),
            P(("grp", "dec"), None, None),
            P("grp", "dec"),
            P("grp", ("stg", "tp"), None),
            P("grp", None),
        ),
        out_specs=(P(("grp", "dec"), ("stg", "tp")), P("grp", ("stg", "tp"), None)),
        check_vma=False,
    )
```

profile of v0, /device:TPU:0, one launch (start us, length us, event | category | flops | bytes accessed | tf_op | source)
XLA Modules:
  0.0 162.5 jit_solution(10861467352135609737)
XLA Ops:
  0.7 1.5 copy-done
  2.2 0.8 slice.8
  3.0 4.1 %collective-permute-start = (bf16[256,896]{1,0:T(8,128)(2,1)}, bf16[256,896]{1,0:T(8,128)(2,1)S(1)}, u32[]{:S(2)}, u32[]{:S(2)}) collective-permute-start(bf16[256,896]{1,0:T(8,128)(2,1)} %slice.8), channel_id=1, source_target_pairs={{0,8},{12,4},{4,0},{8,12},{1,9},{13,5},{5,1},{9,13},{2,10},{14,6},... | collective-permute-start | bytes 1376264 | tf_op jit(solution)/shard_map/ppermute | solution.py:501
  7.1 0.8 slice.9
  7.9 1.9 %collective-permute-start.1 = (bf16[272,896]{1,0:T(8,128)(2,1)}, bf16[272,896]{1,0:T(8,128)(2,1)S(1)}, u32[]{:S(2)}, u32[]{:S(2)}) collective-permute-start(bf16[272,896]{1,0:T(8,128)(2,1)} %slice.9), channel_id=1, source_target_pairs={{0,8},{12,4},{4,0},{8,12},{1,9},{13,5},{5,1},{9,13},{2,10},{14,6},... | collective-permute-start | bytes 1462280 | tf_op jit(solution)/shard_map/ppermute | solution.py:501
  9.9 8.5 %collective-permute-done.refs_1_ = bf16[256,896]{1,0:T(8,128)(2,1)S(1)} collective-permute-done((bf16[256,896]{1,0:T(8,128)(2,1)}, bf16[256,896]{1,0:T(8,128)(2,1)S(1)}, u32[]{:S(2)}, u32[]{:S(2)}) %collective-permute-start) | collective-permute-done | bytes 458784 | tf_op jit(solution)/shard_map/ppermute | solution.py:501
  18.3 5.2 %collective-permute-start.7 = (bf16[272,896]{1,0:T(8,128)(2,1)}, bf16[272,896]{1,0:T(8,128)(2,1)}, u32[]{:S(2)}, u32[]{:S(2)}) collective-permute-start(bf16[272,896]{1,0:T(8,128)(2,1)} %slice.9), channel_id=1, source_target_pairs={{0,0},{4,8},{8,4},{12,12},{1,1},{5,9},{9,5},{13,13},{2,2},{6,10},{... | collective-permute-start | bytes 1462280 | tf_op jit(solution)/shard_map/ppermute | solution.py:518
  23.6 5.0 %collective-permute-start.6 = (bf16[256,896]{1,0:T(8,128)(2,1)}, bf16[256,896]{1,0:T(8,128)(2,1)}, u32[]{:S(2)}, u32[]{:S(2)}) collective-permute-start(bf16[256,896]{1,0:T(8,128)(2,1)} %slice.8), channel_id=1, source_target_pairs={{0,0},{4,8},{8,4},{12,12},{1,1},{5,9},{9,5},{13,13},{2,2},{6,10},{... | collective-permute-start | bytes 1376264 | tf_op jit(solution)/shard_map/ppermute | solution.py:518
  28.7 28.5 %collective-permute-done.1.refs_2_ = bf16[272,896]{1,0:T(8,128)(2,1)S(1)} collective-permute-done((bf16[272,896]{1,0:T(8,128)(2,1)}, bf16[272,896]{1,0:T(8,128)(2,1)S(1)}, u32[]{:S(2)}, u32[]{:S(2)}) %collective-permute-start.1) | collective-permute-done | bytes 487456 | tf_op jit(solution)/shard_map/ppermute | solution.py:501
  57.1 1.5 collective-permute-start.3
  59.3 1.5 collective-permute-start.9
  61.5 0.8 multiply_sine_fusion
  62.2 18.9 %collective-permute-done.2.refs_3_ = bf16[256,896]{1,0:T(8,128)(2,1)} collective-permute-done((bf16[256,896]{1,0:T(8,128)(2,1)S(1)}, bf16[256,896]{1,0:T(8,128)(2,1)}, u32[]{:S(2)}, u32[]{:S(2)}) %collective-permute-start.2) | collective-permute-done | bytes 458784 | tf_op jit(solution)/shard_map/ppermute | solution.py:197
  81.1 2.8 %project.3 = (f32[192,528]{1,0:T(8,128)S(1)}, f32[192,528]{1,0:T(8,128)S(1)}) custom-call(s32[4]{0:T(128)S(1)} %pad_add_fusion.1.ids, bf16[384,1792]{1,0:T(8,128)(2,1)} %refs_0_.3, bf16[256,896]{1,0:T(8,128)(2,1)S(1)} %collective-permute-done.refs_1_, bf16[272,896]{1,0:T(8,128)(2,1)S(1)} %collective-permute-done.1.refs_2_, ...), custom_call_target="tpu_custom_call" | custom-call | flops 726663168 | bytes 1622016 | tf_op jit(solution)/shard_map/project/pallas_call | solution.py:230
  84.0 2.8 %project.5 = (f32[192,528]{1,0:T(8,128)S(1)}, f32[192,528]{1,0:T(8,128)S(1)}) custom-call(s32[4]{0:T(128)S(1)} %pad_add_fusion.1.ids, bf16[384,1792]{1,0:T(8,128)(2,1)} %collective-permute-done.5.refs_1_.refs_0_, bf16[256,896]{1,0:T(8,128)(2,1)S(1)} %collective-permute-done.refs_1_, bf16[272,896]{1,0:T(8,128)(2,1)S(1)} %collective-permute-done.1.refs_2_, ...), custom_call_target="tpu_custom_call" | custom-call | flops 726663168 | bytes 1622016 | tf_op jit(solution)/shard_map/project/pallas_call | solution.py:230
  87.4 11.9 %collective-permute-done.8.refs_4_ = bf16[256,896]{1,0:T(8,128)(2,1)S(1)} collective-permute-done((bf16[256,896]{1,0:T(8,128)(2,1)}, bf16[256,896]{1,0:T(8,128)(2,1)S(1)}, u32[]{:S(2)}, u32[]{:S(2)}) %collective-permute-start.8) | collective-permute-done | bytes 458784 | tf_op jit(solution)/shard_map/ppermute | solution.py:197
  99.3 4.8 %project.4 = (f32[192,528]{1,0:T(8,128)S(1)}, f32[192,528]{1,0:T(8,128)S(1)}, f32[192,528]{1,0:T(8,128)S(1)}, f32[192,528]{1,0:T(8,128)S(1)}) custom-call(s32[4]{0:T(128)S(1)} %pad_add_fusion.1.ids, bf16[384,1792]{1,0:T(8,128)(2,1)} %refs_0_.3, bf16[384,1792]{1,0:T(8,128)(2,1)} %collective-permute-done.5.refs_1_.refs_0_, ...), custom_call_target="tpu_custom_call" | custom-call | flops 1453326336 | bytes 3244032 | tf_op jit(solution)/shard_map/project/pallas_call | solution.py:230
  104.6 1.3 collective-permute-done.10.refs_3_
  106.0 0.7 collective-permute-done.12.refs_7_
  106.7 1.7 %shard_map.113 = (bf16[384,576]{1,0:T(8,128)(2,1)S(1)}, f32[384,576]{1,0:T(8,128)S(1)}, bf16[192,480]{1,0:T(8,128)(2,1)}, f32[192,480]{1,0:T(8,128)S(1)}) custom-call(s32[4]{0:T(128)S(1)} %pad_add_fusion.1.ids, f32[192,528]{1,0:T(8,128)S(1)} %get-tuple-element.34.refs_0_, f32[192,528]{1,0:T(8,128)S(1)} %collective-permute-done.4.refs_1_, ...), custom_call_target="tpu_custom_call" | custom-call | flops 20000000 | bytes 2000000 | tf_op jit(solution)/shard_map/pallas_call | solution.py:451
  108.3 1.5 collective-permute-start.13
  109.8 11.8 %collective-permute-done.13.kv_got.got = bf16[384,576]{1,0:T(8,128)(2,1)S(1)} collective-permute-done((bf16[384,576]{1,0:T(8,128)(2,1)S(1)}, bf16[384,576]{1,0:T(8,128)(2,1)S(1)}, u32[]{:S(2)}, u32[]{:S(2)}) %collective-permute-start.13) | collective-permute-done | bytes 442400 | tf_op jit(solution)/shard_map/ppermute | solution.py:197
  121.6 1.1 shard_map.117.k0_ref
  122.7 1.6 collective-permute-start.14
  124.3 0.8 copy.13
  125.7 4.6 %collective-permute-done.14.q_got = bf16[192,480]{1,0:T(8,128)(2,1)} collective-permute-done((bf16[192,480]{1,0:T(8,128)(2,1)}, bf16[192,480]{1,0:T(8,128)(2,1)}, u32[]{:S(2)}, u32[]{:S(2)}) %collective-permute-start.14) | collective-permute-done | bytes 184352 | tf_op jit(solution)/shard_map/ppermute | solution.py:197
  130.4 1.0 copy-done.4
  131.4 1.1 shard_map.114
  132.4 2.3 %collective-permute-start.15 = (bf16[96,1056]{1,0:T(8,128)(2,1)S(1)}, bf16[96,1056]{1,0:T(8,128)(2,1)S(1)}, u32[]{:S(2)}, u32[]{:S(2)}) collective-permute-start(bf16[96,1056]{1,0:T(8,128)(2,1)S(1)} %get-tuple-element.50), channel_id=1, source_target_pairs={{0,4},{4,0},{8,12},{12,8},{1,5},{5,1},{9,13},{13,9},{2,6},{6,2},{1... | collective-permute-start | bytes 608264 | tf_op jit(solution)/shard_map/ppermute | solution.py:598
  134.8 0.7 add_bitcast_fusion
  135.5 2.5 %collective-permute-start.20 = (s32[1,60]{1,0:T(1,128)S(1)}, s32[1,60]{1,0:T(1,128)S(1)}, u32[]{:S(2)}, u32[]{:S(2)}) collective-permute-start(s32[1,60]{1,0:T(1,128)S(1)} %add_bitcast_fusion), channel_id=1, source_target_pairs={{4,0},{8,4},{12,8},{0,12},{5,1},{9,5},{13,9},{1,13},{6,2},{10,6},{... | collective-permute-start | bytes 728 | tf_op jit(solution)/shard_map/ppermute | solution.py:508
  138.0 1.2 collective-permute-start.22
  139.2 0.7 pad.9.own_ref
  140.1 2.4 %collective-permute-done.21 = s32[1,60]{1,0:T(1,128)S(1)} collective-permute-done((s32[1,60]{1,0:T(1,128)S(1)}, s32[1,60]{1,0:T(1,128)S(1)}, u32[]{:S(2)}, u32[]{:S(2)}) %collective-permute-start.21) | collective-permute-done | bytes 272 | tf_op jit(solution)/shard_map/ppermute | solution.py:508
  142.5 0.9 collective-permute-done.22
  143.4 1.7 %shard_map.118 = (f32[128,1]{1,0:T(8,128)S(1)}, f32[128,1]{1,0:T(8,128)S(1)}, f32[128,512]{1,0:T(8,128)S(1)}, f32[8,768]{1,0:T(8,128)S(1)}) custom-call(s32[4]{0:T(128)S(1)} %pad_add_fusion.1.ids, s32[8,128]{1,0:T(8,128)S(1)} %pad.8.tab_ref, bf16[128,576]{1,0:T(8,128)(2,1)S(1)} %bitcast.14, bf16[1024,576]{1,0:T(8,128)(2,1)S(1)} %bitcast.13, ...), custom_call_target="tpu_custom_call" | custom-call | flops 20000000 | bytes 2000000 | tf_op jit(solution)/shard_map/pallas_call | solution.py:451
  145.2 2.1 %shard_map.119.refs_0_ = bf16[128,640]{1,0:T(8,128)(2,1)S(1)} custom-call(bf16[128,576]{1,0:T(8,128)(2,1)S(1)} %bitcast.15, bf16[384,576]{1,0:T(8,128)(2,1)} %shard_map.117.k0_ref, bf16[384,576]{1,0:T(8,128)(2,1)} %collective-permute-done.19.k1_ref, f32[8,768]{1,0:T(8,128)S(1)} %get-tuple-element.60.bias_ref, f32[128,1]{1,0:T(8,128)S(1)} %get-tuple-element.61.peak_ref, ...), custom_call_target="tpu_custom_call" | custom-call | flops 20000000 | bytes 2000000 | tf_op jit(solution)/shard_map/pallas_call | solution.py:451
  147.3 0.6 collective-permute-start.23
  147.9 0.6 collective-permute-start.24
  148.5 1.9 %collective-permute-start.25 = (bf16[128,640]{1,0:T(8,128)(2,1)S(1)}, bf16[128,640]{1,0:T(8,128)(2,1)S(1)}, u32[]{:S(2)}, u32[]{:S(2)}) collective-permute-start(bf16[128,640]{1,0:T(8,128)(2,1)S(1)} %shard_map.119.refs_0_), channel_id=1, source_target_pairs={{12,0},{0,4},{4,8},{8,12},{13,1},{1,5},{5,9},{9,13},{14,2},{2,6},{... | collective-permute-start | bytes 491528 | tf_op jit(solution)/shard_map/ppermute | solution.py:588
  150.5 0.9 shard_map.115
  151.4 1.6 collective-permute-start.17
  153.0 0.9 collective-permute-start.18
  153.9 2.3 %collective-permute-done.17.refs_2_ = bf16[96,384]{1,0:T(8,128)(2,1)S(1)} collective-permute-done((bf16[96,384]{1,0:T(8,128)(2,1)S(1)}, bf16[96,384]{1,0:T(8,128)(2,1)S(1)}, u32[]{:S(2)}, u32[]{:S(2)}) %collective-permute-start.17) | collective-permute-done | bytes 73760 | tf_op jit(solution)/shard_map/ppermute | solution.py:612
  156.2 1.2 collective-permute-done.18.refs_3_
  157.5 1.3 shard_map.116
  158.8 2.8 %collective-permute-done.24.refs_2_ = bf16[128,640]{1,0:T(8,128)(2,1)S(1)} collective-permute-done((bf16[128,640]{1,0:T(8,128)(2,1)S(1)}, bf16[128,640]{1,0:T(8,128)(2,1)S(1)}, u32[]{:S(2)}, u32[]{:S(2)}) %collective-permute-start.24) | collective-permute-done | bytes 163872 | tf_op jit(solution)/shard_map/ppermute | solution.py:588
  161.6 0.9 shard_map.120
  (53 shorter events, 3.6 us)
Async XLA Ops:
  0.6 1.5 copy-start
  2.2 58.6 %copy-start.6 = (f32[1536]{0:T(1024)S(1)}, f32[1536]{0:T(1024)}, u32[]{:S(2)}) copy-start(f32[1536]{0:T(1024)} %param.12) | copy-start | bytes 18436
  3.0 15.3 %collective-permute-start = (bf16[256,896]{1,0:T(8,128)(2,1)}, bf16[256,896]{1,0:T(8,128)(2,1)S(1)}, u32[]{:S(2)}, u32[]{:S(2)}) collective-permute-start(bf16[256,896]{1,0:T(8,128)(2,1)} %slice.8), channel_id=1, source_target_pairs={{0,8},{12,4},{4,0},{8,12},{1,9},{13,5},{5,1},{9,13},{2,10},{14,6},... | collective-permute-start | bytes 1376264 | tf_op jit(solution)/shard_map/ppermute | solution.py:501
  7.1 76.9 %collective-permute-start.5 = (bf16[384,1792]{1,0:T(8,128)(2,1)}, bf16[384,1792]{1,0:T(8,128)(2,1)}, u32[]{:S(2)}, u32[]{:S(2)}) collective-permute-start(bf16[384,1792]{1,0:T(8,128)(2,1)} %refs_0_.3), channel_id=1, source_target_pairs={{0,4},{4,0},{8,12},{12,8},{1,5},{5,1},{9,13},{13,9},{2,6},{6,2},{1... | collective-permute-start | bytes 4128776 | tf_op jit(solution)/shard_map/ppermute | solution.py:502
  7.9 49.2 %collective-permute-start.1 = (bf16[272,896]{1,0:T(8,128)(2,1)}, bf16[272,896]{1,0:T(8,128)(2,1)S(1)}, u32[]{:S(2)}, u32[]{:S(2)}) collective-permute-start(bf16[272,896]{1,0:T(8,128)(2,1)} %slice.9), channel_id=1, source_target_pairs={{0,8},{12,4},{4,0},{8,12},{1,9},{13,5},{5,1},{9,13},{2,10},{14,6},... | collective-permute-start | bytes 1462280 | tf_op jit(solution)/shard_map/ppermute | solution.py:501
  18.3 40.9 %collective-permute-start.7 = (bf16[272,896]{1,0:T(8,128)(2,1)}, bf16[272,896]{1,0:T(8,128)(2,1)}, u32[]{:S(2)}, u32[]{:S(2)}) collective-permute-start(bf16[272,896]{1,0:T(8,128)(2,1)} %slice.9), channel_id=1, source_target_pairs={{0,0},{4,8},{8,4},{12,12},{1,1},{5,9},{9,5},{13,13},{2,2},{6,10},{... | collective-permute-start | bytes 1462280 | tf_op jit(solution)/shard_map/ppermute | solution.py:518
  23.6 37.2 %collective-permute-start.6 = (bf16[256,896]{1,0:T(8,128)(2,1)}, bf16[256,896]{1,0:T(8,128)(2,1)}, u32[]{:S(2)}, u32[]{:S(2)}) collective-permute-start(bf16[256,896]{1,0:T(8,128)(2,1)} %slice.8), channel_id=1, source_target_pairs={{0,0},{4,8},{8,4},{12,12},{1,1},{5,9},{9,5},{13,13},{2,2},{6,10},{... | collective-permute-start | bytes 1376264 | tf_op jit(solution)/shard_map/ppermute | solution.py:518
  57.1 23.9 %collective-permute-start.3 = (bf16[272,896]{1,0:T(8,128)(2,1)S(1)}, bf16[272,896]{1,0:T(8,128)(2,1)S(1)}, u32[]{:S(2)}, u32[]{:S(2)}) collective-permute-start(bf16[272,896]{1,0:T(8,128)(2,1)S(1)} %collective-permute-done.1.refs_2_), channel_id=1, source_target_pairs={{0,16},{16,0},{1,17},{17,1},{2,18},{18,2},{3,19},{19,3},{4,20},{20... | collective-permute-start | bytes 1462280 | tf_op jit(solution)/shard_map/ppermute | solution.py:197
  58.7 22.3 %collective-permute-start.2 = (bf16[256,896]{1,0:T(8,128)(2,1)S(1)}, bf16[256,896]{1,0:T(8,128)(2,1)}, u32[]{:S(2)}, u32[]{:S(2)}) collective-permute-start(bf16[256,896]{1,0:T(8,128)(2,1)S(1)} %collective-permute-done.refs_1_), channel_id=1, source_target_pairs={{0,16},{16,0},{1,17},{17,1},{2,18},{18,2},{3,19},{19,3},{4,20},{20... | collective-permute-start | bytes 1376264 | tf_op jit(solution)/shard_map/ppermute | solution.py:197
  59.3 40.0 %collective-permute-start.9 = (bf16[272,896]{1,0:T(8,128)(2,1)}, bf16[272,896]{1,0:T(8,128)(2,1)}, u32[]{:S(2)}, u32[]{:S(2)}) collective-permute-start(bf16[272,896]{1,0:T(8,128)(2,1)} %collective-permute-done.7.refs_3_), channel_id=1, source_target_pairs={{0,16},{16,0},{1,17},{17,1},{2,18},{18,2},{3,19},{19,3},{4,20},{20... | collective-permute-start | bytes 1462280 | tf_op jit(solution)/shard_map/ppermute | solution.py:197
  60.8 38.5 %collective-permute-start.8 = (bf16[256,896]{1,0:T(8,128)(2,1)}, bf16[256,896]{1,0:T(8,128)(2,1)S(1)}, u32[]{:S(2)}, u32[]{:S(2)}) collective-permute-start(bf16[256,896]{1,0:T(8,128)(2,1)} %collective-permute-done.6.refs_2_), channel_id=1, source_target_pairs={{0,16},{16,0},{1,17},{17,1},{2,18},{18,2},{3,19},{19,3},{4,20},{20... | collective-permute-start | bytes 1376264 | tf_op jit(solution)/shard_map/ppermute | solution.py:197
  83.9 20.7 %collective-permute-start.4 = (f32[192,528]{1,0:T(8,128)S(1)}, f32[192,528]{1,0:T(8,128)S(1)}, u32[]{:S(2)}, u32[]{:S(2)}) collective-permute-start(f32[192,528]{1,0:T(8,128)S(1)} %get-tuple-element.35), channel_id=1, source_target_pairs={{0,1},{1,0},{2,3},{3,2},{4,5},{5,4},{6,7},{7,6},{8,9},{9,8},{10,11... | collective-permute-start | bytes 1216520 | tf_op jit(solution)/shard_map/ppermute | solution.py:197
  86.9 17.8 %collective-permute-start.11 = (f32[192,528]{1,0:T(8,128)S(1)}, f32[192,528]{1,0:T(8,128)S(1)}, u32[]{:S(2)}, u32[]{:S(2)}) collective-permute-start(f32[192,528]{1,0:T(8,128)S(1)} %get-tuple-element.41), channel_id=1, source_target_pairs={{0,1},{1,0},{2,3},{3,2},{4,5},{5,4},{6,7},{7,6},{8,9},{9,8},{10,11... | collective-permute-start | bytes 1216520 | tf_op jit(solution)/shard_map/ppermute | solution.py:197
  104.0 1.9 %collective-permute-start.10 = (f32[192,528]{1,0:T(8,128)S(1)}, f32[192,528]{1,0:T(8,128)S(1)}, u32[]{:S(2)}, u32[]{:S(2)}) collective-permute-start(f32[192,528]{1,0:T(8,128)S(1)} %get-tuple-element.39), channel_id=1, source_target_pairs={{0,1},{1,0},{2,3},{3,2},{4,5},{5,4},{6,7},{7,6},{8,9},{9,8},{10,11... | collective-permute-start | bytes 1216520 | tf_op jit(solution)/shard_map/ppermute | solution.py:197
  104.1 2.6 %collective-permute-start.12 = (f32[192,528]{1,0:T(8,128)S(1)}, f32[192,528]{1,0:T(8,128)S(1)}, u32[]{:S(2)}, u32[]{:S(2)}) collective-permute-start(f32[192,528]{1,0:T(8,128)S(1)} %get-tuple-element.43), channel_id=1, source_target_pairs={{0,1},{1,0},{2,3},{3,2},{4,5},{5,4},{6,7},{7,6},{8,9},{9,8},{10,11... | collective-permute-start | bytes 1216520 | tf_op jit(solution)/shard_map/ppermute | solution.py:197
  106.7 14.9 %copy-start.5 = (f32[512]{0:T(512)S(1)}, f32[512]{0:T(512)}, u32[]{:S(2)}) copy-start(f32[512]{0:T(512)} %param.13) | copy-start | bytes 6148
  108.3 14.4 %copy-start.3 = (f32[192,480]{1,0:T(8,128)}, f32[192,480]{1,0:T(8,128)S(1)}, u32[]{:S(2)}) copy-start(f32[192,480]{1,0:T(8,128)S(1)} %get-tuple-element.46.q_keep) | copy-start | bytes 1105924
  108.3 17.3 %copy-start.7 = (s32[1,4,8]{2,1,0:T(4,128)S(1)}, s32[1,4,8]{2,1,0:T(4,128)}, u32[]{:S(2)}) copy-start(s32[1,4,8]{2,1,0:T(4,128)} %param.16) | copy-start | bytes 388
  108.3 13.3 %collective-permute-start.13 = (bf16[384,576]{1,0:T(8,128)(2,1)S(1)}, bf16[384,576]{1,0:T(8,128)(2,1)S(1)}, u32[]{:S(2)}, u32[]{:S(2)}) collective-permute-start(bf16[384,576]{1,0:T(8,128)(2,1)S(1)} %get-tuple-element.45), channel_id=1, source_target_pairs={{0,2},{2,0},{1,3},{3,1},{4,6},{6,4},{5,7},{7,5},{8,10},{10,8},{9,1... | collective-permute-start | bytes 1327112 | tf_op jit(solution)/shard_map/ppermute | solution.py:197
  122.7 20.7 %copy-start.2 = (bf16[4,32,576]{2,1,0:T(8,128)(2,1)S(1)}, bf16[4,32,576]{2,1,0:T(8,128)(2,1)}, u32[]{:S(2)}) copy-start(bf16[4,32,576]{2,1,0:T(8,128)(2,1)} %param.18) | copy-start | bytes 442372
  122.7 22.4 %collective-permute-start.19 = (bf16[384,576]{1,0:T(8,128)(2,1)}, bf16[384,576]{1,0:T(8,128)(2,1)}, u32[]{:S(2)}, u32[]{:S(2)}) collective-permute-start(bf16[384,576]{1,0:T(8,128)(2,1)} %shard_map.117.k0_ref), channel_id=1, source_target_pairs={{0,1},{1,0},{2,3},{3,2},{4,5},{5,4},{6,7},{7,6},{8,9},{9,8},{10,11... | collective-permute-start | bytes 1327112 | tf_op jit(solution)/shard_map/ppermute | solution.py:197
  122.7 7.6 %collective-permute-start.14 = (bf16[192,480]{1,0:T(8,128)(2,1)}, bf16[192,480]{1,0:T(8,128)(2,1)}, u32[]{:S(2)}, u32[]{:S(2)}) collective-permute-start(bf16[192,480]{1,0:T(8,128)(2,1)} %get-tuple-element.47), channel_id=1, source_target_pairs={{0,2},{2,0},{1,3},{3,1},{4,6},{6,4},{5,7},{7,5},{8,10},{10,8},{9,1... | collective-permute-start | bytes 552968 | tf_op jit(solution)/shard_map/ppermute | solution.py:197
  125.7 17.7 %copy-start.1 = (bf16[32,32,576]{2,1,0:T(8,128)(2,1)S(1)}, bf16[32,32,576]{2,1,0:T(8,128)(2,1)}, u32[]{:S(2)}) copy-start(bf16[32,32,576]{2,1,0:T(8,128)(2,1)} %param.14) | copy-start | bytes 3538948
  130.4 1.0 copy-start.4
  131.4 3.4 %copy-start.8 = (s32[24]{0:T(128)S(1)}, s32[24]{0:T(128)}, u32[]{:S(2)}) copy-start(s32[24]{0:T(128)} %reshape.97) | copy-start | bytes 292
  132.4 18.0 %collective-permute-start.15 = (bf16[96,1056]{1,0:T(8,128)(2,1)S(1)}, bf16[96,1056]{1,0:T(8,128)(2,1)S(1)}, u32[]{:S(2)}, u32[]{:S(2)}) collective-permute-start(bf16[96,1056]{1,0:T(8,128)(2,1)S(1)} %get-tuple-element.50), channel_id=1, source_target_pairs={{0,4},{4,0},{8,12},{12,8},{1,5},{5,1},{9,13},{13,9},{2,6},{6,2},{1... | collective-permute-start | bytes 608264 | tf_op jit(solution)/shard_map/ppermute | solution.py:598
  135.5 4.5 %collective-permute-start.20 = (s32[1,60]{1,0:T(1,128)S(1)}, s32[1,60]{1,0:T(1,128)S(1)}, u32[]{:S(2)}, u32[]{:S(2)}) collective-permute-start(s32[1,60]{1,0:T(1,128)S(1)} %add_bitcast_fusion), channel_id=1, source_target_pairs={{4,0},{8,4},{12,8},{0,12},{5,1},{9,5},{13,9},{1,13},{6,2},{10,6},{... | collective-permute-start | bytes 728 | tf_op jit(solution)/shard_map/ppermute | solution.py:508
  138.0 4.5 %collective-permute-start.21 = (s32[1,60]{1,0:T(1,128)S(1)}, s32[1,60]{1,0:T(1,128)S(1)}, u32[]{:S(2)}, u32[]{:S(2)}) collective-permute-start(s32[1,60]{1,0:T(1,128)S(1)} %add_bitcast_fusion), channel_id=1, source_target_pairs={{8,0},{12,4},{0,8},{4,12},{9,1},{13,5},{1,9},{5,13},{10,2},{14,6},... | collective-permute-start | bytes 728 | tf_op jit(solution)/shard_map/ppermute | solution.py:508
  138.0 5.4 %collective-permute-start.22 = (s32[1,60]{1,0:T(1,128)S(1)}, s32[1,60]{1,0:T(1,128)S(1)}, u32[]{:S(2)}, u32[]{:S(2)}) collective-permute-start(s32[1,60]{1,0:T(1,128)S(1)} %add_bitcast_fusion), channel_id=1, source_target_pairs={{12,0},{0,4},{4,8},{8,12},{13,1},{1,5},{5,9},{9,13},{14,2},{2,6},{... | collective-permute-start | bytes 728 | tf_op jit(solution)/shard_map/ppermute | solution.py:508
  147.3 11.5 %collective-permute-start.23 = (bf16[128,640]{1,0:T(8,128)(2,1)S(1)}, bf16[128,640]{1,0:T(8,128)(2,1)S(1)}, u32[]{:S(2)}, u32[]{:S(2)}) collective-permute-start(bf16[128,640]{1,0:T(8,128)(2,1)S(1)} %shard_map.119.refs_0_), channel_id=1, source_target_pairs={{4,0},{8,4},{12,8},{0,12},{5,1},{9,5},{13,9},{1,13},{6,2},{10,6},{... | collective-permute-start | bytes 491528 | tf_op jit(solution)/shard_map/ppermute | solution.py:588
  147.9 13.7 %collective-permute-start.24 = (bf16[128,640]{1,0:T(8,128)(2,1)S(1)}, bf16[128,640]{1,0:T(8,128)(2,1)S(1)}, u32[]{:S(2)}, u32[]{:S(2)}) collective-permute-start(bf16[128,640]{1,0:T(8,128)(2,1)S(1)} %shard_map.119.refs_0_), channel_id=1, source_target_pairs={{8,0},{12,4},{0,8},{4,12},{9,1},{13,5},{1,9},{5,13},{10,2},{14,6},... | collective-permute-start | bytes 491528 | tf_op jit(solution)/shard_map/ppermute | solution.py:588
  148.5 13.0 %collective-permute-start.25 = (bf16[128,640]{1,0:T(8,128)(2,1)S(1)}, bf16[128,640]{1,0:T(8,128)(2,1)S(1)}, u32[]{:S(2)}, u32[]{:S(2)}) collective-permute-start(bf16[128,640]{1,0:T(8,128)(2,1)S(1)} %shard_map.119.refs_0_), channel_id=1, source_target_pairs={{12,0},{0,4},{4,8},{8,12},{13,1},{1,5},{5,9},{9,13},{14,2},{2,6},{... | collective-permute-start | bytes 491528 | tf_op jit(solution)/shard_map/ppermute | solution.py:588
  151.4 1.6 %collective-permute-start.16 = (bf16[96,384]{1,0:T(8,128)(2,1)S(1)}, bf16[96,384]{1,0:T(8,128)(2,1)S(1)}, u32[]{:S(2)}, u32[]{:S(2)}) collective-permute-start(bf16[96,384]{1,0:T(8,128)(2,1)S(1)} %get-tuple-element.53), channel_id=1, source_target_pairs={{0,1},{1,0},{2,3},{3,2},{4,5},{5,4},{6,7},{7,6},{8,9},{9,8},{10,11... | collective-permute-start | bytes 221192 | tf_op jit(solution)/shard_map/ppermute | solution.py:612
  151.4 4.8 %collective-permute-start.17 = (bf16[96,384]{1,0:T(8,128)(2,1)S(1)}, bf16[96,384]{1,0:T(8,128)(2,1)S(1)}, u32[]{:S(2)}, u32[]{:S(2)}) collective-permute-start(bf16[96,384]{1,0:T(8,128)(2,1)S(1)} %get-tuple-element.54), channel_id=1, source_target_pairs={{0,2},{1,3},{2,0},{3,1},{4,6},{5,7},{6,4},{7,5},{8,10},{9,11},{10,... | collective-permute-start | bytes 221192 | tf_op jit(solution)/shard_map/ppermute | solution.py:612
  153.0 4.5 %collective-permute-start.18 = (bf16[96,384]{1,0:T(8,128)(2,1)S(1)}, bf16[96,384]{1,0:T(8,128)(2,1)S(1)}, u32[]{:S(2)}, u32[]{:S(2)}) collective-permute-start(bf16[96,384]{1,0:T(8,128)(2,1)S(1)} %get-tuple-element.55), channel_id=1, source_target_pairs={{0,3},{1,2},{2,1},{3,0},{4,7},{5,6},{6,5},{7,4},{8,11},{9,10},{10,... | collective-permute-start | bytes 221192 | tf_op jit(solution)/shard_map/ppermute | solution.py:612
where the time goes:
time: 163 us; the launch traced here: 162 us
  waiting for transfers between devices  95.8 us (59%)
  starting transfers between devices  36.4 us (22%)
  Pallas kernels  21.2 us (13%)
  local copies, waits for them, and re-layouts  6.4 us (4%)
  other arithmetic  1.75 us (1%)
    ppermute x11, waiting for transfers between devices, swap(): return lax.ppermute(a, axis, [(0, 1), (1, 0)])  49.2 us
    ppermute x2, waiting for transfers between devices, pairs_step(): a_z[name] = lax.ppermute(pieces[name], 'dec', a_pairs)  36.9 us
    pallas_call x8, Pallas kernels, call(): pl.pallas_call(kernel, scratch_shapes=scratch, out_shape=shapes, in_specs...  10.8 us
    pallas_call x3, Pallas kernels, matmul(): pl.pallas_call(functools.partial(matmul_kernel, blocks), in_specs=[SMEM]...  10.4 us
    ppermute x2, starting transfers between devices, pairs_step(): b_z[name] = lax.ppermute(held[name], 'dec', b_pairs)  10.3 us
    ppermute x11, starting transfers between devices, swap(): return lax.ppermute(a, axis, [(0, 1), (1, 0)])  8.35 us
    ppermute x2, starting transfers between devices, pairs_step(): a_z[name] = lax.ppermute(pieces[name], 'dec', a_pairs)  5.97 us
    ppermute x3, starting transfers between devices, pairs_step(): lax.ppermute(packed, 'dec', [((i + s) % n, i) for i in range(n)])  3.72 us
  transfers between devices with their start and end apart: 26, of which 14 were waited for; matrix products, arithmetic and copies ran while one was open for 3% of the time, Pallas kernels for 11%

commit v1 on v0

--- a/solution.py
+++ b/solution.py
@@ -205,31 +205,37 @@
     return lax.dot_general(a, b, (((1,), (0,)), ((), ())), preferred_element_type=F32, **kw)
 
 
-def matmul_kernel(blocks, ids, *refs):
-    group, core = ids[0], ids[1]
-    xs, (head_z, tail_z, head_y, tail_y), outs = refs[:blocks], refs[blocks : blocks + 4], refs[blocks + 4 :]
+def matmul_kernel(blocks, own, ids, *refs):
+    group, core, index = ids[0], ids[1], ids[2]
+    xs, refs = refs[:blocks], refs[blocks:]
+    (head_z, tail_z, head_y, tail_y), refs = refs[:4], refs[4:]
+    weight, outs = (refs[0], refs[1:]) if own else (None, refs)
     half = head_z.shape[1]
     split = head_z.shape[0]
     here = pl.ds(pl.multiple_of(group * half, 128), half)
     there = pl.ds(pl.multiple_of((1 - group) * half, 128), half)
-    for i, x_ref in enumerate(xs):
-        send, keep = outs[2 * i], outs[2 * i + 1]
-        rows = send.shape[0]
-        near, far = x_ref[:, here], x_ref[:, there]
-        for z, y, at in ((head_z, head_y, slice(0, split)), (tail_z, tail_y, slice(split, None))):
-            out = dot_t(near, z[...]) + dot_t(far, y[...])
+    outer = (index == 0) | (index == 3)
+    for z, y, at in ((head_z, head_y, slice(0, split)), (tail_z, tail_y, slice(split, None))):
+        w_here, w_there = z[...], y[...]
+        if own:
+            w_here = jnp.where(outer, weight[at, here], w_here)
+            w_there = jnp.where(outer, weight[at, there], w_there)
+        for i, x_ref in enumerate(xs):
+            send, keep = outs[2 * i], outs[2 * i + 1]
+            rows = send.shape[0]
+            out = dot_t(x_ref[:, here], w_here) + dot_t(x_ref[:, there], w_there)
             top, bottom = out[:rows], out[rows:]
             send[:, at] = jnp.where(core == 0, bottom, top)
             keep[:, at] = jnp.where(core == 0, top, bottom)
 
 
-def matmul(ids, xs, weights):
+def matmul(ids, xs, weights, own=()):
     rows, feats = xs[0].shape
     cols = weights[0].shape[0] + weights[1].shape[0]
     blocks = len(xs)
     return pl.pallas_call(
-        functools.partial(matmul_kernel, blocks),
-        in_specs=[SMEM] + [VMEM] * (blocks + 4),
+        functools.partial(matmul_kernel, blocks, bool(own)),
+        in_specs=[SMEM] + [VMEM] * (blocks + 4 + len(own)),
         out_specs=[VMEM] * (2 * blocks),
         out_shape=[jax.ShapeDtypeStruct((rows // 2, cols), F32)] * (2 * blocks),
         cost_estimate=pl.CostEstimate(
@@ -239,7 +245,15 @@
         ),
         compiler_params=pltpu.CompilerParams(vmem_limit_bytes=VMEM_GRANT),
         name="project",
-    )(ids, *xs, *weights)
+    )(ids, *xs, *weights, *own)
+
+
+def turn_kernel(out):
+    source = lax.broadcasted_iota(jnp.int32, out.shape, 0)
+    target = lax.broadcasted_iota(jnp.int32, out.shape, 1)
+    down = (source == target + 1) & (target % 2 == 0)
+    up = (source + 1 == target) & (target % 2 == 1)
+    out[...] = jnp.where(down, -1.0, jnp.where(up, 1.0, 0.0))
 
 
 def old_kernel(n, pages, ids, tab_ref, query_ref, rows_ref, own_ref, peak_ref, total_ref, out_ref, bias_ref):
@@ -491,11 +505,15 @@
     requests, heads, _ = dec_query.shape
     queries = requests * heads
 
-    weight = lax.dynamic_slice_in_dim(proj_weight.T, group * half, half, axis=1)
+    weight = proj_weight.T
     split = cols // 2 // 128 * 128
-    pieces = {"head": weight[:split], "tail": weight[split:]}
+    pieces = {
+        "tail": lax.dynamic_slice(weight, (split, group * half), (cols - split, half)),
+        "head": lax.dynamic_slice(weight, (0, group * half), (split, half)),
+    }
     a_pairs = [(0, 2), (3, 1), (1, 0), (2, 3)]
-    b_pairs = [(0, 0), (1, 2), (2, 1), (3, 3)]
+    b_pairs = [(1, 2), (2, 1)]
+    inner = [(g * n + i, (1 - g) * n + i) for g in range(2) for i in (1, 2)]
     a_z, a_y, b_z, b_y = {}, {}, {}, {}
     for name in ("tail", "head"):
         a_z[name] = lax.ppermute(pieces[name], "dec", a_pairs)
@@ -517,7 +535,7 @@
         a_y[name] = swap(a_z[name], "grp")
         b_z[name] = lax.ppermute(held[name], "dec", b_pairs)
     for name in ("tail", "head"):
-        b_y[name] = swap(b_z[name], "grp")
+        b_y[name] = lax.ppermute(b_z[name], ("grp", "dec"), inner)
     a_weights = (a_z["head"], a_z["tail"], a_y["head"], a_y["tail"])
     b_weights = (b_z["head"], b_z["tail"], b_y["head"], b_y["tail"])
 
@@ -537,19 +555,13 @@
     pair = jnp.arange(ROPE, dtype=jnp.int32) // 2
     frequency = jnp.power(F32(10000.0), -(2 * pair).astype(F32) / ROPE)
     angles = positions[:, None] * frequency[None, :]
-    source = jnp.arange(ROPE, dtype=jnp.int32)[:, None]
-    target = jnp.arange(ROPE, dtype=jnp.int32)[None, :]
-    turn = jnp.where(
-        source == target + 1,
-        jnp.where(target % 2 == 0, -1.0, 0.0),
-        jnp.where((source + 1 == target) & (target % 2 == 1), 1.0, 0.0),
-    )
+    turn = call(turn_kernel, shaped(ROPE, ROPE), [], ())
     early_ids, cos, sin, turn, kv_scale, q_scale = lax.optimization_barrier(
         (ids, jnp.cos(angles), jnp.sin(angles), turn, kv_gain.reshape(1, -1), q_gain.reshape(1, -1))
     )
     a_near = matmul(early_ids, (hidden_x,), a_weights)
     a_far = matmul(ids, (x_far,), a_weights)
-    b_both = matmul(ids, (hidden_x, x_far), b_weights)
+    b_both = matmul(ids, (hidden_x, x_far), b_weights, own=(weight,))
     sums = []
     for (send, keep) in (a_near, b_both[:2], a_far, b_both[2:]):
         sums += [keep, swap(send, "tp")]

time: 163 us -> 159 us (0.975)
  starting transfers between devices: 36.4 us -> 42.5 us
  waiting for transfers between devices: 95.8 us -> 91.2 us
  Pallas kernels: 21.2 us -> 17.8 us
    ppermute x1, starting transfers between devices: 2.33 us -> 16.4 us  [pairs_step(): back = lax.ppermute(back, 'dec', [(0, 1), (1, 0), (2, 3), (3, 2)])]
    ppermute x11 -> x9, waiting for transfers between devices: 49.2 us -> 36.3 us  [swap(): return lax.ppermute(a, axis, [(0, 1), (1, 0)])]
    ppermute x2, starting transfers between devices: 10.3 us -> 2.85 us  [pairs_step(): b_z[name] = lax.ppermute(held[name], 'dec', b_pairs)]
    ppermute x2, waiting for transfers between devices: 36.9 us -> 43.4 us  [pairs_step(): a_z[name] = lax.ppermute(pieces[name], 'dec', a_pairs)]
    dynamic_slice x1 -> x2, local copies, waits for them, and re-layouts: 0.08 us -> 3.8 us  [the longest x1 1.94 us: pairs_step(): lax.dynamic_slice(weight, (0, group * half), (split, half))]
    pallas_call x8 -> x9, Pallas kernels: 10.8 us -> 8.39 us  [call(): pl.pallas_call(kernel, scratch_shapes=scratch, out_shape=shapes, in_specs...]
    ppermute x0 -> x2, starting transfers between devices: none -> 2.15 us  [pairs_step(): b_y[name] = lax.ppermute(b_z[name], ('grp', 'dec'), inner)]
    ppermute x11 -> x9, starting transfers between devices: 8.35 us -> 6.23 us  [swap(): return lax.ppermute(a, axis, [(0, 1), (1, 0)])]
  transfers between devices with their start and end apart: 26 -> 26, of which waited for: 14 -> 13; matrix products, arithmetic and copies ran while one was open for 3% -> 2% of each run, Pallas kernels for 11% -> 9%
where the time goes in v1:
time: 159 us
  waiting for transfers between devices  91.2 us (57%)
  starting transfers between devices  42.5 us (27%)
  Pallas kernels  17.8 us (11%)
  local copies, waits for them, and re-layouts  5.43 us (3%)
    ppermute x2, waiting for transfers between devices, pairs_step(): a_z[name] = lax.ppermute(pieces[name], 'dec', a_pairs)  43.4 us
    ppermute x9, waiting for transfers between devices, swap(): return lax.ppermute(a, axis, [(0, 1), (1, 0)])  36.3 us
    ppermute x1, starting transfers between devices, pairs_step(): back = lax.ppermute(back, 'dec', [(0, 1), (1, 0), (2, 3), (3, 2)])  16.4 us
    pallas_call x3, Pallas kernels, matmul(): pl.pallas_call(functools.partial(matmul_kernel, blocks, bool(own)), in_sp...  9.43 us
    pallas_call x9, Pallas kernels, call(): pl.pallas_call(kernel, scratch_shapes=scratch, out_shape=shapes, in_specs...  8.39 us
    ppermute x9, starting transfers between devices, swap(): return lax.ppermute(a, axis, [(0, 1), (1, 0)])  6.23 us
    ppermute x2, starting transfers between devices, pairs_step(): a_z[name] = lax.ppermute(pieces[name], 'dec', a_pairs)  5.97 us
    ppermute x3, waiting for transfers between devices, pairs_step(): lax.ppermute(packed, 'dec', [((i + s) % n, i) for i in range(n)])  4.73 us
  transfers between devices with their start and end apart: 26, of which 13 were waited for; matrix products, arithmetic and copies ran while one was open for 2% of the time, Pallas kernels for 9%

profile of v1, /device:TPU:0, one launch (start us, length us, event | category | flops | bytes accessed | tf_op | source)
XLA Modules:
  0.0 158.9 jit_solution(12720087324263415673)
XLA Ops:
  0.7 1.9 %dynamic-slice_bitcast_fusion.1 = bf16[256,896]{1,0:T(8,128)(2,1)} fusion(bf16[1792,528]{0,1:T(8,128)(2,1)} %param.11, s32[]{:T(128)S(6)} %select_n.22), kind=kLoop, calls=%fused_computation.1 | loop fusion | bytes 917508 | tf_op jit(solution)/shard_map/dynamic_slice | solution.py:512
  2.6 4.1 %collective-permute-start = (bf16[256,896]{1,0:T(8,128)(2,1)}, bf16[256,896]{1,0:T(8,128)(2,1)}, u32[]{:S(2)}, u32[]{:S(2)}) collective-permute-start(bf16[256,896]{1,0:T(8,128)(2,1)} %dynamic-slice_bitcast_fusion.1), channel_id=1, source_target_pairs={{0,8},{12,4},{4,0},{8,12},{1,9},{13,5},{5,1},{9,13},{2,10},{14,6},... | collective-permute-start | bytes 1376264 | tf_op jit(solution)/shard_map/ppermute | solution.py:519
  6.7 1.9 %dynamic-slice_bitcast_fusion = bf16[272,896]{1,0:T(8,128)(2,1)} fusion(bf16[1792,528]{0,1:T(8,128)(2,1)} %param.11, s32[]{:T(128)S(6)} %select_n.22), kind=kLoop, calls=%fused_computation | loop fusion | bytes 974852 | tf_op jit(solution)/shard_map/dynamic_slice | solution.py:511
  8.5 1.9 %collective-permute-start.1 = (bf16[272,896]{1,0:T(8,128)(2,1)}, bf16[272,896]{1,0:T(8,128)(2,1)S(1)}, u32[]{:S(2)}, u32[]{:S(2)}) collective-permute-start(bf16[272,896]{1,0:T(8,128)(2,1)} %dynamic-slice_bitcast_fusion), channel_id=1, source_target_pairs={{0,8},{12,4},{4,0},{8,12},{1,9},{13,5},{5,1},{9,13},{2,10},{14,6},... | collective-permute-start | bytes 1462280 | tf_op jit(solution)/shard_map/ppermute | solution.py:519
  10.4 7.4 %collective-permute-done.refs_1_ = bf16[256,896]{1,0:T(8,128)(2,1)} collective-permute-done((bf16[256,896]{1,0:T(8,128)(2,1)}, bf16[256,896]{1,0:T(8,128)(2,1)}, u32[]{:S(2)}, u32[]{:S(2)}) %collective-permute-start) | collective-permute-done | bytes 458784 | tf_op jit(solution)/shard_map/ppermute | solution.py:519
  17.9 1.4 collective-permute-start.7
  19.3 1.4 collective-permute-start.6
  20.7 36.0 %collective-permute-done.1.refs_2_ = bf16[272,896]{1,0:T(8,128)(2,1)S(1)} collective-permute-done((bf16[272,896]{1,0:T(8,128)(2,1)}, bf16[272,896]{1,0:T(8,128)(2,1)S(1)}, u32[]{:S(2)}, u32[]{:S(2)}) %collective-permute-start.1) | collective-permute-done | bytes 487456 | tf_op jit(solution)/shard_map/ppermute | solution.py:519
  56.7 1.5 collective-permute-start.3
  58.3 0.5 collective-permute-start.2
  58.8 1.5 collective-permute-start.9
  60.3 0.7 collective-permute-start.8
  61.1 0.8 multiply_sine_fusion
  61.9 16.8 %collective-permute-done.2.refs_3_ = bf16[256,896]{1,0:T(8,128)(2,1)} collective-permute-done((bf16[256,896]{1,0:T(8,128)(2,1)}, bf16[256,896]{1,0:T(8,128)(2,1)}, u32[]{:S(2)}, u32[]{:S(2)}) %collective-permute-start.2) | collective-permute-done | bytes 458784 | tf_op jit(solution)/shard_map/ppermute | solution.py:197
  78.7 2.7 %project.3 = (f32[192,528]{1,0:T(8,128)S(1)}, f32[192,528]{1,0:T(8,128)S(1)}) custom-call(s32[4]{0:T(128)S(1)} %pad_add_fusion.1.ids, bf16[384,1792]{1,0:T(8,128)(2,1)S(1)} %copy-done, bf16[256,896]{1,0:T(8,128)(2,1)} %collective-permute-done.refs_1_, bf16[272,896]{1,0:T(8,128)(2,1)S(1)} %collective-permute-done.1.refs_2_, ...), custom_call_target="tpu_custom_call" | custom-call | flops 726663168 | bytes 1622016 | tf_op jit(solution)/shard_map/project/pallas_call | solution.py:236
  81.5 2.8 %project.5 = (f32[192,528]{1,0:T(8,128)S(1)}, f32[192,528]{1,0:T(8,128)S(1)}) custom-call(s32[4]{0:T(128)S(1)} %pad_add_fusion.1.ids, bf16[384,1792]{1,0:T(8,128)(2,1)S(1)} %collective-permute-done.5.refs_1_.refs_0_, bf16[256,896]{1,0:T(8,128)(2,1)} %collective-permute-done.refs_1_, bf16[272,896]{1,0:T(8,128)(2,1)S(1)} %collective-permute-done.1.refs_2_, ...), custom_call_target="tpu_custom_call" | custom-call | flops 726663168 | bytes 1622016 | tf_op jit(solution)/shard_map/project/pallas_call | solution.py:236
  84.3 0.4 collective-permute-start.11
  84.7 3.9 %project.4 = (f32[192,528]{1,0:T(8,128)S(1)}, f32[192,528]{1,0:T(8,128)S(1)}, f32[192,528]{1,0:T(8,128)S(1)}, f32[192,528]{1,0:T(8,128)S(1)}) custom-call(s32[4]{0:T(128)S(1)} %pad_add_fusion.1.ids, bf16[384,1792]{1,0:T(8,128)(2,1)S(1)} %copy-done, bf16[384,1792]{1,0:T(8,128)(2,1)S(1)} %collective-permute-done.5.refs_1_.refs_0_, ...), custom_call_target="tpu_custom_call" | custom-call | flops 1453326336 | bytes 3244032 | tf_op jit(solution)/shard_map/project/pallas_call | solution.py:236
  88.9 0.4 collective-permute-start.12
  89.2 1.3 collective-permute-done.10.refs_3_
  90.6 0.7 collective-permute-done.12.refs_7_
  91.3 1.7 %shard_map.114 = (bf16[384,576]{1,0:T(8,128)(2,1)S(1)}, f32[384,576]{1,0:T(8,128)S(1)}, bf16[192,480]{1,0:T(8,128)(2,1)}, f32[192,480]{1,0:T(8,128)S(1)}) custom-call(s32[4]{0:T(128)S(1)} %pad_add_fusion.1.ids, f32[192,528]{1,0:T(8,128)S(1)} %get-tuple-element.34.refs_0_, f32[192,528]{1,0:T(8,128)S(1)} %collective-permute-done.4.refs_1_, ...), custom_call_target="tpu_custom_call" | custom-call | flops 20000000 | bytes 2000000 | tf_op jit(solution)/shard_map/pallas_call | solution.py:465
  93.0 1.5 collective-permute-start.13
  94.5 11.8 %collective-permute-done.13.kv_got.got = bf16[384,576]{1,0:T(8,128)(2,1)S(1)} collective-permute-done((bf16[384,576]{1,0:T(8,128)(2,1)S(1)}, bf16[384,576]{1,0:T(8,128)(2,1)S(1)}, u32[]{:S(2)}, u32[]{:S(2)}) %collective-permute-start.13) | collective-permute-done | bytes 442400 | tf_op jit(solution)/shard_map/ppermute | solution.py:197
  106.2 0.3 shard_map.118.k0_ref
  106.7 1.6 collective-permute-start.14
  108.5 5.7 %collective-permute-done.14.q_got = bf16[192,480]{1,0:T(8,128)(2,1)S(1)} collective-permute-done((bf16[192,480]{1,0:T(8,128)(2,1)}, bf16[192,480]{1,0:T(8,128)(2,1)S(1)}, u32[]{:S(2)}, u32[]{:S(2)}) %collective-permute-start.14) | collective-permute-done | bytes 184352 | tf_op jit(solution)/shard_map/ppermute | solution.py:197
  114.2 0.7 shard_map.115
  114.8 16.4 %collective-permute-start.15 = (bf16[96,1056]{1,0:T(8,128)(2,1)S(1)}, bf16[96,1056]{1,0:T(8,128)(2,1)S(1)}, u32[]{:S(2)}, u32[]{:S(2)}) collective-permute-start(bf16[96,1056]{1,0:T(8,128)(2,1)S(1)} %get-tuple-element.50), channel_id=1, source_target_pairs={{0,4},{4,0},{8,12},{12,8},{1,5},{5,1},{9,13},{13,9},{2,6},{6,2},{1... | collective-permute-start | bytes 608264 | tf_op jit(solution)/shard_map/ppermute | solution.py:610
  131.4 2.5 %collective-permute-start.20 = (s32[1,60]{1,0:T(1,128)S(1)}, s32[1,60]{1,0:T(1,128)S(1)}, u32[]{:S(2)}, u32[]{:S(2)}) collective-permute-start(s32[1,60]{1,0:T(1,128)S(1)} %add_bitcast_fusion), channel_id=1, source_target_pairs={{4,0},{8,4},{12,8},{0,12},{5,1},{9,5},{13,9},{1,13},{6,2},{10,6},{... | collective-permute-start | bytes 728 | tf_op jit(solution)/shard_map/ppermute | solution.py:526
  133.8 0.6 collective-permute-start.22
  134.5 2.1 %collective-permute-done.20 = s32[1,60]{1,0:T(1,128)S(1)} collective-permute-done((s32[1,60]{1,0:T(1,128)S(1)}, s32[1,60]{1,0:T(1,128)S(1)}, u32[]{:S(2)}, u32[]{:S(2)}) %collective-permute-start.20) | collective-permute-done | bytes 272 | tf_op jit(solution)/shard_map/ppermute | solution.py:526
  136.5 1.8 %collective-permute-done.21 = s32[1,60]{1,0:T(1,128)S(1)} collective-permute-done((s32[1,60]{1,0:T(1,128)S(1)}, s32[1,60]{1,0:T(1,128)S(1)}, u32[]{:S(2)}, u32[]{:S(2)}) %collective-permute-start.21) | collective-permute-done | bytes 272 | tf_op jit(solution)/shard_map/ppermute | solution.py:526
  138.3 0.9 collective-permute-done.22
  139.2 1.3 copy-done.2
  140.6 1.7 %shard_map.119 = (f32[128,1]{1,0:T(8,128)S(1)}, f32[128,1]{1,0:T(8,128)S(1)}, f32[128,512]{1,0:T(8,128)S(1)}, f32[8,768]{1,0:T(8,128)S(1)}) custom-call(s32[4]{0:T(128)S(1)} %pad_add_fusion.1.ids, s32[8,128]{1,0:T(8,128)S(1)} %pad.8.tab_ref, bf16[128,576]{1,0:T(8,128)(2,1)S(1)} %bitcast.18, bf16[1024,576]{1,0:T(8,128)(2,1)S(1)} %bitcast.17, ...), custom_call_target="tpu_custom_call" | custom-call | flops 20000000 | bytes 2000000 | tf_op jit(solution)/shard_map/pallas_call | solution.py:465
  142.3 0.9 shard_map.120.refs_0_
  143.2 0.9 collective-permute-start.23
  144.0 0.7 collective-permute-start.24
  144.7 1.7 %collective-permute-start.25 = (bf16[128,640]{1,0:T(8,128)(2,1)S(1)}, bf16[128,640]{1,0:T(8,128)(2,1)S(1)}, u32[]{:S(2)}, u32[]{:S(2)}) collective-permute-start(bf16[128,640]{1,0:T(8,128)(2,1)S(1)} %shard_map.120.refs_0_), channel_id=1, source_target_pairs={{12,0},{0,4},{4,8},{8,12},{13,1},{1,5},{5,9},{9,13},{14,2},{2,6},{... | collective-permute-start | bytes 491528 | tf_op jit(solution)/shard_map/ppermute | solution.py:600
  146.4 0.9 shard_map.116
  147.3 1.6 collective-permute-start.17
  148.9 0.9 collective-permute-start.18
  149.8 2.3 %collective-permute-done.17.refs_2_ = bf16[96,384]{1,0:T(8,128)(2,1)S(1)} collective-permute-done((bf16[96,384]{1,0:T(8,128)(2,1)S(1)}, bf16[96,384]{1,0:T(8,128)(2,1)S(1)}, u32[]{:S(2)}, u32[]{:S(2)}) %collective-permute-start.17) | collective-permute-done | bytes 73760 | tf_op jit(solution)/shard_map/ppermute | solution.py:624
  152.1 1.2 collective-permute-done.18.refs_3_
  153.4 1.3 shard_map.117
  154.7 3.2 %collective-permute-done.24.refs_2_ = bf16[128,640]{1,0:T(8,128)(2,1)S(1)} collective-permute-done((bf16[128,640]{1,0:T(8,128)(2,1)S(1)}, bf16[128,640]{1,0:T(8,128)(2,1)S(1)}, u32[]{:S(2)}, u32[]{:S(2)}) %collective-permute-start.24) | collective-permute-done | bytes 163872 | tf_op jit(solution)/shard_map/ppermute | solution.py:600
  157.9 0.9 shard_map.121
  (51 shorter events, 1.0 us)
Async XLA Ops:
  0.6 78.0 %copy-start = (bf16[384,1792]{1,0:T(8,128)(2,1)S(1)}, bf16[384,1792]{1,0:T(8,128)(2,1)}, u32[]{:S(2)}) copy-start(bf16[384,1792]{1,0:T(8,128)(2,1)} %refs_0_.3) | copy-start | bytes 4128772
  0.6 59.6 %copy-start.5 = (f32[1536]{0:T(1024)S(1)}, f32[1536]{0:T(1024)}, u32[]{:S(2)}) copy-start(f32[1536]{0:T(1024)} %param.12) | copy-start | bytes 18436
  2.6 15.3 %collective-permute-start = (bf16[256,896]{1,0:T(8,128)(2,1)}, bf16[256,896]{1,0:T(8,128)(2,1)}, u32[]{:S(2)}, u32[]{:S(2)}) collective-permute-start(bf16[256,896]{1,0:T(8,128)(2,1)} %dynamic-slice_bitcast_fusion.1), channel_id=1, source_target_pairs={{0,8},{12,4},{4,0},{8,12},{1,9},{13,5},{5,1},{9,13},{2,10},{14,6},... | collective-permute-start | bytes 1376264 | tf_op jit(solution)/shard_map/ppermute | solution.py:519
  6.7 74.8 %collective-permute-start.5 = (bf16[384,1792]{1,0:T(8,128)(2,1)}, bf16[384,1792]{1,0:T(8,128)(2,1)S(1)}, u32[]{:S(2)}, u32[]{:S(2)}) collective-permute-start(bf16[384,1792]{1,0:T(8,128)(2,1)} %refs_0_.3), channel_id=1, source_target_pairs={{0,4},{4,0},{8,12},{12,8},{1,5},{5,1},{9,13},{13,9},{2,6},{6,2},{1... | collective-permute-start | bytes 4128776 | tf_op jit(solution)/shard_map/ppermute | solution.py:520
  8.5 48.2 %collective-permute-start.1 = (bf16[272,896]{1,0:T(8,128)(2,1)}, bf16[272,896]{1,0:T(8,128)(2,1)S(1)}, u32[]{:S(2)}, u32[]{:S(2)}) collective-permute-start(bf16[272,896]{1,0:T(8,128)(2,1)} %dynamic-slice_bitcast_fusion), channel_id=1, source_target_pairs={{0,8},{12,4},{4,0},{8,12},{1,9},{13,5},{5,1},{9,13},{2,10},{14,6},... | collective-permute-start | bytes 1462280 | tf_op jit(solution)/shard_map/ppermute | solution.py:519
  17.9 40.9 %collective-permute-start.7 = (bf16[272,896]{1,0:T(8,128)(2,1)}, bf16[272,896]{1,0:T(8,128)(2,1)}, u32[]{:S(2)}, u32[]{:S(2)}) collective-permute-start(bf16[272,896]{1,0:T(8,128)(2,1)} %dynamic-slice_bitcast_fusion), channel_id=1, source_target_pairs={{4,8},{8,4},{5,9},{9,5},{6,10},{10,6},{7,11},{11,7},{20,24},{24,20... | collective-permute-start | bytes 1462280 | tf_op jit(solution)/shard_map/ppermute | solution.py:536
  19.3 41.0 %collective-permute-start.6 = (bf16[256,896]{1,0:T(8,128)(2,1)}, bf16[256,896]{1,0:T(8,128)(2,1)}, u32[]{:S(2)}, u32[]{:S(2)}) collective-permute-start(bf16[256,896]{1,0:T(8,128)(2,1)} %dynamic-slice_bitcast_fusion.1), channel_id=1, source_target_pairs={{4,8},{8,4},{5,9},{9,5},{6,10},{10,6},{7,11},{11,7},{20,24},{24,20... | collective-permute-start | bytes 1376264 | tf_op jit(solution)/shard_map/ppermute | solution.py:536
  56.7 22.0 %collective-permute-start.3 = (bf16[272,896]{1,0:T(8,128)(2,1)S(1)}, bf16[272,896]{1,0:T(8,128)(2,1)}, u32[]{:S(2)}, u32[]{:S(2)}) collective-permute-start(bf16[272,896]{1,0:T(8,128)(2,1)S(1)} %collective-permute-done.1.refs_2_), channel_id=1, source_target_pairs={{0,16},{16,0},{1,17},{17,1},{2,18},{18,2},{3,19},{19,3},{4,20},{20... | collective-permute-start | bytes 1462280 | tf_op jit(solution)/shard_map/ppermute | solution.py:197
  58.3 20.4 %collective-permute-start.2 = (bf16[256,896]{1,0:T(8,128)(2,1)}, bf16[256,896]{1,0:T(8,128)(2,1)}, u32[]{:S(2)}, u32[]{:S(2)}) collective-permute-start(bf16[256,896]{1,0:T(8,128)(2,1)} %collective-permute-done.refs_1_), channel_id=1, source_target_pairs={{0,16},{16,0},{1,17},{17,1},{2,18},{18,2},{3,19},{19,3},{4,20},{20... | collective-permute-start | bytes 1376264 | tf_op jit(solution)/shard_map/ppermute | solution.py:197
  58.8 25.9 %collective-permute-start.9 = (bf16[272,896]{1,0:T(8,128)(2,1)}, bf16[272,896]{1,0:T(8,128)(2,1)}, u32[]{:S(2)}, u32[]{:S(2)}) collective-permute-start(bf16[272,896]{1,0:T(8,128)(2,1)} %collective-permute-done.7.refs_3_), channel_id=1, source_target_pairs={{4,20},{8,24},{20,4},{24,8},{5,21},{9,25},{21,5},{25,9},{6,22},{10... | collective-permute-start | bytes 1462280 | tf_op jit(solution)/shard_map/ppermute | solution.py:538
  60.3 24.4 %collective-permute-start.8 = (bf16[256,896]{1,0:T(8,128)(2,1)}, bf16[256,896]{1,0:T(8,128)(2,1)S(1)}, u32[]{:S(2)}, u32[]{:S(2)}) collective-permute-start(bf16[256,896]{1,0:T(8,128)(2,1)} %collective-permute-done.6.refs_2_), channel_id=1, source_target_pairs={{4,20},{8,24},{20,4},{24,8},{5,21},{9,25},{21,5},{25,9},{6,22},{10... | collective-permute-start | bytes 1376264 | tf_op jit(solution)/shard_map/ppermute | solution.py:538
  81.4 3.4 %copy-start.1 = (bf16[1792,528]{0,1:T(8,128)(2,1)S(1)}, bf16[1792,528]{0,1:T(8,128)(2,1)}, u32[]{:S(2)}) copy-start(bf16[1792,528]{0,1:T(8,128)(2,1)} %param.11) | copy-start | bytes 5677060
  81.4 7.9 %collective-permute-start.4 = (f32[192,528]{1,0:T(8,128)S(1)}, f32[192,528]{1,0:T(8,128)S(1)}, u32[]{:S(2)}, u32[]{:S(2)}) collective-permute-start(f32[192,528]{1,0:T(8,128)S(1)} %get-tuple-element.35), channel_id=1, source_target_pairs={{0,1},{1,0},{2,3},{3,2},{4,5},{5,4},{6,7},{7,6},{8,9},{9,8},{10,11... | collective-permute-start | bytes 1216520 | tf_op jit(solution)/shard_map/ppermute | solution.py:197
  84.3 5.0 %collective-permute-start.11 = (f32[192,528]{1,0:T(8,128)S(1)}, f32[192,528]{1,0:T(8,128)S(1)}, u32[]{:S(2)}, u32[]{:S(2)}) collective-permute-start(f32[192,528]{1,0:T(8,128)S(1)} %get-tuple-element.41), channel_id=1, source_target_pairs={{0,1},{1,0},{2,3},{3,2},{4,5},{5,4},{6,7},{7,6},{8,9},{9,8},{10,11... | collective-permute-start | bytes 1216520 | tf_op jit(solution)/shard_map/ppermute | solution.py:197
  88.7 1.9 %collective-permute-start.10 = (f32[192,528]{1,0:T(8,128)S(1)}, f32[192,528]{1,0:T(8,128)S(1)}, u32[]{:S(2)}, u32[]{:S(2)}) collective-permute-start(f32[192,528]{1,0:T(8,128)S(1)} %get-tuple-element.39), channel_id=1, source_target_pairs={{0,1},{1,0},{2,3},{3,2},{4,5},{5,4},{6,7},{7,6},{8,9},{9,8},{10,11... | collective-permute-start | bytes 1216520 | tf_op jit(solution)/shard_map/ppermute | solution.py:197
  88.9 2.4 %collective-permute-start.12 = (f32[192,528]{1,0:T(8,128)S(1)}, f32[192,528]{1,0:T(8,128)S(1)}, u32[]{:S(2)}, u32[]{:S(2)}) collective-permute-start(f32[192,528]{1,0:T(8,128)S(1)} %get-tuple-element.43), channel_id=1, source_target_pairs={{0,1},{1,0},{2,3},{3,2},{4,5},{5,4},{6,7},{7,6},{8,9},{9,8},{10,11... | collective-permute-start | bytes 1216520 | tf_op jit(solution)/shard_map/ppermute | solution.py:197
  91.3 14.9 %copy-start.4 = (f32[512]{0:T(512)S(1)}, f32[512]{0:T(512)}, u32[]{:S(2)}) copy-start(f32[512]{0:T(512)} %param.13) | copy-start | bytes 6148
  93.0 15.3 %copy-start.8 = (s32[12,2]{0,1:T(2,128)S(1)}, s32[12,2]{0,1:T(2,128)}, u32[]{:S(2)}) copy-start(s32[12,2]{0,1:T(2,128)} %param.15) | copy-start | bytes 292
  93.0 15.4 %copy-start.7 = (s32[1,4,8]{2,1,0:T(4,128)S(1)}, s32[1,4,8]{2,1,0:T(4,128)}, u32[]{:S(2)}) copy-start(s32[1,4,8]{2,1,0:T(4,128)} %param.16) | copy-start | bytes 388
  93.0 13.3 %collective-permute-start.13 = (bf16[384,576]{1,0:T(8,128)(2,1)S(1)}, bf16[384,576]{1,0:T(8,128)(2,1)S(1)}, u32[]{:S(2)}, u32[]{:S(2)}) collective-permute-start(bf16[384,576]{1,0:T(8,128)(2,1)S(1)} %get-tuple-element.45), channel_id=1, source_target_pairs={{0,2},{2,0},{1,3},{3,1},{4,6},{6,4},{5,7},{7,5},{8,10},{10,8},{9,1... | collective-permute-start | bytes 1327112 | tf_op jit(solution)/shard_map/ppermute | solution.py:197
  106.2 25.0 %copy-start.9 = (s32[4,1]{0,1:T(1,128)S(1)}, s32[4,1]{0,1:T(1,128)}, u32[]{:S(2)}) copy-start(s32[4,1]{0,1:T(1,128)} %param.17) | copy-start | bytes 52
  106.2 28.2 %copy-start.6 = (bf16[4,576]{1,0:T(4,128)(2,1)S(1)}, bf16[4,576]{1,0:T(4,128)(2,1)}, u32[]{:S(2)}) copy-start(bf16[4,576]{1,0:T(4,128)(2,1)} %param.19) | copy-start | bytes 13828
  106.2 33.0 %copy-start.3 = (bf16[4,32,576]{2,1,0:T(8,128)(2,1)S(1)}, bf16[4,32,576]{2,1,0:T(8,128)(2,1)}, u32[]{:S(2)}) copy-start(bf16[4,32,576]{2,1,0:T(8,128)(2,1)} %param.18) | copy-start | bytes 442372
  106.6 35.7 %collective-permute-start.19 = (bf16[384,576]{1,0:T(8,128)(2,1)S(1)}, bf16[384,576]{1,0:T(8,128)(2,1)S(1)}, u32[]{:S(2)}, u32[]{:S(2)}) collective-permute-start(bf16[384,576]{1,0:T(8,128)(2,1)S(1)} %shard_map.118.k0_ref), channel_id=1, source_target_pairs={{0,1},{1,0},{2,3},{3,2},{4,5},{5,4},{6,7},{7,6},{8,9},{9,8},{10,11... | collective-permute-start | bytes 1327112 | tf_op jit(solution)/shard_map/ppermute | solution.py:197
  106.7 7.5 %collective-permute-start.14 = (bf16[192,480]{1,0:T(8,128)(2,1)}, bf16[192,480]{1,0:T(8,128)(2,1)S(1)}, u32[]{:S(2)}, u32[]{:S(2)}) collective-permute-start(bf16[192,480]{1,0:T(8,128)(2,1)} %get-tuple-element.47), channel_id=1, source_target_pairs={{0,2},{2,0},{1,3},{3,1},{4,6},{6,4},{5,7},{7,5},{8,10},{10,8},{9,1... | collective-permute-start | bytes 552968 | tf_op jit(solution)/shard_map/ppermute | solution.py:197
  114.8 31.5 %collective-permute-start.15 = (bf16[96,1056]{1,0:T(8,128)(2,1)S(1)}, bf16[96,1056]{1,0:T(8,128)(2,1)S(1)}, u32[]{:S(2)}, u32[]{:S(2)}) collective-permute-start(bf16[96,1056]{1,0:T(8,128)(2,1)S(1)} %get-tuple-element.50), channel_id=1, source_target_pairs={{0,4},{4,0},{8,12},{12,8},{1,5},{5,1},{9,13},{13,9},{2,6},{6,2},{1... | collective-permute-start | bytes 608264 | tf_op jit(solution)/shard_map/ppermute | solution.py:610
  131.4 5.2 %collective-permute-start.20 = (s32[1,60]{1,0:T(1,128)S(1)}, s32[1,60]{1,0:T(1,128)S(1)}, u32[]{:S(2)}, u32[]{:S(2)}) collective-permute-start(s32[1,60]{1,0:T(1,128)S(1)} %add_bitcast_fusion), channel_id=1, source_target_pairs={{4,0},{8,4},{12,8},{0,12},{5,1},{9,5},{13,9},{1,13},{6,2},{10,6},{... | collective-permute-start | bytes 728 | tf_op jit(solution)/shard_map/ppermute | solution.py:526
  133.8 4.5 %collective-permute-start.21 = (s32[1,60]{1,0:T(1,128)S(1)}, s32[1,60]{1,0:T(1,128)S(1)}, u32[]{:S(2)}, u32[]{:S(2)}) collective-permute-start(s32[1,60]{1,0:T(1,128)S(1)} %add_bitcast_fusion), channel_id=1, source_target_pairs={{8,0},{12,4},{0,8},{4,12},{9,1},{13,5},{1,9},{5,13},{10,2},{14,6},... | collective-permute-start | bytes 728 | tf_op jit(solution)/shard_map/ppermute | solution.py:526
  133.8 5.4 %collective-permute-start.22 = (s32[1,60]{1,0:T(1,128)S(1)}, s32[1,60]{1,0:T(1,128)S(1)}, u32[]{:S(2)}, u32[]{:S(2)}) collective-permute-start(s32[1,60]{1,0:T(1,128)S(1)} %add_bitcast_fusion), channel_id=1, source_target_pairs={{12,0},{0,4},{4,8},{8,12},{13,1},{1,5},{5,9},{9,13},{14,2},{2,6},{... | collective-permute-start | bytes 728 | tf_op jit(solution)/shard_map/ppermute | solution.py:526
  139.2 1.3 copy-start.2
  143.2 11.5 %collective-permute-start.23 = (bf16[128,640]{1,0:T(8,128)(2,1)S(1)}, bf16[128,640]{1,0:T(8,128)(2,1)S(1)}, u32[]{:S(2)}, u32[]{:S(2)}) collective-permute-start(bf16[128,640]{1,0:T(8,128)(2,1)S(1)} %shard_map.120.refs_0_), channel_id=1, source_target_pairs={{4,0},{8,4},{12,8},{0,12},{5,1},{9,5},{13,9},{1,13},{6,2},{10,6},{... | collective-permute-start | bytes 491528 | tf_op jit(solution)/shard_map/ppermute | solution.py:600
  144.0 13.9 %collective-permute-start.24 = (bf16[128,640]{1,0:T(8,128)(2,1)S(1)}, bf16[128,640]{1,0:T(8,128)(2,1)S(1)}, u32[]{:S(2)}, u32[]{:S(2)}) collective-permute-start(bf16[128,640]{1,0:T(8,128)(2,1)S(1)} %shard_map.120.refs_0_), channel_id=1, source_target_pairs={{8,0},{12,4},{0,8},{4,12},{9,1},{13,5},{1,9},{5,13},{10,2},{14,6},... | collective-permute-start | bytes 491528 | tf_op jit(solution)/shard_map/ppermute | solution.py:600
  144.7 13.2 %collective-permute-start.25 = (bf16[128,640]{1,0:T(8,128)(2,1)S(1)}, bf16[128,640]{1,0:T(8,128)(2,1)S(1)}, u32[]{:S(2)}, u32[]{:S(2)}) collective-permute-start(bf16[128,640]{1,0:T(8,128)(2,1)S(1)} %shard_map.120.refs_0_), channel_id=1, source_target_pairs={{12,0},{0,4},{4,8},{8,12},{13,1},{1,5},{5,9},{9,13},{14,2},{2,6},{... | collective-permute-start | bytes 491528 | tf_op jit(solution)/shard_map/ppermute | solution.py:600
  147.3 1.6 %collective-permute-start.16 = (bf16[96,384]{1,0:T(8,128)(2,1)S(1)}, bf16[96,384]{1,0:T(8,128)(2,1)S(1)}, u32[]{:S(2)}, u32[]{:S(2)}) collective-permute-start(bf16[96,384]{1,0:T(8,128)(2,1)S(1)} %get-tuple-element.53), channel_id=1, source_target_pairs={{0,1},{1,0},{2,3},{3,2},{4,5},{5,4},{6,7},{7,6},{8,9},{9,8},{10,11... | collective-permute-start | bytes 221192 | tf_op jit(solution)/shard_map/ppermute | solution.py:624
  147.3 4.8 %collective-permute-start.17 = (bf16[96,384]{1,0:T(8,128)(2,1)S(1)}, bf16[96,384]{1,0:T(8,128)(2,1)S(1)}, u32[]{:S(2)}, u32[]{:S(2)}) collective-permute-start(bf16[96,384]{1,0:T(8,128)(2,1)S(1)} %get-tuple-element.54), channel_id=1, source_target_pairs={{0,2},{1,3},{2,0},{3,1},{4,6},{5,7},{6,4},{7,5},{8,10},{9,11},{10,... | collective-permute-start | bytes 221192 | tf_op jit(solution)/shard_map/ppermute | solution.py:624
  148.9 4.5 %collective-permute-start.18 = (bf16[96,384]{1,0:T(8,128)(2,1)S(1)}, bf16[96,384]{1,0:T(8,128)(2,1)S(1)}, u32[]{:S(2)}, u32[]{:S(2)}) collective-permute-start(bf16[96,384]{1,0:T(8,128)(2,1)S(1)} %get-tuple-element.55), channel_id=1, source_target_pairs={{0,3},{1,2},{2,1},{3,0},{4,7},{5,6},{6,5},{7,4},{8,11},{9,10},{10,... | collective-permute-start | bytes 221192 | tf_op jit(solution)/shard_map/ppermute | solution.py:624

commit v2 on v1

--- a/solution.py
+++ b/solution.py
@@ -189,6 +189,7 @@
 VMEM = pl.BlockSpec(memory_space=pltpu.VMEM)
 SMEM = pl.BlockSpec(memory_space=pltpu.SMEM)
 VMEM_GRANT = 16 * 2**20
+GRP, DEC, STG, TP = "grp", "dec", "stg", "tp"
 F32 = jnp.float32
 BF16 = jnp.bfloat16
 
@@ -205,47 +206,85 @@
     return lax.dot_general(a, b, (((1,), (0,)), ((), ())), preferred_element_type=F32, **kw)
 
 
-def matmul_kernel(blocks, own, ids, *refs):
-    group, core, index = ids[0], ids[1], ids[2]
-    xs, refs = refs[:blocks], refs[blocks:]
-    (head_z, tail_z, head_y, tail_y), refs = refs[:4], refs[4:]
-    weight, outs = (refs[0], refs[1:]) if own else (None, refs)
-    half = head_z.shape[1]
-    split = head_z.shape[0]
-    here = pl.ds(pl.multiple_of(group * half, 128), half)
-    there = pl.ds(pl.multiple_of((1 - group) * half, 128), half)
-    outer = (index == 0) | (index == 3)
-    for z, y, at in ((head_z, head_y, slice(0, split)), (tail_z, tail_y, slice(split, None))):
-        w_here, w_there = z[...], y[...]
-        if own:
-            w_here = jnp.where(outer, weight[at, here], w_here)
-            w_there = jnp.where(outer, weight[at, there], w_there)
-        for i, x_ref in enumerate(xs):
-            send, keep = outs[2 * i], outs[2 * i + 1]
-            rows = send.shape[0]
-            out = dot_t(x_ref[:, here], w_here) + dot_t(x_ref[:, there], w_there)
-            top, bottom = out[:rows], out[rows:]
-            send[:, at] = jnp.where(core == 0, bottom, top)
-            keep[:, at] = jnp.where(core == 0, top, bottom)
-
-
-def matmul(ids, xs, weights, own=()):
-    rows, feats = xs[0].shape
-    cols = weights[0].shape[0] + weights[1].shape[0]
-    blocks = len(xs)
+def chosen(outer, own, sent):
+    return jnp.where(outer, own, sent)
+
+
+def halves(ids, x_ref):
+    half = x_ref.shape[1] // 2
+    here = pl.ds(pl.multiple_of(ids[0] * half, 128), half)
+    there = pl.ds(pl.multiple_of((1 - ids[0]) * half, 128), half)
+    return here, there
+
+
+def is_outer(ids):
+    return (ids[2] == 0) | (ids[2] == 3)
+
+
+def put(ids, out, send, keep, start):
+    rows = send.shape[0]
+    top, bottom = out[:rows], out[rows:]
+    at = slice(start, start + out.shape[1])
+    send[:, at] = jnp.where(ids[1] == 0, bottom, top)
+    keep[:, at] = jnp.where(ids[1] == 0, top, bottom)
+
+
+def primary(ids, x_ref, own_ref, parts, send, keep):
+    here, there = halves(ids, x_ref)
+    outer = is_outer(ids)
+    start = 0
+    for z, y in parts:
+        at = slice(start, start + z.shape[0])
+        w_here = chosen(outer, own_ref[at, here], z[...])
+        w_there = chosen(outer, own_ref[at, there], y[...])
+        put(ids, dot_t(x_ref[:, here], w_here) + dot_t(x_ref[:, there], w_there), send, keep, start)
+        start += z.shape[0]
+
+
+def secondary(ids, x_refs, a_part, b_part, at, send, keep, starts):
+    here, there = halves(ids, x_refs[0])
+    outer = is_outer(ids)
+    w_here = chosen(outer, a_part[0][at, :], b_part[0][at, :])
+    w_there = chosen(outer, a_part[1][at, :], b_part[1][at, :])
+    for x_ref, start in zip(x_refs, starts):
+        put(ids, dot_t(x_ref[:, here], w_here) + dot_t(x_ref[:, there], w_there), send, keep, start)
+
+
+def near_kernel(ids, x_ref, own_ref, z0, y0, z1, y1, send, keep):
+    primary(ids, x_ref, own_ref, ((z0, y0), (z1, y1)), send, keep)
+
+
+def far_kernel(keys, ids, x_ref, far_ref, own_ref, z0, y0, z1, y1, bz1, by1, send, keep):
+    cols = own_ref.shape[0]
+    primary(ids, far_ref, own_ref, ((z0, y0), (z1, y1)), send, keep)
+    at = slice(z1.shape[0] - keys, None)
+    starts = (cols, cols + keys)
+    secondary(ids, (x_ref, far_ref), (z1, y1), (bz1, by1), at, send, keep, starts)
+
+
+def rest_kernel(keys, ids, x_ref, far_ref, z0, y0, z1, y1, bz0, by0, bz1, by1, send, keep):
+    head = z0.shape[0]
+    rest = z1.shape[0] - keys
+    wide = send.shape[1] // 2
+    xs = (x_ref, far_ref)
+    secondary(ids, xs, (z0, y0), (bz0, by0), slice(None), send, keep, (0, wide))
+    at = slice(0, rest)
+    secondary(ids, xs, (z1, y1), (bz1, by1), at, send, keep, (head, wide + head))
+
+
+def project(kernel, width, args):
+    rows, feats = args[1].shape
+    shape = jax.ShapeDtypeStruct((rows // 2, width), F32)
     return pl.pallas_call(
-        functools.partial(matmul_kernel, blocks, bool(own)),
-        in_specs=[SMEM] + [VMEM] * (blocks + 4 + len(own)),
-        out_specs=[VMEM] * (2 * blocks),
-        out_shape=[jax.ShapeDtypeStruct((rows // 2, cols), F32)] * (2 * blocks),
+        kernel,
+        in_specs=[SMEM] + [VMEM] * (len(args) - 1),
+        out_specs=[VMEM] * 2,
+        out_shape=[shape] * 2,
         cost_estimate=pl.CostEstimate(
-            flops=2 * rows * feats * cols * blocks,
-            bytes_accessed=8 * rows * cols * blocks,
-            transcendentals=0,
+            flops=2 * rows * feats * width, bytes_accessed=8 * rows * width, transcendentals=0
         ),
         compiler_params=pltpu.CompilerParams(vmem_limit_bytes=VMEM_GRANT),
-        name="project",
-    )(ids, *xs, *weights, *own)
+    )(*args)
 
 
 def turn_kernel(out):
@@ -256,7 +295,7 @@
     out[...] = jnp.where(down, -1.0, jnp.where(up, 1.0, 0.0))
 
 
-def old_kernel(n, pages, ids, tab_ref, query_ref, rows_ref, own_ref, peak_ref, total_ref, out_ref, bias_ref):
+def old_kernel(n, pages, ids, tab_ref, query_ref, rows_ref, own_ref, packed_ref, bias_ref):
     index, core = ids[2], ids[1]
     query = query_ref[...]
     keys = rows_ref.shape[0]
@@ -315,14 +354,13 @@
     peak = jnp.maximum(jnp.max(scores, axis=1, keepdims=True), own)
     weights = jnp.where(wide < 0.0, 0.0, jnp.exp(scores - peak))
     own_weight = jnp.where(index == 0, jnp.exp(own - peak), 0.0)
-    peak_ref[...] = peak
-    total_ref[...] = jnp.sum(weights, axis=1, keepdims=True) + own_weight
+    total = jnp.sum(weights, axis=1, keepdims=True) + own_weight
     out = dot_n(weights.astype(BF16), rows_ref[:, :KVL])
     own_rows = own_ref[:, :KVL].astype(F32)
     latent = jnp.concatenate(
         [jnp.broadcast_to(own_rows[r : r + 1], (heads, KVL)) for r in range(requests)], axis=0
     )
-    out_ref[...] = out + own_weight * latent
+    pack((out + own_weight * latent) / total, peak + jnp.log(total), packed_ref)
 
     width = bias_ref.shape[1]
     half = pages // 2
@@ -345,101 +383,139 @@
     bias_ref[...] = jnp.where(live & (reader == iota(8, width, 0)), 0.0, MASKED)
 
 
-def middle_kernel(ids, *refs):
-    (ak, ar, bk, br, pak, par, pbk, pbr, kv_send, kv_keep, q_send, q_keep) = refs
-    first, stage = ids[2] < 2, ids[3]
-    rows, cols = ak.shape
-    cut = QL - 2 * cols
-    quarter = rows // 2
-    for i, (a0, a1, b0, b1) in enumerate(((ak, ar, bk, br), (pak, par, pbk, pbr))):
-        a = a0[...] + a1[...]
-        b = b0[...] + b1[...]
-        low, high = jnp.where(first, b, a), jnp.where(first, a, b)
-        tail = jnp.concatenate([low[:, cut:], high], axis=1)
+def parted(ids, block):
+    half = block.shape[0] // 2
+    odd, stage = ids[2] % 2 == 1, ids[3]
+    top, bottom = block[:half], block[half:]
+    mine = jnp.where(stage == 0, top, bottom)
+    away = jnp.where(stage == 0, bottom, top)
+    twice = lambda part: jnp.concatenate([part, part], axis=0)
+    return jnp.where(odd, block, twice(mine)), jnp.where(odd, block, twice(away))
+
+
+def cross_near_kernel(ids, kept, got, send, keep):
+    mine, away = parted(ids, kept[...] + got[...])
+    keep[...] = mine
+    send[...] = away.astype(BF16)
+
+
+def cross_far_kernel(cols, ids, kept, got, send, keep):
+    both = kept[...] + got[...]
+    mine, away = parted(ids, both[:, :cols])
+    keep[:, :cols] = mine
+    keep[:, cols:] = both[:, cols:]
+    send[:, :cols] = away.astype(BF16)
+    send[:, cols:] = both[:, cols:].astype(BF16)
+
+
+def cross_rest_kernel(cut, keys, ids, kept, got, kept_far, got_far, send, keep):
+    wide = kept.shape[1] // 2
+    cols = send.shape[1]
+    stage = ids[3]
+    for i in range(2):
+        at = slice(i * wide, i * wide + cut)
+        last = slice(cols + i * keys, cols + (i + 1) * keys)
+        block = jnp.concatenate(
+            [kept[:, at] + got[:, at], kept_far[:, last] + got_far[:, last]], axis=1
+        )
+        half = block.shape[0] // 2
+        top, bottom = block[:half], block[half:]
+        at = slice(i * half, (i + 1) * half)
+        keep[at, :] = jnp.where(stage == 0, top, bottom)
+        send[at, :] = jnp.where(stage == 0, bottom, top).astype(BF16)
+
+
+def keys_kernel(keys, keep0, got0, keep1, got1, cos, sin, turn, gain, out):
+    rows, cols = keep0.shape
+    for i in range(2):
+        last = slice(cols + i * keys, cols + (i + 1) * keys)
+        tail = keep1[:, last] + got1[:, last].astype(F32)
+        if i == 0:
+            block = keep0[...] + got0[...].astype(F32)
+        else:
+            block = keep1[:, :cols] + got1[:, :cols].astype(F32)
+        raw = jnp.concatenate([tail, block], axis=1)
         at = slice(i * rows, (i + 1) * rows)
-        kv_keep[at, :] = tail
-        kv_send[at, :] = tail.astype(BF16)
-        top, bottom = low[:quarter, :cut], low[quarter:, :cut]
-        at = slice(i * quarter, (i + 1) * quarter)
-        q_keep[at, :] = jnp.where(stage == 0, top, bottom)
-        q_send[at, :] = jnp.where(stage == 0, bottom, top).astype(BF16)
-
-
-def keys_kernel(keep, got, cos, sin, turn, gain, out):
-    raw = keep[...] + got[...].astype(F32)
-    latent = raw[:, :KVL]
-    inverse = lax.rsqrt(jnp.sum(latent * latent, axis=1, keepdims=True) / KVL + norm_eps)
-    out[:, :KVL] = (latent * inverse * gain[...]).astype(BF16)
-    rope = raw[:, KVL:]
-    partner = dot_n(rope, turn[...], precision=lax.Precision.HIGHEST)
-    out[:, KVL:] = (rope * cos[...] + partner * sin[...]).astype(BF16)
-
-
-def attend_kernel(query_ref, k0_ref, k1_ref, bias_ref, peak_ref, total_ref, out_ref, packed_ref):
-    query = query_ref[...]
-    keys = k0_ref.shape[0]
-    rows = query.shape[0]
-    requests = bias_ref.shape[0] // 2
-    heads = rows // requests
-    bias = bias_ref[...]
-    wide = jnp.concatenate(
-        [jnp.broadcast_to(bias[r : r + 1], (heads, 2 * keys)) for r in range(requests)], axis=0
-    )
-    scores = jnp.concatenate([dot_t(query, k0_ref[...]), dot_t(query, k1_ref[...])], axis=1)
-    scores = scores * softmax_scale + wide
-    old_peak = peak_ref[...]
-    peak = jnp.maximum(old_peak, jnp.max(scores, axis=1, keepdims=True))
-    weights = jnp.where(wide < 0.0, 0.0, jnp.exp(scores - peak))
-    carried = jnp.exp(old_peak - peak)
-    total = jnp.sum(weights, axis=1, keepdims=True) + total_ref[...] * carried
-    rounded = weights.astype(BF16)
-    out = dot_n(rounded[:, :keys], k0_ref[:, :KVL]) + dot_n(rounded[:, keys:], k1_ref[:, :KVL])
-    out = (out + out_ref[...] * carried) / total
-    level = peak + jnp.log(total)
+        latent = raw[:, :KVL]
+        inverse = lax.rsqrt(jnp.sum(latent * latent, axis=1, keepdims=True) / KVL + norm_eps)
+        out[at, :KVL] = (latent * inverse * gain[...]).astype(BF16)
+        rope = raw[:, KVL:]
+        partner = dot_n(rope, turn[...], precision=lax.Precision.HIGHEST)
+        out[at, KVL:] = (rope * cos[at, :] + partner * sin[at, :]).astype(BF16)
+
+
+def pack(out, level, packed_ref):
     packed_ref[:, :KVL] = out.astype(BF16)
     lead = level.astype(BF16).astype(F32)
     rest = (level - lead).astype(BF16).astype(F32)
     last = level - lead - rest
-    lane = lax.broadcasted_iota(jnp.int32, (rows, 128), 1)
+    lane = lax.broadcasted_iota(jnp.int32, (out.shape[0], 128), 1)
     tail = jnp.where(lane == 0, lead, jnp.where(lane == 1, rest, jnp.where(lane == 2, last, 0.0)))
     packed_ref[:, KVL:] = tail.astype(BF16)
 
 
-def combine_kernel(*refs):
-    parts, out = refs[:-1], refs[-1]
-    levels = [jnp.sum(p[:, KVL:].astype(F32), axis=1, keepdims=True) for p in parts]
-    top = functools.reduce(jnp.maximum, levels)
-    shares = [jnp.exp(level - top) for level in levels]
-    numer = sum(s * p[:, :KVL].astype(F32) for s, p in zip(shares, parts))
-    out[...] = (numer / sum(shares)).astype(BF16)
-
-
-def return_kernel(ids, kv_keep, kv_got, q_keep, q_got, low, high, send):
-    stage = ids[3]
-    rows = kv_keep.shape[0] // 2
-    quarter = rows // 2
-    start = pl.multiple_of(stage * quarter, 32)
+def unpack(packed):
+    level = jnp.sum(packed[:, KVL:].astype(F32), axis=1, keepdims=True)
+    return packed[:, :KVL].astype(F32), level
+
+
+def attend_kernel(query_ref, k0_ref, k1_ref, bias_ref, old_ref, far_ref, packed_ref):
+    query = query_ref[...]
+    keys = k0_ref.shape[0]
+    requests = bias_ref.shape[0] // 2
+    heads = query.shape[0] // requests
+    bias = bias_ref[...]
+    wide = jnp.concatenate(
+        [jnp.broadcast_to(bias[r : r + 1], (heads, 2 * keys)) for r in range(requests)], axis=0
+    )
+    scores = jnp.concatenate([dot_t(query, k0_ref[...]), dot_t(query, k1_ref[...])], axis=1)
+    scores = scores * softmax_scale + wide
+    old, old_level = unpack(old_ref[...])
+    far, far_level = unpack(far_ref[...])
+    peak = jnp.maximum(old_level, far_level)
+    peak = jnp.maximum(peak, jnp.max(scores, axis=1, keepdims=True))
+    weights = jnp.where(wide < 0.0, 0.0, jnp.exp(scores - peak))
+    old_share, far_share = jnp.exp(old_level - peak), jnp.exp(far_level - peak)
+    total = jnp.sum(weights, axis=1, keepdims=True) + old_share + far_share
+    rounded = weights.astype(BF16)
+    out = dot_n(rounded[:, :keys], k0_ref[:, :KVL]) + dot_n(rounded[:, keys:], k1_ref[:, :KVL])
+    out = out + old * old_share + far * far_share
+    pack(out / total, peak + jnp.log(total), packed_ref)
+
+
+def combine_kernel(ids, own, across, partner, other, out):
+    odd = ids[2] % 2 == 1
+    first, level = unpack(jnp.where(odd, own[...], partner[...]))
+    second, other_level = unpack(jnp.where(odd, across[...], other[...]))
+    top = jnp.maximum(level, other_level)
+    share, other_share = jnp.exp(level - top), jnp.exp(other_level - top)
+    out[...] = ((first * share + second * other_share) / (share + other_share)).astype(BF16)
+
+
+def return_kernel(keep0, got0, keep1, got1, keep2, got2, low, high, send):
+    rows, cols = low.shape
     for i in range(2):
-        at = pl.ds(i * rows + start, quarter)
-        wide = kv_keep[at, :] + kv_got[at, :].astype(F32)
-        near = slice(i * quarter, (i + 1) * quarter)
-        short = q_keep[near, :] + q_got[near, :].astype(F32)
+        near = slice(i * rows, (i + 1) * rows)
+        keep, got = (keep0, got0) if i == 0 else (keep1, got1)
+        first = keep[:rows, :cols] + got[:rows, :cols].astype(F32)
+        second = keep2[near, :] + got2[near, :].astype(F32)
         if i == 0:
-            low[...] = short
-            high[...] = wide
+            low[...] = first
+            high[...] = second
         else:
-            send[:, : short.shape[1]] = short.astype(BF16)
-            send[:, short.shape[1] :] = wide.astype(BF16)
+            send[:, :cols] = first.astype(BF16)
+            send[:, cols:] = second.astype(BF16)
 
 
 def query_kernel(ids, low, high, got, gain, *refs):
     sends, scratch = refs[:-1], refs[-1]
     odd = ids[2] % 2 == 1
-    cut = low.shape[1]
-    got_low, got_high = got[:, :cut].astype(F32), got[:, cut:].astype(F32)
+    cols = low.shape[1]
+    cut = QL - 2 * cols
+    got_low, got_high = got[:, :cols].astype(F32), got[:, cols:].astype(F32)
     first = jnp.where(odd, got_low, low[...])
     second = jnp.where(odd, got_high, high[...])
-    third = jnp.where(odd, low[...], got_low)
+    third = jnp.where(odd, high[:, :cut], got_high[:, :cut])
     rows = jnp.concatenate([first, second, third], axis=1)
     inverse = lax.rsqrt(jnp.sum(rows * rows, axis=1, keepdims=True) / QL + norm_eps)
     rows = (rows * inverse * gain[...]).astype(BF16)
@@ -493,9 +569,9 @@
     dec_query,
     new_key,
 ):
-    n = lax.axis_size("dec")
-    group, index = lax.axis_index("grp"), lax.axis_index("dec")
-    stage, core = lax.axis_index("stg"), lax.axis_index("tp")
+    n = lax.axis_size(DEC)
+    group, index = lax.axis_index(GRP), lax.axis_index(DEC)
+    stage, core = lax.axis_index(STG), lax.axis_index(TP)
     ids = jnp.stack([group, core, index, stage]).astype(jnp.int32)
     tokens, feats = hidden_x.shape
     cols = proj_weight.shape[1]
@@ -504,51 +580,47 @@
     pages = page_plan.shape[0]
     requests, heads, _ = dec_query.shape
     queries = requests * heads
+    rows = tokens // 2
+    quarter = rows // 2
 
     weight = proj_weight.T
     split = cols // 2 // 128 * 128
-    pieces = {
-        "tail": lax.dynamic_slice(weight, (split, group * half), (cols - split, half)),
-        "head": lax.dynamic_slice(weight, (0, group * half), (split, half)),
-    }
-    a_pairs = [(0, 2), (3, 1), (1, 0), (2, 3)]
-    b_pairs = [(1, 2), (2, 1)]
+    pieces = [
+        lax.dynamic_slice(weight, (0, group * half), (split, half)),
+        lax.dynamic_slice(weight, (split, group * half), (cols - split, half)),
+    ]
+    partners = [(0, 1), (1, 0), (2, 3), (3, 2)]
     inner = [(g * n + i, (1 - g) * n + i) for g in range(2) for i in (1, 2)]
-    a_z, a_y, b_z, b_y = {}, {}, {}, {}
-    for name in ("tail", "head"):
-        a_z[name] = lax.ppermute(pieces[name], "dec", a_pairs)
-    x_far = lax.ppermute(hidden_x, "dec", [(0, 1), (1, 0), (2, 3), (3, 2)])
+    a_z, a_y, b_z, b_y = [None] * 2, [None] * 2, [None] * 2, [None] * 2
+    for p in (1, 0):
+        a_z[p] = lax.ppermute(pieces[p], DEC, [(0, 2), (3, 1), (1, 0), (2, 3)])
     packed = jnp.concatenate(
         [page_plan.reshape(-1), block_table.reshape(-1), split_lens.reshape(-1)]
     ).reshape(1, -1)
     tables = [packed]
     for s in range(1, n):
-        tables.append(lax.ppermute(packed, "dec", [((i + s) % n, i) for i in range(n)]))
+        tables.append(lax.ppermute(packed, DEC, [((i + s) % n, i) for i in range(n)]))
     tables = jnp.pad(
         jnp.concatenate(tables, axis=0), ((0, 8 - n), (0, -packed.shape[1] % 128))
     )
-    held, held_tail, held_head = pieces, *lax.optimization_barrier(
-        (pieces["tail"], pieces["head"], a_z["head"])
-    )[:2]
-    held = {"tail": held_tail, "head": held_head}
-    for name in ("tail", "head"):
-        a_y[name] = swap(a_z[name], "grp")
-        b_z[name] = lax.ppermute(held[name], "dec", b_pairs)
-    for name in ("tail", "head"):
-        b_y[name] = lax.ppermute(b_z[name], ("grp", "dec"), inner)
-    a_weights = (a_z["head"], a_z["tail"], a_y["head"], a_y["tail"])
-    b_weights = (b_z["head"], b_z["tail"], b_y["head"], b_y["tail"])
-
+    x_far = lax.ppermute(hidden_x, DEC, partners)
+    held = lax.optimization_barrier((pieces[0], pieces[1], a_z[0]))
+    for p in (1, 0):
+        a_y[p] = swap(a_z[p], GRP)
+        b_z[p] = lax.ppermute(held[p], DEC, [(1, 2), (2, 1)])
+    for p in (1, 0):
+        b_y[p] = lax.ppermute(b_z[p], (GRP, DEC), inner)
     query = dec_query.reshape(queries, KVW)
     padded_key = jnp.pad(new_key, ((0, 3 * requests), (0, 0)))
-    peak, total, out, bias = call(
+    old, bias = call(
         functools.partial(old_kernel, n, pages),
-        [shaped(queries, 1), shaped(queries, 1), shaped(queries, KVL), shaped(8, 2 * tokens)],
+        [shaped(queries, KVL + 128, kind=BF16), shaped(8, 2 * tokens)],
         [SMEM, VMEM, VMEM, VMEM, VMEM],
         (ids, tables, query, old_cache.reshape(-1, KVW), padded_key),
     )
 
-    rows = tokens // 2
+    old_far = lax.ppermute(old, DEC, partners)
+
     partner = index + 1 - 2 * (index % 2)
     place = core * rows + jnp.arange(rows, dtype=jnp.int32)
     positions = jnp.concatenate([index * tokens + place, partner * tokens + place]).astype(F32)
@@ -559,55 +631,76 @@
     early_ids, cos, sin, turn, kv_scale, q_scale = lax.optimization_barrier(
         (ids, jnp.cos(angles), jnp.sin(angles), turn, kv_gain.reshape(1, -1), q_gain.reshape(1, -1))
     )
-    a_near = matmul(early_ids, (hidden_x,), a_weights)
-    a_far = matmul(ids, (x_far,), a_weights)
-    b_both = matmul(ids, (hidden_x, x_far), b_weights, own=(weight,))
-    sums = []
-    for (send, keep) in (a_near, b_both[:2], a_far, b_both[2:]):
-        sums += [keep, swap(send, "tp")]
-    rows = tokens // 2
-    quarter = rows // 2
-    kv_send, kv_keep, q_send, q_keep = call(
-        middle_kernel,
-        [
-            shaped(2 * rows, KVW, kind=BF16),
-            shaped(2 * rows, KVW),
-            shaped(rows, cut, kind=BF16),
-            shaped(rows, cut),
-        ],
-        [SMEM] + [VMEM] * 8,
-        (ids, *sums),
-    )
-    kv_got = swap(kv_send, "stg")
-    q_got = swap(q_send, "stg")
+
+    a_refs = (a_z[0], a_y[0], a_z[1], a_y[1])
+    keys = cols - cut
+    wide = -(-cut // 128) * 128
+    send, kept0 = project(near_kernel, cols, (early_ids, hidden_x, weight, *a_refs))
+    other0 = swap(send, TP)
+    send0, keep0 = call(
+        cross_near_kernel,
+        [shaped(rows, cols, kind=BF16), shaped(rows, cols)],
+        [SMEM, VMEM, VMEM],
+        (ids, kept0, other0),
+    )
+    got0 = swap(send0, STG)
+    send, kept1 = project(
+        functools.partial(far_kernel, keys),
+        cols + 2 * keys,
+        (ids, hidden_x, x_far, weight, *a_refs, b_z[1], b_y[1]),
+    )
+    other1 = swap(send, TP)
+    send1, keep1 = call(
+        functools.partial(cross_far_kernel, cols),
+        [shaped(rows, cols + 2 * keys, kind=BF16), shaped(rows, cols + 2 * keys)],
+        [SMEM, VMEM, VMEM],
+        (ids, kept1, other1),
+    )
+    got1 = swap(send1, STG)
+    send, kept2 = project(
+        functools.partial(rest_kernel, keys),
+        2 * wide,
+        (ids, hidden_x, x_far, *a_refs, b_z[0], b_y[0], b_z[1], b_y[1]),
+    )
+    other2 = swap(send, TP)
+    send2, keep2 = call(
+        functools.partial(cross_rest_kernel, cut, keys),
+        [shaped(rows, cols, kind=BF16), shaped(rows, cols)],
+        [SMEM] + [VMEM] * 4,
+        (ids, kept2, other2, kept1, other1),
+    )
+    got2 = swap(send2, STG)
 
     key_rows = call(
-        keys_kernel,
-        shaped(2 * rows, KVW, kind=BF16),
-        [VMEM] * 6,
-        (kv_keep, kv_got, cos, sin, turn, kv_scale),
-    )
-    far_keys = swap(key_rows, "tp")
+        functools.partial(keys_kernel, keys),
+        shaped(tokens, KVW, kind=BF16),
+        [VMEM] * 8,
+        (keep0, got0, keep1, got1, cos, sin, turn, kv_scale),
+    )
+    far_keys = swap(key_rows, TP)
     part_out = call(
         attend_kernel,
         shaped(queries, KVL + 128, kind=BF16),
-        [VMEM] * 7,
-        (query, key_rows, far_keys, bias, peak, total, out),
-    )
-    parts = [part_out]
-    for s in range(1, n):
-        parts.append(
-            lax.ppermute(part_out, "dec", [((i + s) % n, i) for i in range(n)])
-        )
-    attn = call(combine_kernel, shaped(queries, KVL, kind=BF16), [VMEM] * n, tuple(parts))
+        [VMEM] * 6,
+        (query, key_rows, far_keys, bias, old, old_far),
+    )
+    spread = []
+    for pairs in ([(1, 3), (3, 1)], [(1, 0), (3, 2)], [(1, 2), (3, 0)]):
+        spread.append(lax.ppermute(part_out, DEC, pairs))
+    attn = call(
+        combine_kernel,
+        shaped(queries, KVL, kind=BF16),
+        [SMEM] + [VMEM] * 4,
+        (ids, part_out, *spread),
+    )
 
     low, high, back = call(
         return_kernel,
-        [shaped(quarter, cut), shaped(quarter, KVW), shaped(quarter, cut + KVW, kind=BF16)],
-        [SMEM] + [VMEM] * 4,
-        (ids, kv_keep, kv_got, q_keep, q_got),
-    )
-    back = lax.ppermute(back, "dec", [(0, 1), (1, 0), (2, 3), (3, 2)])
+        [shaped(quarter, cols), shaped(quarter, cols), shaped(quarter, 2 * cols, kind=BF16)],
+        [VMEM] * 6,
+        (keep0, got0, keep1, got1, keep2, got2),
+    )
+    back = lax.ppermute(back, DEC, partners)
     lanes = 4
     width = QL // lanes
     tile = shaped(quarter, width, kind=BF16)
@@ -620,9 +713,7 @@
     )
     gots = [blocks[0]]
     for k in range(1, lanes):
-        gots.append(
-            lax.ppermute(blocks[k], ("stg", "tp"), [(i, i ^ k) for i in range(lanes)])
-        )
+        gots.append(lax.ppermute(blocks[k], (STG, TP), [(i, i ^ k) for i in range(lanes)]))
     q_latent = call(
         place_kernel, shaped(tokens, width, kind=BF16), [SMEM] + [VMEM] * lanes, (ids, *gots)
     )

time: 159 us -> 160 us (level)
  the two profiles are of different devices: /device:TPU:0 before, /device:TPU:9 now
where the time goes in v2:
time: 160 us; the launch traced here: 159 us
  waiting for transfers between devices  84.5 us (53%)
  starting transfers between devices  44.8 us (28%)
  Pallas kernels  21.9 us (14%)
  local copies, waits for them, and re-layouts  5.89 us (4%)
    ppermute x2, waiting for transfers between devices, pairs_step(): a_z[p] = lax.ppermute(pieces[p], DEC, [(0, 2), (3, 1), (1, 0), (2, 3)])  43.3 us
    ppermute x9, waiting for transfers between devices, swap(): return lax.ppermute(a, axis, [(0, 1), (1, 0)])  31.2 us
    ppermute x9, starting transfers between devices, swap(): return lax.ppermute(a, axis, [(0, 1), (1, 0)])  14.6 us
    pallas_call x11, Pallas kernels, call(): pl.pallas_call(kernel, scratch_shapes=scratch, out_shape=shapes, in_specs...  11.6 us
    pallas_call x3, Pallas kernels, project(): pl.pallas_call(kernel, in_specs=[SMEM] + [VMEM] * (len(args) - 1), out_sp...  10.3 us
    ppermute x3, starting transfers between devices, pairs_step(): spread.append(lax.ppermute(part_out, DEC, pairs))  8.38 us
    ppermute x1, waiting for transfers between devices, pairs_step(): old_far = lax.ppermute(old, DEC, partners)  6.6 us
    ppermute x2, starting transfers between devices, pairs_step(): b_z[p] = lax.ppermute(held[p], DEC, [(1, 2), (2, 1)])  5.27 us
  transfers between devices with their start and end apart: 27, of which 7 were waited for; matrix products, arithmetic and copies ran while one was open for 1% of the time, Pallas kernels for 13%

profile of v2, /device:TPU:9, one launch (start us, length us, event | category | flops | bytes accessed | tf_op | source)
XLA Modules:
  0.0 159.1 jit_solution(2927298753266454406)
XLA Ops:
  0.6 1.2 dynamic-slice_bitcast_fusion.1
  1.9 2.5 %collective-permute-start.6 = (bf16[384,1792]{1,0:T(8,128)(2,1)}, bf16[384,1792]{1,0:T(8,128)(2,1)S(1)}, u32[]{:S(2)}, u32[]{:S(2)}) collective-permute-start(bf16[384,1792]{1,0:T(8,128)(2,1)} %x_ref.5), channel_id=1, source_target_pairs={{0,4},{4,0},{8,12},{12,8},{1,5},{5,1},{9,13},{13,9},{2,6},{6,2},{1... | collective-permute-start | bytes 4128776 | tf_op jit(solution)/shard_map/ppermute | solution.py:606
  4.3 1.1 dynamic-slice_bitcast_fusion
  5.5 8.8 %collective-permute-done.z0 = bf16[256,896]{1,0:T(8,128)(2,1)} collective-permute-done((bf16[256,896]{1,0:T(8,128)(2,1)S(1)}, bf16[256,896]{1,0:T(8,128)(2,1)}, u32[]{:S(2)}, u32[]{:S(2)}) %collective-permute-start) | collective-permute-done | bytes 458784 | tf_op jit(solution)/shard_map/ppermute | solution.py:596
  14.3 3.2 %collective-permute-start.7 = (bf16[272,896]{1,0:T(8,128)(2,1)S(1)}, bf16[272,896]{1,0:T(8,128)(2,1)}, u32[]{:S(2)}, u32[]{:S(2)}) collective-permute-start(bf16[272,896]{1,0:T(8,128)(2,1)S(1)} %dynamic-slice_bitcast_fusion), channel_id=1, source_target_pairs={{4,8},{8,4},{5,9},{9,5},{6,10},{10,6},{7,11},{11,7},{20,24},{24,20... | collective-permute-start | bytes 1462280 | tf_op jit(solution)/shard_map/ppermute | solution.py:610
  17.5 2.1 %collective-permute-start.11 = (bf16[256,896]{1,0:T(8,128)(2,1)S(1)}, bf16[256,896]{1,0:T(8,128)(2,1)}, u32[]{:S(2)}, u32[]{:S(2)}) collective-permute-start(bf16[256,896]{1,0:T(8,128)(2,1)S(1)} %dynamic-slice_bitcast_fusion.1), channel_id=1, source_target_pairs={{4,8},{8,4},{5,9},{9,5},{6,10},{10,6},{7,11},{11,7},{20,24},{24,20... | collective-permute-start | bytes 1376264 | tf_op jit(solution)/shard_map/ppermute | solution.py:610
  19.6 34.5 %collective-permute-done.2.z1 = bf16[272,896]{1,0:T(8,128)(2,1)S(1)} collective-permute-done((bf16[272,896]{1,0:T(8,128)(2,1)S(1)}, bf16[272,896]{1,0:T(8,128)(2,1)S(1)}, u32[]{:S(2)}, u32[]{:S(2)}) %collective-permute-start.2) | collective-permute-done | bytes 487456 | tf_op jit(solution)/shard_map/ppermute | solution.py:596
  54.1 1.2 collective-permute-start.3
  55.4 2.1 %collective-permute-start.8 = (bf16[272,896]{1,0:T(8,128)(2,1)}, bf16[272,896]{1,0:T(8,128)(2,1)}, u32[]{:S(2)}, u32[]{:S(2)}) collective-permute-start(bf16[272,896]{1,0:T(8,128)(2,1)} %collective-permute-done.7.bz1), channel_id=1, source_target_pairs={{4,20},{8,24},{20,4},{24,8},{5,21},{9,25},{21,5},{25,9},{6,22},{10... | collective-permute-start | bytes 1462280 | tf_op jit(solution)/shard_map/ppermute | solution.py:612
  57.5 1.3 collective-permute-start.1
  58.8 2.1 %collective-permute-start.12 = (bf16[256,896]{1,0:T(8,128)(2,1)}, bf16[256,896]{1,0:T(8,128)(2,1)}, u32[]{:S(2)}, u32[]{:S(2)}) collective-permute-start(bf16[256,896]{1,0:T(8,128)(2,1)} %collective-permute-done.11.bz0), channel_id=1, source_target_pairs={{4,20},{8,24},{20,4},{24,8},{5,21},{9,25},{21,5},{25,9},{6,22},{10... | collective-permute-start | bytes 1376264 | tf_op jit(solution)/shard_map/ppermute | solution.py:612
  61.1 24.5 %collective-permute-done.1.y0 = bf16[256,896]{1,0:T(8,128)(2,1)} collective-permute-done((bf16[256,896]{1,0:T(8,128)(2,1)}, bf16[256,896]{1,0:T(8,128)(2,1)}, u32[]{:S(2)}, u32[]{:S(2)}) %collective-permute-start.1) | collective-permute-done | bytes 458784 | tf_op jit(solution)/shard_map/ppermute | solution.py:198
  85.7 1.5 copy-done.1
  87.2 3.8 %shard_map.116 = (f32[192,624]{1,0:T(8,128)S(1)}, f32[192,624]{1,0:T(8,128)S(1)}) custom-call(s32[4]{0:T(128)S(1)} %pad_add_fusion.1.ids, bf16[384,1792]{1,0:T(8,128)(2,1)S(1)} %copy-done, bf16[384,1792]{1,0:T(8,128)(2,1)S(1)} %collective-permute-done.6.far_ref, bf16[528,1792]{1,0:T(8,128)(2,1)S(1)} %bitcast.16, bf16[256,896]{1,0:T(8,128)(2,1)} %collective-permute-done.z0, ...), custom_call_target="tpu_custom_call" | custom-call | flops 858783744 | bytes 1916928 | tf_op jit(solution)/shard_map/pallas_call | solution.py:278
  91.1 4.4 %collective-permute-start.9 = (f32[192,624]{1,0:T(8,128)S(1)}, f32[192,624]{1,0:T(8,128)S(1)}, u32[]{:S(2)}, u32[]{:S(2)}) collective-permute-start(f32[192,624]{1,0:T(8,128)S(1)} %get-tuple-element.38), channel_id=1, source_target_pairs={{0,1},{1,0},{2,3},{3,2},{4,5},{5,4},{6,7},{7,6},{8,9},{9,8},{10,11... | collective-permute-start | bytes 1437704 | tf_op jit(solution)/shard_map/ppermute | solution.py:198
  95.5 3.7 %shard_map.118 = (f32[192,1024]{1,0:T(8,128)S(1)}, f32[192,1024]{1,0:T(8,128)S(1)}) custom-call(s32[4]{0:T(128)S(1)} %pad_add_fusion.1.ids, bf16[384,1792]{1,0:T(8,128)(2,1)S(1)} %copy-done, bf16[384,1792]{1,0:T(8,128)(2,1)S(1)} %collective-permute-done.6.far_ref, bf16[256,896]{1,0:T(8,128)(2,1)} %collective-permute-done.z0, ...), custom_call_target="tpu_custom_call" | custom-call | flops 1409286144 | bytes 3145728 | tf_op jit(solution)/shard_map/pallas_call | solution.py:278
  99.2 2.4 %collective-permute-start.13 = (f32[192,1024]{1,0:T(8,128)S(1)}, f32[192,1024]{1,0:T(8,128)S(1)}, u32[]{:S(2)}, u32[]{:S(2)}) collective-permute-start(f32[192,1024]{1,0:T(8,128)S(1)} %get-tuple-element.43), channel_id=1, source_target_pairs={{0,1},{1,0},{2,3},{3,2},{4,5},{5,4},{6,7},{7,6},{8,9},{9,8},{10,11... | collective-permute-start | bytes 2359304 | tf_op jit(solution)/shard_map/ppermute | solution.py:198
  101.7 0.8 multiply_sine_fusion
  102.5 2.7 %shard_map.114 = (f32[192,528]{1,0:T(8,128)S(1)}, f32[192,528]{1,0:T(8,128)S(1)}) custom-call(s32[4]{0:T(128)S(1)} %pad_add_fusion.1.ids, bf16[384,1792]{1,0:T(8,128)(2,1)S(1)} %copy-done, bf16[528,1792]{1,0:T(8,128)(2,1)S(1)} %bitcast.17, bf16[256,896]{1,0:T(8,128)(2,1)} %collective-permute-done.z0, bf16[256,896]{1,0:T(8,128)(2,1)} %collective-permute-done.1.y0, ...), custom_call_target="tpu_custom_call" | custom-call | flops 726663168 | bytes 1622016 | tf_op jit(solution)/shard_map/pallas_call | solution.py:278
  105.3 0.7 shard_map.117
  106.0 1.3 collective-permute-start.10
  107.3 0.6 shard_map.115
  107.9 1.2 collective-permute-start.5
  109.1 1.4 shard_map.119
  110.5 0.8 copy-done.5
  111.3 0.4 collective-permute-start.14
  111.7 6.7 %collective-permute-done.5.got0 = bf16[192,528]{1,0:T(8,128)(2,1)S(1)} collective-permute-done((bf16[192,528]{1,0:T(8,128)(2,1)S(1)}, bf16[192,528]{1,0:T(8,128)(2,1)S(1)}, u32[]{:S(2)}, u32[]{:S(2)}) %collective-permute-start.5) | collective-permute-done | bytes 202784 | tf_op jit(solution)/shard_map/ppermute | solution.py:198
  118.4 0.6 shard_map.123.k0_ref
  119.0 2.4 %collective-permute-start.19 = (bf16[384,576]{1,0:T(8,128)(2,1)S(1)}, bf16[384,576]{1,0:T(8,128)(2,1)}, u32[]{:S(2)}, u32[]{:S(2)}) collective-permute-start(bf16[384,576]{1,0:T(8,128)(2,1)S(1)} %shard_map.123.k0_ref), channel_id=1, source_target_pairs={{0,1},{1,0},{2,3},{3,2},{4,5},{5,4},{6,7},{7,6},{8,9},{9,8},{10,11... | collective-permute-start | bytes 1327112 | tf_op jit(solution)/shard_map/ppermute | solution.py:198
  121.7 1.3 collective-permute-start.22
  123.0 1.2 collective-permute-start.20
  124.3 1.0 copy-done.6
  125.3 1.1 shard_map.120
  126.4 2.4 %collective-permute-start.15 = (bf16[96,1056]{1,0:T(8,128)(2,1)S(1)}, bf16[96,1056]{1,0:T(8,128)(2,1)S(1)}, u32[]{:S(2)}, u32[]{:S(2)}) collective-permute-start(bf16[96,1056]{1,0:T(8,128)(2,1)S(1)} %get-tuple-element.48), channel_id=1, source_target_pairs={{0,4},{4,0},{8,12},{12,8},{1,5},{5,1},{9,13},{13,9},{2,6},{6,2},{1... | collective-permute-start | bytes 608264 | tf_op jit(solution)/shard_map/ppermute | solution.py:703
  128.8 1.7 %shard_map.124 = (bf16[128,640]{1,0:T(8,128)(2,1)S(1)}, f32[8,768]{1,0:T(8,128)S(1)}) custom-call(s32[4]{0:T(128)S(1)} %pad_add_fusion.1.ids, s32[8,128]{1,0:T(8,128)S(1)} %pad.8.tab_ref, bf16[128,576]{1,0:T(8,128)(2,1)S(1)} %bitcast.19, bf16[1024,576]{1,0:T(8,128)(2,1)S(1)} %bitcast.18, bf16[16,576]{1,0:T(8,128)(2,1)S(1)} %pad.9.own_ref), custom_call_target="tpu_custom_call" | custom-call | flops 20000000 | bytes 2000000 | tf_op jit(solution)/shard_map/pallas_call | solution.py:541
  130.6 6.6 %collective-permute-done.23.far_ref = bf16[128,640]{1,0:T(8,128)(2,1)S(1)} collective-permute-done((bf16[128,640]{1,0:T(8,128)(2,1)S(1)}, bf16[128,640]{1,0:T(8,128)(2,1)S(1)}, u32[]{:S(2)}, u32[]{:S(2)}) %collective-permute-start.23) | collective-permute-done | bytes 163872 | tf_op jit(solution)/shard_map/ppermute | solution.py:622
  137.2 1.8 %shard_map.125.own = bf16[128,640]{1,0:T(8,128)(2,1)S(1)} custom-call(bf16[128,576]{1,0:T(8,128)(2,1)S(1)} %bitcast.20, bf16[384,576]{1,0:T(8,128)(2,1)S(1)} %shard_map.123.k0_ref, bf16[384,576]{1,0:T(8,128)(2,1)} %collective-permute-done.19.k1_ref, f32[8,768]{1,0:T(8,128)S(1)} %get-tuple-element.58.bias_ref, ...), custom_call_target="tpu_custom_call" | custom-call | flops 20000000 | bytes 2000000 | tf_op jit(solution)/shard_map/pallas_call | solution.py:541
  139.1 1.3 collective-permute-start.26
  140.4 3.1 %collective-permute-start.25 = (bf16[128,640]{1,0:T(8,128)(2,1)S(1)}, bf16[128,640]{1,0:T(8,128)(2,1)S(1)}, u32[]{:S(2)}, u32[]{:S(2)}) collective-permute-start(bf16[128,640]{1,0:T(8,128)(2,1)S(1)} %shard_map.125.own), channel_id=1, source_target_pairs={{4,0},{12,8},{5,1},{13,9},{6,2},{14,10},{7,3},{15,11},{20,16},{28,... | collective-permute-start | bytes 491528 | tf_op jit(solution)/shard_map/ppermute | solution.py:689
  143.5 4.0 %collective-permute-start.24 = (bf16[128,640]{1,0:T(8,128)(2,1)S(1)}, bf16[128,640]{1,0:T(8,128)(2,1)S(1)}, u32[]{:S(2)}, u32[]{:S(2)}) collective-permute-start(bf16[128,640]{1,0:T(8,128)(2,1)S(1)} %shard_map.125.own), channel_id=1, source_target_pairs={{4,12},{12,4},{5,13},{13,5},{6,14},{14,6},{7,15},{15,7},{20,28},{2... | collective-permute-start | bytes 491528 | tf_op jit(solution)/shard_map/ppermute | solution.py:689
  147.5 0.9 shard_map.121
  148.4 2.3 %collective-permute-start.16 = (bf16[96,384]{1,0:T(8,128)(2,1)S(1)}, bf16[96,384]{1,0:T(8,128)(2,1)S(1)}, u32[]{:S(2)}, u32[]{:S(2)}) collective-permute-start(bf16[96,384]{1,0:T(8,128)(2,1)S(1)} %get-tuple-element.51), channel_id=1, source_target_pairs={{0,1},{1,0},{2,3},{3,2},{4,5},{5,4},{6,7},{7,6},{8,9},{9,8},{10,11... | collective-permute-start | bytes 221192 | tf_op jit(solution)/shard_map/ppermute | solution.py:716
  150.8 1.2 collective-permute-start.17
  152.0 1.1 collective-permute-start.18
  153.1 1.4 collective-permute-done.17.refs_2_
  154.5 1.9 %collective-permute-done.18.refs_3_ = bf16[96,384]{1,0:T(8,128)(2,1)S(1)} collective-permute-done((bf16[96,384]{1,0:T(8,128)(2,1)S(1)}, bf16[96,384]{1,0:T(8,128)(2,1)S(1)}, u32[]{:S(2)}, u32[]{:S(2)}) %collective-permute-start.18) | collective-permute-done | bytes 73760 | tf_op jit(solution)/shard_map/ppermute | solution.py:716
  156.4 1.3 shard_map.122
  157.8 1.4 shard_map.126
  (61 shorter events, 1.0 us)
Async XLA Ops:
  0.6 85.0 %copy-start = (bf16[384,1792]{1,0:T(8,128)(2,1)S(1)}, bf16[384,1792]{1,0:T(8,128)(2,1)}, u32[]{:S(2)}) copy-start(bf16[384,1792]{1,0:T(8,128)(2,1)} %x_ref.5) | copy-start | bytes 4128772
  1.8 12.5 %collective-permute-start = (bf16[256,896]{1,0:T(8,128)(2,1)S(1)}, bf16[256,896]{1,0:T(8,128)(2,1)}, u32[]{:S(2)}, u32[]{:S(2)}) collective-permute-start(bf16[256,896]{1,0:T(8,128)(2,1)S(1)} %dynamic-slice_bitcast_fusion.1), channel_id=1, source_target_pairs={{0,8},{12,4},{4,0},{8,12},{1,9},{13,5},{5,1},{9,13},{2,10},{14,6},... | collective-permute-start | bytes 1376264 | tf_op jit(solution)/shard_map/ppermute | solution.py:596
  1.9 83.8 %collective-permute-start.6 = (bf16[384,1792]{1,0:T(8,128)(2,1)}, bf16[384,1792]{1,0:T(8,128)(2,1)S(1)}, u32[]{:S(2)}, u32[]{:S(2)}) collective-permute-start(bf16[384,1792]{1,0:T(8,128)(2,1)} %x_ref.5), channel_id=1, source_target_pairs={{0,4},{4,0},{8,12},{12,8},{1,5},{5,1},{9,13},{13,9},{2,6},{6,2},{1... | collective-permute-start | bytes 4128776 | tf_op jit(solution)/shard_map/ppermute | solution.py:606
  5.4 48.7 %collective-permute-start.2 = (bf16[272,896]{1,0:T(8,128)(2,1)S(1)}, bf16[272,896]{1,0:T(8,128)(2,1)S(1)}, u32[]{:S(2)}, u32[]{:S(2)}) collective-permute-start(bf16[272,896]{1,0:T(8,128)(2,1)S(1)} %dynamic-slice_bitcast_fusion), channel_id=1, source_target_pairs={{0,8},{12,4},{4,0},{8,12},{1,9},{13,5},{5,1},{9,13},{2,10},{14,6},... | collective-permute-start | bytes 1462280 | tf_op jit(solution)/shard_map/ppermute | solution.py:596
  14.3 41.1 %collective-permute-start.7 = (bf16[272,896]{1,0:T(8,128)(2,1)S(1)}, bf16[272,896]{1,0:T(8,128)(2,1)}, u32[]{:S(2)}, u32[]{:S(2)}) collective-permute-start(bf16[272,896]{1,0:T(8,128)(2,1)S(1)} %dynamic-slice_bitcast_fusion), channel_id=1, source_target_pairs={{4,8},{8,4},{5,9},{9,5},{6,10},{10,6},{7,11},{11,7},{20,24},{24,20... | collective-permute-start | bytes 1462280 | tf_op jit(solution)/shard_map/ppermute | solution.py:610
  17.5 41.3 %collective-permute-start.11 = (bf16[256,896]{1,0:T(8,128)(2,1)S(1)}, bf16[256,896]{1,0:T(8,128)(2,1)}, u32[]{:S(2)}, u32[]{:S(2)}) collective-permute-start(bf16[256,896]{1,0:T(8,128)(2,1)S(1)} %dynamic-slice_bitcast_fusion.1), channel_id=1, source_target_pairs={{4,8},{8,4},{5,9},{9,5},{6,10},{10,6},{7,11},{11,7},{20,24},{24,20... | collective-permute-start | bytes 1376264 | tf_op jit(solution)/shard_map/ppermute | solution.py:610
  54.1 31.5 %collective-permute-start.3 = (bf16[272,896]{1,0:T(8,128)(2,1)S(1)}, bf16[272,896]{1,0:T(8,128)(2,1)}, u32[]{:S(2)}, u32[]{:S(2)}) collective-permute-start(bf16[272,896]{1,0:T(8,128)(2,1)S(1)} %collective-permute-done.2.z1), channel_id=1, source_target_pairs={{0,16},{16,0},{1,17},{17,1},{2,18},{18,2},{3,19},{19,3},{4,20},{20... | collective-permute-start | bytes 1462280 | tf_op jit(solution)/shard_map/ppermute | solution.py:198
  55.4 30.3 %collective-permute-start.8 = (bf16[272,896]{1,0:T(8,128)(2,1)}, bf16[272,896]{1,0:T(8,128)(2,1)}, u32[]{:S(2)}, u32[]{:S(2)}) collective-permute-start(bf16[272,896]{1,0:T(8,128)(2,1)} %collective-permute-done.7.bz1), channel_id=1, source_target_pairs={{4,20},{8,24},{20,4},{24,8},{5,21},{9,25},{21,5},{25,9},{6,22},{10... | collective-permute-start | bytes 1462280 | tf_op jit(solution)/shard_map/ppermute | solution.py:612
  57.5 28.2 %collective-permute-start.1 = (bf16[256,896]{1,0:T(8,128)(2,1)}, bf16[256,896]{1,0:T(8,128)(2,1)}, u32[]{:S(2)}, u32[]{:S(2)}) collective-permute-start(bf16[256,896]{1,0:T(8,128)(2,1)} %collective-permute-done.z0), channel_id=1, source_target_pairs={{0,16},{16,0},{1,17},{17,1},{2,18},{18,2},{3,19},{19,3},{4,20},{20... | collective-permute-start | bytes 1376264 | tf_op jit(solution)/shard_map/ppermute | solution.py:198
  58.8 36.7 %collective-permute-start.12 = (bf16[256,896]{1,0:T(8,128)(2,1)}, bf16[256,896]{1,0:T(8,128)(2,1)}, u32[]{:S(2)}, u32[]{:S(2)}) collective-permute-start(bf16[256,896]{1,0:T(8,128)(2,1)} %collective-permute-done.11.bz0), channel_id=1, source_target_pairs={{4,20},{8,24},{20,4},{24,8},{5,21},{9,25},{21,5},{25,9},{6,22},{10... | collective-permute-start | bytes 1376264 | tf_op jit(solution)/shard_map/ppermute | solution.py:612
  85.7 1.5 copy-start.1
  91.0 11.4 %copy-start.8 = (f32[1536]{0:T(1024)S(1)}, f32[1536]{0:T(1024)}, u32[]{:S(2)}) copy-start(f32[1536]{0:T(1024)} %param.12) | copy-start | bytes 18436
  91.1 11.4 %copy-start.2 = (bf16[1792,528]{0,1:T(8,128)(2,1)S(1)}, bf16[1792,528]{0,1:T(8,128)(2,1)}, u32[]{:S(2)}) copy-start(bf16[1792,528]{0,1:T(8,128)(2,1)} %param.11) | copy-start | bytes 5677060
  91.1 14.2 %collective-permute-start.9 = (f32[192,624]{1,0:T(8,128)S(1)}, f32[192,624]{1,0:T(8,128)S(1)}, u32[]{:S(2)}, u32[]{:S(2)}) collective-permute-start(f32[192,624]{1,0:T(8,128)S(1)} %get-tuple-element.38), channel_id=1, source_target_pairs={{0,1},{1,0},{2,3},{3,2},{4,5},{5,4},{6,7},{7,6},{8,9},{9,8},{10,11... | collective-permute-start | bytes 1437704 | tf_op jit(solution)/shard_map/ppermute | solution.py:198
  99.2 9.8 %collective-permute-start.13 = (f32[192,1024]{1,0:T(8,128)S(1)}, f32[192,1024]{1,0:T(8,128)S(1)}, u32[]{:S(2)}, u32[]{:S(2)}) collective-permute-start(f32[192,1024]{1,0:T(8,128)S(1)} %get-tuple-element.43), channel_id=1, source_target_pairs={{0,1},{1,0},{2,3},{3,2},{4,5},{5,4},{6,7},{7,6},{8,9},{9,8},{10,11... | collective-permute-start | bytes 2359304 | tf_op jit(solution)/shard_map/ppermute | solution.py:198
  105.2 2.0 %collective-permute-start.4 = (f32[192,528]{1,0:T(8,128)S(1)}, f32[192,528]{1,0:T(8,128)S(1)}, u32[]{:S(2)}, u32[]{:S(2)}) collective-permute-start(f32[192,528]{1,0:T(8,128)S(1)} %get-tuple-element.33), channel_id=1, source_target_pairs={{0,1},{1,0},{2,3},{3,2},{4,5},{5,4},{6,7},{7,6},{8,9},{9,8},{10,11... | collective-permute-start | bytes 1216520 | tf_op jit(solution)/shard_map/ppermute | solution.py:198
  106.0 12.4 %copy-start.7 = (f32[512]{0:T(512)S(1)}, f32[512]{0:T(512)}, u32[]{:S(2)}) copy-start(f32[512]{0:T(512)} %param.13) | copy-start | bytes 6148
  106.0 12.4 %collective-permute-start.10 = (bf16[192,624]{1,0:T(8,128)(2,1)S(1)}, bf16[192,624]{1,0:T(8,128)(2,1)S(1)}, u32[]{:S(2)}, u32[]{:S(2)}) collective-permute-start(bf16[192,624]{1,0:T(8,128)(2,1)S(1)} %get-tuple-element.40), channel_id=1, source_target_pairs={{0,2},{2,0},{1,3},{3,1},{4,6},{6,4},{5,7},{7,5},{8,10},{10,8},{9,1... | collective-permute-start | bytes 718856 | tf_op jit(solution)/shard_map/ppermute | solution.py:198
  107.9 10.4 %collective-permute-start.5 = (bf16[192,528]{1,0:T(8,128)(2,1)S(1)}, bf16[192,528]{1,0:T(8,128)(2,1)S(1)}, u32[]{:S(2)}, u32[]{:S(2)}) collective-permute-start(bf16[192,528]{1,0:T(8,128)(2,1)S(1)} %get-tuple-element.35), channel_id=1, source_target_pairs={{0,2},{2,0},{1,3},{3,1},{4,6},{6,4},{5,7},{7,5},{8,10},{10,8},{9,1... | collective-permute-start | bytes 608264 | tf_op jit(solution)/shard_map/ppermute | solution.py:198
  109.1 12.2 %copy-start.10 = (s32[1,4,8]{2,1,0:T(4,128)S(1)}, s32[1,4,8]{2,1,0:T(4,128)}, u32[]{:S(2)}) copy-start(s32[1,4,8]{2,1,0:T(4,128)} %param.16) | copy-start | bytes 388
  109.1 12.3 %copy-start.11 = (s32[12,2]{0,1:T(2,128)S(1)}, s32[12,2]{0,1:T(2,128)}, u32[]{:S(2)}) copy-start(s32[12,2]{0,1:T(2,128)} %param.15) | copy-start | bytes 292
  109.1 12.5 %copy-start.12 = (s32[4,1]{0,1:T(1,128)S(1)}, s32[4,1]{0,1:T(1,128)}, u32[]{:S(2)}) copy-start(s32[4,1]{0,1:T(1,128)} %param.17) | copy-start | bytes 52
  109.1 15.1 %copy-start.9 = (bf16[4,576]{1,0:T(4,128)(2,1)S(1)}, bf16[4,576]{1,0:T(4,128)(2,1)}, u32[]{:S(2)}) copy-start(bf16[4,576]{1,0:T(4,128)(2,1)} %param.19) | copy-start | bytes 13828
  110.5 0.8 copy-start.5
  111.3 12.9 %collective-permute-start.14 = (bf16[192,528]{1,0:T(8,128)(2,1)}, bf16[192,528]{1,0:T(8,128)(2,1)}, u32[]{:S(2)}, u32[]{:S(2)}) collective-permute-start(bf16[192,528]{1,0:T(8,128)(2,1)} %get-tuple-element.45), channel_id=1, source_target_pairs={{0,2},{2,0},{1,3},{3,1},{4,6},{6,4},{5,7},{7,5},{8,10},{10,8},{9,1... | collective-permute-start | bytes 608264 | tf_op jit(solution)/shard_map/ppermute | solution.py:198
  118.3 10.5 %copy-start.3 = (bf16[32,32,576]{2,1,0:T(8,128)(2,1)S(1)}, bf16[32,32,576]{2,1,0:T(8,128)(2,1)}, u32[]{:S(2)}) copy-start(bf16[32,32,576]{2,1,0:T(8,128)(2,1)} %param.14) | copy-start | bytes 3538948
  118.4 10.5 %copy-start.4 = (bf16[4,32,576]{2,1,0:T(8,128)(2,1)S(1)}, bf16[4,32,576]{2,1,0:T(8,128)(2,1)}, u32[]{:S(2)}) copy-start(bf16[4,32,576]{2,1,0:T(8,128)(2,1)} %param.18) | copy-start | bytes 442372
  119.0 18.3 %collective-permute-start.19 = (bf16[384,576]{1,0:T(8,128)(2,1)S(1)}, bf16[384,576]{1,0:T(8,128)(2,1)}, u32[]{:S(2)}, u32[]{:S(2)}) collective-permute-start(bf16[384,576]{1,0:T(8,128)(2,1)S(1)} %shard_map.123.k0_ref), channel_id=1, source_target_pairs={{0,1},{1,0},{2,3},{3,2},{4,5},{5,4},{6,7},{7,6},{8,9},{9,8},{10,11... | collective-permute-start | bytes 1327112 | tf_op jit(solution)/shard_map/ppermute | solution.py:198
  121.7 7.1 %collective-permute-start.22 = (s32[1,60]{1,0:T(1,128)S(1)}, s32[1,60]{1,0:T(1,128)S(1)}, u32[]{:S(2)}, u32[]{:S(2)}) collective-permute-start(s32[1,60]{1,0:T(1,128)S(1)} %add_bitcast_fusion), channel_id=1, source_target_pairs={{12,0},{0,4},{4,8},{8,12},{13,1},{1,5},{5,9},{9,13},{14,2},{2,6},{... | collective-permute-start | bytes 728 | tf_op jit(solution)/shard_map/ppermute | solution.py:602
  123.0 5.8 %collective-permute-start.21 = (s32[1,60]{1,0:T(1,128)S(1)}, s32[1,60]{1,0:T(1,128)S(1)}, u32[]{:S(2)}, u32[]{:S(2)}) collective-permute-start(s32[1,60]{1,0:T(1,128)S(1)} %add_bitcast_fusion), channel_id=1, source_target_pairs={{8,0},{12,4},{0,8},{4,12},{9,1},{13,5},{1,9},{5,13},{10,2},{14,6},... | collective-permute-start | bytes 728 | tf_op jit(solution)/shard_map/ppermute | solution.py:602
  123.0 5.8 %collective-permute-start.20 = (s32[1,60]{1,0:T(1,128)S(1)}, s32[1,60]{1,0:T(1,128)S(1)}, u32[]{:S(2)}, u32[]{:S(2)}) collective-permute-start(s32[1,60]{1,0:T(1,128)S(1)} %add_bitcast_fusion), channel_id=1, source_target_pairs={{4,0},{8,4},{12,8},{0,12},{5,1},{9,5},{13,9},{1,13},{6,2},{10,6},{... | collective-permute-start | bytes 728 | tf_op jit(solution)/shard_map/ppermute | solution.py:602
  124.2 1.0 copy-start.6
  126.4 21.1 %collective-permute-start.15 = (bf16[96,1056]{1,0:T(8,128)(2,1)S(1)}, bf16[96,1056]{1,0:T(8,128)(2,1)S(1)}, u32[]{:S(2)}, u32[]{:S(2)}) collective-permute-start(bf16[96,1056]{1,0:T(8,128)(2,1)S(1)} %get-tuple-element.48), channel_id=1, source_target_pairs={{0,4},{4,0},{8,12},{12,8},{1,5},{5,1},{9,13},{13,9},{2,6},{6,2},{1... | collective-permute-start | bytes 608264 | tf_op jit(solution)/shard_map/ppermute | solution.py:703
  130.5 6.7 %collective-permute-start.23 = (bf16[128,640]{1,0:T(8,128)(2,1)S(1)}, bf16[128,640]{1,0:T(8,128)(2,1)S(1)}, u32[]{:S(2)}, u32[]{:S(2)}) collective-permute-start(bf16[128,640]{1,0:T(8,128)(2,1)S(1)} %get-tuple-element.59.old_ref), channel_id=1, source_target_pairs={{0,4},{4,0},{8,12},{12,8},{1,5},{5,1},{9,13},{13,9},{2,6},{6,2},{1... | collective-permute-start | bytes 491528 | tf_op jit(solution)/shard_map/ppermute | solution.py:622
  139.1 18.7 %collective-permute-start.26 = (bf16[128,640]{1,0:T(8,128)(2,1)S(1)}, bf16[128,640]{1,0:T(8,128)(2,1)S(1)}, u32[]{:S(2)}, u32[]{:S(2)}) collective-permute-start(bf16[128,640]{1,0:T(8,128)(2,1)S(1)} %shard_map.125.own), channel_id=1, source_target_pairs={{4,8},{12,0},{5,9},{13,1},{6,10},{14,2},{7,11},{15,3},{20,24},{28,... | collective-permute-start | bytes 491528 | tf_op jit(solution)/shard_map/ppermute | solution.py:689
  140.4 17.4 %collective-permute-start.25 = (bf16[128,640]{1,0:T(8,128)(2,1)S(1)}, bf16[128,640]{1,0:T(8,128)(2,1)S(1)}, u32[]{:S(2)}, u32[]{:S(2)}) collective-permute-start(bf16[128,640]{1,0:T(8,128)(2,1)S(1)} %shard_map.125.own), channel_id=1, source_target_pairs={{4,0},{12,8},{5,1},{13,9},{6,2},{14,10},{7,3},{15,11},{20,16},{28,... | collective-permute-start | bytes 491528 | tf_op jit(solution)/shard_map/ppermute | solution.py:689
  143.5 14.3 %collective-permute-start.24 = (bf16[128,640]{1,0:T(8,128)(2,1)S(1)}, bf16[128,640]{1,0:T(8,128)(2,1)S(1)}, u32[]{:S(2)}, u32[]{:S(2)}) collective-permute-start(bf16[128,640]{1,0:T(8,128)(2,1)S(1)} %shard_map.125.own), channel_id=1, source_target_pairs={{4,12},{12,4},{5,13},{13,5},{6,14},{14,6},{7,15},{15,7},{20,28},{2... | collective-permute-start | bytes 491528 | tf_op jit(solution)/shard_map/ppermute | solution.py:689
  148.4 3.6 %collective-permute-start.16 = (bf16[96,384]{1,0:T(8,128)(2,1)S(1)}, bf16[96,384]{1,0:T(8,128)(2,1)S(1)}, u32[]{:S(2)}, u32[]{:S(2)}) collective-permute-start(bf16[96,384]{1,0:T(8,128)(2,1)S(1)} %get-tuple-element.51), channel_id=1, source_target_pairs={{0,1},{1,0},{2,3},{3,2},{4,5},{5,4},{6,7},{7,6},{8,9},{9,8},{10,11... | collective-permute-start | bytes 221192 | tf_op jit(solution)/shard_map/ppermute | solution.py:716
  150.8 3.7 %collective-permute-start.17 = (bf16[96,384]{1,0:T(8,128)(2,1)S(1)}, bf16[96,384]{1,0:T(8,128)(2,1)S(1)}, u32[]{:S(2)}, u32[]{:S(2)}) collective-permute-start(bf16[96,384]{1,0:T(8,128)(2,1)S(1)} %get-tuple-element.52), channel_id=1, source_target_pairs={{0,2},{1,3},{2,0},{3,1},{4,6},{5,7},{6,4},{7,5},{8,10},{9,11},{10,... | collective-permute-start | bytes 221192 | tf_op jit(solution)/shard_map/ppermute | solution.py:716
  152.0 4.4 %collective-permute-start.18 = (bf16[96,384]{1,0:T(8,128)(2,1)S(1)}, bf16[96,384]{1,0:T(8,128)(2,1)S(1)}, u32[]{:S(2)}, u32[]{:S(2)}) collective-permute-start(bf16[96,384]{1,0:T(8,128)(2,1)S(1)} %get-tuple-element.53), channel_id=1, source_target_pairs={{0,3},{1,2},{2,1},{3,0},{4,7},{5,6},{6,5},{7,4},{8,11},{9,10},{10,... | collective-permute-start | bytes 221192 | tf_op jit(solution)/shard_map/ppermute | solution.py:716

commit v3 on v2

--- a/solution.py
+++ b/solution.py
@@ -221,15 +221,17 @@
     return (ids[2] == 0) | (ids[2] == 3)
 
 
-def put(ids, out, send, keep, start):
-    rows = send.shape[0]
-    top, bottom = out[:rows], out[rows:]
-    at = slice(start, start + out.shape[1])
-    send[:, at] = jnp.where(ids[1] == 0, bottom, top)
-    keep[:, at] = jnp.where(ids[1] == 0, top, bottom)
-
-
-def primary(ids, x_ref, own_ref, parts, send, keep):
+def put(ids, out, send, keep, chunk, column, row=0):
+    part = chunk // 2
+    columns = slice(column, column + out.shape[1])
+    for c in range(out.shape[0] // chunk):
+        top, bottom = out[c * chunk : c * chunk + part], out[c * chunk + part : (c + 1) * chunk]
+        at = slice(row + c * part, row + (c + 1) * part)
+        send[at, columns] = jnp.where(ids[1] == 0, bottom, top)
+        keep[at, columns] = jnp.where(ids[1] == 0, top, bottom)
+
+
+def primary(ids, x_ref, own_ref, parts, send, keep, chunk):
     here, there = halves(ids, x_ref)
     outer = is_outer(ids)
     start = 0
@@ -237,51 +239,87 @@
         at = slice(start, start + z.shape[0])
         w_here = chosen(outer, own_ref[at, here], z[...])
         w_there = chosen(outer, own_ref[at, there], y[...])
-        put(ids, dot_t(x_ref[:, here], w_here) + dot_t(x_ref[:, there], w_there), send, keep, start)
+        out = dot_t(x_ref[:, here], w_here) + dot_t(x_ref[:, there], w_there)
+        put(ids, out, send, keep, chunk, start)
         start += z.shape[0]
 
 
-def secondary(ids, x_refs, a_part, b_part, at, send, keep, starts):
+def secondary(ids, x_refs, w_here, w_there, outs, chunk, places):
     here, there = halves(ids, x_refs[0])
+    for x_ref, (column, step, row) in zip(x_refs, places):
+        out = dot_t(x_ref[:, here], w_here) + dot_t(x_ref[:, there], w_there)
+        for c in range(out.shape[0] // chunk):
+            piece = out[c * chunk : (c + 1) * chunk]
+            put(ids, piece, *outs, chunk, column + c * step, row + (0 if step else c * chunk // 2))
+
+
+def near_kernel(chunk, ids, x_ref, own_ref, z0, y0, z1, y1, send, keep):
+    primary(ids, x_ref, own_ref, ((z0, y0), (z1, y1)), send, keep, chunk)
+
+
+def far_kernel(chunk, ids, far_ref, own_ref, z0, y0, z1, y1, send, keep):
+    primary(ids, far_ref, own_ref, ((z0, y0), (z1, y1)), send, keep, chunk)
+
+
+def last_kernel(chunk, keys, ids, x_ref, far0, far1, own_ref, z0, y0, z1, y1, bz1, by1, send, keep):
+    cols = own_ref.shape[0]
+    primary(ids, far1, own_ref, ((z0, y0), (z1, y1)), send, keep, chunk)
     outer = is_outer(ids)
-    w_here = chosen(outer, a_part[0][at, :], b_part[0][at, :])
-    w_there = chosen(outer, a_part[1][at, :], b_part[1][at, :])
-    for x_ref, start in zip(x_refs, starts):
-        put(ids, dot_t(x_ref[:, here], w_here) + dot_t(x_ref[:, there], w_there), send, keep, start)
-
-
-def near_kernel(ids, x_ref, own_ref, z0, y0, z1, y1, send, keep):
-    primary(ids, x_ref, own_ref, ((z0, y0), (z1, y1)), send, keep)
-
-
-def far_kernel(keys, ids, x_ref, far_ref, own_ref, z0, y0, z1, y1, bz1, by1, send, keep):
-    cols = own_ref.shape[0]
-    primary(ids, far_ref, own_ref, ((z0, y0), (z1, y1)), send, keep)
     at = slice(z1.shape[0] - keys, None)
-    starts = (cols, cols + keys)
-    secondary(ids, (x_ref, far_ref), (z1, y1), (bz1, by1), at, send, keep, starts)
-
-
-def rest_kernel(keys, ids, x_ref, far_ref, z0, y0, z1, y1, bz0, by0, bz1, by1, send, keep):
-    head = z0.shape[0]
-    rest = z1.shape[0] - keys
+    w_here = chosen(outer, z1[at, :], bz1[at, :])
+    w_there = chosen(outer, y1[at, :], by1[at, :])
+    places = [(cols, keys, 0), (cols + 2 * keys, keys, 0), (cols + 3 * keys, keys, 0)]
+    secondary(ids, (x_ref, far0, far1), w_here, w_there, (send, keep), chunk, places)
+
+
+def rest_kernel(
+    chunk, keys, ids, x_ref, far0, far1, z0, y0, z1, y1, whole, bz0, by0, bz1, by1, send, keep
+):
+    outer = is_outer(ids)
+    head, direct = z0.shape[0], whole.shape[0]
     wide = send.shape[1] // 2
-    xs = (x_ref, far_ref)
-    secondary(ids, xs, (z0, y0), (bz0, by0), slice(None), send, keep, (0, wide))
-    at = slice(0, rest)
-    secondary(ids, xs, (z1, y1), (bz1, by1), at, send, keep, (head, wide + head))
-
-
-def project(kernel, width, args):
-    rows, feats = args[1].shape
-    shape = jax.ShapeDtypeStruct((rows // 2, width), F32)
+    here, there = halves(ids, x_ref)
+    xs = (x_ref, far0, far1)
+    rest = slice(0, z1.shape[0] - keys)
+    late = slice(direct, None)
+    for column, w_here, w_there in (
+        (
+            0,
+            jnp.concatenate(
+                [
+                    chosen(outer, z0[:direct, :], whole[:, here]),
+                    chosen(outer, z0[late, :], bz0[...]),
+                ],
+                axis=0,
+            ),
+            jnp.concatenate(
+                [
+                    chosen(outer, y0[:direct, :], whole[:, there]),
+                    chosen(outer, y0[late, :], by0[...]),
+                ],
+                axis=0,
+            ),
+        ),
+        (
+            head,
+            chosen(outer, z1[rest, :], bz1[rest, :]),
+            chosen(outer, y1[rest, :], by1[rest, :]),
+        ),
+    ):
+        places = [(column, 0, 0), (wide + column, 0, 0), (wide + column, 0, chunk // 2)]
+        secondary(ids, xs, w_here, w_there, (send, keep), chunk, places)
+
+
+def project(kernel, rows, width, args):
+    feats = args[1].shape[1]
+    shape = jax.ShapeDtypeStruct((rows, width), F32)
     return pl.pallas_call(
         kernel,
         in_specs=[SMEM] + [VMEM] * (len(args) - 1),
         out_specs=[VMEM] * 2,
         out_shape=[shape] * 2,
         cost_estimate=pl.CostEstimate(
-            flops=2 * rows * feats * width, bytes_accessed=8 * rows * width, transcendentals=0
+            flops=4 * rows * feats * width, bytes_accessed=8 * rows * width, transcendentals=0
         ),
         compiler_params=pltpu.CompilerParams(vmem_limit_bytes=VMEM_GRANT),
     )(*args)
@@ -365,7 +403,9 @@
     width = bias_ref.shape[1]
     half = pages // 2
     spot = iota(1, width, 1) // PAGE
-    which = jnp.where(spot // pages == 1, 1 - core, core) * half + spot % half
+    place = spot % half
+    taker = jnp.where(spot // pages == 1, 1 - core, core)
+    which = (place // (half // 2)) * half + taker * (half // 2) + place % (half // 2)
     partner = (spot % pages) // half == 1
     line = iota(base, width, 0)
     plan = jnp.where(partner, columns[n - 1][:base, :], columns[0][:base, :])
@@ -383,59 +423,56 @@
     bias_ref[...] = jnp.where(live & (reader == iota(8, width, 0)), 0.0, MASKED)
 
 
-def parted(ids, block):
+def lane_rows(ids, block):
     half = block.shape[0] // 2
-    odd, stage = ids[2] % 2 == 1, ids[3]
     top, bottom = block[:half], block[half:]
-    mine = jnp.where(stage == 0, top, bottom)
-    away = jnp.where(stage == 0, bottom, top)
-    twice = lambda part: jnp.concatenate([part, part], axis=0)
-    return jnp.where(odd, block, twice(mine)), jnp.where(odd, block, twice(away))
-
-
-def cross_near_kernel(ids, kept, got, send, keep):
-    mine, away = parted(ids, kept[...] + got[...])
-    keep[...] = mine
-    send[...] = away.astype(BF16)
-
-
-def cross_far_kernel(cols, ids, kept, got, send, keep):
+    stage = ids[3]
+    return jnp.where(stage == 0, top, bottom), jnp.where(stage == 0, bottom, top)
+
+
+def cross_kernel(cols, part, ids, kept, got, send, keep):
+    odd = ids[2] % 2 == 1
     both = kept[...] + got[...]
-    mine, away = parted(ids, both[:, :cols])
-    keep[:, :cols] = mine
-    keep[:, cols:] = both[:, cols:]
-    send[:, :cols] = away.astype(BF16)
-    send[:, cols:] = both[:, cols:].astype(BF16)
-
-
-def cross_rest_kernel(cut, keys, ids, kept, got, kept_far, got_far, send, keep):
+    for c in range(both.shape[0] // part):
+        at = slice(c * part, (c + 1) * part)
+        block = both[at, :cols]
+        mine, away = lane_rows(ids, block)
+        keep[at, :cols] = jnp.where(odd, block, jnp.concatenate([mine, mine], axis=0))
+        send[at, :cols] = jnp.where(odd, block, jnp.concatenate([away, away], axis=0)).astype(BF16)
+    if both.shape[1] > cols:
+        keep[:, cols:] = both[:, cols:]
+        send[:, cols:] = both[:, cols:].astype(BF16)
+
+
+def cross_rest_kernel(cut, keys, ids, kept, got, kept_last, got_last, send, keep):
     wide = kept.shape[1] // 2
     cols = send.shape[1]
-    stage = ids[3]
-    for i in range(2):
-        at = slice(i * wide, i * wide + cut)
+    part = kept.shape[0] // 2
+    half = part // 2
+    for i in range(4):
+        side, c = divmod(i, 2)
+        rows, at = slice(c * part, (c + 1) * part), slice(side * wide, side * wide + cut)
         last = slice(cols + i * keys, cols + (i + 1) * keys)
         block = jnp.concatenate(
-            [kept[:, at] + got[:, at], kept_far[:, last] + got_far[:, last]], axis=1
+            [kept[rows, at] + got[rows, at], kept_last[:, last] + got_last[:, last]], axis=1
         )
-        half = block.shape[0] // 2
-        top, bottom = block[:half], block[half:]
+        mine, away = lane_rows(ids, block)
         at = slice(i * half, (i + 1) * half)
-        keep[at, :] = jnp.where(stage == 0, top, bottom)
-        send[at, :] = jnp.where(stage == 0, bottom, top).astype(BF16)
-
-
-def keys_kernel(keys, keep0, got0, keep1, got1, cos, sin, turn, gain, out):
-    rows, cols = keep0.shape
-    for i in range(2):
+        keep[at, :] = mine
+        send[at, :] = away.astype(BF16)
+
+
+def keys_kernel(keys, keep0, got0, keep1, got1, keep2, got2, cos, sin, turn, gain, out):
+    cols = keep0.shape[1]
+    part = keep1.shape[0]
+    for i in range(4):
         last = slice(cols + i * keys, cols + (i + 1) * keys)
-        tail = keep1[:, last] + got1[:, last].astype(F32)
-        if i == 0:
-            block = keep0[...] + got0[...].astype(F32)
-        else:
-            block = keep1[:, :cols] + got1[:, :cols].astype(F32)
+        tail = keep2[:, last] + got2[:, last].astype(F32)
+        keep, got = ((keep0, got0), (keep0, got0), (keep1, got1), (keep2, got2))[i]
+        rows = slice(part, 2 * part) if i == 1 else slice(0, part)
+        block = keep[rows, :cols] + got[rows, :cols].astype(F32)
         raw = jnp.concatenate([tail, block], axis=1)
-        at = slice(i * rows, (i + 1) * rows)
+        at = slice(i * part, (i + 1) * part)
         latent = raw[:, :KVL]
         inverse = lax.rsqrt(jnp.sum(latent * latent, axis=1, keepdims=True) / KVL + norm_eps)
         out[at, :KVL] = (latent * inverse * gain[...]).astype(BF16)
@@ -492,19 +529,23 @@
     out[...] = ((first * share + second * other_share) / (share + other_share)).astype(BF16)
 
 
-def return_kernel(keep0, got0, keep1, got1, keep2, got2, low, high, send):
+def return_kernel(keep0, got0, keep1, got1, keep2, got2, keep3, got3, low, high, send):
     rows, cols = low.shape
-    for i in range(2):
-        near = slice(i * rows, (i + 1) * rows)
-        keep, got = (keep0, got0) if i == 0 else (keep1, got1)
-        first = keep[:rows, :cols] + got[:rows, :cols].astype(F32)
-        second = keep2[near, :] + got2[near, :].astype(F32)
-        if i == 0:
-            low[...] = first
-            high[...] = second
+    half = rows // 2
+    part = keep1.shape[0]
+    for i in range(4):
+        keep, got = ((keep0, got0), (keep0, got0), (keep1, got1), (keep2, got2))[i]
+        start = part if i == 1 else 0
+        from_rows, at = slice(start, start + half), slice(i * half, (i + 1) * half)
+        first = keep[from_rows, :cols] + got[from_rows, :cols].astype(F32)
+        second = keep3[at, :] + got3[at, :].astype(F32)
+        if i < 2:
+            low[at, :] = first
+            high[at, :] = second
         else:
-            send[:, :cols] = first.astype(BF16)
-            send[:, cols:] = second.astype(BF16)
+            at = slice((i - 2) * half, (i - 1) * half)
+            send[at, :cols] = first.astype(BF16)
+            send[at, cols:] = second.astype(BF16)
 
 
 def query_kernel(ids, low, high, got, gain, *refs):
@@ -529,12 +570,15 @@
 
 def place_kernel(ids, *refs):
     gots, out = refs[:-1], refs[-1]
-    rows = gots[0].shape[0]
+    half = gots[0].shape[0] // 2
+    chunk = out.shape[0] // 2
     lane = 2 * ids[3] + ids[1]
     for k, got in enumerate(gots):
         source = jnp.bitwise_xor(lane, k)
-        order = 2 * (source % 2) + source // 2
-        out[pl.ds(pl.multiple_of(order * rows, 32), rows), :] = got[...]
+        start = (source % 2) * (2 * half) + (source // 2) * half
+        for c in range(2):
+            at = pl.ds(pl.multiple_of(c * chunk + start, 16), half)
+            out[at, :] = got[c * half : (c + 1) * half, :]
 
 
 def call(kernel, shapes, specs, args, scratch=()):
@@ -603,11 +647,17 @@
     tables = jnp.pad(
         jnp.concatenate(tables, axis=0), ((0, 8 - n), (0, -packed.shape[1] % 128))
     )
-    x_far = lax.ppermute(hidden_x, DEC, partners)
-    held = lax.optimization_barrier((pieces[0], pieces[1], a_z[0]))
+    x_far = []
+    for c in range(2):
+        x_far.append(lax.ppermute(hidden_x[c * rows : (c + 1) * rows], DEC, partners))
+    direct = split // 2
+    held = lax.optimization_barrier(
+        (pieces[0][direct:], pieces[1], weight[:direct], a_z[0])
+    )
     for p in (1, 0):
         a_y[p] = swap(a_z[p], GRP)
         b_z[p] = lax.ppermute(held[p], DEC, [(1, 2), (2, 1)])
+    b_whole = lax.ppermute(held[2], DEC, [(1, 2), (2, 1)])
     for p in (1, 0):
         b_y[p] = lax.ppermute(b_z[p], (GRP, DEC), inner)
     query = dec_query.reshape(queries, KVW)
@@ -622,7 +672,8 @@
     old_far = lax.ppermute(old, DEC, partners)
 
     partner = index + 1 - 2 * (index % 2)
-    place = core * rows + jnp.arange(rows, dtype=jnp.int32)
+    place = jnp.arange(rows, dtype=jnp.int32)
+    place = place + core * quarter + (place // quarter) * quarter
     positions = jnp.concatenate([index * tokens + place, partner * tokens + place]).astype(F32)
     pair = jnp.arange(ROPE, dtype=jnp.int32) // 2
     frequency = jnp.power(F32(10000.0), -(2 * pair).astype(F32) / ROPE)
@@ -635,47 +686,51 @@
     a_refs = (a_z[0], a_y[0], a_z[1], a_y[1])
     keys = cols - cut
     wide = -(-cut // 128) * 128
-    send, kept0 = project(near_kernel, cols, (early_ids, hidden_x, weight, *a_refs))
-    other0 = swap(send, TP)
-    send0, keep0 = call(
-        cross_near_kernel,
-        [shaped(rows, cols, kind=BF16), shaped(rows, cols)],
-        [SMEM, VMEM, VMEM],
-        (ids, kept0, other0),
-    )
-    got0 = swap(send0, STG)
-    send, kept1 = project(
-        functools.partial(far_kernel, keys),
-        cols + 2 * keys,
-        (ids, hidden_x, x_far, weight, *a_refs, b_z[1], b_y[1]),
-    )
-    other1 = swap(send, TP)
-    send1, keep1 = call(
-        functools.partial(cross_far_kernel, cols),
-        [shaped(rows, cols + 2 * keys, kind=BF16), shaped(rows, cols + 2 * keys)],
-        [SMEM, VMEM, VMEM],
-        (ids, kept1, other1),
-    )
-    got1 = swap(send1, STG)
-    send, kept2 = project(
-        functools.partial(rest_kernel, keys),
+    last = cols + 4 * keys
+
+    def crossed(kernel, rows, width, args):
+        send, kept = project(kernel, rows, width, args)
+        other = swap(send, TP)
+        send, keep = call(
+            functools.partial(cross_kernel, cols, quarter),
+            [shaped(rows, width, kind=BF16), shaped(rows, width)],
+            [SMEM, VMEM, VMEM],
+            (ids, kept, other),
+        )
+        return (keep, swap(send, STG)), (kept, other)
+
+    near, _ = crossed(
+        functools.partial(near_kernel, rows), rows, cols, (early_ids, hidden_x, weight, *a_refs)
+    )
+    far, _ = crossed(
+        functools.partial(far_kernel, rows), quarter, cols, (ids, x_far[0], weight, *a_refs)
+    )
+    final, final_sums = crossed(
+        functools.partial(last_kernel, rows, keys),
+        quarter,
+        last,
+        (ids, hidden_x, *x_far, weight, *a_refs, b_z[1], b_y[1]),
+    )
+    send, kept = project(
+        functools.partial(rest_kernel, rows, keys),
+        rows,
         2 * wide,
-        (ids, hidden_x, x_far, *a_refs, b_z[0], b_y[0], b_z[1], b_y[1]),
-    )
-    other2 = swap(send, TP)
-    send2, keep2 = call(
+        (ids, hidden_x, *x_far, *a_refs, b_whole, b_z[0], b_y[0], b_z[1], b_y[1]),
+    )
+    other = swap(send, TP)
+    send, kept = call(
         functools.partial(cross_rest_kernel, cut, keys),
         [shaped(rows, cols, kind=BF16), shaped(rows, cols)],
         [SMEM] + [VMEM] * 4,
-        (ids, kept2, other2, kept1, other1),
-    )
-    got2 = swap(send2, STG)
+        (ids, kept, other, *final_sums),
+    )
+    rest = (kept, swap(send, STG))
 
     key_rows = call(
         functools.partial(keys_kernel, keys),
         shaped(tokens, KVW, kind=BF16),
-        [VMEM] * 8,
-        (keep0, got0, keep1, got1, cos, sin, turn, kv_scale),
+        [VMEM] * 10,
+        (*near, *far, *final, cos, sin, turn, kv_scale),
     )
     far_keys = swap(key_rows, TP)
     part_out = call(
@@ -697,8 +752,8 @@
     low, high, back = call(
         return_kernel,
         [shaped(quarter, cols), shaped(quarter, cols), shaped(quarter, 2 * cols, kind=BF16)],
-        [VMEM] * 6,
-        (keep0, got0, keep1, got1, keep2, got2),
+        [VMEM] * 8,
+        (*near, *far, *final, *rest),
     )
     back = lax.ppermute(back, DEC, partners)
     lanes = 4

time: 160 us -> 166 us (1.038)
  the two profiles are of different devices: /device:TPU:9 before, /device:TPU:0 now
where the time goes in v3:
time: 166 us
  waiting for transfers between devices  77.6 us (47%)
  starting transfers between devices  47.3 us (28%)
  Pallas kernels  25.5 us (15%)
  local copies, waits for them, and re-layouts  12.4 us (7%)
  other arithmetic  1.73 us (1%)
    ppermute x2, waiting for transfers between devices, pairs_step(): a_z[p] = lax.ppermute(pieces[p], DEC, [(0, 2), (3, 1), (1, 0), (2, 3)])  39.2 us
    ppermute x11, waiting for transfers between devices, swap(): return lax.ppermute(a, axis, [(0, 1), (1, 0)])  28.8 us
    ppermute x3, starting transfers between devices, pairs_step(): lax.ppermute(packed, DEC, [((i + s) % n, i) for i in range(n)])  20.7 us
    pallas_call x4, Pallas kernels, project(): pl.pallas_call(kernel, in_specs=[SMEM] + [VMEM] * (len(args) - 1), out_sp...  14.4 us
    pallas_call x12, Pallas kernels, call(): pl.pallas_call(kernel, scratch_shapes=scratch, out_shape=shapes, in_specs...  11.2 us
    ppermute x3, waiting for transfers between devices, pairs_step(): spread.append(lax.ppermute(part_out, DEC, pairs))  8.64 us
    ppermute x11, starting transfers between devices, swap(): return lax.ppermute(a, axis, [(0, 1), (1, 0)])  8.28 us
    ppermute x2, starting transfers between devices, pairs_step(): a_z[p] = lax.ppermute(pieces[p], DEC, [(0, 2), (3, 1), (1, 0), (2, 3)])  5.69 us
  transfers between devices with their start and end apart: 31, of which 8 were waited for; matrix products, arithmetic and copies ran while one was open for 7% of the time, Pallas kernels for 12%

profile of v3, /device:TPU:0, one launch (start us, length us, event | category | flops | bytes accessed | tf_op | source)
XLA Modules:
  0.0 165.6 jit_solution(2159428970178637547)
XLA Ops:
  0.6 1.2 dynamic-slice_bitcast_fusion.1
  1.8 4.1 %collective-permute-start = (bf16[256,896]{1,0:T(8,128)(2,1)S(1)}, bf16[256,896]{1,0:T(8,128)(2,1)}, u32[]{:S(2)}, u32[]{:S(2)}) collective-permute-start(bf16[256,896]{1,0:T(8,128)(2,1)S(1)} %dynamic-slice_bitcast_fusion.1), channel_id=1, source_target_pairs={{0,8},{12,4},{4,0},{8,12},{1,9},{13,5},{5,1},{9,13},{2,10},{14,6},... | collective-permute-start | bytes 1376264 | tf_op jit(solution)/shard_map/ppermute | solution.py:640
  6.0 2.5 %fusion.8 = (bf16[192,1792]{1,0:T(8,128)(2,1)}, bf16[192,1792]{1,0:T(8,128)(2,1)}) fusion(bf16[384,1792]{1,0:T(8,128)(2,1)} %x_ref.5), kind=kLoop, calls=%fused_computation.25 | loop fusion | bytes 2752512 | tf_op jit(solution)/shard_map/slice | solution.py:652
  8.5 2.0 %collective-permute-start.9 = (bf16[192,1792]{1,0:T(8,128)(2,1)}, bf16[192,1792]{1,0:T(8,128)(2,1)}, u32[]{:S(2)}, u32[]{:S(2)}) collective-permute-start(bf16[192,1792]{1,0:T(8,128)(2,1)} %get-tuple-element.70), channel_id=1, source_target_pairs={{0,4},{4,0},{8,12},{12,8},{1,5},{5,1},{9,13},{13,9},{2,6},{6,2},{1... | collective-permute-start | bytes 2064392 | tf_op jit(solution)/shard_map/ppermute | solution.py:652
  10.5 0.8 dynamic-slice_bitcast_fusion
  11.3 1.6 collective-permute-start.2
  12.9 0.7 slice.16
  13.6 0.8 slice.17
  14.4 2.5 %collective-permute-done.z0 = bf16[256,896]{1,0:T(8,128)(2,1)} collective-permute-done((bf16[256,896]{1,0:T(8,128)(2,1)S(1)}, bf16[256,896]{1,0:T(8,128)(2,1)}, u32[]{:S(2)}, u32[]{:S(2)}) %collective-permute-start) | collective-permute-done | bytes 458784 | tf_op jit(solution)/shard_map/ppermute | solution.py:640
  16.9 1.4 collective-permute-start.10
  18.3 0.7 collective-permute-start.15
  19.0 36.8 %collective-permute-done.2.z1 = bf16[272,896]{1,0:T(8,128)(2,1)} collective-permute-done((bf16[272,896]{1,0:T(8,128)(2,1)}, bf16[272,896]{1,0:T(8,128)(2,1)}, u32[]{:S(2)}, u32[]{:S(2)}) %collective-permute-start.2) | collective-permute-done | bytes 487456 | tf_op jit(solution)/shard_map/ppermute | solution.py:640
  55.8 1.5 collective-permute-start.3
  57.3 1.5 collective-permute-start.11
  59.4 0.7 collective-permute-start.14
  61.5 0.8 multiply_sine_fusion
  62.3 15.6 %collective-permute-done.1.y0 = bf16[256,896]{1,0:T(8,128)(2,1)S(1)} collective-permute-done((bf16[256,896]{1,0:T(8,128)(2,1)}, bf16[256,896]{1,0:T(8,128)(2,1)S(1)}, u32[]{:S(2)}, u32[]{:S(2)}) %collective-permute-start.1) | collective-permute-done | bytes 458784 | tf_op jit(solution)/shard_map/ppermute | solution.py:198
  77.9 5.0 %shard_map.120 = (f32[192,1024]{1,0:T(8,128)}, f32[192,1024]{1,0:T(8,128)S(1)}) custom-call(s32[4]{0:T(128)S(1)} %pad_add_fusion.1.ids, bf16[384,1792]{1,0:T(8,128)(2,1)S(1)} %copy-done.1, bf16[192,1792]{1,0:T(8,128)(2,1)} %collective-permute-done.6.far_ref.far0, bf16[192,1792]{1,0:T(8,128)(2,1)} %collective-permute-done.9.far1, ...), custom_call_target="tpu_custom_call" | custom-call | flops 1409286144 | bytes 1572864 | tf_op jit(solution)/shard_map/pallas_call | solution.py:316
  82.9 3.0 %shard_map.114 = (f32[192,528]{1,0:T(8,128)S(1)}, f32[192,528]{1,0:T(8,128)S(1)}) custom-call(s32[4]{0:T(128)S(1)} %pad_add_fusion.1.ids, bf16[384,1792]{1,0:T(8,128)(2,1)S(1)} %copy-done.1, bf16[528,1792]{1,0:T(8,128)(2,1)S(1)} %bitcast.17, bf16[256,896]{1,0:T(8,128)(2,1)} %collective-permute-done.z0, bf16[256,896]{1,0:T(8,128)(2,1)S(1)} %collective-permute-done.1.y0, ...), custom_call_target="tpu_custom_call" | custom-call | flops 726663168 | bytes 811008 | tf_op jit(solution)/shard_map/pallas_call | solution.py:316
  86.3 3.8 %shard_map.118 = (f32[96,720]{1,0:T(8,128)S(1)}, f32[96,720]{1,0:T(8,128)S(1)}) custom-call(s32[4]{0:T(128)S(1)} %pad_add_fusion.1.ids, bf16[384,1792]{1,0:T(8,128)(2,1)S(1)} %copy-done.1, bf16[192,1792]{1,0:T(8,128)(2,1)} %collective-permute-done.6.far_ref.far0, bf16[192,1792]{1,0:T(8,128)(2,1)} %collective-permute-done.9.far1, ...), custom_call_target="tpu_custom_call" | custom-call | flops 495452160 | bytes 552960 | tf_op jit(solution)/shard_map/pallas_call | solution.py:316
  90.4 2.5 %shard_map.116 = (f32[96,528]{1,0:T(8,128)S(1)}, f32[96,528]{1,0:T(8,128)S(1)}) custom-call(s32[4]{0:T(128)S(1)} %pad_add_fusion.1.ids, bf16[192,1792]{1,0:T(8,128)(2,1)} %collective-permute-done.6.far_ref.far0, bf16[528,1792]{1,0:T(8,128)(2,1)S(1)} %bitcast.19, bf16[256,896]{1,0:T(8,128)(2,1)} %collective-permute-done.z0, ...), custom_call_target="tpu_custom_call" | custom-call | flops 363331584 | bytes 405504 | tf_op jit(solution)/shard_map/pallas_call | solution.py:316
  93.9 1.5 collective-permute-start.5
  97.3 1.5 collective-permute-start.8
  98.8 9.1 %collective-permute-done.8.got1 = bf16[96,528]{1,0:T(8,128)(2,1)S(1)} collective-permute-done((bf16[96,528]{1,0:T(8,128)(2,1)S(1)}, bf16[96,528]{1,0:T(8,128)(2,1)S(1)}, u32[]{:S(2)}, u32[]{:S(2)}) %collective-permute-start.8) | collective-permute-done | bytes 101408 | tf_op jit(solution)/shard_map/ppermute | solution.py:198
  107.9 0.7 shard_map.125.k0_ref
  108.6 0.7 copy-done.5
  109.3 1.4 copy.13
  110.7 1.3 reshape.65
  112.6 0.8 add_bitcast_fusion
  113.4 3.5 %collective-permute-start.24 = (s32[1,60]{1,0:T(1,128)S(1)}, s32[1,60]{1,0:T(1,128)S(1)}, u32[]{:S(2)}, u32[]{:S(2)}) collective-permute-start(s32[1,60]{1,0:T(1,128)S(1)} %add_bitcast_fusion), channel_id=1, source_target_pairs={{4,0},{8,4},{12,8},{0,12},{5,1},{9,5},{13,9},{1,13},{6,2},{10,6},{... | collective-permute-start | bytes 728 | tf_op jit(solution)/shard_map/ppermute | solution.py:646
  116.8 15.7 %collective-permute-start.25 = (s32[1,60]{1,0:T(1,128)S(1)}, s32[1,60]{1,0:T(1,128)S(1)}, u32[]{:S(2)}, u32[]{:S(2)}) collective-permute-start(s32[1,60]{1,0:T(1,128)S(1)} %add_bitcast_fusion), channel_id=1, source_target_pairs={{8,0},{12,4},{0,8},{4,12},{9,1},{13,5},{1,9},{5,13},{10,2},{14,6},... | collective-permute-start | bytes 728 | tf_op jit(solution)/shard_map/ppermute | solution.py:646
  132.5 1.6 collective-permute-start.26
  134.1 0.7 pad.9.own_ref
  134.8 1.1 copy-done.8
  135.9 1.4 shard_map.121
  137.3 1.6 collective-permute-start.18
  138.9 1.7 %shard_map.126 = (bf16[128,640]{1,0:T(8,128)(2,1)S(1)}, f32[8,768]{1,0:T(8,128)S(1)}) custom-call(s32[4]{0:T(128)S(1)} %pad_add_fusion.1.ids, s32[8,128]{1,0:T(8,128)S(1)} %pad.8.tab_ref, bf16[128,576]{1,0:T(8,128)(2,1)S(1)} %bitcast.21, bf16[1024,576]{1,0:T(8,128)(2,1)S(1)} %bitcast.20, bf16[16,576]{1,0:T(8,128)(2,1)S(1)} %pad.9.own_ref), custom_call_target="tpu_custom_call" | custom-call | flops 20000000 | bytes 2000000 | tf_op jit(solution)/shard_map/pallas_call | solution.py:585
  140.7 4.2 %collective-permute-done.18.got3 = bf16[192,528]{1,0:T(8,128)(2,1)S(1)} collective-permute-done((bf16[192,528]{1,0:T(8,128)(2,1)S(1)}, bf16[192,528]{1,0:T(8,128)(2,1)S(1)}, u32[]{:S(2)}, u32[]{:S(2)}) %collective-permute-start.18) | collective-permute-done | bytes 202784 | tf_op jit(solution)/shard_map/ppermute | solution.py:198
  145.4 0.8 collective-permute-done.27.far_ref
  146.2 1.8 %shard_map.127.own = bf16[128,640]{1,0:T(8,128)(2,1)S(1)} custom-call(bf16[128,576]{1,0:T(8,128)(2,1)S(1)} %bitcast.22, bf16[384,576]{1,0:T(8,128)(2,1)S(1)} %shard_map.125.k0_ref, bf16[384,576]{1,0:T(8,128)(2,1)} %collective-permute-done.23.k1_ref, f32[8,768]{1,0:T(8,128)S(1)} %get-tuple-element.68.bias_ref, ...), custom_call_target="tpu_custom_call" | custom-call | flops 20000000 | bytes 2000000 | tf_op jit(solution)/shard_map/pallas_call | solution.py:585
  148.7 1.3 collective-permute-start.29
  150.0 1.3 collective-permute-start.30
  151.4 0.9 shard_map.123
  152.4 1.4 collective-permute-start.21
  154.2 3.5 %collective-permute-done.29.partner = bf16[128,640]{1,0:T(8,128)(2,1)S(1)} collective-permute-done((bf16[128,640]{1,0:T(8,128)(2,1)S(1)}, bf16[128,640]{1,0:T(8,128)(2,1)S(1)}, u32[]{:S(2)}, u32[]{:S(2)}) %collective-permute-start.29) | collective-permute-done | bytes 163872 | tf_op jit(solution)/shard_map/ppermute | solution.py:744
  157.8 5.1 %collective-permute-done.30.other = bf16[128,640]{1,0:T(8,128)(2,1)S(1)} collective-permute-done((bf16[128,640]{1,0:T(8,128)(2,1)S(1)}, bf16[128,640]{1,0:T(8,128)(2,1)S(1)}, u32[]{:S(2)}, u32[]{:S(2)}) %collective-permute-start.30) | collective-permute-done | bytes 163872 | tf_op jit(solution)/shard_map/ppermute | solution.py:744
  162.9 1.4 shard_map.128
  164.3 1.3 shard_map.124
  (80 shorter events, 7.9 us)
Async XLA Ops:
  0.6 9.9 %copy-start = (bf16[1792,528]{0,1:T(8,128)(2,1)S(1)}, bf16[1792,528]{0,1:T(8,128)(2,1)}, u32[]{:S(2)}) copy-start(bf16[1792,528]{0,1:T(8,128)(2,1)} %param.11) | copy-start | bytes 5677060
  1.8 15.0 %collective-permute-start = (bf16[256,896]{1,0:T(8,128)(2,1)S(1)}, bf16[256,896]{1,0:T(8,128)(2,1)}, u32[]{:S(2)}, u32[]{:S(2)}) collective-permute-start(bf16[256,896]{1,0:T(8,128)(2,1)S(1)} %dynamic-slice_bitcast_fusion.1), channel_id=1, source_target_pairs={{0,8},{12,4},{4,0},{8,12},{1,9},{13,5},{5,1},{9,13},{2,10},{14,6},... | collective-permute-start | bytes 1376264 | tf_op jit(solution)/shard_map/ppermute | solution.py:640
  8.5 50.3 %copy-start.14 = (f32[1536]{0:T(1024)S(1)}, f32[1536]{0:T(1024)}, u32[]{:S(2)}) copy-start(f32[1536]{0:T(1024)} %param.12) | copy-start | bytes 18436
  8.5 69.4 %copy-start.1 = (bf16[384,1792]{1,0:T(8,128)(2,1)S(1)}, bf16[384,1792]{1,0:T(8,128)(2,1)}, u32[]{:S(2)}) copy-start(bf16[384,1792]{1,0:T(8,128)(2,1)} %x_ref.5) | copy-start | bytes 4128772
  8.5 50.9 %collective-permute-start.6 = (bf16[192,1792]{1,0:T(8,128)(2,1)}, bf16[192,1792]{1,0:T(8,128)(2,1)}, u32[]{:S(2)}, u32[]{:S(2)}) collective-permute-start(bf16[192,1792]{1,0:T(8,128)(2,1)} %get-tuple-element.71), channel_id=1, source_target_pairs={{0,4},{4,0},{8,12},{12,8},{1,5},{5,1},{9,13},{13,9},{2,6},{6,2},{1... | collective-permute-start | bytes 2064392 | tf_op jit(solution)/shard_map/ppermute | solution.py:652
  8.5 51.6 %collective-permute-start.9 = (bf16[192,1792]{1,0:T(8,128)(2,1)}, bf16[192,1792]{1,0:T(8,128)(2,1)}, u32[]{:S(2)}, u32[]{:S(2)}) collective-permute-start(bf16[192,1792]{1,0:T(8,128)(2,1)} %get-tuple-element.70), channel_id=1, source_target_pairs={{0,4},{4,0},{8,12},{12,8},{1,5},{5,1},{9,13},{13,9},{2,6},{6,2},{1... | collective-permute-start | bytes 2064392 | tf_op jit(solution)/shard_map/ppermute | solution.py:652
  11.3 44.5 %collective-permute-start.2 = (bf16[272,896]{1,0:T(8,128)(2,1)}, bf16[272,896]{1,0:T(8,128)(2,1)}, u32[]{:S(2)}, u32[]{:S(2)}) collective-permute-start(bf16[272,896]{1,0:T(8,128)(2,1)} %dynamic-slice_bitcast_fusion), channel_id=1, source_target_pairs={{0,8},{12,4},{4,0},{8,12},{1,9},{13,5},{5,1},{9,13},{2,10},{14,6},... | collective-permute-start | bytes 1462280 | tf_op jit(solution)/shard_map/ppermute | solution.py:640
  16.9 40.4 %collective-permute-start.10 = (bf16[272,896]{1,0:T(8,128)(2,1)}, bf16[272,896]{1,0:T(8,128)(2,1)}, u32[]{:S(2)}, u32[]{:S(2)}) collective-permute-start(bf16[272,896]{1,0:T(8,128)(2,1)} %dynamic-slice_bitcast_fusion), channel_id=1, source_target_pairs={{4,8},{8,4},{5,9},{9,5},{6,10},{10,6},{7,11},{11,7},{20,24},{24,20... | collective-permute-start | bytes 1462280 | tf_op jit(solution)/shard_map/ppermute | solution.py:659
  18.3 42.5 %collective-permute-start.15 = (bf16[128,896]{1,0:T(8,128)(2,1)}, bf16[128,896]{1,0:T(8,128)(2,1)S(1)}, u32[]{:S(2)}, u32[]{:S(2)}) collective-permute-start(bf16[128,896]{1,0:T(8,128)(2,1)} %slice.16), channel_id=1, source_target_pairs={{4,8},{8,4},{5,9},{9,5},{6,10},{10,6},{7,11},{11,7},{20,24},{24,20... | collective-permute-start | bytes 688136 | tf_op jit(solution)/shard_map/ppermute | solution.py:659
  55.8 22.1 %collective-permute-start.3 = (bf16[272,896]{1,0:T(8,128)(2,1)}, bf16[272,896]{1,0:T(8,128)(2,1)}, u32[]{:S(2)}, u32[]{:S(2)}) collective-permute-start(bf16[272,896]{1,0:T(8,128)(2,1)} %collective-permute-done.2.z1), channel_id=1, source_target_pairs={{0,16},{16,0},{1,17},{17,1},{2,18},{18,2},{3,19},{19,3},{4,20},{20... | collective-permute-start | bytes 1462280 | tf_op jit(solution)/shard_map/ppermute | solution.py:198
  57.3 20.6 %collective-permute-start.11 = (bf16[272,896]{1,0:T(8,128)(2,1)}, bf16[272,896]{1,0:T(8,128)(2,1)}, u32[]{:S(2)}, u32[]{:S(2)}) collective-permute-start(bf16[272,896]{1,0:T(8,128)(2,1)} %collective-permute-done.10.bz1), channel_id=1, source_target_pairs={{4,20},{8,24},{20,4},{24,8},{5,21},{9,25},{21,5},{25,9},{6,22},{10... | collective-permute-start | bytes 1462280 | tf_op jit(solution)/shard_map/ppermute | solution.py:662
  59.4 18.5 %collective-permute-start.14 = (bf16[128,1792]{1,0:T(8,128)(2,1)}, bf16[128,1792]{1,0:T(8,128)(2,1)S(1)}, u32[]{:S(2)}, u32[]{:S(2)}) collective-permute-start(bf16[128,1792]{1,0:T(8,128)(2,1)} %slice.17), channel_id=1, source_target_pairs={{4,8},{8,4},{5,9},{9,5},{6,10},{10,6},{7,11},{11,7},{20,24},{24,20... | collective-permute-start | bytes 1376264 | tf_op jit(solution)/shard_map/ppermute | solution.py:660
  60.1 17.7 %collective-permute-start.1 = (bf16[256,896]{1,0:T(8,128)(2,1)}, bf16[256,896]{1,0:T(8,128)(2,1)S(1)}, u32[]{:S(2)}, u32[]{:S(2)}) collective-permute-start(bf16[256,896]{1,0:T(8,128)(2,1)} %collective-permute-done.z0), channel_id=1, source_target_pairs={{0,16},{16,0},{1,17},{17,1},{2,18},{18,2},{3,19},{19,3},{4,20},{20... | collective-permute-start | bytes 1376264 | tf_op jit(solution)/shard_map/ppermute | solution.py:198
  60.8 17.0 %collective-permute-start.16 = (bf16[128,896]{1,0:T(8,128)(2,1)S(1)}, bf16[128,896]{1,0:T(8,128)(2,1)S(1)}, u32[]{:S(2)}, u32[]{:S(2)}) collective-permute-start(bf16[128,896]{1,0:T(8,128)(2,1)S(1)} %collective-permute-done.15.bz0), channel_id=1, source_target_pairs={{4,20},{8,24},{20,4},{24,8},{5,21},{9,25},{21,5},{25,9},{6,22},{10... | collective-permute-start | bytes 688136 | tf_op jit(solution)/shard_map/ppermute | solution.py:662
  82.9 3.0 %copy-start.7 = (f32[192,1024]{1,0:T(8,128)}, f32[192,1024]{1,0:T(8,128)S(1)}, u32[]{:S(2)}) copy-start(f32[192,1024]{1,0:T(8,128)S(1)} %get-tuple-element.52.kept) | copy-start | bytes 2359300
  82.9 51.9 %collective-permute-start.17 = (f32[192,1024]{1,0:T(8,128)}, f32[192,1024]{1,0:T(8,128)}, u32[]{:S(2)}, u32[]{:S(2)}) collective-permute-start(f32[192,1024]{1,0:T(8,128)} %get-tuple-element.53), channel_id=1, source_target_pairs={{0,1},{1,0},{2,3},{3,2},{4,5},{5,4},{6,7},{7,6},{8,9},{9,8},{10,11... | collective-permute-start | bytes 2359304 | tf_op jit(solution)/shard_map/ppermute | solution.py:198
  86.0 7.3 %collective-permute-start.4 = (f32[192,528]{1,0:T(8,128)S(1)}, f32[192,528]{1,0:T(8,128)S(1)}, u32[]{:S(2)}, u32[]{:S(2)}) collective-permute-start(f32[192,528]{1,0:T(8,128)S(1)} %get-tuple-element.38), channel_id=1, source_target_pairs={{0,1},{1,0},{2,3},{3,2},{4,5},{5,4},{6,7},{7,6},{8,9},{9,8},{10,11... | collective-permute-start | bytes 1216520 | tf_op jit(solution)/shard_map/ppermute | solution.py:198
  90.1 5.4 %copy-start.3 = (f32[96,720]{1,0:T(8,128)}, f32[96,720]{1,0:T(8,128)S(1)}, u32[]{:S(2)}) copy-start(f32[96,720]{1,0:T(8,128)S(1)} %get-tuple-element.46.kept.kept_last) | copy-start | bytes 829444
  90.1 5.3 %collective-permute-start.12 = (f32[96,720]{1,0:T(8,128)S(1)}, f32[96,720]{1,0:T(8,128)S(1)}, u32[]{:S(2)}, u32[]{:S(2)}) collective-permute-start(f32[96,720]{1,0:T(8,128)S(1)} %get-tuple-element.47), channel_id=1, source_target_pairs={{0,1},{1,0},{2,3},{3,2},{4,5},{5,4},{6,7},{7,6},{8,9},{9,8},{10,11... | collective-permute-start | bytes 829448 | tf_op jit(solution)/shard_map/ppermute | solution.py:198
  92.9 15.0 %copy-start.13 = (f32[512]{0:T(512)S(1)}, f32[512]{0:T(512)}, u32[]{:S(2)}) copy-start(f32[512]{0:T(512)} %param.13) | copy-start | bytes 6148
  93.0 3.7 %collective-permute-start.7 = (f32[96,528]{1,0:T(8,128)S(1)}, f32[96,528]{1,0:T(8,128)S(1)}, u32[]{:S(2)}, u32[]{:S(2)}) collective-permute-start(f32[96,528]{1,0:T(8,128)S(1)} %get-tuple-element.42), channel_id=1, source_target_pairs={{0,1},{1,0},{2,3},{3,2},{4,5},{5,4},{6,7},{7,6},{8,9},{9,8},{10,11... | collective-permute-start | bytes 608264 | tf_op jit(solution)/shard_map/ppermute | solution.py:198
  93.9 18.1 %copy-start.15 = (s32[1,4,8]{2,1,0:T(4,128)S(1)}, s32[1,4,8]{2,1,0:T(4,128)}, u32[]{:S(2)}) copy-start(s32[1,4,8]{2,1,0:T(4,128)} %param.16) | copy-start | bytes 388
  93.9 14.0 %collective-permute-start.5 = (bf16[192,528]{1,0:T(8,128)(2,1)S(1)}, bf16[192,528]{1,0:T(8,128)(2,1)S(1)}, u32[]{:S(2)}, u32[]{:S(2)}) collective-permute-start(bf16[192,528]{1,0:T(8,128)(2,1)S(1)} %get-tuple-element.40), channel_id=1, source_target_pairs={{0,2},{2,0},{1,3},{3,1},{4,6},{6,4},{5,7},{7,5},{8,10},{10,8},{9,1... | collective-permute-start | bytes 608264 | tf_op jit(solution)/shard_map/ppermute | solution.py:198
  96.1 38.7 %copy-start.4 = (f32[96,720]{1,0:T(8,128)S(1)}, f32[96,720]{1,0:T(8,128)}, u32[]{:S(2)}) copy-start(f32[96,720]{1,0:T(8,128)} %copy-done.3) | copy-start | bytes 829444
  96.1 11.8 %collective-permute-start.13 = (bf16[96,720]{1,0:T(8,128)(2,1)S(1)}, bf16[96,720]{1,0:T(8,128)(2,1)S(1)}, u32[]{:S(2)}, u32[]{:S(2)}) collective-permute-start(bf16[96,720]{1,0:T(8,128)(2,1)S(1)} %get-tuple-element.49), channel_id=1, source_target_pairs={{0,2},{2,0},{1,3},{3,1},{4,6},{6,4},{5,7},{7,5},{8,10},{10,8},{9,1... | collective-permute-start | bytes 414728 | tf_op jit(solution)/shard_map/ppermute | solution.py:198
  97.3 10.6 %collective-permute-start.8 = (bf16[96,528]{1,0:T(8,128)(2,1)S(1)}, bf16[96,528]{1,0:T(8,128)(2,1)S(1)}, u32[]{:S(2)}, u32[]{:S(2)}) collective-permute-start(bf16[96,528]{1,0:T(8,128)(2,1)S(1)} %get-tuple-element.44), channel_id=1, source_target_pairs={{0,2},{2,0},{1,3},{3,1},{4,6},{6,4},{5,7},{7,5},{8,10},{10,8},{9,1... | collective-permute-start | bytes 304136 | tf_op jit(solution)/shard_map/ppermute | solution.py:198
  107.9 0.7 copy-start.10
  107.9 31.0 %copy-start.2 = (bf16[32,32,576]{2,1,0:T(8,128)(2,1)S(1)}, bf16[32,32,576]{2,1,0:T(8,128)(2,1)}, u32[]{:S(2)}) copy-start(bf16[32,32,576]{2,1,0:T(8,128)(2,1)} %param.14) | copy-start | bytes 3538948
  108.6 0.7 copy-start.5
  109.3 36.9 %collective-permute-start.23 = (bf16[384,576]{1,0:T(8,128)(2,1)S(1)}, bf16[384,576]{1,0:T(8,128)(2,1)}, u32[]{:S(2)}, u32[]{:S(2)}) collective-permute-start(bf16[384,576]{1,0:T(8,128)(2,1)S(1)} %shard_map.125.k0_ref), channel_id=1, source_target_pairs={{0,1},{1,0},{2,3},{3,2},{4,5},{5,4},{6,7},{7,6},{8,9},{9,8},{10,11... | collective-permute-start | bytes 1327112 | tf_op jit(solution)/shard_map/ppermute | solution.py:198
  112.6 32.3 %copy-start.6 = (f32[96,528]{1,0:T(8,128)S(1)}, f32[96,528]{1,0:T(8,128)}, u32[]{:S(2)}) copy-start(f32[96,528]{1,0:T(8,128)} %copy-done.5) | copy-start | bytes 608260
  113.4 25.5 %collective-permute-start.24 = (s32[1,60]{1,0:T(1,128)S(1)}, s32[1,60]{1,0:T(1,128)S(1)}, u32[]{:S(2)}, u32[]{:S(2)}) collective-permute-start(s32[1,60]{1,0:T(1,128)S(1)} %add_bitcast_fusion), channel_id=1, source_target_pairs={{4,0},{8,4},{12,8},{0,12},{5,1},{9,5},{13,9},{1,13},{6,2},{10,6},{... | collective-permute-start | bytes 728 | tf_op jit(solution)/shard_map/ppermute | solution.py:646
  116.8 22.0 %collective-permute-start.25 = (s32[1,60]{1,0:T(1,128)S(1)}, s32[1,60]{1,0:T(1,128)S(1)}, u32[]{:S(2)}, u32[]{:S(2)}) collective-permute-start(s32[1,60]{1,0:T(1,128)S(1)} %add_bitcast_fusion), channel_id=1, source_target_pairs={{8,0},{12,4},{0,8},{4,12},{9,1},{13,5},{1,9},{5,13},{10,2},{14,6},... | collective-permute-start | bytes 728 | tf_op jit(solution)/shard_map/ppermute | solution.py:646
  132.5 6.3 %collective-permute-start.26 = (s32[1,60]{1,0:T(1,128)S(1)}, s32[1,60]{1,0:T(1,128)S(1)}, u32[]{:S(2)}, u32[]{:S(2)}) collective-permute-start(s32[1,60]{1,0:T(1,128)S(1)} %add_bitcast_fusion), channel_id=1, source_target_pairs={{12,0},{0,4},{4,8},{8,12},{13,1},{1,5},{5,9},{9,13},{14,2},{2,6},{... | collective-permute-start | bytes 728 | tf_op jit(solution)/shard_map/ppermute | solution.py:646
  134.8 1.1 copy-start.8
  135.9 3.0 %copy-start.9 = (bf16[4,32,576]{2,1,0:T(8,128)(2,1)S(1)}, bf16[4,32,576]{2,1,0:T(8,128)(2,1)}, u32[]{:S(2)}) copy-start(bf16[4,32,576]{2,1,0:T(8,128)(2,1)} %param.18) | copy-start | bytes 442372
  135.9 9.0 %copy-start.11 = (bf16[96,720]{1,0:T(8,128)(2,1)S(1)}, bf16[96,720]{1,0:T(8,128)(2,1)}, u32[]{:S(2)}) copy-start(bf16[96,720]{1,0:T(8,128)(2,1)} %copy-done.10) | copy-start | bytes 414724
  137.3 7.6 %collective-permute-start.18 = (bf16[192,528]{1,0:T(8,128)(2,1)S(1)}, bf16[192,528]{1,0:T(8,128)(2,1)S(1)}, u32[]{:S(2)}, u32[]{:S(2)}) collective-permute-start(bf16[192,528]{1,0:T(8,128)(2,1)S(1)} %get-tuple-element.55), channel_id=1, source_target_pairs={{0,2},{2,0},{1,3},{3,1},{4,6},{6,4},{5,7},{7,5},{8,10},{10,8},{9,1... | collective-permute-start | bytes 608264 | tf_op jit(solution)/shard_map/ppermute | solution.py:198
  140.6 5.6 %collective-permute-start.27 = (bf16[128,640]{1,0:T(8,128)(2,1)S(1)}, bf16[128,640]{1,0:T(8,128)(2,1)S(1)}, u32[]{:S(2)}, u32[]{:S(2)}) collective-permute-start(bf16[128,640]{1,0:T(8,128)(2,1)S(1)} %get-tuple-element.69.old_ref), channel_id=1, source_target_pairs={{0,4},{4,0},{8,12},{12,8},{1,5},{5,1},{9,13},{13,9},{2,6},{6,2},{1... | collective-permute-start | bytes 491528 | tf_op jit(solution)/shard_map/ppermute | solution.py:672
  144.9 6.5 %copy-start.12 = (f32[1,1536]{1,0:T(1,128)S(1)}, f32[1,1536]{1,0:T(1,128)}, u32[]{:S(2)}) copy-start(f32[1,1536]{1,0:T(1,128)} %reshape.63.gain) | copy-start | bytes 18436
  145.0 6.3 %collective-permute-start.19 = (bf16[96,1056]{1,0:T(8,128)(2,1)S(1)}, bf16[96,1056]{1,0:T(8,128)(2,1)S(1)}, u32[]{:S(2)}, u32[]{:S(2)}) collective-permute-start(bf16[96,1056]{1,0:T(8,128)(2,1)S(1)} %get-tuple-element.58), channel_id=1, source_target_pairs={{0,4},{4,0},{8,12},{12,8},{1,5},{5,1},{9,13},{13,9},{2,6},{6,2},{1... | collective-permute-start | bytes 608264 | tf_op jit(solution)/shard_map/ppermute | solution.py:758
  148.1 5.8 %collective-permute-start.28 = (bf16[128,640]{1,0:T(8,128)(2,1)S(1)}, bf16[128,640]{1,0:T(8,128)(2,1)S(1)}, u32[]{:S(2)}, u32[]{:S(2)}) collective-permute-start(bf16[128,640]{1,0:T(8,128)(2,1)S(1)} %shard_map.127.own), channel_id=1, source_target_pairs={{4,12},{12,4},{5,13},{13,5},{6,14},{14,6},{7,15},{15,7},{20,28},{2... | collective-permute-start | bytes 491528 | tf_op jit(solution)/shard_map/ppermute | solution.py:744
  148.7 9.0 %collective-permute-start.29 = (bf16[128,640]{1,0:T(8,128)(2,1)S(1)}, bf16[128,640]{1,0:T(8,128)(2,1)S(1)}, u32[]{:S(2)}, u32[]{:S(2)}) collective-permute-start(bf16[128,640]{1,0:T(8,128)(2,1)S(1)} %shard_map.127.own), channel_id=1, source_target_pairs={{4,0},{12,8},{5,1},{13,9},{6,2},{14,10},{7,3},{15,11},{20,16},{28,... | collective-permute-start | bytes 491528 | tf_op jit(solution)/shard_map/ppermute | solution.py:744
  150.0 12.8 %collective-permute-start.30 = (bf16[128,640]{1,0:T(8,128)(2,1)S(1)}, bf16[128,640]{1,0:T(8,128)(2,1)S(1)}, u32[]{:S(2)}, u32[]{:S(2)}) collective-permute-start(bf16[128,640]{1,0:T(8,128)(2,1)S(1)} %shard_map.127.own), channel_id=1, source_target_pairs={{4,8},{12,0},{5,9},{13,1},{6,10},{14,2},{7,11},{15,3},{20,24},{28,... | collective-permute-start | bytes 491528 | tf_op jit(solution)/shard_map/ppermute | solution.py:744
  152.3 11.9 %collective-permute-start.20 = (bf16[96,384]{1,0:T(8,128)(2,1)S(1)}, bf16[96,384]{1,0:T(8,128)(2,1)S(1)}, u32[]{:S(2)}, u32[]{:S(2)}) collective-permute-start(bf16[96,384]{1,0:T(8,128)(2,1)S(1)} %get-tuple-element.61), channel_id=1, source_target_pairs={{0,1},{1,0},{2,3},{3,2},{4,5},{5,4},{6,7},{7,6},{8,9},{9,8},{10,11... | collective-permute-start | bytes 221192 | tf_op jit(solution)/shard_map/ppermute | solution.py:771
  152.4 11.9 %collective-permute-start.21 = (bf16[96,384]{1,0:T(8,128)(2,1)S(1)}, bf16[96,384]{1,0:T(8,128)(2,1)S(1)}, u32[]{:S(2)}, u32[]{:S(2)}) collective-permute-start(bf16[96,384]{1,0:T(8,128)(2,1)S(1)} %get-tuple-element.62), channel_id=1, source_target_pairs={{0,2},{1,3},{2,0},{3,1},{4,6},{5,7},{6,4},{7,5},{8,10},{9,11},{10,... | collective-permute-start | bytes 221192 | tf_op jit(solution)/shard_map/ppermute | solution.py:771
  153.8 10.4 %collective-permute-start.22 = (bf16[96,384]{1,0:T(8,128)(2,1)S(1)}, bf16[96,384]{1,0:T(8,128)(2,1)S(1)}, u32[]{:S(2)}, u32[]{:S(2)}) collective-permute-start(bf16[96,384]{1,0:T(8,128)(2,1)S(1)} %get-tuple-element.63), channel_id=1, source_target_pairs={{0,3},{1,2},{2,1},{3,0},{4,7},{5,6},{6,5},{7,4},{8,11},{9,10},{10,... | collective-permute-start | bytes 221192 | tf_op jit(solution)/shard_map/ppermute | solution.py:771

commit v4 on v2

--- a/solution.py
+++ b/solution.py
@@ -190,6 +190,7 @@
 SMEM = pl.BlockSpec(memory_space=pltpu.SMEM)
 VMEM_GRANT = 16 * 2**20
 GRP, DEC, STG, TP = "grp", "dec", "stg", "tp"
+TILE = 256
 F32 = jnp.float32
 BF16 = jnp.bfloat16
 
@@ -241,13 +242,9 @@
         start += z.shape[0]
 
 
-def secondary(ids, x_refs, a_part, b_part, at, send, keep, starts):
-    here, there = halves(ids, x_refs[0])
-    outer = is_outer(ids)
-    w_here = chosen(outer, a_part[0][at, :], b_part[0][at, :])
-    w_there = chosen(outer, a_part[1][at, :], b_part[1][at, :])
-    for x_ref, start in zip(x_refs, starts):
-        put(ids, dot_t(x_ref[:, here], w_here) + dot_t(x_ref[:, there], w_there), send, keep, start)
+def projected(ids, x_ref, w_here, w_there):
+    here, there = halves(ids, x_ref)
+    return dot_t(x_ref[:, here], w_here) + dot_t(x_ref[:, there], w_there)
 
 
 def near_kernel(ids, x_ref, own_ref, z0, y0, z1, y1, send, keep):
@@ -255,21 +252,30 @@
 
 
 def far_kernel(keys, ids, x_ref, far_ref, own_ref, z0, y0, z1, y1, bz1, by1, send, keep):
-    cols = own_ref.shape[0]
-    primary(ids, far_ref, own_ref, ((z0, y0), (z1, y1)), send, keep)
-    at = slice(z1.shape[0] - keys, None)
-    starts = (cols, cols + keys)
-    secondary(ids, (x_ref, far_ref), (z1, y1), (bz1, by1), at, send, keep, starts)
-
-
-def rest_kernel(keys, ids, x_ref, far_ref, z0, y0, z1, y1, bz0, by0, bz1, by1, send, keep):
-    head = z0.shape[0]
-    rest = z1.shape[0] - keys
-    wide = send.shape[1] // 2
-    xs = (x_ref, far_ref)
-    secondary(ids, xs, (z0, y0), (bz0, by0), slice(None), send, keep, (0, wide))
-    at = slice(0, rest)
-    secondary(ids, xs, (z1, y1), (bz1, by1), at, send, keep, (head, wide + head))
+    cols, head = own_ref.shape[0], z0.shape[0]
+    full = z1.shape[0] // TILE * TILE
+    outer = is_outer(ids)
+    here, there = halves(ids, x_ref)
+    primary(
+        ids, far_ref, own_ref, ((z0, y0), (z1.at[:full, :], y1.at[:full, :])), send, keep
+    )
+    at, left, own = slice(z1.shape[0] - keys, None), slice(full, None), slice(head + full, None)
+    k_here = chosen(outer, z1[at, :], bz1[at, :])
+    k_there = chosen(outer, y1[at, :], by1[at, :])
+    w_here = jnp.concatenate([chosen(outer, own_ref[own, here], z1[left, :]), k_here], axis=0)
+    w_there = jnp.concatenate([chosen(outer, own_ref[own, there], y1[left, :]), k_there], axis=0)
+    out = projected(ids, far_ref, w_here, w_there)
+    put(ids, out[:, : cols - head - full], send, keep, head + full)
+    put(ids, out[:, cols - head - full :], send, keep, cols + keys)
+    put(ids, projected(ids, x_ref, k_here, k_there), send, keep, cols)
+
+
+def rest_kernel(used, ids, x_ref, far_ref, z, y, bz, by, send, keep):
+    outer = is_outer(ids)
+    w_here = chosen(outer, z[:used, :], bz[:used, :])
+    w_there = chosen(outer, y[:used, :], by[:used, :])
+    put(ids, projected(ids, x_ref, w_here, w_there), send, keep, 0)
+    put(ids, projected(ids, far_ref, w_here, w_there), send, keep, send.shape[1] - used)
 
 
 def project(kernel, width, args):
@@ -285,6 +291,25 @@
         ),
         compiler_params=pltpu.CompilerParams(vmem_limit_bytes=VMEM_GRANT),
     )(*args)
+
+
+def share_kernel(ids, weight, out):
+    out[...] = weight[...]
+
+
+def share(ids, weight):
+    rows, feats = weight.shape
+    return pl.pallas_call(
+        share_kernel,
+        grid_spec=pltpu.PrefetchScalarGridSpec(
+            num_scalar_prefetch=1,
+            grid=(1,),
+            in_specs=[pl.BlockSpec((rows, feats // 2), lambda i, ids: (0, ids[0]))],
+            out_specs=pl.BlockSpec((rows, feats // 2), lambda i, ids: (0, 0)),
+        ),
+        out_shape=jax.ShapeDtypeStruct((rows, feats // 2), weight.dtype),
+        compiler_params=pltpu.CompilerParams(vmem_limit_bytes=VMEM_GRANT),
+    )(ids, weight)
 
 
 def turn_kernel(out):
@@ -408,16 +433,20 @@
     send[:, cols:] = both[:, cols:].astype(BF16)
 
 
-def cross_rest_kernel(cut, keys, ids, kept, got, kept_far, got_far, send, keep):
-    wide = kept.shape[1] // 2
+def cross_rest_kernel(
+    head, rest, keys, ids, kept_tail, got_tail, kept_head, got_head, kept_far, got_far, send, keep
+):
     cols = send.shape[1]
     stage = ids[3]
     for i in range(2):
-        at = slice(i * wide, i * wide + cut)
-        last = slice(cols + i * keys, cols + (i + 1) * keys)
-        block = jnp.concatenate(
-            [kept[:, at] + got[:, at], kept_far[:, last] + got_far[:, last]], axis=1
-        )
+        start = i * (kept_head.shape[1] - head)
+        at = slice(start, start + head)
+        first = kept_head[:, at] + got_head[:, at]
+        start = i * (kept_tail.shape[1] - rest)
+        at = slice(start, start + rest)
+        second = kept_tail[:, at] + got_tail[:, at]
+        at = slice(cols + i * keys, cols + (i + 1) * keys)
+        block = jnp.concatenate([first, second, kept_far[:, at] + got_far[:, at]], axis=1)
         half = block.shape[0] // 2
         top, bottom = block[:half], block[half:]
         at = slice(i * half, (i + 1) * half)
@@ -492,27 +521,25 @@
     out[...] = ((first * share + second * other_share) / (share + other_share)).astype(BF16)
 
 
-def return_kernel(keep0, got0, keep1, got1, keep2, got2, low, high, send):
+def return_first_kernel(keep0, got0, keep1, got1, low, send):
     rows, cols = low.shape
-    for i in range(2):
-        near = slice(i * rows, (i + 1) * rows)
-        keep, got = (keep0, got0) if i == 0 else (keep1, got1)
-        first = keep[:rows, :cols] + got[:rows, :cols].astype(F32)
-        second = keep2[near, :] + got2[near, :].astype(F32)
-        if i == 0:
-            low[...] = first
-            high[...] = second
-        else:
-            send[:, :cols] = first.astype(BF16)
-            send[:, cols:] = second.astype(BF16)
-
-
-def query_kernel(ids, low, high, got, gain, *refs):
+    low[...] = keep0[:rows, :] + got0[:rows, :].astype(F32)
+    send[...] = (keep1[:rows, :cols] + got1[:rows, :cols].astype(F32)).astype(BF16)
+
+
+def return_second_kernel(keep, got, high, send):
+    rows = high.shape[0]
+    both = keep[...] + got[...].astype(F32)
+    high[...] = both[:rows]
+    send[...] = both[rows:].astype(BF16)
+
+
+def query_kernel(ids, low, high, got_first, got_second, gain, *refs):
     sends, scratch = refs[:-1], refs[-1]
     odd = ids[2] % 2 == 1
     cols = low.shape[1]
     cut = QL - 2 * cols
-    got_low, got_high = got[:, :cols].astype(F32), got[:, cols:].astype(F32)
+    got_low, got_high = got_first[...].astype(F32), got_second[...].astype(F32)
     first = jnp.where(odd, got_low, low[...])
     second = jnp.where(odd, got_high, high[...])
     third = jnp.where(odd, high[:, :cut], got_high[:, :cut])
@@ -573,10 +600,9 @@
     group, index = lax.axis_index(GRP), lax.axis_index(DEC)
     stage, core = lax.axis_index(STG), lax.axis_index(TP)
     ids = jnp.stack([group, core, index, stage]).astype(jnp.int32)
-    tokens, feats = hidden_x.shape
+    tokens, _ = hidden_x.shape
     cols = proj_weight.shape[1]
     cut = QL - 2 * cols
-    half = feats // 2
     pages = page_plan.shape[0]
     requests, heads, _ = dec_query.shape
     queries = requests * heads
@@ -585,12 +611,8 @@
 
     weight = proj_weight.T
     split = cols // 2 // 128 * 128
-    pieces = [
-        lax.dynamic_slice(weight, (0, group * half), (split, half)),
-        lax.dynamic_slice(weight, (split, group * half), (cols - split, half)),
-    ]
+    pieces = [share(ids, weight[:split]), share(ids, weight[split:])]
     partners = [(0, 1), (1, 0), (2, 3), (3, 2)]
-    inner = [(g * n + i, (1 - g) * n + i) for g in range(2) for i in (1, 2)]
     a_z, a_y, b_z, b_y = [None] * 2, [None] * 2, [None] * 2, [None] * 2
     for p in (1, 0):
         a_z[p] = lax.ppermute(pieces[p], DEC, [(0, 2), (3, 1), (1, 0), (2, 3)])
@@ -609,7 +631,7 @@
         a_y[p] = swap(a_z[p], GRP)
         b_z[p] = lax.ppermute(held[p], DEC, [(1, 2), (2, 1)])
     for p in (1, 0):
-        b_y[p] = lax.ppermute(b_z[p], (GRP, DEC), inner)
+        b_y[p] = swap(b_z[p], GRP)
     query = dec_query.reshape(queries, KVW)
     padded_key = jnp.pad(new_key, ((0, 3 * requests), (0, 0)))
     old, bias = call(
@@ -634,7 +656,6 @@
 
     a_refs = (a_z[0], a_y[0], a_z[1], a_y[1])
     keys = cols - cut
-    wide = -(-cut // 128) * 128
     send, kept0 = project(near_kernel, cols, (early_ids, hidden_x, weight, *a_refs))
     other0 = swap(send, TP)
     send0, keep0 = call(
@@ -657,17 +678,20 @@
         (ids, kept1, other1),
     )
     got1 = swap(send1, STG)
-    send, kept2 = project(
-        functools.partial(rest_kernel, keys),
-        2 * wide,
-        (ids, hidden_x, x_far, *a_refs, b_z[0], b_y[0], b_z[1], b_y[1]),
-    )
-    other2 = swap(send, TP)
+    used = (cols - split - keys, split)
+    rest = []
+    for k, p in enumerate((1, 0)):
+        send, kept = project(
+            functools.partial(rest_kernel, used[k]),
+            -(-used[k] // 128) * 128 + used[k],
+            (ids, hidden_x, x_far, a_z[p], a_y[p], b_z[p], b_y[p]),
+        )
+        rest += [kept, swap(send, TP)]
     send2, keep2 = call(
-        functools.partial(cross_rest_kernel, cut, keys),
+        functools.partial(cross_rest_kernel, split, used[0], keys),
         [shaped(rows, cols, kind=BF16), shaped(rows, cols)],
-        [SMEM] + [VMEM] * 4,
-        (ids, kept2, other2, kept1, other1),
+        [SMEM] + [VMEM] * 6,
+        (ids, *rest, kept1, other1),
     )
     got2 = swap(send2, STG)
 
@@ -694,21 +718,28 @@
         (ids, part_out, *spread),
     )
 
-    low, high, back = call(
-        return_kernel,
-        [shaped(quarter, cols), shaped(quarter, cols), shaped(quarter, 2 * cols, kind=BF16)],
-        [VMEM] * 6,
-        (keep0, got0, keep1, got1, keep2, got2),
-    )
-    back = lax.ppermute(back, DEC, partners)
+    low, back0 = call(
+        return_first_kernel,
+        [shaped(quarter, cols), shaped(quarter, cols, kind=BF16)],
+        [VMEM] * 4,
+        (keep0, got0, keep1, got1),
+    )
+    back0 = lax.ppermute(back0, DEC, partners)
+    high, back1 = call(
+        return_second_kernel,
+        [shaped(quarter, cols), shaped(quarter, cols, kind=BF16)],
+        [VMEM] * 2,
+        (keep2, got2),
+    )
+    back1 = lax.ppermute(back1, DEC, partners)
     lanes = 4
     width = QL // lanes
     tile = shaped(quarter, width, kind=BF16)
     blocks = call(
         query_kernel,
         [tile] * lanes,
-        [SMEM] + [VMEM] * 4,
-        (ids, low, high, back, q_scale),
+        [SMEM] + [VMEM] * 5,
+        (ids, low, high, back0, back1, q_scale),
         scratch=[pltpu.VMEM((quarter, QL), BF16)],
     )
     gots = [blocks[0]]

time: 160 us -> 167 us (1.044)
  the two profiles are of different devices: /device:TPU:9 before, /device:TPU:13 now
where the time goes in v4:
time: 167 us
  waiting for transfers between devices  89.4 us (54%)
  starting transfers between devices  40.4 us (24%)
  Pallas kernels  26.6 us (16%)
  local copies, waits for them, and re-layouts  7.84 us (5%)
  other arithmetic  1.67 us (1%)
    ppermute x2, waiting for transfers between devices, pairs_step(): a_z[p] = lax.ppermute(pieces[p], DEC, [(0, 2), (3, 1), (1, 0), (2, 3)])  44.9 us
    ppermute x12, waiting for transfers between devices, swap(): return lax.ppermute(a, axis, [(0, 1), (1, 0)])  28.1 us
    pallas_call x4, Pallas kernels, project(): pl.pallas_call(kernel, in_specs=[SMEM] + [VMEM] * (len(args) - 1), out_sp...  14.2 us
    ppermute x12, starting transfers between devices, swap(): return lax.ppermute(a, axis, [(0, 1), (1, 0)])  11.3 us
    pallas_call x12, Pallas kernels, call(): pl.pallas_call(kernel, scratch_shapes=scratch, out_shape=shapes, in_specs...  10.5 us
    ppermute x2, waiting for transfers between devices, pairs_step(): b_z[p] = lax.ppermute(held[p], DEC, [(1, 2), (2, 1)])  8.6 us
    ppermute x3, starting transfers between devices, pairs_step(): spread.append(lax.ppermute(part_out, DEC, pairs))  8.38 us
    ppermute x2, starting transfers between devices, pairs_step(): b_z[p] = lax.ppermute(held[p], DEC, [(1, 2), (2, 1)])  6.39 us
  transfers between devices with their start and end apart: 29, of which 10 were waited for; matrix products, arithmetic and copies ran while one was open for 3% of the time, Pallas kernels for 14%

profile of v4, /device:TPU:13, one launch (start us, length us, event | category | flops | bytes accessed | tf_op | source)
XLA Modules:
  0.0 166.9 jit_solution(2346430054515272055)
XLA Ops:
  0.6 1.3 slice.8.weight
  2.1 1.4 shard_map.114
  3.6 2.3 %collective-permute-start.6 = (bf16[384,1792]{1,0:T(8,128)(2,1)S(1)}, bf16[384,1792]{1,0:T(8,128)(2,1)}, u32[]{:S(2)}, u32[]{:S(2)}) collective-permute-start(bf16[384,1792]{1,0:T(8,128)(2,1)S(1)} %copy-done), channel_id=1, source_target_pairs={{0,4},{4,0},{8,12},{12,8},{1,5},{5,1},{9,13},{13,9},{2,6},{6,2},{1... | collective-permute-start | bytes 4128776 | tf_op jit(solution)/shard_map/ppermute | solution.py:628
  5.9 1.3 slice.9.weight
  7.9 8.2 %collective-permute-done.z0.z = bf16[256,896]{1,0:T(8,128)(2,1)} collective-permute-done((bf16[256,896]{1,0:T(8,128)(2,1)}, bf16[256,896]{1,0:T(8,128)(2,1)}, u32[]{:S(2)}, u32[]{:S(2)}) %collective-permute-start) | collective-permute-done | bytes 458784 | tf_op jit(solution)/shard_map/ppermute | solution.py:618
  16.1 3.2 %collective-permute-start.7 = (bf16[272,896]{1,0:T(8,128)(2,1)S(1)}, bf16[272,896]{1,0:T(8,128)(2,1)}, u32[]{:S(2)}, u32[]{:S(2)}) collective-permute-start(bf16[272,896]{1,0:T(8,128)(2,1)S(1)} %shard_map.115), channel_id=1, source_target_pairs={{4,8},{8,4},{5,9},{9,5},{6,10},{10,6},{7,11},{11,7},{20,24},{24,20... | collective-permute-start | bytes 1462280 | tf_op jit(solution)/shard_map/ppermute | solution.py:632
  19.3 36.7 %collective-permute-done.2.z1.z = bf16[272,896]{1,0:T(8,128)(2,1)} collective-permute-done((bf16[272,896]{1,0:T(8,128)(2,1)S(1)}, bf16[272,896]{1,0:T(8,128)(2,1)}, u32[]{:S(2)}, u32[]{:S(2)}) %collective-permute-start.2) | collective-permute-done | bytes 487456 | tf_op jit(solution)/shard_map/ppermute | solution.py:618
  56.2 1.2 collective-permute-start.8
  57.5 3.2 %collective-permute-start.12 = (bf16[256,896]{1,0:T(8,128)(2,1)}, bf16[256,896]{1,0:T(8,128)(2,1)}, u32[]{:S(2)}, u32[]{:S(2)}) collective-permute-start(bf16[256,896]{1,0:T(8,128)(2,1)} %shard_map.114), channel_id=1, source_target_pairs={{4,8},{8,4},{5,9},{9,5},{6,10},{10,6},{7,11},{11,7},{20,24},{24,20... | collective-permute-start | bytes 1376264 | tf_op jit(solution)/shard_map/ppermute | solution.py:632
  61.1 8.6 %collective-permute-done.12.bz = bf16[256,896]{1,0:T(8,128)(2,1)} collective-permute-done((bf16[256,896]{1,0:T(8,128)(2,1)}, bf16[256,896]{1,0:T(8,128)(2,1)}, u32[]{:S(2)}, u32[]{:S(2)}) %collective-permute-start.12) | collective-permute-done | bytes 458784 | tf_op jit(solution)/shard_map/ppermute | solution.py:632
  69.9 17.9 %collective-permute-done.1.y0.y = bf16[256,896]{1,0:T(8,128)(2,1)} collective-permute-done((bf16[256,896]{1,0:T(8,128)(2,1)}, bf16[256,896]{1,0:T(8,128)(2,1)}, u32[]{:S(2)}, u32[]{:S(2)}) %collective-permute-start.1) | collective-permute-done | bytes 458784 | tf_op jit(solution)/shard_map/ppermute | solution.py:199
  87.8 4.1 %shard_map.118 = (f32[192,624]{1,0:T(8,128)S(1)}, f32[192,624]{1,0:T(8,128)S(1)}) custom-call(s32[4]{0:T(128)S(1)} %pad_add_fusion.1.ids, bf16[384,1792]{1,0:T(8,128)(2,1)S(1)} %copy-done, bf16[384,1792]{1,0:T(8,128)(2,1)} %collective-permute-done.6.far_ref, bf16[528,1792]{1,0:T(8,128)(2,1)S(1)} %bitcast.14, bf16[256,896]{1,0:T(8,128)(2,1)} %collective-permute-done.z0.z, ...), custom_call_target="tpu_custom_call" | custom-call | flops 858783744 | bytes 1916928 | tf_op jit(solution)/shard_map/pallas_call | solution.py:284
  91.9 4.4 %collective-permute-start.9 = (f32[192,624]{1,0:T(8,128)S(1)}, f32[192,624]{1,0:T(8,128)S(1)}, u32[]{:S(2)}, u32[]{:S(2)}) collective-permute-start(f32[192,624]{1,0:T(8,128)S(1)} %get-tuple-element.41), channel_id=1, source_target_pairs={{0,1},{1,0},{2,3},{3,2},{4,5},{5,4},{6,7},{7,6},{8,9},{9,8},{10,11... | collective-permute-start | bytes 1437704 | tf_op jit(solution)/shard_map/ppermute | solution.py:199
  96.3 0.8 multiply_sine_fusion
  97.1 2.9 %shard_map.116 = (f32[192,528]{1,0:T(8,128)S(1)}, f32[192,528]{1,0:T(8,128)S(1)}) custom-call(s32[4]{0:T(128)S(1)} %pad_add_fusion.1.ids, bf16[384,1792]{1,0:T(8,128)(2,1)S(1)} %copy-done, bf16[528,1792]{1,0:T(8,128)(2,1)S(1)} %bitcast.15, bf16[256,896]{1,0:T(8,128)(2,1)} %collective-permute-done.z0.z, bf16[256,896]{1,0:T(8,128)(2,1)} %collective-permute-done.1.y0.y, ...), custom_call_target="tpu_custom_call" | custom-call | flops 726663168 | bytes 1622016 | tf_op jit(solution)/shard_map/pallas_call | solution.py:284
  100.1 3.5 %shard_map.122 = (f32[192,512]{1,0:T(8,128)}, f32[192,512]{1,0:T(8,128)S(1)}) custom-call(s32[4]{0:T(128)S(1)} %pad_add_fusion.1.ids, bf16[384,1792]{1,0:T(8,128)(2,1)S(1)} %copy-done, bf16[384,1792]{1,0:T(8,128)(2,1)} %collective-permute-done.6.far_ref, bf16[256,896]{1,0:T(8,128)(2,1)} %collective-permute-done.z0.z, ...), custom_call_target="tpu_custom_call" | custom-call | flops 704643072 | bytes 1572864 | tf_op jit(solution)/shard_map/pallas_call | solution.py:284
  104.1 3.7 %shard_map.121 = (f32[192,480]{1,0:T(8,128)}, f32[192,480]{1,0:T(8,128)S(1)}) custom-call(s32[4]{0:T(128)S(1)} %pad_add_fusion.1.ids, bf16[384,1792]{1,0:T(8,128)(2,1)S(1)} %copy-done, bf16[384,1792]{1,0:T(8,128)(2,1)} %collective-permute-done.6.far_ref, bf16[272,896]{1,0:T(8,128)(2,1)} %collective-permute-done.2.z1.z, ...), custom_call_target="tpu_custom_call" | custom-call | flops 660602880 | bytes 1474560 | tf_op jit(solution)/shard_map/pallas_call | solution.py:284
  108.0 0.7 shard_map.119
  108.7 1.3 collective-permute-start.10
  111.0 10.2 %collective-permute-done.5.got0 = bf16[192,528]{1,0:T(8,128)(2,1)S(1)} collective-permute-done((bf16[192,528]{1,0:T(8,128)(2,1)S(1)}, bf16[192,528]{1,0:T(8,128)(2,1)S(1)}, u32[]{:S(2)}, u32[]{:S(2)}) %collective-permute-start.5) | collective-permute-done | bytes 202784 | tf_op jit(solution)/shard_map/ppermute | solution.py:199
  121.8 0.7 copy-done.7
  122.5 1.2 collective-permute-start.21
  123.8 0.8 copy.13
  125.2 1.0 copy-done.5
  126.3 1.0 copy-done.11
  127.2 1.0 copy-done.13
  128.2 1.3 shard_map.123
  129.6 1.3 collective-permute-start.15
  130.9 0.7 add_bitcast_fusion
  131.6 1.3 collective-permute-start.24
  133.1 1.4 collective-permute-start.22
  134.5 1.7 %collective-permute-done.23 = s32[1,60]{1,0:T(1,128)S(1)} collective-permute-done((s32[1,60]{1,0:T(1,128)S(1)}, s32[1,60]{1,0:T(1,128)S(1)}, u32[]{:S(2)}, u32[]{:S(2)}) %collective-permute-start.23) | collective-permute-done | bytes 272 | tf_op jit(solution)/shard_map/ppermute | solution.py:624
  136.3 1.7 %shard_map.128 = (bf16[128,640]{1,0:T(8,128)(2,1)S(1)}, f32[8,768]{1,0:T(8,128)S(1)}) custom-call(s32[4]{0:T(128)S(1)} %pad_add_fusion.1.ids, s32[8,128]{1,0:T(8,128)S(1)} %pad.8.tab_ref, bf16[128,576]{1,0:T(8,128)(2,1)S(1)} %bitcast.17, bf16[1024,576]{1,0:T(8,128)(2,1)S(1)} %bitcast.16, bf16[16,576]{1,0:T(8,128)(2,1)S(1)} %pad.9.own_ref), custom_call_target="tpu_custom_call" | custom-call | flops 20000000 | bytes 2000000 | tf_op jit(solution)/shard_map/pallas_call | solution.py:568
  138.0 1.0 collective-permute-start.25
  139.7 1.0 collective-permute-start.16
  140.7 1.5 collective-permute-done.25.far_ref
  142.3 1.8 %shard_map.129.own = bf16[128,640]{1,0:T(8,128)(2,1)S(1)} custom-call(bf16[128,576]{1,0:T(8,128)(2,1)S(1)} %bitcast.18, bf16[384,576]{1,0:T(8,128)(2,1)S(1)} %shard_map.127.k0_ref, bf16[384,576]{1,0:T(8,128)(2,1)} %collective-permute-done.21.k1_ref, f32[8,768]{1,0:T(8,128)S(1)} %get-tuple-element.64.bias_ref, ...), custom_call_target="tpu_custom_call" | custom-call | flops 20000000 | bytes 2000000 | tf_op jit(solution)/shard_map/pallas_call | solution.py:568
  144.1 4.0 %collective-permute-start.28 = (bf16[128,640]{1,0:T(8,128)(2,1)S(1)}, bf16[128,640]{1,0:T(8,128)(2,1)S(1)}, u32[]{:S(2)}, u32[]{:S(2)}) collective-permute-start(bf16[128,640]{1,0:T(8,128)(2,1)S(1)} %shard_map.129.own), channel_id=1, source_target_pairs={{4,8},{12,0},{5,9},{13,1},{6,10},{14,2},{7,11},{15,3},{20,24},{28,... | collective-permute-start | bytes 491528 | tf_op jit(solution)/shard_map/ppermute | solution.py:713
  148.1 1.3 collective-permute-start.27
  149.4 3.1 %collective-permute-start.26 = (bf16[128,640]{1,0:T(8,128)(2,1)S(1)}, bf16[128,640]{1,0:T(8,128)(2,1)S(1)}, u32[]{:S(2)}, u32[]{:S(2)}) collective-permute-start(bf16[128,640]{1,0:T(8,128)(2,1)S(1)} %shard_map.129.own), channel_id=1, source_target_pairs={{4,12},{12,4},{5,13},{13,5},{6,14},{14,6},{7,15},{15,7},{20,28},{2... | collective-permute-start | bytes 491528 | tf_op jit(solution)/shard_map/ppermute | solution.py:713
  152.5 0.9 shard_map.125
  153.4 5.2 %collective-permute-start.18 = (bf16[96,384]{1,0:T(8,128)(2,1)S(1)}, bf16[96,384]{1,0:T(8,128)(2,1)S(1)}, u32[]{:S(2)}, u32[]{:S(2)}) collective-permute-start(bf16[96,384]{1,0:T(8,128)(2,1)S(1)} %get-tuple-element.57), channel_id=1, source_target_pairs={{0,1},{1,0},{2,3},{3,2},{4,5},{5,4},{6,7},{7,6},{8,9},{9,8},{10,11... | collective-permute-start | bytes 221192 | tf_op jit(solution)/shard_map/ppermute | solution.py:747
  158.9 0.7 collective-permute-done.18.refs_1_
  159.6 0.8 collective-permute-start.20
  160.4 2.0 %collective-permute-done.19.refs_2_ = bf16[96,384]{1,0:T(8,128)(2,1)S(1)} collective-permute-done((bf16[96,384]{1,0:T(8,128)(2,1)S(1)}, bf16[96,384]{1,0:T(8,128)(2,1)S(1)}, u32[]{:S(2)}, u32[]{:S(2)}) %collective-permute-start.19) | collective-permute-done | bytes 73760 | tf_op jit(solution)/shard_map/ppermute | solution.py:747
  162.4 1.8 %collective-permute-done.20.refs_3_ = bf16[96,384]{1,0:T(8,128)(2,1)S(1)} collective-permute-done((bf16[96,384]{1,0:T(8,128)(2,1)S(1)}, bf16[96,384]{1,0:T(8,128)(2,1)S(1)}, u32[]{:S(2)}, u32[]{:S(2)}) %collective-permute-start.20) | collective-permute-done | bytes 73760 | tf_op jit(solution)/shard_map/ppermute | solution.py:747
  164.2 1.3 shard_map.126
  165.5 1.4 shard_map.130
  (81 shorter events, 6.0 us)
Async XLA Ops:
  0.6 3.0 %copy-start = (bf16[384,1792]{1,0:T(8,128)(2,1)S(1)}, bf16[384,1792]{1,0:T(8,128)(2,1)}, u32[]{:S(2)}) copy-start(bf16[384,1792]{1,0:T(8,128)(2,1)} %x_ref.7) | copy-start | bytes 4128772
  3.5 84.3 %copy-start.1 = (bf16[1792,528]{0,1:T(8,128)(2,1)S(1)}, bf16[1792,528]{0,1:T(8,128)(2,1)}, u32[]{:S(2)}) copy-start(bf16[1792,528]{0,1:T(8,128)(2,1)} %param.11) | copy-start | bytes 5677060
  3.5 12.6 %collective-permute-start = (bf16[256,896]{1,0:T(8,128)(2,1)}, bf16[256,896]{1,0:T(8,128)(2,1)}, u32[]{:S(2)}, u32[]{:S(2)}) collective-permute-start(bf16[256,896]{1,0:T(8,128)(2,1)} %shard_map.114), channel_id=1, source_target_pairs={{0,8},{12,4},{4,0},{8,12},{1,9},{13,5},{5,1},{9,13},{2,10},{14,6},... | collective-permute-start | bytes 1376264 | tf_op jit(solution)/shard_map/ppermute | solution.py:618
  3.6 84.1 %collective-permute-start.6 = (bf16[384,1792]{1,0:T(8,128)(2,1)S(1)}, bf16[384,1792]{1,0:T(8,128)(2,1)}, u32[]{:S(2)}, u32[]{:S(2)}) collective-permute-start(bf16[384,1792]{1,0:T(8,128)(2,1)S(1)} %copy-done), channel_id=1, source_target_pairs={{0,4},{4,0},{8,12},{12,8},{1,5},{5,1},{9,13},{13,9},{2,6},{6,2},{1... | collective-permute-start | bytes 4128776 | tf_op jit(solution)/shard_map/ppermute | solution.py:628
  7.8 48.2 %collective-permute-start.2 = (bf16[272,896]{1,0:T(8,128)(2,1)S(1)}, bf16[272,896]{1,0:T(8,128)(2,1)}, u32[]{:S(2)}, u32[]{:S(2)}) collective-permute-start(bf16[272,896]{1,0:T(8,128)(2,1)S(1)} %shard_map.115), channel_id=1, source_target_pairs={{0,8},{12,4},{4,0},{8,12},{1,9},{13,5},{5,1},{9,13},{2,10},{14,6},... | collective-permute-start | bytes 1462280 | tf_op jit(solution)/shard_map/ppermute | solution.py:618
  16.1 40.2 %collective-permute-start.7 = (bf16[272,896]{1,0:T(8,128)(2,1)S(1)}, bf16[272,896]{1,0:T(8,128)(2,1)}, u32[]{:S(2)}, u32[]{:S(2)}) collective-permute-start(bf16[272,896]{1,0:T(8,128)(2,1)S(1)} %shard_map.115), channel_id=1, source_target_pairs={{4,8},{8,4},{5,9},{9,5},{6,10},{10,6},{7,11},{11,7},{20,24},{24,20... | collective-permute-start | bytes 1462280 | tf_op jit(solution)/shard_map/ppermute | solution.py:632
  56.0 31.8 %collective-permute-start.3 = (bf16[272,896]{1,0:T(8,128)(2,1)}, bf16[272,896]{1,0:T(8,128)(2,1)}, u32[]{:S(2)}, u32[]{:S(2)}) collective-permute-start(bf16[272,896]{1,0:T(8,128)(2,1)} %collective-permute-done.2.z1.z), channel_id=1, source_target_pairs={{0,16},{16,0},{1,17},{17,1},{2,18},{18,2},{3,19},{19,3},{4,20},{20... | collective-permute-start | bytes 1462280 | tf_op jit(solution)/shard_map/ppermute | solution.py:199
  56.2 31.5 %collective-permute-start.8 = (bf16[272,896]{1,0:T(8,128)(2,1)}, bf16[272,896]{1,0:T(8,128)(2,1)}, u32[]{:S(2)}, u32[]{:S(2)}) collective-permute-start(bf16[272,896]{1,0:T(8,128)(2,1)} %collective-permute-done.7.bz1.bz), channel_id=1, source_target_pairs={{0,16},{16,0},{1,17},{17,1},{2,18},{18,2},{3,19},{19,3},{4,20},{20... | collective-permute-start | bytes 1462280 | tf_op jit(solution)/shard_map/ppermute | solution.py:199
  57.5 12.2 %collective-permute-start.12 = (bf16[256,896]{1,0:T(8,128)(2,1)}, bf16[256,896]{1,0:T(8,128)(2,1)}, u32[]{:S(2)}, u32[]{:S(2)}) collective-permute-start(bf16[256,896]{1,0:T(8,128)(2,1)} %shard_map.114), channel_id=1, source_target_pairs={{4,8},{8,4},{5,9},{9,5},{6,10},{10,6},{7,11},{11,7},{20,24},{24,20... | collective-permute-start | bytes 1376264 | tf_op jit(solution)/shard_map/ppermute | solution.py:632
  60.7 27.1 %collective-permute-start.1 = (bf16[256,896]{1,0:T(8,128)(2,1)}, bf16[256,896]{1,0:T(8,128)(2,1)}, u32[]{:S(2)}, u32[]{:S(2)}) collective-permute-start(bf16[256,896]{1,0:T(8,128)(2,1)} %collective-permute-done.z0.z), channel_id=1, source_target_pairs={{0,16},{16,0},{1,17},{17,1},{2,18},{18,2},{3,19},{19,3},{4,20},{20... | collective-permute-start | bytes 1376264 | tf_op jit(solution)/shard_map/ppermute | solution.py:199
  61.1 36.0 %copy-start.15 = (f32[1536]{0:T(1024)S(1)}, f32[1536]{0:T(1024)}, u32[]{:S(2)}) copy-start(f32[1536]{0:T(1024)} %param.12) | copy-start | bytes 18436
  69.7 30.4 %collective-permute-start.13 = (bf16[256,896]{1,0:T(8,128)(2,1)}, bf16[256,896]{1,0:T(8,128)(2,1)S(1)}, u32[]{:S(2)}, u32[]{:S(2)}) collective-permute-start(bf16[256,896]{1,0:T(8,128)(2,1)} %collective-permute-done.12.bz), channel_id=1, source_target_pairs={{0,16},{16,0},{1,17},{17,1},{2,18},{18,2},{3,19},{19,3},{4,20},{20... | collective-permute-start | bytes 1376264 | tf_op jit(solution)/shard_map/ppermute | solution.py:199
  91.9 16.2 %copy-start.2 = (f32[192,624]{1,0:T(8,128)}, f32[192,624]{1,0:T(8,128)S(1)}, u32[]{:S(2)}) copy-start(f32[192,624]{1,0:T(8,128)S(1)} %get-tuple-element.40.kept.kept_far) | copy-start | bytes 1437700
  91.9 16.2 %collective-permute-start.9 = (f32[192,624]{1,0:T(8,128)S(1)}, f32[192,624]{1,0:T(8,128)S(1)}, u32[]{:S(2)}, u32[]{:S(2)}) collective-permute-start(f32[192,624]{1,0:T(8,128)S(1)} %get-tuple-element.41), channel_id=1, source_target_pairs={{0,1},{1,0},{2,3},{3,2},{4,5},{5,4},{6,7},{7,6},{8,9},{9,8},{10,11... | collective-permute-start | bytes 1437704 | tf_op jit(solution)/shard_map/ppermute | solution.py:199
  100.0 10.0 %collective-permute-start.4 = (f32[192,528]{1,0:T(8,128)S(1)}, f32[192,528]{1,0:T(8,128)S(1)}, u32[]{:S(2)}, u32[]{:S(2)}) collective-permute-start(f32[192,528]{1,0:T(8,128)S(1)} %get-tuple-element.36), channel_id=1, source_target_pairs={{0,1},{1,0},{2,3},{3,2},{4,5},{5,4},{6,7},{7,6},{8,9},{9,8},{10,11... | collective-permute-start | bytes 1216520 | tf_op jit(solution)/shard_map/ppermute | solution.py:199
  103.6 4.2 %copy-start.10 = (f32[192,512]{1,0:T(8,128)}, f32[192,512]{1,0:T(8,128)S(1)}, u32[]{:S(2)}) copy-start(f32[192,512]{1,0:T(8,128)S(1)} %get-tuple-element.48.kept_head) | copy-start | bytes 1179652
  103.6 21.6 %collective-permute-start.14 = (f32[192,512]{1,0:T(8,128)}, f32[192,512]{1,0:T(8,128)}, u32[]{:S(2)}, u32[]{:S(2)}) collective-permute-start(f32[192,512]{1,0:T(8,128)} %get-tuple-element.49), channel_id=1, source_target_pairs={{0,1},{1,0},{2,3},{3,2},{4,5},{5,4},{6,7},{7,6},{8,9},{9,8},{10,11... | collective-permute-start | bytes 1179656 | tf_op jit(solution)/shard_map/ppermute | solution.py:199
  107.8 14.0 %copy-start.12 = (f32[192,480]{1,0:T(8,128)}, f32[192,480]{1,0:T(8,128)S(1)}, u32[]{:S(2)}) copy-start(f32[192,480]{1,0:T(8,128)S(1)} %get-tuple-element.45.kept_tail) | copy-start | bytes 1105924
  107.8 13.4 %copy-start.14 = (f32[512]{0:T(512)S(1)}, f32[512]{0:T(512)}, u32[]{:S(2)}) copy-start(f32[512]{0:T(512)} %param.13) | copy-start | bytes 6148
  107.8 17.4 %collective-permute-start.11 = (f32[192,480]{1,0:T(8,128)}, f32[192,480]{1,0:T(8,128)}, u32[]{:S(2)}, u32[]{:S(2)}) collective-permute-start(f32[192,480]{1,0:T(8,128)} %get-tuple-element.46), channel_id=1, source_target_pairs={{0,1},{1,0},{2,3},{3,2},{4,5},{5,4},{6,7},{7,6},{8,9},{9,8},{10,11... | collective-permute-start | bytes 1105928 | tf_op jit(solution)/shard_map/ppermute | solution.py:199
  108.0 13.8 %copy-start.4 = (f32[192,624]{1,0:T(8,128)}, f32[192,624]{1,0:T(8,128)S(1)}, u32[]{:S(2)}) copy-start(f32[192,624]{1,0:T(8,128)S(1)} %collective-permute-done.9.got.got_far) | copy-start | bytes 1437700
  108.7 12.5 %collective-permute-start.10 = (bf16[192,624]{1,0:T(8,128)(2,1)S(1)}, bf16[192,624]{1,0:T(8,128)(2,1)S(1)}, u32[]{:S(2)}, u32[]{:S(2)}) collective-permute-start(bf16[192,624]{1,0:T(8,128)(2,1)S(1)} %get-tuple-element.43), channel_id=1, source_target_pairs={{0,2},{2,0},{1,3},{3,1},{4,6},{6,4},{5,7},{7,5},{8,10},{10,8},{9,1... | collective-permute-start | bytes 718856 | tf_op jit(solution)/shard_map/ppermute | solution.py:199
  110.6 13.1 %copy-start.17 = (s32[1,4,8]{2,1,0:T(4,128)S(1)}, s32[1,4,8]{2,1,0:T(4,128)}, u32[]{:S(2)}) copy-start(s32[1,4,8]{2,1,0:T(4,128)} %param.16) | copy-start | bytes 388
  110.6 14.6 %copy-start.3 = (f32[192,624]{1,0:T(8,128)S(1)}, f32[192,624]{1,0:T(8,128)}, u32[]{:S(2)}) copy-start(f32[192,624]{1,0:T(8,128)} %copy-done.2) | copy-start | bytes 1437700
  110.6 10.5 %collective-permute-start.5 = (bf16[192,528]{1,0:T(8,128)(2,1)S(1)}, bf16[192,528]{1,0:T(8,128)(2,1)S(1)}, u32[]{:S(2)}, u32[]{:S(2)}) collective-permute-start(bf16[192,528]{1,0:T(8,128)(2,1)S(1)} %get-tuple-element.38), channel_id=1, source_target_pairs={{0,2},{2,0},{1,3},{3,1},{4,6},{6,4},{5,7},{7,5},{8,10},{10,8},{9,1... | collective-permute-start | bytes 608264 | tf_op jit(solution)/shard_map/ppermute | solution.py:199
  121.2 15.1 %copy-start.6 = (bf16[32,32,576]{2,1,0:T(8,128)(2,1)S(1)}, bf16[32,32,576]{2,1,0:T(8,128)(2,1)}, u32[]{:S(2)}) copy-start(bf16[32,32,576]{2,1,0:T(8,128)(2,1)} %param.14) | copy-start | bytes 3538948
  121.8 0.7 copy-start.7
  122.5 12.0 %copy-start.16 = (bf16[4,576]{1,0:T(4,128)(2,1)S(1)}, bf16[4,576]{1,0:T(4,128)(2,1)}, u32[]{:S(2)}) copy-start(bf16[4,576]{1,0:T(4,128)(2,1)} %param.19) | copy-start | bytes 13828
  122.5 19.7 %collective-permute-start.21 = (bf16[384,576]{1,0:T(8,128)(2,1)S(1)}, bf16[384,576]{1,0:T(8,128)(2,1)}, u32[]{:S(2)}, u32[]{:S(2)}) collective-permute-start(bf16[384,576]{1,0:T(8,128)(2,1)S(1)} %shard_map.127.k0_ref), channel_id=1, source_target_pairs={{0,1},{1,0},{2,3},{3,2},{4,5},{5,4},{6,7},{7,6},{8,9},{9,8},{10,11... | collective-permute-start | bytes 1327112 | tf_op jit(solution)/shard_map/ppermute | solution.py:199
  125.2 5.7 %copy-start.18 = (s32[24]{0:T(128)S(1)}, s32[24]{0:T(128)}, u32[]{:S(2)}) copy-start(s32[24]{0:T(128)} %reshape.65) | copy-start | bytes 292
  125.2 1.0 copy-start.5
  126.3 1.0 copy-start.11
  127.2 1.0 copy-start.13
  128.2 8.0 %copy-start.9 = (bf16[4,32,576]{2,1,0:T(8,128)(2,1)S(1)}, bf16[4,32,576]{2,1,0:T(8,128)(2,1)}, u32[]{:S(2)}) copy-start(bf16[4,32,576]{2,1,0:T(8,128)(2,1)} %param.18) | copy-start | bytes 442372
  129.6 10.1 %copy-start.8 = (bf16[192,528]{1,0:T(8,128)(2,1)S(1)}, bf16[192,528]{1,0:T(8,128)(2,1)}, u32[]{:S(2)}) copy-start(bf16[192,528]{1,0:T(8,128)(2,1)} %copy-done.7) | copy-start | bytes 608260
  129.6 9.4 %collective-permute-start.15 = (bf16[192,528]{1,0:T(8,128)(2,1)S(1)}, bf16[192,528]{1,0:T(8,128)(2,1)S(1)}, u32[]{:S(2)}, u32[]{:S(2)}) collective-permute-start(bf16[192,528]{1,0:T(8,128)(2,1)S(1)} %get-tuple-element.51), channel_id=1, source_target_pairs={{0,2},{2,0},{1,3},{3,1},{4,6},{6,4},{5,7},{7,5},{8,10},{10,8},{9,1... | collective-permute-start | bytes 608264 | tf_op jit(solution)/shard_map/ppermute | solution.py:199
  131.6 2.9 %collective-permute-start.24 = (s32[1,60]{1,0:T(1,128)S(1)}, s32[1,60]{1,0:T(1,128)S(1)}, u32[]{:S(2)}, u32[]{:S(2)}) collective-permute-start(s32[1,60]{1,0:T(1,128)S(1)} %add_bitcast_fusion), channel_id=1, source_target_pairs={{12,0},{0,4},{4,8},{8,12},{13,1},{1,5},{5,9},{9,13},{14,2},{2,6},{... | collective-permute-start | bytes 728 | tf_op jit(solution)/shard_map/ppermute | solution.py:624
  132.9 3.3 %collective-permute-start.23 = (s32[1,60]{1,0:T(1,128)S(1)}, s32[1,60]{1,0:T(1,128)S(1)}, u32[]{:S(2)}, u32[]{:S(2)}) collective-permute-start(s32[1,60]{1,0:T(1,128)S(1)} %add_bitcast_fusion), channel_id=1, source_target_pairs={{8,0},{12,4},{0,8},{4,12},{9,1},{13,5},{1,9},{5,13},{10,2},{14,6},... | collective-permute-start | bytes 728 | tf_op jit(solution)/shard_map/ppermute | solution.py:624
  133.1 3.2 %collective-permute-start.22 = (s32[1,60]{1,0:T(1,128)S(1)}, s32[1,60]{1,0:T(1,128)S(1)}, u32[]{:S(2)}, u32[]{:S(2)}) collective-permute-start(s32[1,60]{1,0:T(1,128)S(1)} %add_bitcast_fusion), channel_id=1, source_target_pairs={{4,0},{8,4},{12,8},{0,12},{5,1},{9,5},{13,9},{1,13},{6,2},{10,6},{... | collective-permute-start | bytes 728 | tf_op jit(solution)/shard_map/ppermute | solution.py:624
  138.0 4.2 %collective-permute-start.25 = (bf16[128,640]{1,0:T(8,128)(2,1)S(1)}, bf16[128,640]{1,0:T(8,128)(2,1)S(1)}, u32[]{:S(2)}, u32[]{:S(2)}) collective-permute-start(bf16[128,640]{1,0:T(8,128)(2,1)S(1)} %get-tuple-element.65.old_ref), channel_id=1, source_target_pairs={{0,4},{4,0},{8,12},{12,8},{1,5},{5,1},{9,13},{13,9},{2,6},{6,2},{1... | collective-permute-start | bytes 491528 | tf_op jit(solution)/shard_map/ppermute | solution.py:644
  139.1 13.4 %collective-permute-start.17 = (bf16[96,528]{1,0:T(8,128)(2,1)S(1)}, bf16[96,528]{1,0:T(8,128)(2,1)S(1)}, u32[]{:S(2)}, u32[]{:S(2)}) collective-permute-start(bf16[96,528]{1,0:T(8,128)(2,1)S(1)} %get-tuple-element.54), channel_id=1, source_target_pairs={{0,4},{4,0},{8,12},{12,8},{1,5},{5,1},{9,13},{13,9},{2,6},{6,2},{1... | collective-permute-start | bytes 304136 | tf_op jit(solution)/shard_map/ppermute | solution.py:734
  139.7 12.8 %collective-permute-start.16 = (bf16[96,528]{1,0:T(8,128)(2,1)S(1)}, bf16[96,528]{1,0:T(8,128)(2,1)S(1)}, u32[]{:S(2)}, u32[]{:S(2)}) collective-permute-start(bf16[96,528]{1,0:T(8,128)(2,1)S(1)} %get-tuple-element.53), channel_id=1, source_target_pairs={{0,4},{4,0},{8,12},{12,8},{1,5},{5,1},{9,13},{13,9},{2,6},{6,2},{1... | collective-permute-start | bytes 304136 | tf_op jit(solution)/shard_map/ppermute | solution.py:727
  144.1 21.4 %collective-permute-start.28 = (bf16[128,640]{1,0:T(8,128)(2,1)S(1)}, bf16[128,640]{1,0:T(8,128)(2,1)S(1)}, u32[]{:S(2)}, u32[]{:S(2)}) collective-permute-start(bf16[128,640]{1,0:T(8,128)(2,1)S(1)} %shard_map.129.own), channel_id=1, source_target_pairs={{4,8},{12,0},{5,9},{13,1},{6,10},{14,2},{7,11},{15,3},{20,24},{28,... | collective-permute-start | bytes 491528 | tf_op jit(solution)/shard_map/ppermute | solution.py:713
  148.1 17.4 %collective-permute-start.27 = (bf16[128,640]{1,0:T(8,128)(2,1)S(1)}, bf16[128,640]{1,0:T(8,128)(2,1)S(1)}, u32[]{:S(2)}, u32[]{:S(2)}) collective-permute-start(bf16[128,640]{1,0:T(8,128)(2,1)S(1)} %shard_map.129.own), channel_id=1, source_target_pairs={{4,0},{12,8},{5,1},{13,9},{6,2},{14,10},{7,3},{15,11},{20,16},{28,... | collective-permute-start | bytes 491528 | tf_op jit(solution)/shard_map/ppermute | solution.py:713
  149.4 16.1 %collective-permute-start.26 = (bf16[128,640]{1,0:T(8,128)(2,1)S(1)}, bf16[128,640]{1,0:T(8,128)(2,1)S(1)}, u32[]{:S(2)}, u32[]{:S(2)}) collective-permute-start(bf16[128,640]{1,0:T(8,128)(2,1)S(1)} %shard_map.129.own), channel_id=1, source_target_pairs={{4,12},{12,4},{5,13},{13,5},{6,14},{14,6},{7,15},{15,7},{20,28},{2... | collective-permute-start | bytes 491528 | tf_op jit(solution)/shard_map/ppermute | solution.py:713
  153.4 6.2 %collective-permute-start.18 = (bf16[96,384]{1,0:T(8,128)(2,1)S(1)}, bf16[96,384]{1,0:T(8,128)(2,1)S(1)}, u32[]{:S(2)}, u32[]{:S(2)}) collective-permute-start(bf16[96,384]{1,0:T(8,128)(2,1)S(1)} %get-tuple-element.57), channel_id=1, source_target_pairs={{0,1},{1,0},{2,3},{3,2},{4,5},{5,4},{6,7},{7,6},{8,9},{9,8},{10,11... | collective-permute-start | bytes 221192 | tf_op jit(solution)/shard_map/ppermute | solution.py:747
  158.7 3.7 %collective-permute-start.19 = (bf16[96,384]{1,0:T(8,128)(2,1)S(1)}, bf16[96,384]{1,0:T(8,128)(2,1)S(1)}, u32[]{:S(2)}, u32[]{:S(2)}) collective-permute-start(bf16[96,384]{1,0:T(8,128)(2,1)S(1)} %get-tuple-element.58), channel_id=1, source_target_pairs={{0,2},{1,3},{2,0},{3,1},{4,6},{5,7},{6,4},{7,5},{8,10},{9,11},{10,... | collective-permute-start | bytes 221192 | tf_op jit(solution)/shard_map/ppermute | solution.py:747
  159.6 4.7 %collective-permute-start.20 = (bf16[96,384]{1,0:T(8,128)(2,1)S(1)}, bf16[96,384]{1,0:T(8,128)(2,1)S(1)}, u32[]{:S(2)}, u32[]{:S(2)}) collective-permute-start(bf16[96,384]{1,0:T(8,128)(2,1)S(1)} %get-tuple-element.59), channel_id=1, source_target_pairs={{0,3},{1,2},{2,1},{3,0},{4,7},{5,6},{6,5},{7,4},{8,11},{9,10},{10,... | collective-permute-start | bytes 221192 | tf_op jit(solution)/shard_map/ppermute | solution.py:747

commit v5 on v4

--- a/solution.py
+++ b/solution.py
@@ -189,6 +189,7 @@
 VMEM = pl.BlockSpec(memory_space=pltpu.VMEM)
 SMEM = pl.BlockSpec(memory_space=pltpu.SMEM)
 VMEM_GRANT = 16 * 2**20
+VMEM_ALL = 62 * 2**20
 GRP, DEC, STG, TP = "grp", "dec", "stg", "tp"
 TILE = 256
 F32 = jnp.float32
@@ -293,22 +294,27 @@
     )(*args)
 
 
-def share_kernel(ids, weight, out):
-    out[...] = weight[...]
-
-
-def share(ids, weight):
+def share_kernel(ids, weight, head, tail, sems):
+    split, half = head.shape
+    columns = pl.ds(pl.multiple_of(ids[0] * half, 128), half)
+    first = pltpu.make_async_copy(weight.at[split:, columns], tail, sems.at[0])
+    second = pltpu.make_async_copy(weight.at[:split, columns], head, sems.at[1])
+    first.start()
+    second.start()
+    first.wait()
+    second.wait()
+
+
+def share(ids, weight, split):
     rows, feats = weight.shape
+    sizes = (split, rows - split)
     return pl.pallas_call(
         share_kernel,
-        grid_spec=pltpu.PrefetchScalarGridSpec(
-            num_scalar_prefetch=1,
-            grid=(1,),
-            in_specs=[pl.BlockSpec((rows, feats // 2), lambda i, ids: (0, ids[0]))],
-            out_specs=pl.BlockSpec((rows, feats // 2), lambda i, ids: (0, 0)),
-        ),
-        out_shape=jax.ShapeDtypeStruct((rows, feats // 2), weight.dtype),
-        compiler_params=pltpu.CompilerParams(vmem_limit_bytes=VMEM_GRANT),
+        in_specs=[SMEM, pl.BlockSpec(memory_space=pltpu.HBM)],
+        out_specs=[VMEM] * 2,
+        out_shape=[jax.ShapeDtypeStruct((size, feats // 2), weight.dtype) for size in sizes],
+        scratch_shapes=[pltpu.SemaphoreType.DMA((2,))],
+        compiler_params=pltpu.CompilerParams(vmem_limit_bytes=VMEM_ALL),
     )(ids, weight)
 
 
@@ -512,13 +518,16 @@
     pack(out / total, peak + jnp.log(total), packed_ref)
 
 
-def combine_kernel(ids, own, across, partner, other, out):
-    odd = ids[2] % 2 == 1
-    first, level = unpack(jnp.where(odd, own[...], partner[...]))
-    second, other_level = unpack(jnp.where(odd, across[...], other[...]))
+def combine_kernel(own, across, out):
+    first, level = unpack(own[...])
+    second, other_level = unpack(across[...])
     top = jnp.maximum(level, other_level)
     share, other_share = jnp.exp(level - top), jnp.exp(other_level - top)
     out[...] = ((first * share + second * other_share) / (share + other_share)).astype(BF16)
+
+
+def final_kernel(ids, own, partner, out):
+    out[...] = jnp.where(ids[2] % 2 == 1, own[...], partner[...])
 
 
 def return_first_kernel(keep0, got0, keep1, got1, low, send):
@@ -611,7 +620,7 @@
 
     weight = proj_weight.T
     split = cols // 2 // 128 * 128
-    pieces = [share(ids, weight[:split]), share(ids, weight[split:])]
+    pieces = share(ids, weight, split)
     partners = [(0, 1), (1, 0), (2, 3), (3, 2)]
     a_z, a_y, b_z, b_y = [None] * 2, [None] * 2, [None] * 2, [None] * 2
     for p in (1, 0):
@@ -708,14 +717,14 @@
         [VMEM] * 6,
         (query, key_rows, far_keys, bias, old, old_far),
     )
-    spread = []
-    for pairs in ([(1, 3), (3, 1)], [(1, 0), (3, 2)], [(1, 2), (3, 0)]):
-        spread.append(lax.ppermute(part_out, DEC, pairs))
+    across = lax.ppermute(part_out, DEC, [(1, 3), (3, 1)])
+    merged = call(combine_kernel, shaped(queries, KVL, kind=BF16), [VMEM] * 2, (part_out, across))
+    given = lax.ppermute(merged, DEC, partners)
     attn = call(
-        combine_kernel,
+        final_kernel,
         shaped(queries, KVL, kind=BF16),
-        [SMEM] + [VMEM] * 4,
-        (ids, part_out, *spread),
+        [SMEM] + [VMEM] * 2,
+        (ids, merged, given),
     )
 
     low, back0 = call(

time: 167 us -> 159 us (0.952)
  the two profiles are of different devices: /device:TPU:13 before, /device:TPU:0 now
where the time goes in v5:
time: 159 us
  waiting for transfers between devices  92.9 us (58%)
  starting transfers between devices  34.7 us (22%)
  Pallas kernels  24.9 us (16%)
  local copies, waits for them, and re-layouts  3.91 us (2%)
    ppermute x2, waiting for transfers between devices, pairs_step(): a_z[p] = lax.ppermute(pieces[p], DEC, [(0, 2), (3, 1), (1, 0), (2, 3)])  46.7 us
    ppermute x12, waiting for transfers between devices, swap(): return lax.ppermute(a, axis, [(0, 1), (1, 0)])  37.8 us
    pallas_call x4, Pallas kernels, project(): pl.pallas_call(kernel, in_specs=[SMEM] + [VMEM] * (len(args) - 1), out_sp...  12.5 us
    ppermute x12, starting transfers between devices, swap(): return lax.ppermute(a, axis, [(0, 1), (1, 0)])  9.94 us
    pallas_call x13, Pallas kernels, call(): pl.pallas_call(kernel, scratch_shapes=scratch, out_shape=shapes, in_specs...  9.39 us
    ppermute x2, starting transfers between devices, pairs_step(): a_z[p] = lax.ppermute(pieces[p], DEC, [(0, 2), (3, 1), (1, 0), (2, 3)])  6.03 us
    ppermute x3, starting transfers between devices, pairs_step(): lax.ppermute(packed, DEC, [((i + s) % n, i) for i in range(n)])  5.56 us
    ppermute x1, starting transfers between devices, pairs_step(): given = lax.ppermute(merged, DEC, partners)  4.78 us
  transfers between devices with their start and end apart: 28, of which 10 were waited for; matrix products, arithmetic and copies ran while one was open for 1% of the time, Pallas kernels for 13%

profile of v5, /device:TPU:0, one launch (start us, length us, event | category | flops | bytes accessed | tf_op | source)
XLA Modules:
  0.0 159.0 jit_solution(9924044892378083366)
XLA Ops:
  0.6 0.6 pad_add_fusion.1.ids
  1.3 2.9 %shard_map.114 = (bf16[256,896]{1,0:T(8,128)(2,1)}, bf16[272,896]{1,0:T(8,128)(2,1)}) custom-call(s32[4]{0:T(128)} %pad_add_fusion.1.ids, bf16[528,1792]{1,0:T(8,128)(2,1)} %bitcast.12), custom_call_target="tpu_custom_call" | custom-call | tf_op jit(solution)/shard_map/pallas_call | solution.py:311
  4.2 4.1 %collective-permute-start = (bf16[256,896]{1,0:T(8,128)(2,1)}, bf16[256,896]{1,0:T(8,128)(2,1)}, u32[]{:S(2)}, u32[]{:S(2)}) collective-permute-start(bf16[256,896]{1,0:T(8,128)(2,1)} %get-tuple-element.51), channel_id=1, source_target_pairs={{0,8},{12,4},{4,0},{8,12},{1,9},{13,5},{5,1},{9,13},{2,10},{14,6},... | collective-permute-start | bytes 1376264 | tf_op jit(solution)/shard_map/ppermute | solution.py:627
  8.3 1.9 %collective-permute-start.2 = (bf16[272,896]{1,0:T(8,128)(2,1)}, bf16[272,896]{1,0:T(8,128)(2,1)S(1)}, u32[]{:S(2)}, u32[]{:S(2)}) collective-permute-start(bf16[272,896]{1,0:T(8,128)(2,1)} %get-tuple-element.43), channel_id=1, source_target_pairs={{0,8},{12,4},{4,0},{8,12},{1,9},{13,5},{5,1},{9,13},{2,10},{14,6},... | collective-permute-start | bytes 1462280 | tf_op jit(solution)/shard_map/ppermute | solution.py:627
  10.2 9.3 %collective-permute-done.z0.z = bf16[256,896]{1,0:T(8,128)(2,1)} collective-permute-done((bf16[256,896]{1,0:T(8,128)(2,1)}, bf16[256,896]{1,0:T(8,128)(2,1)}, u32[]{:S(2)}, u32[]{:S(2)}) %collective-permute-start) | collective-permute-done | bytes 458784 | tf_op jit(solution)/shard_map/ppermute | solution.py:627
  19.5 1.4 collective-permute-start.7
  21.0 37.4 %collective-permute-done.2.z1.z = bf16[272,896]{1,0:T(8,128)(2,1)S(1)} collective-permute-done((bf16[272,896]{1,0:T(8,128)(2,1)}, bf16[272,896]{1,0:T(8,128)(2,1)S(1)}, u32[]{:S(2)}, u32[]{:S(2)}) %collective-permute-start.2) | collective-permute-done | bytes 487456 | tf_op jit(solution)/shard_map/ppermute | solution.py:627
  58.4 1.5 collective-permute-start.3
  60.4 1.5 collective-permute-start.1
  62.0 0.7 collective-permute-start.12
  62.7 28.1 %collective-permute-done.1.y0.y = bf16[256,896]{1,0:T(8,128)(2,1)} collective-permute-done((bf16[256,896]{1,0:T(8,128)(2,1)}, bf16[256,896]{1,0:T(8,128)(2,1)}, u32[]{:S(2)}, u32[]{:S(2)}) %collective-permute-start.1) | collective-permute-done | bytes 458784 | tf_op jit(solution)/shard_map/ppermute | solution.py:200
  90.8 1.5 copy-done.1
  92.3 3.6 %shard_map.117 = (f32[192,624]{1,0:T(8,128)S(1)}, f32[192,624]{1,0:T(8,128)S(1)}) custom-call(s32[4]{0:T(128)S(1)} %copy-done.21, bf16[384,1792]{1,0:T(8,128)(2,1)S(1)} %copy-done, bf16[384,1792]{1,0:T(8,128)(2,1)S(1)} %collective-permute-done.6.far_ref, bf16[528,1792]{1,0:T(8,128)(2,1)S(1)} %bitcast.13, bf16[256,896]{1,0:T(8,128)(2,1)} %collective-permute-done.z0.z, ...), custom_call_target="tpu_custom_call" | custom-call | flops 858783744 | bytes 1916928 | tf_op jit(solution)/shard_map/pallas_call | solution.py:285
  96.0 0.8 multiply_sine_fusion
  96.8 2.7 %shard_map.115 = (f32[192,528]{1,0:T(8,128)S(1)}, f32[192,528]{1,0:T(8,128)S(1)}) custom-call(s32[4]{0:T(128)S(1)} %copy-done.21, bf16[384,1792]{1,0:T(8,128)(2,1)S(1)} %copy-done, bf16[528,1792]{1,0:T(8,128)(2,1)S(1)} %bitcast.14, bf16[256,896]{1,0:T(8,128)(2,1)} %collective-permute-done.z0.z, bf16[256,896]{1,0:T(8,128)(2,1)} %collective-permute-done.1.y0.y, ...), custom_call_target="tpu_custom_call" | custom-call | flops 726663168 | bytes 1622016 | tf_op jit(solution)/shard_map/pallas_call | solution.py:285
  99.6 0.6 collective-permute-start.4
  100.1 1.5 collective-permute-start.13
  101.7 0.7 shard_map.118
  102.5 1.5 collective-permute-start.10
  104.0 0.6 shard_map.116
  104.6 0.6 collective-permute-start.5
  105.2 7.4 %collective-permute-done.13.by = bf16[256,896]{1,0:T(8,128)(2,1)S(1)} collective-permute-done((bf16[256,896]{1,0:T(8,128)(2,1)S(1)}, bf16[256,896]{1,0:T(8,128)(2,1)S(1)}, u32[]{:S(2)}, u32[]{:S(2)}) %collective-permute-start.13) | collective-permute-done | bytes 458784 | tf_op jit(solution)/shard_map/ppermute | solution.py:200
  112.6 3.0 %shard_map.121 = (f32[192,512]{1,0:T(8,128)}, f32[192,512]{1,0:T(8,128)S(1)}) custom-call(s32[4]{0:T(128)S(1)} %copy-done.21, bf16[384,1792]{1,0:T(8,128)(2,1)S(1)} %copy-done, bf16[384,1792]{1,0:T(8,128)(2,1)S(1)} %collective-permute-done.6.far_ref, bf16[256,896]{1,0:T(8,128)(2,1)} %collective-permute-done.z0.z, ...), custom_call_target="tpu_custom_call" | custom-call | flops 704643072 | bytes 1572864 | tf_op jit(solution)/shard_map/pallas_call | solution.py:285
  115.6 3.2 %shard_map.120 = (f32[192,480]{1,0:T(8,128)}, f32[192,480]{1,0:T(8,128)S(1)}) custom-call(s32[4]{0:T(128)S(1)} %copy-done.21, bf16[384,1792]{1,0:T(8,128)(2,1)S(1)} %copy-done, bf16[384,1792]{1,0:T(8,128)(2,1)S(1)} %collective-permute-done.6.far_ref, bf16[272,896]{1,0:T(8,128)(2,1)S(1)} %collective-permute-done.2.z1.z, ...), custom_call_target="tpu_custom_call" | custom-call | flops 660602880 | bytes 1474560 | tf_op jit(solution)/shard_map/pallas_call | solution.py:285
  118.8 0.8 copy-done.19
  120.1 0.6 shard_map.126.k0_ref
  121.4 2.3 %collective-permute-start.24 = (s32[1,60]{1,0:T(1,128)S(1)}, s32[1,60]{1,0:T(1,128)S(1)}, u32[]{:S(2)}, u32[]{:S(2)}) collective-permute-start(s32[1,60]{1,0:T(1,128)S(1)} %add_bitcast_fusion), channel_id=1, source_target_pairs={{12,0},{0,4},{4,8},{8,12},{13,1},{1,5},{5,9},{9,13},{14,2},{2,6},{... | collective-permute-start | bytes 728 | tf_op jit(solution)/shard_map/ppermute | solution.py:633
  123.7 1.7 %collective-permute-start.23 = (s32[1,60]{1,0:T(1,128)S(1)}, s32[1,60]{1,0:T(1,128)S(1)}, u32[]{:S(2)}, u32[]{:S(2)}) collective-permute-start(s32[1,60]{1,0:T(1,128)S(1)} %add_bitcast_fusion), channel_id=1, source_target_pairs={{8,0},{12,4},{0,8},{4,12},{9,1},{13,5},{1,9},{5,13},{10,2},{14,6},... | collective-permute-start | bytes 728 | tf_op jit(solution)/shard_map/ppermute | solution.py:633
  125.4 1.4 collective-permute-done.24
  126.8 1.6 %collective-permute-start.22 = (s32[1,60]{1,0:T(1,128)S(1)}, s32[1,60]{1,0:T(1,128)S(1)}, u32[]{:S(2)}, u32[]{:S(2)}) collective-permute-start(s32[1,60]{1,0:T(1,128)S(1)} %add_bitcast_fusion), channel_id=1, source_target_pairs={{4,0},{8,4},{12,8},{0,12},{5,1},{9,5},{13,9},{1,13},{6,2},{10,6},{... | collective-permute-start | bytes 728 | tf_op jit(solution)/shard_map/ppermute | solution.py:633
  128.4 1.9 %collective-permute-done.22 = s32[1,60]{1,0:T(1,128)S(1)} collective-permute-done((s32[1,60]{1,0:T(1,128)S(1)}, s32[1,60]{1,0:T(1,128)S(1)}, u32[]{:S(2)}, u32[]{:S(2)}) %collective-permute-start.22) | collective-permute-done | bytes 272 | tf_op jit(solution)/shard_map/ppermute | solution.py:633
  130.4 1.7 %shard_map.127 = (bf16[128,640]{1,0:T(8,128)(2,1)S(1)}, f32[8,768]{1,0:T(8,128)S(1)}) custom-call(s32[4]{0:T(128)S(1)} %copy-done.21, s32[8,128]{1,0:T(8,128)S(1)} %pad.8.tab_ref, bf16[128,576]{1,0:T(8,128)(2,1)S(1)} %bitcast.16, bf16[1024,576]{1,0:T(8,128)(2,1)S(1)} %bitcast.15, bf16[16,576]{1,0:T(8,128)(2,1)S(1)} %pad.9.own_ref), custom_call_target="tpu_custom_call" | custom-call | flops 20000000 | bytes 2000000 | tf_op jit(solution)/shard_map/pallas_call | solution.py:577
  132.1 0.5 collective-permute-start.25
  132.6 1.0 copy-done.20
  133.6 1.3 shard_map.122
  135.0 1.6 collective-permute-start.15
  136.5 0.9 collective-permute-done.25.far_ref
  137.5 0.8 shard_map.128.own
  138.3 0.7 collective-permute-start.26
  139.0 2.3 %collective-permute-done.15.got = bf16[192,528]{1,0:T(8,128)(2,1)S(1)} collective-permute-done((bf16[192,528]{1,0:T(8,128)(2,1)S(1)}, bf16[192,528]{1,0:T(8,128)(2,1)S(1)}, u32[]{:S(2)}, u32[]{:S(2)}) %collective-permute-start.15) | collective-permute-done | bytes 202784 | tf_op jit(solution)/shard_map/ppermute | solution.py:200
  141.3 3.0 %collective-permute-start.17 = (bf16[96,528]{1,0:T(8,128)(2,1)S(1)}, bf16[96,528]{1,0:T(8,128)(2,1)S(1)}, u32[]{:S(2)}, u32[]{:S(2)}) collective-permute-start(bf16[96,528]{1,0:T(8,128)(2,1)S(1)} %get-tuple-element.58), channel_id=1, source_target_pairs={{0,4},{4,0},{8,12},{12,8},{1,5},{5,1},{9,13},{13,9},{2,6},{6,2},{1... | collective-permute-start | bytes 304136 | tf_op jit(solution)/shard_map/ppermute | solution.py:743
  144.6 4.8 %collective-permute-start.27 = (bf16[128,512]{1,0:T(8,128)(2,1)S(1)}, bf16[128,512]{1,0:T(8,128)(2,1)S(1)}, u32[]{:S(2)}, u32[]{:S(2)}) collective-permute-start(bf16[128,512]{1,0:T(8,128)(2,1)S(1)} %shard_map.129.own), channel_id=1, source_target_pairs={{0,4},{4,0},{8,12},{12,8},{1,5},{5,1},{9,13},{13,9},{2,6},{6,2},{1... | collective-permute-start | bytes 393224 | tf_op jit(solution)/shard_map/ppermute | solution.py:722
  149.4 0.9 shard_map.124
  150.4 1.6 collective-permute-start.19
  152.3 2.9 %collective-permute-done.19.refs_2_ = bf16[96,384]{1,0:T(8,128)(2,1)S(1)} collective-permute-done((bf16[96,384]{1,0:T(8,128)(2,1)S(1)}, bf16[96,384]{1,0:T(8,128)(2,1)S(1)}, u32[]{:S(2)}, u32[]{:S(2)}) %collective-permute-start.19) | collective-permute-done | bytes 73760 | tf_op jit(solution)/shard_map/ppermute | solution.py:756
  155.2 1.2 collective-permute-done.20.refs_3_
  156.5 1.3 shard_map.125
  157.8 1.2 shard_map.130
  (95 shorter events, 2.8 us)
Async XLA Ops:
  0.6 7.7 %copy-start = (bf16[384,1792]{1,0:T(8,128)(2,1)S(1)}, bf16[384,1792]{1,0:T(8,128)(2,1)}, u32[]{:S(2)}) copy-start(bf16[384,1792]{1,0:T(8,128)(2,1)} %x_ref.7) | copy-start | bytes 4128772
  1.3 89.5 %copy-start.21 = (s32[4]{0:T(128)S(1)}, s32[4]{0:T(128)}, u32[]{:S(2)}) copy-start(s32[4]{0:T(128)} %pad_add_fusion.1.ids) | copy-start | bytes 52
  4.2 15.3 %collective-permute-start = (bf16[256,896]{1,0:T(8,128)(2,1)}, bf16[256,896]{1,0:T(8,128)(2,1)}, u32[]{:S(2)}, u32[]{:S(2)}) collective-permute-start(bf16[256,896]{1,0:T(8,128)(2,1)} %get-tuple-element.51), channel_id=1, source_target_pairs={{0,8},{12,4},{4,0},{8,12},{1,9},{13,5},{5,1},{9,13},{2,10},{14,6},... | collective-permute-start | bytes 1376264 | tf_op jit(solution)/shard_map/ppermute | solution.py:627
  8.3 82.4 %collective-permute-start.6 = (bf16[384,1792]{1,0:T(8,128)(2,1)S(1)}, bf16[384,1792]{1,0:T(8,128)(2,1)S(1)}, u32[]{:S(2)}, u32[]{:S(2)}) collective-permute-start(bf16[384,1792]{1,0:T(8,128)(2,1)S(1)} %copy-done), channel_id=1, source_target_pairs={{0,4},{4,0},{8,12},{12,8},{1,5},{5,1},{9,13},{13,9},{2,6},{6,2},{1... | collective-permute-start | bytes 4128776 | tf_op jit(solution)/shard_map/ppermute | solution.py:637
  8.3 50.0 %collective-permute-start.2 = (bf16[272,896]{1,0:T(8,128)(2,1)}, bf16[272,896]{1,0:T(8,128)(2,1)S(1)}, u32[]{:S(2)}, u32[]{:S(2)}) collective-permute-start(bf16[272,896]{1,0:T(8,128)(2,1)} %get-tuple-element.43), channel_id=1, source_target_pairs={{0,8},{12,4},{4,0},{8,12},{1,9},{13,5},{5,1},{9,13},{2,10},{14,6},... | collective-permute-start | bytes 1462280 | tf_op jit(solution)/shard_map/ppermute | solution.py:627
  19.5 40.3 %collective-permute-start.7 = (bf16[272,896]{1,0:T(8,128)(2,1)}, bf16[272,896]{1,0:T(8,128)(2,1)}, u32[]{:S(2)}, u32[]{:S(2)}) collective-permute-start(bf16[272,896]{1,0:T(8,128)(2,1)} %get-tuple-element.43), channel_id=1, source_target_pairs={{4,8},{8,4},{5,9},{9,5},{6,10},{10,6},{7,11},{11,7},{20,24},{24,20... | collective-permute-start | bytes 1462280 | tf_op jit(solution)/shard_map/ppermute | solution.py:641
  58.4 32.4 %collective-permute-start.3 = (bf16[272,896]{1,0:T(8,128)(2,1)S(1)}, bf16[272,896]{1,0:T(8,128)(2,1)}, u32[]{:S(2)}, u32[]{:S(2)}) collective-permute-start(bf16[272,896]{1,0:T(8,128)(2,1)S(1)} %collective-permute-done.2.z1.z), channel_id=1, source_target_pairs={{0,16},{16,0},{1,17},{17,1},{2,18},{18,2},{3,19},{19,3},{4,20},{20... | collective-permute-start | bytes 1462280 | tf_op jit(solution)/shard_map/ppermute | solution.py:200
  59.9 30.9 %collective-permute-start.8 = (bf16[272,896]{1,0:T(8,128)(2,1)}, bf16[272,896]{1,0:T(8,128)(2,1)}, u32[]{:S(2)}, u32[]{:S(2)}) collective-permute-start(bf16[272,896]{1,0:T(8,128)(2,1)} %collective-permute-done.7.bz1.bz), channel_id=1, source_target_pairs={{0,16},{16,0},{1,17},{17,1},{2,18},{18,2},{3,19},{19,3},{4,20},{20... | collective-permute-start | bytes 1462280 | tf_op jit(solution)/shard_map/ppermute | solution.py:200
  60.4 30.4 %collective-permute-start.1 = (bf16[256,896]{1,0:T(8,128)(2,1)}, bf16[256,896]{1,0:T(8,128)(2,1)}, u32[]{:S(2)}, u32[]{:S(2)}) collective-permute-start(bf16[256,896]{1,0:T(8,128)(2,1)} %collective-permute-done.z0.z), channel_id=1, source_target_pairs={{0,16},{16,0},{1,17},{17,1},{2,18},{18,2},{3,19},{19,3},{4,20},{20... | collective-permute-start | bytes 1376264 | tf_op jit(solution)/shard_map/ppermute | solution.py:200
  62.0 38.1 %collective-permute-start.12 = (bf16[256,896]{1,0:T(8,128)(2,1)}, bf16[256,896]{1,0:T(8,128)(2,1)S(1)}, u32[]{:S(2)}, u32[]{:S(2)}) collective-permute-start(bf16[256,896]{1,0:T(8,128)(2,1)} %get-tuple-element.51), channel_id=1, source_target_pairs={{4,8},{8,4},{5,9},{9,5},{6,10},{10,6},{7,11},{11,7},{20,24},{24,20... | collective-permute-start | bytes 1376264 | tf_op jit(solution)/shard_map/ppermute | solution.py:641
  92.3 4.5 %copy-start.23 = (f32[1536]{0:T(1024)S(1)}, f32[1536]{0:T(1024)}, u32[]{:S(2)}) copy-start(f32[1536]{0:T(1024)} %param.12) | copy-start | bytes 18436
  92.3 4.5 %copy-start.2 = (bf16[1792,528]{0,1:T(8,128)(2,1)S(1)}, bf16[1792,528]{0,1:T(8,128)(2,1)}, u32[]{:S(2)}) copy-start(bf16[1792,528]{0,1:T(8,128)(2,1)} %param.11) | copy-start | bytes 5677060
  95.9 5.7 %copy-start.3 = (f32[192,624]{1,0:T(8,128)}, f32[192,624]{1,0:T(8,128)S(1)}, u32[]{:S(2)}) copy-start(f32[192,624]{1,0:T(8,128)S(1)} %get-tuple-element.44.kept.kept_far) | copy-start | bytes 1437700
  95.9 5.7 %collective-permute-start.9 = (f32[192,624]{1,0:T(8,128)S(1)}, f32[192,624]{1,0:T(8,128)S(1)}, u32[]{:S(2)}, u32[]{:S(2)}) collective-permute-start(f32[192,624]{1,0:T(8,128)S(1)} %get-tuple-element.45), channel_id=1, source_target_pairs={{0,1},{1,0},{2,3},{3,2},{4,5},{5,4},{6,7},{7,6},{8,9},{9,8},{10,11... | collective-permute-start | bytes 1437704 | tf_op jit(solution)/shard_map/ppermute | solution.py:200
  99.6 4.4 %collective-permute-start.4 = (f32[192,528]{1,0:T(8,128)S(1)}, f32[192,528]{1,0:T(8,128)S(1)}, u32[]{:S(2)}, u32[]{:S(2)}) collective-permute-start(f32[192,528]{1,0:T(8,128)S(1)} %get-tuple-element.40), channel_id=1, source_target_pairs={{0,1},{1,0},{2,3},{3,2},{4,5},{5,4},{6,7},{7,6},{8,9},{9,8},{10,11... | collective-permute-start | bytes 1216520 | tf_op jit(solution)/shard_map/ppermute | solution.py:200
  100.1 12.5 %collective-permute-start.13 = (bf16[256,896]{1,0:T(8,128)(2,1)S(1)}, bf16[256,896]{1,0:T(8,128)(2,1)S(1)}, u32[]{:S(2)}, u32[]{:S(2)}) collective-permute-start(bf16[256,896]{1,0:T(8,128)(2,1)S(1)} %collective-permute-done.12.bz), channel_id=1, source_target_pairs={{0,16},{16,0},{1,17},{17,1},{2,18},{18,2},{3,19},{19,3},{4,20},{20... | collective-permute-start | bytes 1376264 | tf_op jit(solution)/shard_map/ppermute | solution.py:200
  102.5 17.6 %copy-start.7 = (f32[192,624]{1,0:T(8,128)}, f32[192,624]{1,0:T(8,128)S(1)}, u32[]{:S(2)}) copy-start(f32[192,624]{1,0:T(8,128)S(1)} %get-tuple-element.46.keep1) | copy-start | bytes 1437700
  102.5 17.6 %collective-permute-start.10 = (bf16[192,624]{1,0:T(8,128)(2,1)S(1)}, bf16[192,624]{1,0:T(8,128)(2,1)S(1)}, u32[]{:S(2)}, u32[]{:S(2)}) collective-permute-start(bf16[192,624]{1,0:T(8,128)(2,1)S(1)} %get-tuple-element.47), channel_id=1, source_target_pairs={{0,2},{2,0},{1,3},{3,1},{4,6},{6,4},{5,7},{7,5},{8,10},{10,8},{9,1... | collective-permute-start | bytes 718856 | tf_op jit(solution)/shard_map/ppermute | solution.py:200
  104.6 15.5 %copy-start.9 = (f32[192,528]{1,0:T(8,128)}, f32[192,528]{1,0:T(8,128)S(1)}, u32[]{:S(2)}) copy-start(f32[192,528]{1,0:T(8,128)S(1)} %get-tuple-element.41.keep0) | copy-start | bytes 1216516
  104.6 15.4 %collective-permute-start.5 = (bf16[192,528]{1,0:T(8,128)(2,1)S(1)}, bf16[192,528]{1,0:T(8,128)(2,1)S(1)}, u32[]{:S(2)}, u32[]{:S(2)}) collective-permute-start(bf16[192,528]{1,0:T(8,128)(2,1)S(1)} %get-tuple-element.42), channel_id=1, source_target_pairs={{0,2},{2,0},{1,3},{3,1},{4,6},{6,4},{5,7},{7,5},{8,10},{10,8},{9,1... | collective-permute-start | bytes 608264 | tf_op jit(solution)/shard_map/ppermute | solution.py:200
  115.6 3.2 %copy-start.17 = (f32[192,512]{1,0:T(8,128)}, f32[192,512]{1,0:T(8,128)S(1)}, u32[]{:S(2)}) copy-start(f32[192,512]{1,0:T(8,128)S(1)} %get-tuple-element.52.kept_head) | copy-start | bytes 1179652
  115.6 4.5 %copy-start.22 = (f32[512]{0:T(512)S(1)}, f32[512]{0:T(512)}, u32[]{:S(2)}) copy-start(f32[512]{0:T(512)} %param.13) | copy-start | bytes 6148
  115.6 17.0 %collective-permute-start.14 = (f32[192,512]{1,0:T(8,128)}, f32[192,512]{1,0:T(8,128)}, u32[]{:S(2)}, u32[]{:S(2)}) collective-permute-start(f32[192,512]{1,0:T(8,128)} %get-tuple-element.53), channel_id=1, source_target_pairs={{0,1},{1,0},{2,3},{3,2},{4,5},{5,4},{6,7},{7,6},{8,9},{9,8},{10,11... | collective-permute-start | bytes 1179656 | tf_op jit(solution)/shard_map/ppermute | solution.py:200
  119.6 1.7 %copy-start.27 = (s32[4,1]{0,1:T(1,128)S(1)}, s32[4,1]{0,1:T(1,128)}, u32[]{:S(2)}) copy-start(s32[4,1]{0,1:T(1,128)} %param.17) | copy-start | bytes 52
  119.6 8.8 %copy-start.24 = (bf16[4,576]{1,0:T(4,128)(2,1)S(1)}, bf16[4,576]{1,0:T(4,128)(2,1)}, u32[]{:S(2)}) copy-start(bf16[4,576]{1,0:T(4,128)(2,1)} %param.19) | copy-start | bytes 13828
  119.6 10.7 %copy-start.11 = (bf16[32,32,576]{2,1,0:T(8,128)(2,1)S(1)}, bf16[32,32,576]{2,1,0:T(8,128)(2,1)}, u32[]{:S(2)}) copy-start(bf16[32,32,576]{2,1,0:T(8,128)(2,1)} %param.14) | copy-start | bytes 3538948
  119.6 10.7 %copy-start.16 = (bf16[4,32,576]{2,1,0:T(8,128)(2,1)S(1)}, bf16[4,32,576]{2,1,0:T(8,128)(2,1)}, u32[]{:S(2)}) copy-start(bf16[4,32,576]{2,1,0:T(8,128)(2,1)} %param.18) | copy-start | bytes 442372
  119.6 13.0 %collective-permute-start.11 = (f32[192,480]{1,0:T(8,128)}, f32[192,480]{1,0:T(8,128)}, u32[]{:S(2)}, u32[]{:S(2)}) collective-permute-start(f32[192,480]{1,0:T(8,128)} %get-tuple-element.50), channel_id=1, source_target_pairs={{0,1},{1,0},{2,3},{3,2},{4,5},{5,4},{6,7},{7,6},{8,9},{9,8},{10,11... | collective-permute-start | bytes 1105928 | tf_op jit(solution)/shard_map/ppermute | solution.py:200
  120.9 11.7 %copy-start.4 = (f32[192,624]{1,0:T(8,128)S(1)}, f32[192,624]{1,0:T(8,128)}, u32[]{:S(2)}) copy-start(f32[192,624]{1,0:T(8,128)} %copy-done.3) | copy-start | bytes 1437700
  120.9 11.7 %copy-start.6 = (f32[192,624]{1,0:T(8,128)S(1)}, f32[192,624]{1,0:T(8,128)}, u32[]{:S(2)}) copy-start(f32[192,624]{1,0:T(8,128)} %copy-done.5) | copy-start | bytes 1437700
  120.9 16.6 %collective-permute-start.21 = (bf16[384,576]{1,0:T(8,128)(2,1)S(1)}, bf16[384,576]{1,0:T(8,128)(2,1)S(1)}, u32[]{:S(2)}, u32[]{:S(2)}) collective-permute-start(bf16[384,576]{1,0:T(8,128)(2,1)S(1)} %shard_map.126.k0_ref), channel_id=1, source_target_pairs={{0,1},{1,0},{2,3},{3,2},{4,5},{5,4},{6,7},{7,6},{8,9},{9,8},{10,11... | collective-permute-start | bytes 1327112 | tf_op jit(solution)/shard_map/ppermute | solution.py:200
  121.3 11.3 %copy-start.18 = (f32[192,512]{1,0:T(8,128)S(1)}, f32[192,512]{1,0:T(8,128)}, u32[]{:S(2)}) copy-start(f32[192,512]{1,0:T(8,128)} %copy-done.17) | copy-start | bytes 1179652
  121.4 5.4 %collective-permute-start.24 = (s32[1,60]{1,0:T(1,128)S(1)}, s32[1,60]{1,0:T(1,128)S(1)}, u32[]{:S(2)}, u32[]{:S(2)}) collective-permute-start(s32[1,60]{1,0:T(1,128)S(1)} %add_bitcast_fusion), channel_id=1, source_target_pairs={{12,0},{0,4},{4,8},{8,12},{13,1},{1,5},{5,9},{9,13},{14,2},{2,6},{... | collective-permute-start | bytes 728 | tf_op jit(solution)/shard_map/ppermute | solution.py:633
  123.7 4.7 %collective-permute-start.23 = (s32[1,60]{1,0:T(1,128)S(1)}, s32[1,60]{1,0:T(1,128)S(1)}, u32[]{:S(2)}, u32[]{:S(2)}) collective-permute-start(s32[1,60]{1,0:T(1,128)S(1)} %add_bitcast_fusion), channel_id=1, source_target_pairs={{8,0},{12,4},{0,8},{4,12},{9,1},{13,5},{1,9},{5,13},{10,2},{14,6},... | collective-permute-start | bytes 728 | tf_op jit(solution)/shard_map/ppermute | solution.py:633
  126.8 3.6 %collective-permute-start.22 = (s32[1,60]{1,0:T(1,128)S(1)}, s32[1,60]{1,0:T(1,128)S(1)}, u32[]{:S(2)}, u32[]{:S(2)}) collective-permute-start(s32[1,60]{1,0:T(1,128)S(1)} %add_bitcast_fusion), channel_id=1, source_target_pairs={{4,0},{8,4},{12,8},{0,12},{5,1},{9,5},{13,9},{1,13},{6,2},{10,6},{... | collective-permute-start | bytes 728 | tf_op jit(solution)/shard_map/ppermute | solution.py:633
  132.1 5.4 %collective-permute-start.25 = (bf16[128,640]{1,0:T(8,128)(2,1)S(1)}, bf16[128,640]{1,0:T(8,128)(2,1)S(1)}, u32[]{:S(2)}, u32[]{:S(2)}) collective-permute-start(bf16[128,640]{1,0:T(8,128)(2,1)S(1)} %get-tuple-element.69.old_ref), channel_id=1, source_target_pairs={{0,4},{4,0},{8,12},{12,8},{1,5},{5,1},{9,13},{13,9},{2,6},{6,2},{1... | collective-permute-start | bytes 491528 | tf_op jit(solution)/shard_map/ppermute | solution.py:653
  134.9 9.4 %copy-start.8 = (f32[192,624]{1,0:T(8,128)S(1)}, f32[192,624]{1,0:T(8,128)}, u32[]{:S(2)}) copy-start(f32[192,624]{1,0:T(8,128)} %copy-done.7) | copy-start | bytes 1437700
  134.9 9.4 %copy-start.10 = (f32[192,528]{1,0:T(8,128)S(1)}, f32[192,528]{1,0:T(8,128)}, u32[]{:S(2)}) copy-start(f32[192,528]{1,0:T(8,128)} %copy-done.9) | copy-start | bytes 1216516
  134.9 9.4 %copy-start.13 = (bf16[192,624]{1,0:T(8,128)(2,1)S(1)}, bf16[192,624]{1,0:T(8,128)(2,1)}, u32[]{:S(2)}) copy-start(bf16[192,624]{1,0:T(8,128)(2,1)} %copy-done.12) | copy-start | bytes 718852
  134.9 9.4 %copy-start.15 = (bf16[192,528]{1,0:T(8,128)(2,1)S(1)}, bf16[192,528]{1,0:T(8,128)(2,1)}, u32[]{:S(2)}) copy-start(bf16[192,528]{1,0:T(8,128)(2,1)} %copy-done.14) | copy-start | bytes 608260
  135.0 6.3 %collective-permute-start.15 = (bf16[192,528]{1,0:T(8,128)(2,1)S(1)}, bf16[192,528]{1,0:T(8,128)(2,1)S(1)}, u32[]{:S(2)}, u32[]{:S(2)}) collective-permute-start(bf16[192,528]{1,0:T(8,128)(2,1)S(1)} %get-tuple-element.55), channel_id=1, source_target_pairs={{0,2},{2,0},{1,3},{3,1},{4,6},{6,4},{5,7},{7,5},{8,10},{10,8},{9,1... | collective-permute-start | bytes 608264 | tf_op jit(solution)/shard_map/ppermute | solution.py:200
  138.3 6.2 %collective-permute-start.26 = (bf16[128,640]{1,0:T(8,128)(2,1)S(1)}, bf16[128,640]{1,0:T(8,128)(2,1)S(1)}, u32[]{:S(2)}, u32[]{:S(2)}) collective-permute-start(bf16[128,640]{1,0:T(8,128)(2,1)S(1)} %shard_map.128.own), channel_id=1, source_target_pairs={{4,12},{12,4},{5,13},{13,5},{6,14},{14,6},{7,15},{15,7},{20,28},{2... | collective-permute-start | bytes 491528 | tf_op jit(solution)/shard_map/ppermute | solution.py:720
  141.3 8.2 %collective-permute-start.17 = (bf16[96,528]{1,0:T(8,128)(2,1)S(1)}, bf16[96,528]{1,0:T(8,128)(2,1)S(1)}, u32[]{:S(2)}, u32[]{:S(2)}) collective-permute-start(bf16[96,528]{1,0:T(8,128)(2,1)S(1)} %get-tuple-element.58), channel_id=1, source_target_pairs={{0,4},{4,0},{8,12},{12,8},{1,5},{5,1},{9,13},{13,9},{2,6},{6,2},{1... | collective-permute-start | bytes 304136 | tf_op jit(solution)/shard_map/ppermute | solution.py:743
  144.4 5.1 %collective-permute-start.16 = (bf16[96,528]{1,0:T(8,128)(2,1)S(1)}, bf16[96,528]{1,0:T(8,128)(2,1)S(1)}, u32[]{:S(2)}, u32[]{:S(2)}) collective-permute-start(bf16[96,528]{1,0:T(8,128)(2,1)S(1)} %get-tuple-element.57), channel_id=1, source_target_pairs={{0,4},{4,0},{8,12},{12,8},{1,5},{5,1},{9,13},{13,9},{2,6},{6,2},{1... | collective-permute-start | bytes 304136 | tf_op jit(solution)/shard_map/ppermute | solution.py:736
  144.6 13.1 %collective-permute-start.27 = (bf16[128,512]{1,0:T(8,128)(2,1)S(1)}, bf16[128,512]{1,0:T(8,128)(2,1)S(1)}, u32[]{:S(2)}, u32[]{:S(2)}) collective-permute-start(bf16[128,512]{1,0:T(8,128)(2,1)S(1)} %shard_map.129.own), channel_id=1, source_target_pairs={{0,4},{4,0},{8,12},{12,8},{1,5},{5,1},{9,13},{13,9},{2,6},{6,2},{1... | collective-permute-start | bytes 393224 | tf_op jit(solution)/shard_map/ppermute | solution.py:722
  150.3 1.9 %collective-permute-start.18 = (bf16[96,384]{1,0:T(8,128)(2,1)S(1)}, bf16[96,384]{1,0:T(8,128)(2,1)S(1)}, u32[]{:S(2)}, u32[]{:S(2)}) collective-permute-start(bf16[96,384]{1,0:T(8,128)(2,1)S(1)} %get-tuple-element.61), channel_id=1, source_target_pairs={{0,1},{1,0},{2,3},{3,2},{4,5},{5,4},{6,7},{7,6},{8,9},{9,8},{10,11... | collective-permute-start | bytes 221192 | tf_op jit(solution)/shard_map/ppermute | solution.py:756
  150.4 4.8 %collective-permute-start.19 = (bf16[96,384]{1,0:T(8,128)(2,1)S(1)}, bf16[96,384]{1,0:T(8,128)(2,1)S(1)}, u32[]{:S(2)}, u32[]{:S(2)}) collective-permute-start(bf16[96,384]{1,0:T(8,128)(2,1)S(1)} %get-tuple-element.62), channel_id=1, source_target_pairs={{0,2},{1,3},{2,0},{3,1},{4,6},{5,7},{6,4},{7,5},{8,10},{9,11},{10,... | collective-permute-start | bytes 221192 | tf_op jit(solution)/shard_map/ppermute | solution.py:756
  152.0 4.5 %collective-permute-start.20 = (bf16[96,384]{1,0:T(8,128)(2,1)S(1)}, bf16[96,384]{1,0:T(8,128)(2,1)S(1)}, u32[]{:S(2)}, u32[]{:S(2)}) collective-permute-start(bf16[96,384]{1,0:T(8,128)(2,1)S(1)} %get-tuple-element.63), channel_id=1, source_target_pairs={{0,3},{1,2},{2,1},{3,0},{4,7},{5,6},{6,5},{7,4},{8,11},{9,10},{10,... | collective-permute-start | bytes 221192 | tf_op jit(solution)/shard_map/ppermute | solution.py:756
  (8 other events, 8.5 us)

commit v6 on v5

--- a/solution.py
+++ b/solution.py
@@ -189,7 +189,6 @@
 VMEM = pl.BlockSpec(memory_space=pltpu.VMEM)
 SMEM = pl.BlockSpec(memory_space=pltpu.SMEM)
 VMEM_GRANT = 16 * 2**20
-VMEM_ALL = 62 * 2**20
 GRP, DEC, STG, TP = "grp", "dec", "stg", "tp"
 TILE = 256
 F32 = jnp.float32
@@ -292,30 +291,6 @@
         ),
         compiler_params=pltpu.CompilerParams(vmem_limit_bytes=VMEM_GRANT),
     )(*args)
-
-
-def share_kernel(ids, weight, head, tail, sems):
-    split, half = head.shape
-    columns = pl.ds(pl.multiple_of(ids[0] * half, 128), half)
-    first = pltpu.make_async_copy(weight.at[split:, columns], tail, sems.at[0])
-    second = pltpu.make_async_copy(weight.at[:split, columns], head, sems.at[1])
-    first.start()
-    second.start()
-    first.wait()
-    second.wait()
-
-
-def share(ids, weight, split):
-    rows, feats = weight.shape
-    sizes = (split, rows - split)
-    return pl.pallas_call(
-        share_kernel,
-        in_specs=[SMEM, pl.BlockSpec(memory_space=pltpu.HBM)],
-        out_specs=[VMEM] * 2,
-        out_shape=[jax.ShapeDtypeStruct((size, feats // 2), weight.dtype) for size in sizes],
-        scratch_shapes=[pltpu.SemaphoreType.DMA((2,))],
-        compiler_params=pltpu.CompilerParams(vmem_limit_bytes=VMEM_ALL),
-    )(ids, weight)
 
 
 def turn_kernel(out):
@@ -427,7 +402,7 @@
 def cross_near_kernel(ids, kept, got, send, keep):
     mine, away = parted(ids, kept[...] + got[...])
     keep[...] = mine
-    send[...] = away.astype(BF16)
+    send[...] = away
 
 
 def cross_far_kernel(cols, ids, kept, got, send, keep):
@@ -435,8 +410,8 @@
     mine, away = parted(ids, both[:, :cols])
     keep[:, :cols] = mine
     keep[:, cols:] = both[:, cols:]
-    send[:, :cols] = away.astype(BF16)
-    send[:, cols:] = both[:, cols:].astype(BF16)
+    send[:, :cols] = away
+    send[:, cols:] = both[:, cols:]
 
 
 def cross_rest_kernel(
@@ -464,11 +439,11 @@
     rows, cols = keep0.shape
     for i in range(2):
         last = slice(cols + i * keys, cols + (i + 1) * keys)
-        tail = keep1[:, last] + got1[:, last].astype(F32)
+        tail = keep1[:, last] + got1[:, last]
         if i == 0:
-            block = keep0[...] + got0[...].astype(F32)
+            block = keep0[...] + got0[...]
         else:
-            block = keep1[:, :cols] + got1[:, :cols].astype(F32)
+            block = keep1[:, :cols] + got1[:, :cols]
         raw = jnp.concatenate([tail, block], axis=1)
         at = slice(i * rows, (i + 1) * rows)
         latent = raw[:, :KVL]
@@ -479,14 +454,15 @@
         out[at, KVL:] = (rope * cos[at, :] + partner * sin[at, :]).astype(BF16)
 
 
-def pack(out, level, packed_ref):
-    packed_ref[:, :KVL] = out.astype(BF16)
+def pack(out, level, *packed_refs):
     lead = level.astype(BF16).astype(F32)
     rest = (level - lead).astype(BF16).astype(F32)
     last = level - lead - rest
     lane = lax.broadcasted_iota(jnp.int32, (out.shape[0], 128), 1)
     tail = jnp.where(lane == 0, lead, jnp.where(lane == 1, rest, jnp.where(lane == 2, last, 0.0)))
-    packed_ref[:, KVL:] = tail.astype(BF16)
+    for packed_ref in packed_refs:
+        packed_ref[:, :KVL] = out.astype(packed_ref.dtype)
+        packed_ref[:, KVL:] = tail.astype(packed_ref.dtype)
 
 
 def unpack(packed):
@@ -494,7 +470,7 @@
     return packed[:, :KVL].astype(F32), level
 
 
-def attend_kernel(query_ref, k0_ref, k1_ref, bias_ref, old_ref, far_ref, packed_ref):
+def attend_kernel(query_ref, k0_ref, k1_ref, bias_ref, old_ref, far_ref, own_ref, packed_ref):
     query = query_ref[...]
     keys = k0_ref.shape[0]
     requests = bias_ref.shape[0] // 2
@@ -515,7 +491,7 @@
     rounded = weights.astype(BF16)
     out = dot_n(rounded[:, :keys], k0_ref[:, :KVL]) + dot_n(rounded[:, keys:], k1_ref[:, :KVL])
     out = out + old * old_share + far * far_share
-    pack(out / total, peak + jnp.log(total), packed_ref)
+    pack(out / total, peak + jnp.log(total), own_ref, packed_ref)
 
 
 def combine_kernel(own, across, out):
@@ -532,8 +508,8 @@
 
 def return_first_kernel(keep0, got0, keep1, got1, low, send):
     rows, cols = low.shape
-    low[...] = keep0[:rows, :] + got0[:rows, :].astype(F32)
-    send[...] = (keep1[:rows, :cols] + got1[:rows, :cols].astype(F32)).astype(BF16)
+    low[...] = keep0[:rows, :] + got0[:rows, :]
+    send[...] = (keep1[:rows, :cols] + got1[:rows, :cols]).astype(BF16)
 
 
 def return_second_kernel(keep, got, high, send):
@@ -609,9 +585,10 @@
     group, index = lax.axis_index(GRP), lax.axis_index(DEC)
     stage, core = lax.axis_index(STG), lax.axis_index(TP)
     ids = jnp.stack([group, core, index, stage]).astype(jnp.int32)
-    tokens, _ = hidden_x.shape
+    tokens, feats = hidden_x.shape
     cols = proj_weight.shape[1]
     cut = QL - 2 * cols
+    half = feats // 2
     pages = page_plan.shape[0]
     requests, heads, _ = dec_query.shape
     queries = requests * heads
@@ -620,7 +597,10 @@
 
     weight = proj_weight.T
     split = cols // 2 // 128 * 128
-    pieces = share(ids, weight, split)
+    pieces = [
+        lax.dynamic_slice(weight, (0, group * half), (split, half)),
+        lax.dynamic_slice(weight, (split, group * half), (cols - split, half)),
+    ]
     partners = [(0, 1), (1, 0), (2, 3), (3, 2)]
     a_z, a_y, b_z, b_y = [None] * 2, [None] * 2, [None] * 2, [None] * 2
     for p in (1, 0):
@@ -645,7 +625,7 @@
     padded_key = jnp.pad(new_key, ((0, 3 * requests), (0, 0)))
     old, bias = call(
         functools.partial(old_kernel, n, pages),
-        [shaped(queries, KVL + 128, kind=BF16), shaped(8, 2 * tokens)],
+        [shaped(queries, KVL + 128), shaped(8, 2 * tokens)],
         [SMEM, VMEM, VMEM, VMEM, VMEM],
         (ids, tables, query, old_cache.reshape(-1, KVW), padded_key),
     )
@@ -669,7 +649,7 @@
     other0 = swap(send, TP)
     send0, keep0 = call(
         cross_near_kernel,
-        [shaped(rows, cols, kind=BF16), shaped(rows, cols)],
+        [shaped(rows, cols)] * 2,
         [SMEM, VMEM, VMEM],
         (ids, kept0, other0),
     )
@@ -682,7 +662,7 @@
     other1 = swap(send, TP)
     send1, keep1 = call(
         functools.partial(cross_far_kernel, cols),
-        [shaped(rows, cols + 2 * keys, kind=BF16), shaped(rows, cols + 2 * keys)],
+        [shaped(rows, cols + 2 * keys)] * 2,
         [SMEM, VMEM, VMEM],
         (ids, kept1, other1),
     )
@@ -711,14 +691,14 @@
         (keep0, got0, keep1, got1, cos, sin, turn, kv_scale),
     )
     far_keys = swap(key_rows, TP)
-    part_out = call(
+    own_out, part_out = call(
         attend_kernel,
-        shaped(queries, KVL + 128, kind=BF16),
+        [shaped(queries, KVL + 128), shaped(queries, KVL + 128, kind=BF16)],
         [VMEM] * 6,
         (query, key_rows, far_keys, bias, old, old_far),
     )
     across = lax.ppermute(part_out, DEC, [(1, 3), (3, 1)])
-    merged = call(combine_kernel, shaped(queries, KVL, kind=BF16), [VMEM] * 2, (part_out, across))
+    merged = call(combine_kernel, shaped(queries, KVL, kind=BF16), [VMEM] * 2, (own_out, across))
     given = lax.ppermute(merged, DEC, partners)
     attn = call(
         final_kernel,

time: 159 us -> 169 us (1.063)
  waiting for transfers between devices: 92.9 us -> 97.5 us
  starting transfers between devices: 34.7 us -> 38.1 us
  local copies, waits for them, and re-layouts: 3.91 us -> 5.7 us
    ppermute x1, waiting for transfers between devices: 0.93 us -> 5.64 us  [pairs_step(): old_far = lax.ppermute(old, DEC, partners)]
    pallas_call x13, Pallas kernels: 9.39 us -> 12.8 us  [call(): pl.pallas_call(kernel, scratch_shapes=scratch, out_shape=shapes, in_specs...]
    pallas_call x1 -> x0, Pallas kernels: 2.94 us -> none  [share(): pl.pallas_call(share_kernel, in_specs=[SMEM, pl.BlockSpec(memory_space=pl...]
    dynamic_slice x0 -> x2, local copies, waits for them, and re-layouts: none -> 2.23 us  [the longest x1 1.17 us: pairs_step(): lax.dynamic_slice(weight, (0, group * half), (split, half))]
    ppermute x1, starting transfers between devices: 3.01 us -> 5.01 us  [pairs_step(): back1 = lax.ppermute(back1, DEC, partners)]
    ppermute x1, waiting for transfers between devices: 0.01 us -> 1.7 us  [pairs_step(): back0 = lax.ppermute(back0, DEC, partners)]
    unnamed x57 -> x43, local copies, waits for them, and re-layouts: 3.72 us -> 3.28 us
  transfers between devices with their start and end apart: 28 -> 28, of which waited for: 10 -> 11; matrix products, arithmetic and copies ran while one was open for 1% -> 2% of each run, Pallas kernels for 13% -> 14%
where the time goes in v6:
time: 169 us; the launch traced here: 168 us
  waiting for transfers between devices  97.5 us (58%)
  starting transfers between devices  38.1 us (23%)
  Pallas kernels  24.1 us (14%)
  local copies, waits for them, and re-layouts  5.7 us (3%)
  other arithmetic  1.69 us (1%)
    ppermute x2, waiting for transfers between devices, pairs_step(): a_z[p] = lax.ppermute(pieces[p], DEC, [(0, 2), (3, 1), (1, 0), (2, 3)])  45.2 us
    ppermute x12, waiting for transfers between devices, swap(): return lax.ppermute(a, axis, [(0, 1), (1, 0)])  38.6 us
    pallas_call x13, Pallas kernels, call(): pl.pallas_call(kernel, scratch_shapes=scratch, out_shape=shapes, in_specs...  12.8 us
    pallas_call x4, Pallas kernels, project(): pl.pallas_call(kernel, in_specs=[SMEM] + [VMEM] * (len(args) - 1), out_sp...  11.2 us
    ppermute x12, starting transfers between devices, swap(): return lax.ppermute(a, axis, [(0, 1), (1, 0)])  9.92 us
    ppermute x3, starting transfers between devices, pairs_step(): lax.ppermute(packed, DEC, [((i + s) % n, i) for i in range(n)])  7.15 us
    ppermute x2, starting transfers between devices, pairs_step(): a_z[p] = lax.ppermute(pieces[p], DEC, [(0, 2), (3, 1), (1, 0), (2, 3)])  6.08 us
    ppermute x1, waiting for transfers between devices, pairs_step(): old_far = lax.ppermute(old, DEC, partners)  5.64 us
  transfers between devices with their start and end apart: 28, of which 11 were waited for; matrix products, arithmetic and copies ran while one was open for 2% of the time, Pallas kernels for 14%

profile of v6, /device:TPU:0, one launch (start us, length us, event | category | flops | bytes accessed | tf_op | source)
XLA Modules:
  0.0 168.1 jit_solution(5637708113911516394)
XLA Ops:
  0.6 1.2 dynamic-slice_bitcast_fusion.1
  1.8 4.1 %collective-permute-start = (bf16[256,896]{1,0:T(8,128)(2,1)S(1)}, bf16[256,896]{1,0:T(8,128)(2,1)}, u32[]{:S(2)}, u32[]{:S(2)}) collective-permute-start(bf16[256,896]{1,0:T(8,128)(2,1)S(1)} %dynamic-slice_bitcast_fusion.1), channel_id=1, source_target_pairs={{0,8},{12,4},{4,0},{8,12},{1,9},{13,5},{5,1},{9,13},{2,10},{14,6},... | collective-permute-start | bytes 1376264 | tf_op jit(solution)/shard_map/ppermute | solution.py:607
  5.9 1.1 dynamic-slice_bitcast_fusion
  7.0 2.0 %collective-permute-start.2 = (bf16[272,896]{1,0:T(8,128)(2,1)S(1)}, bf16[272,896]{1,0:T(8,128)(2,1)S(1)}, u32[]{:S(2)}, u32[]{:S(2)}) collective-permute-start(bf16[272,896]{1,0:T(8,128)(2,1)S(1)} %dynamic-slice_bitcast_fusion), channel_id=1, source_target_pairs={{0,8},{12,4},{4,0},{8,12},{1,9},{13,5},{5,1},{9,13},{2,10},{14,6},... | collective-permute-start | bytes 1462280 | tf_op jit(solution)/shard_map/ppermute | solution.py:607
  9.0 7.9 %collective-permute-done.z0.z = bf16[256,896]{1,0:T(8,128)(2,1)} collective-permute-done((bf16[256,896]{1,0:T(8,128)(2,1)S(1)}, bf16[256,896]{1,0:T(8,128)(2,1)}, u32[]{:S(2)}, u32[]{:S(2)}) %collective-permute-start) | collective-permute-done | bytes 458784 | tf_op jit(solution)/shard_map/ppermute | solution.py:607
  16.9 1.5 collective-permute-start.7
  18.3 37.3 %collective-permute-done.2.z1.z = bf16[272,896]{1,0:T(8,128)(2,1)S(1)} collective-permute-done((bf16[272,896]{1,0:T(8,128)(2,1)S(1)}, bf16[272,896]{1,0:T(8,128)(2,1)S(1)}, u32[]{:S(2)}, u32[]{:S(2)}) %collective-permute-start.2) | collective-permute-done | bytes 487456 | tf_op jit(solution)/shard_map/ppermute | solution.py:607
  55.7 1.5 collective-permute-start.3
  57.7 1.5 collective-permute-start.1
  59.4 1.4 collective-permute-start.12
  60.8 27.3 %collective-permute-done.1.y0.y = bf16[256,896]{1,0:T(8,128)(2,1)} collective-permute-done((bf16[256,896]{1,0:T(8,128)(2,1)}, bf16[256,896]{1,0:T(8,128)(2,1)}, u32[]{:S(2)}, u32[]{:S(2)}) %collective-permute-start.1) | collective-permute-done | bytes 458784 | tf_op jit(solution)/shard_map/ppermute | solution.py:199
  88.1 1.5 copy-done.1
  89.6 3.6 %shard_map.116 = (f32[192,624]{1,0:T(8,128)S(1)}, f32[192,624]{1,0:T(8,128)S(1)}) custom-call(s32[4]{0:T(128)S(1)} %pad_add_fusion.1.ids, bf16[384,1792]{1,0:T(8,128)(2,1)S(1)} %copy-done, bf16[384,1792]{1,0:T(8,128)(2,1)S(1)} %collective-permute-done.6.far_ref, bf16[528,1792]{1,0:T(8,128)(2,1)S(1)} %bitcast.16, bf16[256,896]{1,0:T(8,128)(2,1)} %collective-permute-done.z0.z, ...), custom_call_target="tpu_custom_call" | custom-call | flops 858783744 | bytes 1916928 | tf_op jit(solution)/shard_map/pallas_call | solution.py:284
  93.3 1.4 multiply_sine_fusion
  94.8 2.7 %shard_map.114 = (f32[192,528]{1,0:T(8,128)S(1)}, f32[192,528]{1,0:T(8,128)S(1)}) custom-call(s32[4]{0:T(128)S(1)} %pad_add_fusion.1.ids, bf16[384,1792]{1,0:T(8,128)(2,1)S(1)} %copy-done, bf16[528,1792]{1,0:T(8,128)(2,1)S(1)} %bitcast.17, bf16[256,896]{1,0:T(8,128)(2,1)} %collective-permute-done.z0.z, bf16[256,896]{1,0:T(8,128)(2,1)} %collective-permute-done.1.y0.y, ...), custom_call_target="tpu_custom_call" | custom-call | flops 726663168 | bytes 1622016 | tf_op jit(solution)/shard_map/pallas_call | solution.py:284
  97.6 0.6 collective-permute-start.4
  98.2 1.5 collective-permute-start.13
  99.7 1.4 shard_map.117
  101.1 0.8 copy-done.3
  101.9 1.5 collective-permute-start.10
  103.4 1.4 shard_map.115
  104.8 0.8 copy-done.5
  106.4 4.6 %collective-permute-done.13.by = bf16[256,896]{1,0:T(8,128)(2,1)} collective-permute-done((bf16[256,896]{1,0:T(8,128)(2,1)}, bf16[256,896]{1,0:T(8,128)(2,1)}, u32[]{:S(2)}, u32[]{:S(2)}) %collective-permute-start.13) | collective-permute-done | bytes 458784 | tf_op jit(solution)/shard_map/ppermute | solution.py:199
  111.0 2.5 %shard_map.120 = (f32[192,512]{1,0:T(8,128)S(1)}, f32[192,512]{1,0:T(8,128)S(1)}) custom-call(s32[4]{0:T(128)S(1)} %pad_add_fusion.1.ids, bf16[384,1792]{1,0:T(8,128)(2,1)S(1)} %copy-done, bf16[384,1792]{1,0:T(8,128)(2,1)S(1)} %collective-permute-done.6.far_ref, bf16[256,896]{1,0:T(8,128)(2,1)} %collective-permute-done.z0.z, ...), custom_call_target="tpu_custom_call" | custom-call | flops 704643072 | bytes 1572864 | tf_op jit(solution)/shard_map/pallas_call | solution.py:284
  113.6 2.4 %shard_map.119 = (f32[192,480]{1,0:T(8,128)S(1)}, f32[192,480]{1,0:T(8,128)S(1)}) custom-call(s32[4]{0:T(128)S(1)} %pad_add_fusion.1.ids, bf16[384,1792]{1,0:T(8,128)(2,1)S(1)} %copy-done, bf16[384,1792]{1,0:T(8,128)(2,1)S(1)} %collective-permute-done.6.far_ref, bf16[272,896]{1,0:T(8,128)(2,1)S(1)} %collective-permute-done.2.z1.z, ...), custom_call_target="tpu_custom_call" | custom-call | flops 660602880 | bytes 1474560 | tf_op jit(solution)/shard_map/pallas_call | solution.py:284
  116.6 2.4 %collective-permute-start.24 = (s32[1,60]{1,0:T(1,128)S(1)}, s32[1,60]{1,0:T(1,128)S(1)}, u32[]{:S(2)}, u32[]{:S(2)}) collective-permute-start(s32[1,60]{1,0:T(1,128)S(1)} %add_bitcast_fusion), channel_id=1, source_target_pairs={{12,0},{0,4},{4,8},{8,12},{13,1},{1,5},{5,9},{9,13},{14,2},{2,6},{... | collective-permute-start | bytes 728 | tf_op jit(solution)/shard_map/ppermute | solution.py:613
  119.0 6.7 %collective-permute-done.5.got0 = f32[192,528]{1,0:T(8,128)} collective-permute-done((f32[192,528]{1,0:T(8,128)}, f32[192,528]{1,0:T(8,128)}, u32[]{:S(2)}, u32[]{:S(2)}) %collective-permute-start.5) | collective-permute-done | bytes 405536 | tf_op jit(solution)/shard_map/ppermute | solution.py:199
  125.7 1.9 %shard_map.125.k0_ref = bf16[384,576]{1,0:T(8,128)(2,1)S(1)} custom-call(f32[192,528]{1,0:T(8,128)S(1)} %copy-done.6, f32[192,528]{1,0:T(8,128)} %collective-permute-done.5.got0, f32[192,624]{1,0:T(8,128)S(1)} %copy-done.4, f32[192,624]{1,0:T(8,128)} %collective-permute-done.10.got1, f32[384,64]{1,0:T(8,128)S(1)} %copy-done.12, ...), custom_call_target="tpu_custom_call" | custom-call | flops 20000000 | bytes 2000000 | tf_op jit(solution)/shard_map/pallas_call | solution.py:553
  127.7 3.4 %collective-permute-start.23 = (s32[1,60]{1,0:T(1,128)S(1)}, s32[1,60]{1,0:T(1,128)S(1)}, u32[]{:S(2)}, u32[]{:S(2)}) collective-permute-start(s32[1,60]{1,0:T(1,128)S(1)} %add_bitcast_fusion), channel_id=1, source_target_pairs={{8,0},{12,4},{0,8},{4,12},{9,1},{13,5},{1,9},{5,13},{10,2},{14,6},... | collective-permute-start | bytes 728 | tf_op jit(solution)/shard_map/ppermute | solution.py:613
  131.1 1.3 collective-permute-start.22
  132.7 2.0 %collective-permute-done.22 = s32[1,60]{1,0:T(1,128)S(1)} collective-permute-done((s32[1,60]{1,0:T(1,128)S(1)}, s32[1,60]{1,0:T(1,128)S(1)}, u32[]{:S(2)}, u32[]{:S(2)}) %collective-permute-start.22) | collective-permute-done | bytes 272 | tf_op jit(solution)/shard_map/ppermute | solution.py:613
  134.8 1.7 %shard_map.126 = (f32[128,640]{1,0:T(8,128)S(1)}, f32[8,768]{1,0:T(8,128)S(1)}) custom-call(s32[4]{0:T(128)S(1)} %pad_add_fusion.1.ids, s32[8,128]{1,0:T(8,128)S(1)} %pad.8.tab_ref, bf16[128,576]{1,0:T(8,128)(2,1)S(1)} %bitcast.19, bf16[1024,576]{1,0:T(8,128)(2,1)S(1)} %bitcast.18, bf16[16,576]{1,0:T(8,128)(2,1)S(1)} %pad.9.own_ref), custom_call_target="tpu_custom_call" | custom-call | flops 20000000 | bytes 2000000 | tf_op jit(solution)/shard_map/pallas_call | solution.py:553
  136.5 0.7 collective-permute-start.25
  137.3 0.7 shard_map.121
  138.0 1.6 collective-permute-start.15
  139.5 5.6 %collective-permute-done.25.far_ref = f32[128,640]{1,0:T(8,128)S(1)} collective-permute-done((f32[128,640]{1,0:T(8,128)S(1)}, f32[128,640]{1,0:T(8,128)S(1)}, u32[]{:S(2)}, u32[]{:S(2)}) %collective-permute-start.25) | collective-permute-done | bytes 327712 | tf_op jit(solution)/shard_map/ppermute | solution.py:633
  145.2 0.8 shard_map.127
  146.0 0.7 collective-permute-start.26
  146.8 5.0 %collective-permute-start.17 = (bf16[96,528]{1,0:T(8,128)(2,1)S(1)}, bf16[96,528]{1,0:T(8,128)(2,1)S(1)}, u32[]{:S(2)}, u32[]{:S(2)}) collective-permute-start(bf16[96,528]{1,0:T(8,128)(2,1)S(1)} %get-tuple-element.56), channel_id=1, source_target_pairs={{0,4},{4,0},{8,12},{12,8},{1,5},{5,1},{9,13},{13,9},{2,6},{6,2},{1... | collective-permute-start | bytes 304136 | tf_op jit(solution)/shard_map/ppermute | solution.py:723
  151.8 1.2 shard_map.118
  153.3 3.6 %collective-permute-start.27 = (bf16[128,512]{1,0:T(8,128)(2,1)S(1)}, bf16[128,512]{1,0:T(8,128)(2,1)S(1)}, u32[]{:S(2)}, u32[]{:S(2)}) collective-permute-start(bf16[128,512]{1,0:T(8,128)(2,1)S(1)} %shard_map.128.own), channel_id=1, source_target_pairs={{0,4},{4,0},{8,12},{12,8},{1,5},{5,1},{9,13},{13,9},{2,6},{6,2},{1... | collective-permute-start | bytes 393224 | tf_op jit(solution)/shard_map/ppermute | solution.py:702
  156.9 1.7 %collective-permute-done.16.got_first = bf16[96,528]{1,0:T(8,128)(2,1)S(1)} collective-permute-done((bf16[96,528]{1,0:T(8,128)(2,1)S(1)}, bf16[96,528]{1,0:T(8,128)(2,1)S(1)}, u32[]{:S(2)}, u32[]{:S(2)}) %collective-permute-start.16) | collective-permute-done | bytes 101408 | tf_op jit(solution)/shard_map/ppermute | solution.py:716
  158.6 0.9 shard_map.123
  159.6 1.6 collective-permute-start.19
  161.4 2.9 %collective-permute-done.19.refs_2_ = bf16[96,384]{1,0:T(8,128)(2,1)S(1)} collective-permute-done((bf16[96,384]{1,0:T(8,128)(2,1)S(1)}, bf16[96,384]{1,0:T(8,128)(2,1)S(1)}, u32[]{:S(2)}, u32[]{:S(2)}) %collective-permute-start.19) | collective-permute-done | bytes 73760 | tf_op jit(solution)/shard_map/ppermute | solution.py:736
  164.4 1.3 collective-permute-done.20.refs_3_
  165.6 1.3 shard_map.124
  166.9 1.2 shard_map.129
  (82 shorter events, 3.3 us)
Async XLA Ops:
  0.6 87.5 %copy-start = (bf16[384,1792]{1,0:T(8,128)(2,1)S(1)}, bf16[384,1792]{1,0:T(8,128)(2,1)}, u32[]{:S(2)}) copy-start(bf16[384,1792]{1,0:T(8,128)(2,1)} %x_ref.7) | copy-start | bytes 4128772
  1.8 55.4 %copy-start.15 = (bf16[256,896]{1,0:T(8,128)(2,1)}, bf16[256,896]{1,0:T(8,128)(2,1)S(1)}, u32[]{:S(2)}) copy-start(bf16[256,896]{1,0:T(8,128)(2,1)S(1)} %dynamic-slice_bitcast_fusion.1) | copy-start | bytes 1376260
  1.8 15.0 %collective-permute-start = (bf16[256,896]{1,0:T(8,128)(2,1)S(1)}, bf16[256,896]{1,0:T(8,128)(2,1)}, u32[]{:S(2)}, u32[]{:S(2)}) collective-permute-start(bf16[256,896]{1,0:T(8,128)(2,1)S(1)} %dynamic-slice_bitcast_fusion.1), channel_id=1, source_target_pairs={{0,8},{12,4},{4,0},{8,12},{1,9},{13,5},{5,1},{9,13},{2,10},{14,6},... | collective-permute-start | bytes 1376264 | tf_op jit(solution)/shard_map/ppermute | solution.py:607
  5.9 82.1 %collective-permute-start.6 = (bf16[384,1792]{1,0:T(8,128)(2,1)}, bf16[384,1792]{1,0:T(8,128)(2,1)S(1)}, u32[]{:S(2)}, u32[]{:S(2)}) collective-permute-start(bf16[384,1792]{1,0:T(8,128)(2,1)} %x_ref.7), channel_id=1, source_target_pairs={{0,4},{4,0},{8,12},{12,8},{1,5},{5,1},{9,13},{13,9},{2,6},{6,2},{1... | collective-permute-start | bytes 4128776 | tf_op jit(solution)/shard_map/ppermute | solution.py:617
  7.0 48.6 %collective-permute-start.2 = (bf16[272,896]{1,0:T(8,128)(2,1)S(1)}, bf16[272,896]{1,0:T(8,128)(2,1)S(1)}, u32[]{:S(2)}, u32[]{:S(2)}) collective-permute-start(bf16[272,896]{1,0:T(8,128)(2,1)S(1)} %dynamic-slice_bitcast_fusion), channel_id=1, source_target_pairs={{0,8},{12,4},{4,0},{8,12},{1,9},{13,5},{5,1},{9,13},{2,10},{14,6},... | collective-permute-start | bytes 1462280 | tf_op jit(solution)/shard_map/ppermute | solution.py:607
  16.9 40.3 %collective-permute-start.7 = (bf16[272,896]{1,0:T(8,128)(2,1)S(1)}, bf16[272,896]{1,0:T(8,128)(2,1)}, u32[]{:S(2)}, u32[]{:S(2)}) collective-permute-start(bf16[272,896]{1,0:T(8,128)(2,1)S(1)} %dynamic-slice_bitcast_fusion), channel_id=1, source_target_pairs={{4,8},{8,4},{5,9},{9,5},{6,10},{10,6},{7,11},{11,7},{20,24},{24,20... | collective-permute-start | bytes 1462280 | tf_op jit(solution)/shard_map/ppermute | solution.py:621
  55.7 32.4 %collective-permute-start.3 = (bf16[272,896]{1,0:T(8,128)(2,1)S(1)}, bf16[272,896]{1,0:T(8,128)(2,1)}, u32[]{:S(2)}, u32[]{:S(2)}) collective-permute-start(bf16[272,896]{1,0:T(8,128)(2,1)S(1)} %collective-permute-done.2.z1.z), channel_id=1, source_target_pairs={{0,16},{16,0},{1,17},{17,1},{2,18},{18,2},{3,19},{19,3},{4,20},{20... | collective-permute-start | bytes 1462280 | tf_op jit(solution)/shard_map/ppermute | solution.py:199
  57.2 30.9 %collective-permute-start.8 = (bf16[272,896]{1,0:T(8,128)(2,1)}, bf16[272,896]{1,0:T(8,128)(2,1)}, u32[]{:S(2)}, u32[]{:S(2)}) collective-permute-start(bf16[272,896]{1,0:T(8,128)(2,1)} %collective-permute-done.7.bz1.bz), channel_id=1, source_target_pairs={{0,16},{16,0},{1,17},{17,1},{2,18},{18,2},{3,19},{19,3},{4,20},{20... | collective-permute-start | bytes 1462280 | tf_op jit(solution)/shard_map/ppermute | solution.py:199
  57.7 30.4 %collective-permute-start.1 = (bf16[256,896]{1,0:T(8,128)(2,1)}, bf16[256,896]{1,0:T(8,128)(2,1)}, u32[]{:S(2)}, u32[]{:S(2)}) collective-permute-start(bf16[256,896]{1,0:T(8,128)(2,1)} %collective-permute-done.z0.z), channel_id=1, source_target_pairs={{0,16},{16,0},{1,17},{17,1},{2,18},{18,2},{3,19},{19,3},{4,20},{20... | collective-permute-start | bytes 1376264 | tf_op jit(solution)/shard_map/ppermute | solution.py:199
  59.4 38.8 %collective-permute-start.12 = (bf16[256,896]{1,0:T(8,128)(2,1)}, bf16[256,896]{1,0:T(8,128)(2,1)}, u32[]{:S(2)}, u32[]{:S(2)}) collective-permute-start(bf16[256,896]{1,0:T(8,128)(2,1)} %copy-done.15), channel_id=1, source_target_pairs={{4,8},{8,4},{5,9},{9,5},{6,10},{10,6},{7,11},{11,7},{20,24},{24,20... | collective-permute-start | bytes 1376264 | tf_op jit(solution)/shard_map/ppermute | solution.py:621
  88.1 1.5 copy-start.1
  89.6 5.2 %copy-start.16 = (f32[1536]{0:T(1024)S(1)}, f32[1536]{0:T(1024)}, u32[]{:S(2)}) copy-start(f32[1536]{0:T(1024)} %param.12) | copy-start | bytes 18436
  89.6 5.2 %copy-start.2 = (bf16[1792,528]{0,1:T(8,128)(2,1)S(1)}, bf16[1792,528]{0,1:T(8,128)(2,1)}, u32[]{:S(2)}) copy-start(bf16[1792,528]{0,1:T(8,128)(2,1)} %param.11) | copy-start | bytes 5677060
  93.3 6.4 %copy-start.7 = (f32[192,624]{1,0:T(8,128)}, f32[192,624]{1,0:T(8,128)S(1)}, u32[]{:S(2)}) copy-start(f32[192,624]{1,0:T(8,128)S(1)} %get-tuple-element.42.kept.kept_far) | copy-start | bytes 1437700
  93.3 6.4 %collective-permute-start.9 = (f32[192,624]{1,0:T(8,128)S(1)}, f32[192,624]{1,0:T(8,128)S(1)}, u32[]{:S(2)}, u32[]{:S(2)}) collective-permute-start(f32[192,624]{1,0:T(8,128)S(1)} %get-tuple-element.43), channel_id=1, source_target_pairs={{0,1},{1,0},{2,3},{3,2},{4,5},{5,4},{6,7},{7,6},{8,9},{9,8},{10,11... | collective-permute-start | bytes 1437704 | tf_op jit(solution)/shard_map/ppermute | solution.py:199
  97.6 8.6 %copy-start.18 = (s32[1,4,8]{2,1,0:T(4,128)S(1)}, s32[1,4,8]{2,1,0:T(4,128)}, u32[]{:S(2)}) copy-start(s32[1,4,8]{2,1,0:T(4,128)} %param.16) | copy-start | bytes 388
  97.6 8.6 %copy-start.19 = (s32[12,2]{0,1:T(2,128)S(1)}, s32[12,2]{0,1:T(2,128)}, u32[]{:S(2)}) copy-start(s32[12,2]{0,1:T(2,128)} %param.15) | copy-start | bytes 292
  97.6 5.8 %collective-permute-start.4 = (f32[192,528]{1,0:T(8,128)S(1)}, f32[192,528]{1,0:T(8,128)S(1)}, u32[]{:S(2)}, u32[]{:S(2)}) collective-permute-start(f32[192,528]{1,0:T(8,128)S(1)} %get-tuple-element.38), channel_id=1, source_target_pairs={{0,1},{1,0},{2,3},{3,2},{4,5},{5,4},{6,7},{7,6},{8,9},{9,8},{10,11... | collective-permute-start | bytes 1216520 | tf_op jit(solution)/shard_map/ppermute | solution.py:199
  98.2 12.8 %collective-permute-start.13 = (bf16[256,896]{1,0:T(8,128)(2,1)}, bf16[256,896]{1,0:T(8,128)(2,1)}, u32[]{:S(2)}, u32[]{:S(2)}) collective-permute-start(bf16[256,896]{1,0:T(8,128)(2,1)} %collective-permute-done.12.bz), channel_id=1, source_target_pairs={{0,16},{16,0},{1,17},{17,1},{2,18},{18,2},{3,19},{19,3},{4,20},{20... | collective-permute-start | bytes 1376264 | tf_op jit(solution)/shard_map/ppermute | solution.py:199
  99.7 5.1 %copy-start.9 = (f32[192,624]{1,0:T(8,128)}, f32[192,624]{1,0:T(8,128)S(1)}, u32[]{:S(2)}) copy-start(f32[192,624]{1,0:T(8,128)S(1)} %collective-permute-done.9.got.got_far) | copy-start | bytes 1437700
  101.9 23.8 %collective-permute-start.10 = (f32[192,624]{1,0:T(8,128)}, f32[192,624]{1,0:T(8,128)}, u32[]{:S(2)}, u32[]{:S(2)}) collective-permute-start(f32[192,624]{1,0:T(8,128)} %get-tuple-element.45), channel_id=1, source_target_pairs={{0,2},{2,0},{1,3},{3,1},{4,6},{6,4},{5,7},{7,5},{8,10},{10,8},{9,1... | collective-permute-start | bytes 1437704 | tf_op jit(solution)/shard_map/ppermute | solution.py:199
  104.8 0.8 copy-start.5
  105.6 20.1 %collective-permute-start.5 = (f32[192,528]{1,0:T(8,128)}, f32[192,528]{1,0:T(8,128)}, u32[]{:S(2)}, u32[]{:S(2)}) collective-permute-start(f32[192,528]{1,0:T(8,128)} %get-tuple-element.40), channel_id=1, source_target_pairs={{0,2},{2,0},{1,3},{3,1},{4,6},{6,4},{5,7},{7,5},{8,10},{10,8},{9,1... | collective-permute-start | bytes 1216520 | tf_op jit(solution)/shard_map/ppermute | solution.py:199
  113.5 3.1 %copy-start.20 = (s32[4,1]{0,1:T(1,128)S(1)}, s32[4,1]{0,1:T(1,128)}, u32[]{:S(2)}) copy-start(s32[4,1]{0,1:T(1,128)} %param.17) | copy-start | bytes 52
  113.5 12.2 %copy-start.4 = (f32[192,624]{1,0:T(8,128)S(1)}, f32[192,624]{1,0:T(8,128)}, u32[]{:S(2)}) copy-start(f32[192,624]{1,0:T(8,128)} %copy-done.3) | copy-start | bytes 1437700
  113.5 12.2 %copy-start.6 = (f32[192,528]{1,0:T(8,128)S(1)}, f32[192,528]{1,0:T(8,128)}, u32[]{:S(2)}) copy-start(f32[192,528]{1,0:T(8,128)} %copy-done.5) | copy-start | bytes 1216516
  113.5 12.2 %copy-start.12 = (f32[384,64]{1,0:T(8,128)S(1)}, f32[384,64]{1,0:T(8,128)}, u32[]{:S(2)}) copy-start(f32[384,64]{1,0:T(8,128)} %get-tuple-element.62.cos) | copy-start | bytes 294916
  113.5 12.2 %copy-start.14 = (f32[512]{0:T(512)S(1)}, f32[512]{0:T(512)}, u32[]{:S(2)}) copy-start(f32[512]{0:T(512)} %param.13) | copy-start | bytes 6148
  113.5 23.7 %collective-permute-start.14 = (f32[192,512]{1,0:T(8,128)S(1)}, f32[192,512]{1,0:T(8,128)S(1)}, u32[]{:S(2)}, u32[]{:S(2)}) collective-permute-start(f32[192,512]{1,0:T(8,128)S(1)} %get-tuple-element.51), channel_id=1, source_target_pairs={{0,1},{1,0},{2,3},{3,2},{4,5},{5,4},{6,7},{7,6},{8,9},{9,8},{10,11... | collective-permute-start | bytes 1179656 | tf_op jit(solution)/shard_map/ppermute | solution.py:199
  116.0 16.5 %copy-start.17 = (bf16[4,576]{1,0:T(4,128)(2,1)S(1)}, bf16[4,576]{1,0:T(4,128)(2,1)}, u32[]{:S(2)}) copy-start(bf16[4,576]{1,0:T(4,128)(2,1)} %param.19) | copy-start | bytes 13828
  116.0 18.7 %copy-start.11 = (bf16[32,32,576]{2,1,0:T(8,128)(2,1)S(1)}, bf16[32,32,576]{2,1,0:T(8,128)(2,1)}, u32[]{:S(2)}) copy-start(bf16[32,32,576]{2,1,0:T(8,128)(2,1)} %param.14) | copy-start | bytes 3538948
  116.0 18.7 %copy-start.13 = (bf16[4,32,576]{2,1,0:T(8,128)(2,1)S(1)}, bf16[4,32,576]{2,1,0:T(8,128)(2,1)}, u32[]{:S(2)}) copy-start(bf16[4,32,576]{2,1,0:T(8,128)(2,1)} %param.18) | copy-start | bytes 442372
  116.0 21.2 %collective-permute-start.11 = (f32[192,480]{1,0:T(8,128)S(1)}, f32[192,480]{1,0:T(8,128)S(1)}, u32[]{:S(2)}, u32[]{:S(2)}) collective-permute-start(f32[192,480]{1,0:T(8,128)S(1)} %get-tuple-element.48), channel_id=1, source_target_pairs={{0,1},{1,0},{2,3},{3,2},{4,5},{5,4},{6,7},{7,6},{8,9},{9,8},{10,11... | collective-permute-start | bytes 1105928 | tf_op jit(solution)/shard_map/ppermute | solution.py:199
  116.6 14.5 %collective-permute-start.24 = (s32[1,60]{1,0:T(1,128)S(1)}, s32[1,60]{1,0:T(1,128)S(1)}, u32[]{:S(2)}, u32[]{:S(2)}) collective-permute-start(s32[1,60]{1,0:T(1,128)S(1)} %add_bitcast_fusion), channel_id=1, source_target_pairs={{12,0},{0,4},{4,8},{8,12},{13,1},{1,5},{5,9},{9,13},{14,2},{2,6},{... | collective-permute-start | bytes 728 | tf_op jit(solution)/shard_map/ppermute | solution.py:613
  125.7 11.5 %copy-start.8 = (f32[192,624]{1,0:T(8,128)S(1)}, f32[192,624]{1,0:T(8,128)}, u32[]{:S(2)}) copy-start(f32[192,624]{1,0:T(8,128)} %copy-done.7) | copy-start | bytes 1437700
  125.7 11.5 %copy-start.10 = (f32[192,624]{1,0:T(8,128)S(1)}, f32[192,624]{1,0:T(8,128)}, u32[]{:S(2)}) copy-start(f32[192,624]{1,0:T(8,128)} %copy-done.9) | copy-start | bytes 1437700
  127.6 17.6 %collective-permute-start.21 = (bf16[384,576]{1,0:T(8,128)(2,1)S(1)}, bf16[384,576]{1,0:T(8,128)(2,1)S(1)}, u32[]{:S(2)}, u32[]{:S(2)}) collective-permute-start(bf16[384,576]{1,0:T(8,128)(2,1)S(1)} %shard_map.125.k0_ref), channel_id=1, source_target_pairs={{0,1},{1,0},{2,3},{3,2},{4,5},{5,4},{6,7},{7,6},{8,9},{9,8},{10,11... | collective-permute-start | bytes 1327112 | tf_op jit(solution)/shard_map/ppermute | solution.py:199
  127.7 5.0 %collective-permute-start.23 = (s32[1,60]{1,0:T(1,128)S(1)}, s32[1,60]{1,0:T(1,128)S(1)}, u32[]{:S(2)}, u32[]{:S(2)}) collective-permute-start(s32[1,60]{1,0:T(1,128)S(1)} %add_bitcast_fusion), channel_id=1, source_target_pairs={{8,0},{12,4},{0,8},{4,12},{9,1},{13,5},{1,9},{5,13},{10,2},{14,6},... | collective-permute-start | bytes 728 | tf_op jit(solution)/shard_map/ppermute | solution.py:613
  131.1 3.6 %collective-permute-start.22 = (s32[1,60]{1,0:T(1,128)S(1)}, s32[1,60]{1,0:T(1,128)S(1)}, u32[]{:S(2)}, u32[]{:S(2)}) collective-permute-start(s32[1,60]{1,0:T(1,128)S(1)} %add_bitcast_fusion), channel_id=1, source_target_pairs={{4,0},{8,4},{12,8},{0,12},{5,1},{9,5},{13,9},{1,13},{6,2},{10,6},{... | collective-permute-start | bytes 728 | tf_op jit(solution)/shard_map/ppermute | solution.py:613
  136.5 8.7 %collective-permute-start.25 = (f32[128,640]{1,0:T(8,128)S(1)}, f32[128,640]{1,0:T(8,128)S(1)}, u32[]{:S(2)}, u32[]{:S(2)}) collective-permute-start(f32[128,640]{1,0:T(8,128)S(1)} %get-tuple-element.67.old_ref), channel_id=1, source_target_pairs={{0,4},{4,0},{8,12},{12,8},{1,5},{5,1},{9,13},{13,9},{2,6},{6,2},{1... | collective-permute-start | bytes 983048 | tf_op jit(solution)/shard_map/ppermute | solution.py:633
  138.0 8.7 %collective-permute-start.15 = (bf16[192,528]{1,0:T(8,128)(2,1)S(1)}, bf16[192,528]{1,0:T(8,128)(2,1)S(1)}, u32[]{:S(2)}, u32[]{:S(2)}) collective-permute-start(bf16[192,528]{1,0:T(8,128)(2,1)S(1)} %get-tuple-element.53), channel_id=1, source_target_pairs={{0,2},{2,0},{1,3},{3,1},{4,6},{6,4},{5,7},{7,5},{8,10},{10,8},{9,1... | collective-permute-start | bytes 608264 | tf_op jit(solution)/shard_map/ppermute | solution.py:199
  146.0 7.1 %collective-permute-start.26 = (bf16[128,640]{1,0:T(8,128)(2,1)S(1)}, bf16[128,640]{1,0:T(8,128)(2,1)S(1)}, u32[]{:S(2)}, u32[]{:S(2)}) collective-permute-start(bf16[128,640]{1,0:T(8,128)(2,1)S(1)} %get-tuple-element.69), channel_id=1, source_target_pairs={{4,12},{12,4},{5,13},{13,5},{6,14},{14,6},{7,15},{15,7},{20,28},{2... | collective-permute-start | bytes 491528 | tf_op jit(solution)/shard_map/ppermute | solution.py:700
  146.8 10.2 %collective-permute-start.17 = (bf16[96,528]{1,0:T(8,128)(2,1)S(1)}, bf16[96,528]{1,0:T(8,128)(2,1)S(1)}, u32[]{:S(2)}, u32[]{:S(2)}) collective-permute-start(bf16[96,528]{1,0:T(8,128)(2,1)S(1)} %get-tuple-element.56), channel_id=1, source_target_pairs={{0,4},{4,0},{8,12},{12,8},{1,5},{5,1},{9,13},{13,9},{2,6},{6,2},{1... | collective-permute-start | bytes 304136 | tf_op jit(solution)/shard_map/ppermute | solution.py:723
  153.0 5.6 %collective-permute-start.16 = (bf16[96,528]{1,0:T(8,128)(2,1)S(1)}, bf16[96,528]{1,0:T(8,128)(2,1)S(1)}, u32[]{:S(2)}, u32[]{:S(2)}) collective-permute-start(bf16[96,528]{1,0:T(8,128)(2,1)S(1)} %get-tuple-element.55), channel_id=1, source_target_pairs={{0,4},{4,0},{8,12},{12,8},{1,5},{5,1},{9,13},{13,9},{2,6},{6,2},{1... | collective-permute-start | bytes 304136 | tf_op jit(solution)/shard_map/ppermute | solution.py:716
  153.3 13.7 %collective-permute-start.27 = (bf16[128,512]{1,0:T(8,128)(2,1)S(1)}, bf16[128,512]{1,0:T(8,128)(2,1)S(1)}, u32[]{:S(2)}, u32[]{:S(2)}) collective-permute-start(bf16[128,512]{1,0:T(8,128)(2,1)S(1)} %shard_map.128.own), channel_id=1, source_target_pairs={{0,4},{4,0},{8,12},{12,8},{1,5},{5,1},{9,13},{13,9},{2,6},{6,2},{1... | collective-permute-start | bytes 393224 | tf_op jit(solution)/shard_map/ppermute | solution.py:702
  159.5 1.9 %collective-permute-start.18 = (bf16[96,384]{1,0:T(8,128)(2,1)S(1)}, bf16[96,384]{1,0:T(8,128)(2,1)S(1)}, u32[]{:S(2)}, u32[]{:S(2)}) collective-permute-start(bf16[96,384]{1,0:T(8,128)(2,1)S(1)} %get-tuple-element.59), channel_id=1, source_target_pairs={{0,1},{1,0},{2,3},{3,2},{4,5},{5,4},{6,7},{7,6},{8,9},{9,8},{10,11... | collective-permute-start | bytes 221192 | tf_op jit(solution)/shard_map/ppermute | solution.py:736
  159.6 4.8 %collective-permute-start.19 = (bf16[96,384]{1,0:T(8,128)(2,1)S(1)}, bf16[96,384]{1,0:T(8,128)(2,1)S(1)}, u32[]{:S(2)}, u32[]{:S(2)}) collective-permute-start(bf16[96,384]{1,0:T(8,128)(2,1)S(1)} %get-tuple-element.60), channel_id=1, source_target_pairs={{0,2},{1,3},{2,0},{3,1},{4,6},{5,7},{6,4},{7,5},{8,10},{9,11},{10,... | collective-permute-start | bytes 221192 | tf_op jit(solution)/shard_map/ppermute | solution.py:736
  161.1 4.5 %collective-permute-start.20 = (bf16[96,384]{1,0:T(8,128)(2,1)S(1)}, bf16[96,384]{1,0:T(8,128)(2,1)S(1)}, u32[]{:S(2)}, u32[]{:S(2)}) collective-permute-start(bf16[96,384]{1,0:T(8,128)(2,1)S(1)} %get-tuple-element.61), channel_id=1, source_target_pairs={{0,3},{1,2},{2,1},{3,0},{4,7},{5,6},{6,5},{7,4},{8,11},{9,10},{10,... | collective-permute-start | bytes 221192 | tf_op jit(solution)/shard_map/ppermute | solution.py:736
  (1 other events, 0.8 us)

commit v7 on v6

--- a/solution.py
+++ b/solution.py
@@ -222,15 +222,22 @@
     return (ids[2] == 0) | (ids[2] == 3)
 
 
-def put(ids, out, send, keep, start):
-    rows = send.shape[0]
-    top, bottom = out[:rows], out[rows:]
-    at = slice(start, start + out.shape[1])
-    send[:, at] = jnp.where(ids[1] == 0, bottom, top)
-    keep[:, at] = jnp.where(ids[1] == 0, top, bottom)
-
-
-def primary(ids, x_ref, own_ref, parts, send, keep):
+def put(ids, out, send, keep, chunk, column):
+    part = chunk // 2
+    columns = slice(column, column + out.shape[1])
+    for c in range(out.shape[0] // chunk):
+        top, bottom = out[c * chunk : c * chunk + part], out[c * chunk + part : (c + 1) * chunk]
+        at = slice(c * part, (c + 1) * part)
+        send[at, columns] = jnp.where(ids[1] == 0, bottom, top)
+        keep[at, columns] = jnp.where(ids[1] == 0, top, bottom)
+
+
+def projected(ids, x_ref, w_here, w_there):
+    here, there = halves(ids, x_ref)
+    return dot_t(x_ref[:, here], w_here) + dot_t(x_ref[:, there], w_there)
+
+
+def primary(ids, x_ref, own_ref, parts, send, keep, chunk):
     here, there = halves(ids, x_ref)
     outer = is_outer(ids)
     start = 0
@@ -238,56 +245,57 @@
         at = slice(start, start + z.shape[0])
         w_here = chosen(outer, own_ref[at, here], z[...])
         w_there = chosen(outer, own_ref[at, there], y[...])
-        put(ids, dot_t(x_ref[:, here], w_here) + dot_t(x_ref[:, there], w_there), send, keep, start)
+        put(ids, projected(ids, x_ref, w_here, w_there), send, keep, chunk, start)
         start += z.shape[0]
 
 
-def projected(ids, x_ref, w_here, w_there):
-    here, there = halves(ids, x_ref)
-    return dot_t(x_ref[:, here], w_here) + dot_t(x_ref[:, there], w_there)
-
-
-def near_kernel(ids, x_ref, own_ref, z0, y0, z1, y1, send, keep):
-    primary(ids, x_ref, own_ref, ((z0, y0), (z1, y1)), send, keep)
-
-
-def far_kernel(keys, ids, x_ref, far_ref, own_ref, z0, y0, z1, y1, bz1, by1, send, keep):
+def primary_kernel(chunk, ids, x_ref, own_ref, z0, y0, z1, y1, send, keep):
+    primary(ids, x_ref, own_ref, ((z0, y0), (z1, y1)), send, keep, chunk)
+
+
+def last_kernel(chunk, keys, ids, x_ref, far0, far1, own_ref, z0, y0, z1, y1, bz1, by1, send, keep):
     cols, head = own_ref.shape[0], z0.shape[0]
     full = z1.shape[0] // TILE * TILE
     outer = is_outer(ids)
     here, there = halves(ids, x_ref)
-    primary(
-        ids, far_ref, own_ref, ((z0, y0), (z1.at[:full, :], y1.at[:full, :])), send, keep
-    )
+    parts = ((z0, y0), (z1.at[:full, :], y1.at[:full, :]))
+    primary(ids, far1, own_ref, parts, send, keep, chunk)
     at, left, own = slice(z1.shape[0] - keys, None), slice(full, None), slice(head + full, None)
     k_here = chosen(outer, z1[at, :], bz1[at, :])
     k_there = chosen(outer, y1[at, :], by1[at, :])
     w_here = jnp.concatenate([chosen(outer, own_ref[own, here], z1[left, :]), k_here], axis=0)
     w_there = jnp.concatenate([chosen(outer, own_ref[own, there], y1[left, :]), k_there], axis=0)
-    out = projected(ids, far_ref, w_here, w_there)
-    put(ids, out[:, : cols - head - full], send, keep, head + full)
-    put(ids, out[:, cols - head - full :], send, keep, cols + keys)
-    put(ids, projected(ids, x_ref, k_here, k_there), send, keep, cols)
-
-
-def rest_kernel(used, ids, x_ref, far_ref, z, y, bz, by, send, keep):
+    out = projected(ids, far1, w_here, w_there)
+    put(ids, out[:, : cols - head - full], send, keep, chunk, head + full)
+    put(ids, out[:, cols - head - full :], send, keep, chunk, cols + 3 * keys)
+    out = projected(ids, x_ref, k_here, k_there)
+    put(ids, out[:chunk], send, keep, chunk, cols)
+    put(ids, out[chunk:], send, keep, chunk, cols + keys)
+    put(ids, projected(ids, far0, k_here, k_there), send, keep, chunk, cols + 2 * keys)
+
+
+def rest_kernel(chunk, used, ids, x_ref, far0, far1, z, y, bz, by, send, keep, rows):
     outer = is_outer(ids)
     w_here = chosen(outer, z[:used, :], bz[:used, :])
     w_there = chosen(outer, y[:used, :], by[:used, :])
-    put(ids, projected(ids, x_ref, w_here, w_there), send, keep, 0)
-    put(ids, projected(ids, far_ref, w_here, w_there), send, keep, send.shape[1] - used)
-
-
-def project(kernel, width, args):
-    rows, feats = args[1].shape
-    shape = jax.ShapeDtypeStruct((rows // 2, width), F32)
+    put(ids, projected(ids, x_ref, w_here, w_there), send, keep, chunk, 0)
+    rows[:chunk, :] = far0[...]
+    rows[chunk:, :] = far1[...]
+    out = projected(ids, rows, w_here, w_there)
+    put(ids, out, send, keep, chunk, send.shape[1] - used)
+
+
+def project(kernel, rows, width, args, scratch=()):
+    feats = args[1].shape[1]
+    shape = jax.ShapeDtypeStruct((rows, width), F32)
     return pl.pallas_call(
         kernel,
         in_specs=[SMEM] + [VMEM] * (len(args) - 1),
         out_specs=[VMEM] * 2,
         out_shape=[shape] * 2,
+        scratch_shapes=scratch,
         cost_estimate=pl.CostEstimate(
-            flops=2 * rows * feats * width, bytes_accessed=8 * rows * width, transcendentals=0
+            flops=4 * rows * feats * width, bytes_accessed=8 * rows * width, transcendentals=0
         ),
         compiler_params=pltpu.CompilerParams(vmem_limit_bytes=VMEM_GRANT),
     )(*args)
@@ -371,7 +379,9 @@
     width = bias_ref.shape[1]
     half = pages // 2
     spot = iota(1, width, 1) // PAGE
-    which = jnp.where(spot // pages == 1, 1 - core, core) * half + spot % half
+    place = spot % half
+    taker = jnp.where(spot // pages == 1, 1 - core, core)
+    which = (place // (half // 2)) * half + taker * (half // 2) + place % (half // 2)
     partner = (spot % pages) // half == 1
     line = iota(base, width, 0)
     plan = jnp.where(partner, columns[n - 1][:base, :], columns[0][:base, :])
@@ -389,63 +399,61 @@
     bias_ref[...] = jnp.where(live & (reader == iota(8, width, 0)), 0.0, MASKED)
 
 
-def parted(ids, block):
+def lane_rows(ids, block):
     half = block.shape[0] // 2
-    odd, stage = ids[2] % 2 == 1, ids[3]
     top, bottom = block[:half], block[half:]
-    mine = jnp.where(stage == 0, top, bottom)
-    away = jnp.where(stage == 0, bottom, top)
-    twice = lambda part: jnp.concatenate([part, part], axis=0)
-    return jnp.where(odd, block, twice(mine)), jnp.where(odd, block, twice(away))
-
-
-def cross_near_kernel(ids, kept, got, send, keep):
-    mine, away = parted(ids, kept[...] + got[...])
-    keep[...] = mine
-    send[...] = away
-
-
-def cross_far_kernel(cols, ids, kept, got, send, keep):
+    stage = ids[3]
+    return jnp.where(stage == 0, top, bottom), jnp.where(stage == 0, bottom, top)
+
+
+def cross_kernel(cols, part, ids, kept, got, send, keep):
+    odd = ids[2] % 2 == 1
     both = kept[...] + got[...]
-    mine, away = parted(ids, both[:, :cols])
-    keep[:, :cols] = mine
-    keep[:, cols:] = both[:, cols:]
-    send[:, :cols] = away
-    send[:, cols:] = both[:, cols:]
+    for c in range(both.shape[0] // part):
+        at = slice(c * part, (c + 1) * part)
+        block = both[at, :cols]
+        mine, away = lane_rows(ids, block)
+        keep[at, :cols] = jnp.where(odd, block, jnp.concatenate([mine, mine], axis=0))
+        send[at, :cols] = jnp.where(odd, block, jnp.concatenate([away, away], axis=0))
+    if both.shape[1] > cols:
+        keep[:, cols:] = both[:, cols:]
+        send[:, cols:] = both[:, cols:]
 
 
 def cross_rest_kernel(
-    head, rest, keys, ids, kept_tail, got_tail, kept_head, got_head, kept_far, got_far, send, keep
+    head, rest, keys, ids, kept_tail, got_tail, kept_head, got_head, kept_last, got_last, send, keep
 ):
     cols = send.shape[1]
-    stage = ids[3]
-    for i in range(2):
-        start = i * (kept_head.shape[1] - head)
+    part = kept_head.shape[0] // 2
+    half = part // 2
+    for i in range(4):
+        side, c = divmod(i, 2)
+        rows = slice(c * part, (c + 1) * part)
+        start = side * (kept_head.shape[1] - head)
         at = slice(start, start + head)
-        first = kept_head[:, at] + got_head[:, at]
-        start = i * (kept_tail.shape[1] - rest)
+        first = kept_head[rows, at] + got_head[rows, at]
+        start = side * (kept_tail.shape[1] - rest)
         at = slice(start, start + rest)
-        second = kept_tail[:, at] + got_tail[:, at]
+        second = kept_tail[rows, at] + got_tail[rows, at]
         at = slice(cols + i * keys, cols + (i + 1) * keys)
-        block = jnp.concatenate([first, second, kept_far[:, at] + got_far[:, at]], axis=1)
-        half = block.shape[0] // 2
-        top, bottom = block[:half], block[half:]
+        third = kept_last[:, at] + got_last[:, at]
+        mine, away = lane_rows(ids, jnp.concatenate([first, second, third], axis=1))
         at = slice(i * half, (i + 1) * half)
-        keep[at, :] = jnp.where(stage == 0, top, bottom)
-        send[at, :] = jnp.where(stage == 0, bottom, top).astype(BF16)
-
-
-def keys_kernel(keys, keep0, got0, keep1, got1, cos, sin, turn, gain, out):
-    rows, cols = keep0.shape
-    for i in range(2):
+        keep[at, :] = mine
+        send[at, :] = away.astype(BF16)
+
+
+def keys_kernel(keys, keep0, got0, keep1, got1, keep2, got2, cos, sin, turn, gain, out):
+    cols = keep0.shape[1]
+    part = keep1.shape[0]
+    for i in range(4):
         last = slice(cols + i * keys, cols + (i + 1) * keys)
-        tail = keep1[:, last] + got1[:, last]
-        if i == 0:
-            block = keep0[...] + got0[...]
-        else:
-            block = keep1[:, :cols] + got1[:, :cols]
+        tail = keep2[:, last] + got2[:, last]
+        keep, got = ((keep0, got0), (keep0, got0), (keep1, got1), (keep2, got2))[i]
+        rows = slice(part, 2 * part) if i == 1 else slice(0, part)
+        block = keep[rows, :cols] + got[rows, :cols]
         raw = jnp.concatenate([tail, block], axis=1)
-        at = slice(i * rows, (i + 1) * rows)
+        at = slice(i * part, (i + 1) * part)
         latent = raw[:, :KVL]
         inverse = lax.rsqrt(jnp.sum(latent * latent, axis=1, keepdims=True) / KVL + norm_eps)
         out[at, :KVL] = (latent * inverse * gain[...]).astype(BF16)
@@ -502,14 +510,14 @@
     out[...] = ((first * share + second * other_share) / (share + other_share)).astype(BF16)
 
 
-def final_kernel(ids, own, partner, out):
-    out[...] = jnp.where(ids[2] % 2 == 1, own[...], partner[...])
-
-
-def return_first_kernel(keep0, got0, keep1, got1, low, send):
+def return_first_kernel(keep0, got0, keep1, got1, keep2, got2, low, send):
     rows, cols = low.shape
-    low[...] = keep0[:rows, :] + got0[:rows, :]
-    send[...] = (keep1[:rows, :cols] + got1[:rows, :cols]).astype(BF16)
+    half = rows // 2
+    part = keep1.shape[0]
+    for c, (keep, got) in enumerate(((keep1, got1), (keep2, got2))):
+        at, near = slice(c * half, (c + 1) * half), slice(c * part, c * part + half)
+        low[at, :] = keep0[near, :] + got0[near, :]
+        send[at, :] = (keep[:half, :cols] + got[:half, :cols]).astype(BF16)
 
 
 def return_second_kernel(keep, got, high, send):
@@ -541,12 +549,15 @@
 
 def place_kernel(ids, *refs):
     gots, out = refs[:-1], refs[-1]
-    rows = gots[0].shape[0]
+    half = gots[0].shape[0] // 2
+    chunk = out.shape[0] // 2
     lane = 2 * ids[3] + ids[1]
     for k, got in enumerate(gots):
         source = jnp.bitwise_xor(lane, k)
-        order = 2 * (source % 2) + source // 2
-        out[pl.ds(pl.multiple_of(order * rows, 32), rows), :] = got[...]
+        start = (source % 2) * (2 * half) + (source // 2) * half
+        for c in range(2):
+            at = pl.ds(pl.multiple_of(c * chunk + start, 16), half)
+            out[at, :] = got[c * half : (c + 1) * half, :]
 
 
 def call(kernel, shapes, specs, args, scratch=()):
@@ -614,7 +625,9 @@
     tables = jnp.pad(
         jnp.concatenate(tables, axis=0), ((0, 8 - n), (0, -packed.shape[1] % 128))
     )
-    x_far = lax.ppermute(hidden_x, DEC, partners)
+    x_far = []
+    for c in range(2):
+        x_far.append(lax.ppermute(hidden_x[c * rows : (c + 1) * rows], DEC, partners))
     held = lax.optimization_barrier((pieces[0], pieces[1], a_z[0]))
     for p in (1, 0):
         a_y[p] = swap(a_z[p], GRP)
@@ -633,7 +646,8 @@
     old_far = lax.ppermute(old, DEC, partners)
 
     partner = index + 1 - 2 * (index % 2)
-    place = core * rows + jnp.arange(rows, dtype=jnp.int32)
+    place = jnp.arange(rows, dtype=jnp.int32)
+    place = place + core * quarter + (place // quarter) * quarter
     positions = jnp.concatenate([index * tokens + place, partner * tokens + place]).astype(F32)
     pair = jnp.arange(ROPE, dtype=jnp.int32) // 2
     frequency = jnp.power(F32(10000.0), -(2 * pair).astype(F32) / ROPE)
@@ -645,50 +659,54 @@
 
     a_refs = (a_z[0], a_y[0], a_z[1], a_y[1])
     keys = cols - cut
-    send, kept0 = project(near_kernel, cols, (early_ids, hidden_x, weight, *a_refs))
-    other0 = swap(send, TP)
-    send0, keep0 = call(
-        cross_near_kernel,
-        [shaped(rows, cols)] * 2,
-        [SMEM, VMEM, VMEM],
-        (ids, kept0, other0),
-    )
-    got0 = swap(send0, STG)
-    send, kept1 = project(
-        functools.partial(far_kernel, keys),
-        cols + 2 * keys,
-        (ids, hidden_x, x_far, weight, *a_refs, b_z[1], b_y[1]),
-    )
-    other1 = swap(send, TP)
-    send1, keep1 = call(
-        functools.partial(cross_far_kernel, cols),
-        [shaped(rows, cols + 2 * keys)] * 2,
-        [SMEM, VMEM, VMEM],
-        (ids, kept1, other1),
-    )
-    got1 = swap(send1, STG)
+
+    def crossed(kernel, count, width, args):
+        send, kept = project(kernel, count, width, args)
+        other = swap(send, TP)
+        send, keep = call(
+            functools.partial(cross_kernel, cols, quarter),
+            [shaped(count, width)] * 2,
+            [SMEM, VMEM, VMEM],
+            (ids, kept, other),
+        )
+        return (keep, swap(send, STG)), (kept, other)
+
+    near, _ = crossed(
+        functools.partial(primary_kernel, rows), rows, cols, (early_ids, hidden_x, weight, *a_refs)
+    )
+    far, _ = crossed(
+        functools.partial(primary_kernel, rows), quarter, cols, (ids, x_far[0], weight, *a_refs)
+    )
+    last, last_sums = crossed(
+        functools.partial(last_kernel, rows, keys),
+        quarter,
+        cols + 4 * keys,
+        (ids, hidden_x, *x_far, weight, *a_refs, b_z[1], b_y[1]),
+    )
     used = (cols - split - keys, split)
     rest = []
     for k, p in enumerate((1, 0)):
         send, kept = project(
-            functools.partial(rest_kernel, used[k]),
+            functools.partial(rest_kernel, rows, used[k]),
+            rows,
             -(-used[k] // 128) * 128 + used[k],
-            (ids, hidden_x, x_far, a_z[p], a_y[p], b_z[p], b_y[p]),
+            (ids, hidden_x, *x_far, a_z[p], a_y[p], b_z[p], b_y[p]),
+            scratch=[pltpu.VMEM((tokens, feats), BF16)],
         )
         rest += [kept, swap(send, TP)]
     send2, keep2 = call(
         functools.partial(cross_rest_kernel, split, used[0], keys),
         [shaped(rows, cols, kind=BF16), shaped(rows, cols)],
         [SMEM] + [VMEM] * 6,
-        (ids, *rest, kept1, other1),
+        (ids, *rest, *last_sums),
     )
     got2 = swap(send2, STG)
 
     key_rows = call(
         functools.partial(keys_kernel, keys),
         shaped(tokens, KVW, kind=BF16),
-        [VMEM] * 8,
-        (keep0, got0, keep1, got1, cos, sin, turn, kv_scale),
+        [VMEM] * 10,
+        (*near, *far, *last, cos, sin, turn, kv_scale),
     )
     far_keys = swap(key_rows, TP)
     own_out, part_out = call(
@@ -700,18 +718,13 @@
     across = lax.ppermute(part_out, DEC, [(1, 3), (3, 1)])
     merged = call(combine_kernel, shaped(queries, KVL, kind=BF16), [VMEM] * 2, (own_out, across))
     given = lax.ppermute(merged, DEC, partners)
-    attn = call(
-        final_kernel,
-        shaped(queries, KVL, kind=BF16),
-        [SMEM] + [VMEM] * 2,
-        (ids, merged, given),
-    )
+    attn = jnp.where(index % 2 == 1, merged, given)
 
     low, back0 = call(
         return_first_kernel,
         [shaped(quarter, cols), shaped(quarter, cols, kind=BF16)],
-        [VMEM] * 4,
-        (keep0, got0, keep1, got1),
+        [VMEM] * 6,
+        (*near, *far, *last),
     )
     back0 = lax.ppermute(back0, DEC, partners)
     high, back1 = call(

time: 169 us -> 131 us (0.78)
  waiting for transfers between devices: 97.5 us -> 50.7 us
  starting transfers between devices: 38.1 us -> 44.5 us
    ppermute x2, waiting for transfers between devices: 45.2 us -> 9.58 us  [pairs_step(): a_z[p] = lax.ppermute(pieces[p], DEC, [(0, 2), (3, 1), (1, 0), (2, 3)])]
    ppermute x12 -> x14, waiting for transfers between devices: 38.6 us -> 19.9 us  [swap(): return lax.ppermute(a, axis, [(0, 1), (1, 0)])]
    ppermute x1 -> x2, waiting for transfers between devices: 0.01 us -> 9.5 us  [pairs_step(): x_far.append(lax.ppermute(hidden_x[c * rows:(c + 1) * rows], DEC, partners))]
    ppermute x1, starting transfers between devices: 5.01 us -> 0.09 us  [pairs_step(): back1 = lax.ppermute(back1, DEC, partners)]
    ppermute x1, starting transfers between devices: 0.08 us -> 4.95 us  [pairs_step(): back0 = lax.ppermute(back0, DEC, partners)]
    ppermute x1 -> x2, starting transfers between devices: 0.01 us -> 4.49 us  [pairs_step(): x_far.append(lax.ppermute(hidden_x[c * rows:(c + 1) * rows], DEC, partners))]
    pallas_call x4 -> x5, Pallas kernels: 11.2 us -> 15.7 us  [project(): pl.pallas_call(kernel, in_specs=[SMEM] + [VMEM] * (len(args) - 1), out_sp...]
    pallas_call x13, Pallas kernels: 12.8 us -> 9.72 us  [call(): pl.pallas_call(kernel, scratch_shapes=scratch, out_shape=shapes, in_specs...]
  transfers between devices with their start and end apart: 28 -> 31, of which waited for: 11 -> 12; matrix products, arithmetic and copies ran while one was open for 2% -> 4% of each run, Pallas kernels for 14% -> 20%
where the time goes in v7:
time: 131 us; the launch traced here: 130 us
  waiting for transfers between devices  50.7 us (39%)
  starting transfers between devices  44.5 us (34%)
  Pallas kernels  25.4 us (19%)
  local copies, waits for them, and re-layouts  6.31 us (5%)
  other arithmetic  2.38 us (2%)
    ppermute x14, waiting for transfers between devices, swap(): return lax.ppermute(a, axis, [(0, 1), (1, 0)])  19.9 us
    pallas_call x5, Pallas kernels, project(): pl.pallas_call(kernel, in_specs=[SMEM] + [VMEM] * (len(args) - 1), out_sp...  15.7 us
    ppermute x14, starting transfers between devices, swap(): return lax.ppermute(a, axis, [(0, 1), (1, 0)])  12.6 us
    pallas_call x13, Pallas kernels, call(): pl.pallas_call(kernel, scratch_shapes=scratch, out_shape=shapes, in_specs...  9.72 us
    ppermute x2, waiting for transfers between devices, pairs_step(): a_z[p] = lax.ppermute(pieces[p], DEC, [(0, 2), (3, 1), (1, 0), (2, 3)])  9.58 us
    ppermute x2, waiting for transfers between devices, pairs_step(): x_far.append(lax.ppermute(hidden_x[c * rows:(c + 1) * rows], DEC, partners))  9.5 us
    ppermute x3, starting transfers between devices, pairs_step(): lax.ppermute(packed, DEC, [((i + s) % n, i) for i in range(n)])  5.72 us
    ppermute x2, starting transfers between devices, pairs_step(): a_z[p] = lax.ppermute(pieces[p], DEC, [(0, 2), (3, 1), (1, 0), (2, 3)])  5.64 us
  transfers between devices with their start and end apart: 31, of which 12 were waited for; matrix products, arithmetic and copies ran while one was open for 4% of the time, Pallas kernels for 20%

profile of v7, /device:TPU:0, one launch (start us, length us, event | category | flops | bytes accessed | tf_op | source)
XLA Modules:
  0.0 130.4 jit_solution(13761321504088135959)
XLA Ops:
  0.6 1.9 %dynamic-slice_bitcast_fusion.1 = bf16[256,896]{1,0:T(8,128)(2,1)} fusion(bf16[1792,528]{0,1:T(8,128)(2,1)} %param.11, s32[]{:T(128)S(6)} %select_n.42), kind=kLoop, calls=%fused_computation.1 | loop fusion | bytes 917508 | tf_op jit(solution)/shard_map/dynamic_slice | solution.py:612
  2.6 4.1 %collective-permute-start = (bf16[256,896]{1,0:T(8,128)(2,1)}, bf16[256,896]{1,0:T(8,128)(2,1)}, u32[]{:S(2)}, u32[]{:S(2)}) collective-permute-start(bf16[256,896]{1,0:T(8,128)(2,1)} %dynamic-slice_bitcast_fusion.1), channel_id=1, source_target_pairs={{0,8},{12,4},{4,0},{8,12},{1,9},{13,5},{5,1},{9,13},{2,10},{14,6},... | collective-permute-start | bytes 1376264 | tf_op jit(solution)/shard_map/ppermute | solution.py:618
  6.6 1.9 %dynamic-slice_bitcast_fusion = bf16[272,896]{1,0:T(8,128)(2,1)} fusion(bf16[1792,528]{0,1:T(8,128)(2,1)} %param.11, s32[]{:T(128)S(6)} %select_n.42), kind=kLoop, calls=%fused_computation | loop fusion | bytes 974852 | tf_op jit(solution)/shard_map/dynamic_slice | solution.py:613
  8.5 1.6 %collective-permute-start.2 = (bf16[272,896]{1,0:T(8,128)(2,1)}, bf16[272,896]{1,0:T(8,128)(2,1)}, u32[]{:S(2)}, u32[]{:S(2)}) collective-permute-start(bf16[272,896]{1,0:T(8,128)(2,1)} %dynamic-slice_bitcast_fusion), channel_id=1, source_target_pairs={{0,8},{12,4},{4,0},{8,12},{1,9},{13,5},{5,1},{9,13},{2,10},{14,6},... | collective-permute-start | bytes 1462280 | tf_op jit(solution)/shard_map/ppermute | solution.py:618
  10.1 7.8 %collective-permute-done.z0.z = bf16[256,896]{1,0:T(8,128)(2,1)} collective-permute-done((bf16[256,896]{1,0:T(8,128)(2,1)}, bf16[256,896]{1,0:T(8,128)(2,1)}, u32[]{:S(2)}, u32[]{:S(2)}) %collective-permute-start) | collective-permute-done | bytes 458784 | tf_op jit(solution)/shard_map/ppermute | solution.py:618
  17.9 1.4 %collective-permute-start.10 = (bf16[272,896]{1,0:T(8,128)(2,1)}, bf16[272,896]{1,0:T(8,128)(2,1)}, u32[]{:S(2)}, u32[]{:S(2)}) collective-permute-start(bf16[272,896]{1,0:T(8,128)(2,1)} %dynamic-slice_bitcast_fusion), channel_id=1, source_target_pairs={{4,8},{8,4},{5,9},{9,5},{6,10},{10,6},{7,11},{11,7},{20,24},{24,20... | collective-permute-start | bytes 1462280 | tf_op jit(solution)/shard_map/ppermute | solution.py:634
  19.3 1.5 %collective-permute-start.1 = (bf16[256,896]{1,0:T(8,128)(2,1)}, bf16[256,896]{1,0:T(8,128)(2,1)}, u32[]{:S(2)}, u32[]{:S(2)}) collective-permute-start(bf16[256,896]{1,0:T(8,128)(2,1)} %collective-permute-done.z0.z), channel_id=1, source_target_pairs={{0,16},{16,0},{1,17},{17,1},{2,18},{18,2},{3,19},{19,3},{4,20},{20... | collective-permute-start | bytes 1376264 | tf_op jit(solution)/shard_map/ppermute | solution.py:199
  20.8 1.2 fusion.8
  22.0 4.5 %collective-permute-start.9 = (bf16[192,1792]{1,0:T(8,128)(2,1)}, bf16[192,1792]{1,0:T(8,128)(2,1)}, u32[]{:S(2)}, u32[]{:S(2)}) collective-permute-start(bf16[192,1792]{1,0:T(8,128)(2,1)} %get-tuple-element.78), channel_id=1, source_target_pairs={{0,4},{4,0},{8,12},{12,8},{1,5},{5,1},{9,13},{13,9},{2,6},{6,2},{1... | collective-permute-start | bytes 2064392 | tf_op jit(solution)/shard_map/ppermute | solution.py:630
  26.5 1.8 %collective-permute-done.2.z1.z = bf16[272,896]{1,0:T(8,128)(2,1)} collective-permute-done((bf16[272,896]{1,0:T(8,128)(2,1)}, bf16[272,896]{1,0:T(8,128)(2,1)}, u32[]{:S(2)}, u32[]{:S(2)}) %collective-permute-start.2) | collective-permute-done | bytes 487456 | tf_op jit(solution)/shard_map/ppermute | solution.py:618
  28.3 1.5 %collective-permute-start.3 = (bf16[272,896]{1,0:T(8,128)(2,1)}, bf16[272,896]{1,0:T(8,128)(2,1)}, u32[]{:S(2)}, u32[]{:S(2)}) collective-permute-start(bf16[272,896]{1,0:T(8,128)(2,1)} %collective-permute-done.2.z1.z), channel_id=1, source_target_pairs={{0,16},{16,0},{1,17},{17,1},{2,18},{18,2},{3,19},{19,3},{4,20},{20... | collective-permute-start | bytes 1462280 | tf_op jit(solution)/shard_map/ppermute | solution.py:199
  30.0 0.7 collective-permute-done.1.y0.y
  30.7 1.4 %collective-permute-start.15 = (bf16[256,896]{1,0:T(8,128)(2,1)}, bf16[256,896]{1,0:T(8,128)(2,1)}, u32[]{:S(2)}, u32[]{:S(2)}) collective-permute-start(bf16[256,896]{1,0:T(8,128)(2,1)} %dynamic-slice_bitcast_fusion.1), channel_id=1, source_target_pairs={{4,8},{8,4},{5,9},{9,5},{6,10},{10,6},{7,11},{11,7},{20,24},{24,20... | collective-permute-start | bytes 1376264 | tf_op jit(solution)/shard_map/ppermute | solution.py:634
  32.3 1.6 %collective-permute-start.11 = (bf16[272,896]{1,0:T(8,128)(2,1)}, bf16[272,896]{1,0:T(8,128)(2,1)S(1)}, u32[]{:S(2)}, u32[]{:S(2)}) collective-permute-start(bf16[272,896]{1,0:T(8,128)(2,1)} %collective-permute-done.10.bz1.bz), channel_id=1, source_target_pairs={{0,16},{16,0},{1,17},{17,1},{2,18},{18,2},{3,19},{19,3},{4,20},{20... | collective-permute-start | bytes 1462280 | tf_op jit(solution)/shard_map/ppermute | solution.py:199
  33.8 1.4 %multiply_sine_fusion = (f32[384,64]{1,0:T(8,128)S(1)}, f32[384,64]{1,0:T(8,128)}) fusion(f32[64]{0:T(128)S(1)} %fusion.6, f32[384]{0:T(512)S(1)} %add_convert_fusion), kind=kLoop, calls=%fused_computation.2 | loop fusion | flops 24576 | bytes 198400 | tf_op jit(solution)/shard_map/sin | solution.py:657
  35.3 7.4 %collective-permute-done.3.y1.y = bf16[272,896]{1,0:T(8,128)(2,1)} collective-permute-done((bf16[272,896]{1,0:T(8,128)(2,1)}, bf16[272,896]{1,0:T(8,128)(2,1)}, u32[]{:S(2)}, u32[]{:S(2)}) %collective-permute-start.3) | collective-permute-done | bytes 487456 | tf_op jit(solution)/shard_map/ppermute | solution.py:199
  42.7 2.9 %shard_map.114 = (f32[192,528]{1,0:T(8,128)S(1)}, f32[192,528]{1,0:T(8,128)S(1)}) custom-call(s32[4]{0:T(128)S(1)} %pad_add_fusion.1.ids, bf16[384,1792]{1,0:T(8,128)(2,1)S(1)} %copy-done, bf16[528,1792]{1,0:T(8,128)(2,1)S(1)} %bitcast.16, bf16[256,896]{1,0:T(8,128)(2,1)} %collective-permute-done.z0.z, bf16[256,896]{1,0:T(8,128)(2,1)} %collective-permute-done.1.y0.y, ...), custom_call_target="tpu_custom_call" | custom-call | flops 726663168 | bytes 811008 | tf_op jit(solution)/shard_map/pallas_call | solution.py:291
  45.6 1.6 %collective-permute-start.16 = (bf16[256,896]{1,0:T(8,128)(2,1)}, bf16[256,896]{1,0:T(8,128)(2,1)}, u32[]{:S(2)}, u32[]{:S(2)}) collective-permute-start(bf16[256,896]{1,0:T(8,128)(2,1)} %collective-permute-done.15.bz), channel_id=1, source_target_pairs={{0,16},{16,0},{1,17},{17,1},{2,18},{18,2},{3,19},{19,3},{4,20},{20... | collective-permute-start | bytes 1376264 | tf_op jit(solution)/shard_map/ppermute | solution.py:199
  47.2 9.5 %collective-permute-done.6.x_ref.far0 = bf16[192,1792]{1,0:T(8,128)(2,1)} collective-permute-done((bf16[192,1792]{1,0:T(8,128)(2,1)}, bf16[192,1792]{1,0:T(8,128)(2,1)}, u32[]{:S(2)}, u32[]{:S(2)}) %collective-permute-start.6) | collective-permute-done | bytes 688160 | tf_op jit(solution)/shard_map/ppermute | solution.py:630
  56.7 3.8 %shard_map.118 = (f32[96,720]{1,0:T(8,128)S(1)}, f32[96,720]{1,0:T(8,128)S(1)}) custom-call(s32[4]{0:T(128)S(1)} %pad_add_fusion.1.ids, bf16[384,1792]{1,0:T(8,128)(2,1)S(1)} %copy-done, bf16[192,1792]{1,0:T(8,128)(2,1)} %collective-permute-done.6.x_ref.far0, bf16[192,1792]{1,0:T(8,128)(2,1)} %collective-permute-done.9.far1, bf16[528,1792]{1,0:T(8,128)(2,1)S(1)} %bitcast.17, ...), custom_call_target="tpu_custom_call" | custom-call | flops 495452160 | bytes 552960 | tf_op jit(solution)/shard_map/pallas_call | solution.py:291
  60.6 3.4 %shard_map.116 = (f32[96,528]{1,0:T(8,128)}, f32[96,528]{1,0:T(8,128)S(1)}) custom-call(s32[4]{0:T(128)S(1)} %pad_add_fusion.1.ids, bf16[192,1792]{1,0:T(8,128)(2,1)} %collective-permute-done.6.x_ref.far0, bf16[528,1792]{1,0:T(8,128)(2,1)S(1)} %bitcast.18, bf16[256,896]{1,0:T(8,128)(2,1)} %collective-permute-done.z0.z, ...), custom_call_target="tpu_custom_call" | custom-call | flops 363331584 | bytes 405504 | tf_op jit(solution)/shard_map/pallas_call | solution.py:291
  64.5 1.4 %shard_map.115 = (f32[192,528]{1,0:T(8,128)}, f32[192,528]{1,0:T(8,128)S(1)}) custom-call(s32[4]{0:T(128)S(1)} %pad_add_fusion.1.ids, f32[192,528]{1,0:T(8,128)S(1)} %get-tuple-element.41.kept, f32[192,528]{1,0:T(8,128)S(1)} %collective-permute-done.4.got), custom_call_target="tpu_custom_call" | custom-call | flops 20000000 | bytes 2000000 | tf_op jit(solution)/shard_map/pallas_call | solution.py:564
  65.8 1.5 %collective-permute-start.5 = (f32[192,528]{1,0:T(8,128)}, f32[192,528]{1,0:T(8,128)S(1)}, u32[]{:S(2)}, u32[]{:S(2)}) collective-permute-start(f32[192,528]{1,0:T(8,128)} %get-tuple-element.44), channel_id=1, source_target_pairs={{0,2},{2,0},{1,3},{3,1},{4,6},{6,4},{5,7},{7,5},{8,10},{10,8},{9,1... | collective-permute-start | bytes 1216520 | tf_op jit(solution)/shard_map/ppermute | solution.py:199
  67.3 1.3 %shard_map.119 = (f32[96,720]{1,0:T(8,128)}, f32[96,720]{1,0:T(8,128)S(1)}) custom-call(s32[4]{0:T(128)S(1)} %pad_add_fusion.1.ids, f32[96,720]{1,0:T(8,128)S(1)} %get-tuple-element.50.kept.kept_last, f32[96,720]{1,0:T(8,128)S(1)} %collective-permute-done.12.got.got_last), custom_call_target="tpu_custom_call" | custom-call | flops 20000000 | bytes 2000000 | tf_op jit(solution)/shard_map/pallas_call | solution.py:564
  69.5 0.9 copy-done.12
  71.0 1.6 %collective-permute-start.8 = (f32[96,528]{1,0:T(8,128)S(1)}, f32[96,528]{1,0:T(8,128)S(1)}, u32[]{:S(2)}, u32[]{:S(2)}) collective-permute-start(f32[96,528]{1,0:T(8,128)S(1)} %get-tuple-element.48), channel_id=1, source_target_pairs={{0,2},{2,0},{1,3},{3,1},{4,6},{6,4},{5,7},{7,5},{8,10},{10,8},{9,1... | collective-permute-start | bytes 608264 | tf_op jit(solution)/shard_map/ppermute | solution.py:199
  72.6 2.9 %shard_map.122 = (f32[192,512]{1,0:T(8,128)S(1)}, f32[192,512]{1,0:T(8,128)S(1)}) custom-call(s32[4]{0:T(128)S(1)} %pad_add_fusion.1.ids, bf16[384,1792]{1,0:T(8,128)(2,1)S(1)} %copy-done, bf16[192,1792]{1,0:T(8,128)(2,1)} %collective-permute-done.6.x_ref.far0, bf16[192,1792]{1,0:T(8,128)(2,1)} %collective-permute-done.9.far1, ...), custom_call_target="tpu_custom_call" | custom-call | flops 704643072 | bytes 786432 | tf_op jit(solution)/shard_map/pallas_call | solution.py:291
  75.6 2.8 %shard_map.121 = (f32[192,480]{1,0:T(8,128)S(1)}, f32[192,480]{1,0:T(8,128)S(1)}) custom-call(s32[4]{0:T(128)S(1)} %pad_add_fusion.1.ids, bf16[384,1792]{1,0:T(8,128)(2,1)S(1)} %copy-done, bf16[192,1792]{1,0:T(8,128)(2,1)} %collective-permute-done.6.x_ref.far0, bf16[192,1792]{1,0:T(8,128)(2,1)} %collective-permute-done.9.far1, ...), custom_call_target="tpu_custom_call" | custom-call | flops 660602880 | bytes 737280 | tf_op jit(solution)/shard_map/pallas_call | solution.py:291
  79.1 11.7 %collective-permute-done.8.got1 = f32[96,528]{1,0:T(8,128)S(1)} collective-permute-done((f32[96,528]{1,0:T(8,128)S(1)}, f32[96,528]{1,0:T(8,128)S(1)}, u32[]{:S(2)}, u32[]{:S(2)}) %collective-permute-start.8) | collective-permute-done | bytes 202784 | tf_op jit(solution)/shard_map/ppermute | solution.py:199
  90.8 2.5 %collective-permute-start.27 = (s32[1,60]{1,0:T(1,128)S(1)}, s32[1,60]{1,0:T(1,128)S(1)}, u32[]{:S(2)}, u32[]{:S(2)}) collective-permute-start(s32[1,60]{1,0:T(1,128)S(1)} %add_bitcast_fusion), channel_id=1, source_target_pairs={{12,0},{0,4},{4,8},{8,12},{13,1},{1,5},{5,9},{9,13},{14,2},{2,6},{... | collective-permute-start | bytes 728 | tf_op jit(solution)/shard_map/ppermute | solution.py:624
  94.1 1.6 %collective-permute-start.26 = (s32[1,60]{1,0:T(1,128)S(1)}, s32[1,60]{1,0:T(1,128)S(1)}, u32[]{:S(2)}, u32[]{:S(2)}) collective-permute-start(s32[1,60]{1,0:T(1,128)S(1)} %add_bitcast_fusion), channel_id=1, source_target_pairs={{8,0},{12,4},{0,8},{4,12},{9,1},{13,5},{1,9},{5,13},{10,2},{14,6},... | collective-permute-start | bytes 728 | tf_op jit(solution)/shard_map/ppermute | solution.py:624
  96.2 1.6 %collective-permute-start.25 = (s32[1,60]{1,0:T(1,128)S(1)}, s32[1,60]{1,0:T(1,128)S(1)}, u32[]{:S(2)}, u32[]{:S(2)}) collective-permute-start(s32[1,60]{1,0:T(1,128)S(1)} %add_bitcast_fusion), channel_id=1, source_target_pairs={{4,0},{8,4},{12,8},{0,12},{5,1},{9,5},{13,9},{1,13},{6,2},{10,6},{... | collective-permute-start | bytes 728 | tf_op jit(solution)/shard_map/ppermute | solution.py:624
  97.9 0.8 collective-permute-done.26
  98.6 1.1 collective-permute-done.25
  99.8 1.8 %shard_map.128 = (f32[128,640]{1,0:T(8,128)S(1)}, f32[8,768]{1,0:T(8,128)S(1)}) custom-call(s32[4]{0:T(128)S(1)} %pad_add_fusion.1.ids, s32[8,128]{1,0:T(8,128)S(1)} %pad.8.tab_ref, bf16[128,576]{1,0:T(8,128)(2,1)S(1)} %bitcast.20, bf16[1024,576]{1,0:T(8,128)(2,1)S(1)} %bitcast.19, bf16[16,576]{1,0:T(8,128)(2,1)S(1)} %pad.9.own_ref), custom_call_target="tpu_custom_call" | custom-call | flops 20000000 | bytes 2000000 | tf_op jit(solution)/shard_map/pallas_call | solution.py:564
  101.6 0.7 collective-permute-start.28
  102.4 0.7 shard_map.123
  103.1 1.6 %collective-permute-start.18 = (bf16[192,528]{1,0:T(8,128)(2,1)S(1)}, bf16[192,528]{1,0:T(8,128)(2,1)S(1)}, u32[]{:S(2)}, u32[]{:S(2)}) collective-permute-start(bf16[192,528]{1,0:T(8,128)(2,1)S(1)} %get-tuple-element.61), channel_id=1, source_target_pairs={{0,2},{2,0},{1,3},{3,1},{4,6},{6,4},{5,7},{7,5},{8,10},{10,8},{9,1... | collective-permute-start | bytes 608264 | tf_op jit(solution)/shard_map/ppermute | solution.py:199
  104.6 5.1 %collective-permute-done.28.far_ref = f32[128,640]{1,0:T(8,128)S(1)} collective-permute-done((f32[128,640]{1,0:T(8,128)S(1)}, f32[128,640]{1,0:T(8,128)S(1)}, u32[]{:S(2)}, u32[]{:S(2)}) %collective-permute-start.28) | collective-permute-done | bytes 327712 | tf_op jit(solution)/shard_map/ppermute | solution.py:646
  109.8 0.8 shard_map.129
  111.3 5.0 %collective-permute-start.19 = (bf16[96,528]{1,0:T(8,128)(2,1)S(1)}, bf16[96,528]{1,0:T(8,128)(2,1)S(1)}, u32[]{:S(2)}, u32[]{:S(2)}) collective-permute-start(bf16[96,528]{1,0:T(8,128)(2,1)S(1)} %get-tuple-element.63), channel_id=1, source_target_pairs={{0,4},{4,0},{8,12},{12,8},{1,5},{5,1},{9,13},{13,9},{2,6},{6,2},{1... | collective-permute-start | bytes 304136 | tf_op jit(solution)/shard_map/ppermute | solution.py:729
  116.6 4.8 %collective-permute-start.30 = (bf16[128,512]{1,0:T(8,128)(2,1)S(1)}, bf16[128,512]{1,0:T(8,128)(2,1)S(1)}, u32[]{:S(2)}, u32[]{:S(2)}) collective-permute-start(bf16[128,512]{1,0:T(8,128)(2,1)S(1)} %shard_map.130), channel_id=1, source_target_pairs={{0,4},{4,0},{8,12},{12,8},{1,5},{5,1},{9,13},{13,9},{2,6},{6,2},{1... | collective-permute-start | bytes 393224 | tf_op jit(solution)/shard_map/ppermute | solution.py:720
  121.4 0.9 shard_map.125
  122.4 1.5 %collective-permute-start.22 = (bf16[96,384]{1,0:T(8,128)(2,1)S(1)}, bf16[96,384]{1,0:T(8,128)(2,1)S(1)}, u32[]{:S(2)}, u32[]{:S(2)}) collective-permute-start(bf16[96,384]{1,0:T(8,128)(2,1)S(1)} %get-tuple-element.68), channel_id=1, source_target_pairs={{0,2},{1,3},{2,0},{3,1},{4,6},{5,7},{6,4},{7,5},{8,10},{9,11},{10,... | collective-permute-start | bytes 221192 | tf_op jit(solution)/shard_map/ppermute | solution.py:749
  124.2 3.0 %collective-permute-done.22.refs_2_ = bf16[96,384]{1,0:T(8,128)(2,1)S(1)} collective-permute-done((bf16[96,384]{1,0:T(8,128)(2,1)S(1)}, bf16[96,384]{1,0:T(8,128)(2,1)S(1)}, u32[]{:S(2)}, u32[]{:S(2)}) %collective-permute-start.22) | collective-permute-done | bytes 73760 | tf_op jit(solution)/shard_map/ppermute | solution.py:749
  127.2 1.3 collective-permute-done.23.refs_3_
  128.4 1.3 shard_map.126
  129.7 0.7 broadcast_select_fusion
  (87 shorter events, 5.7 us)
Async XLA Ops:
  0.6 20.2 %copy-start = (bf16[384,1792]{1,0:T(8,128)(2,1)S(1)}, bf16[384,1792]{1,0:T(8,128)(2,1)}, u32[]{:S(2)}) copy-start(bf16[384,1792]{1,0:T(8,128)(2,1)} %x_ref.7) | copy-start | bytes 4128772
  2.6 29.6 %copy-start.14 = (f32[1536]{0:T(1024)S(1)}, f32[1536]{0:T(1024)}, u32[]{:S(2)}) copy-start(f32[1536]{0:T(1024)} %param.12) | copy-start | bytes 18436
  2.6 15.3 %collective-permute-start = (bf16[256,896]{1,0:T(8,128)(2,1)}, bf16[256,896]{1,0:T(8,128)(2,1)}, u32[]{:S(2)}, u32[]{:S(2)}) collective-permute-start(bf16[256,896]{1,0:T(8,128)(2,1)} %dynamic-slice_bitcast_fusion.1), channel_id=1, source_target_pairs={{0,8},{12,4},{4,0},{8,12},{1,9},{13,5},{5,1},{9,13},{2,10},{14,6},... | collective-permute-start | bytes 1376264 | tf_op jit(solution)/shard_map/ppermute | solution.py:618
  8.5 34.2 %copy-start.1 = (bf16[1792,528]{0,1:T(8,128)(2,1)S(1)}, bf16[1792,528]{0,1:T(8,128)(2,1)}, u32[]{:S(2)}) copy-start(bf16[1792,528]{0,1:T(8,128)(2,1)} %param.11) | copy-start | bytes 5677060
  8.5 19.8 %collective-permute-start.2 = (bf16[272,896]{1,0:T(8,128)(2,1)}, bf16[272,896]{1,0:T(8,128)(2,1)}, u32[]{:S(2)}, u32[]{:S(2)}) collective-permute-start(bf16[272,896]{1,0:T(8,128)(2,1)} %dynamic-slice_bitcast_fusion), channel_id=1, source_target_pairs={{0,8},{12,4},{4,0},{8,12},{1,9},{13,5},{5,1},{9,13},{2,10},{14,6},... | collective-permute-start | bytes 1462280 | tf_op jit(solution)/shard_map/ppermute | solution.py:618
  17.9 14.4 %collective-permute-start.10 = (bf16[272,896]{1,0:T(8,128)(2,1)}, bf16[272,896]{1,0:T(8,128)(2,1)}, u32[]{:S(2)}, u32[]{:S(2)}) collective-permute-start(bf16[272,896]{1,0:T(8,128)(2,1)} %dynamic-slice_bitcast_fusion), channel_id=1, source_target_pairs={{4,8},{8,4},{5,9},{9,5},{6,10},{10,6},{7,11},{11,7},{20,24},{24,20... | collective-permute-start | bytes 1462280 | tf_op jit(solution)/shard_map/ppermute | solution.py:634
  19.3 11.4 %collective-permute-start.1 = (bf16[256,896]{1,0:T(8,128)(2,1)}, bf16[256,896]{1,0:T(8,128)(2,1)}, u32[]{:S(2)}, u32[]{:S(2)}) collective-permute-start(bf16[256,896]{1,0:T(8,128)(2,1)} %collective-permute-done.z0.z), channel_id=1, source_target_pairs={{0,16},{16,0},{1,17},{17,1},{2,18},{18,2},{3,19},{19,3},{4,20},{20... | collective-permute-start | bytes 1376264 | tf_op jit(solution)/shard_map/ppermute | solution.py:199
  22.0 25.2 %collective-permute-start.9 = (bf16[192,1792]{1,0:T(8,128)(2,1)}, bf16[192,1792]{1,0:T(8,128)(2,1)}, u32[]{:S(2)}, u32[]{:S(2)}) collective-permute-start(bf16[192,1792]{1,0:T(8,128)(2,1)} %get-tuple-element.78), channel_id=1, source_target_pairs={{0,4},{4,0},{8,12},{12,8},{1,5},{5,1},{9,13},{13,9},{2,6},{6,2},{1... | collective-permute-start | bytes 2064392 | tf_op jit(solution)/shard_map/ppermute | solution.py:630
  26.5 30.2 %collective-permute-start.6 = (bf16[192,1792]{1,0:T(8,128)(2,1)}, bf16[192,1792]{1,0:T(8,128)(2,1)}, u32[]{:S(2)}, u32[]{:S(2)}) collective-permute-start(bf16[192,1792]{1,0:T(8,128)(2,1)} %get-tuple-element.79), channel_id=1, source_target_pairs={{0,4},{4,0},{8,12},{12,8},{1,5},{5,1},{9,13},{13,9},{2,6},{6,2},{1... | collective-permute-start | bytes 2064392 | tf_op jit(solution)/shard_map/ppermute | solution.py:630
  28.3 14.3 %collective-permute-start.3 = (bf16[272,896]{1,0:T(8,128)(2,1)}, bf16[272,896]{1,0:T(8,128)(2,1)}, u32[]{:S(2)}, u32[]{:S(2)}) collective-permute-start(bf16[272,896]{1,0:T(8,128)(2,1)} %collective-permute-done.2.z1.z), channel_id=1, source_target_pairs={{0,16},{16,0},{1,17},{17,1},{2,18},{18,2},{3,19},{19,3},{4,20},{20... | collective-permute-start | bytes 1462280 | tf_op jit(solution)/shard_map/ppermute | solution.py:199
  30.7 14.9 %collective-permute-start.15 = (bf16[256,896]{1,0:T(8,128)(2,1)}, bf16[256,896]{1,0:T(8,128)(2,1)}, u32[]{:S(2)}, u32[]{:S(2)}) collective-permute-start(bf16[256,896]{1,0:T(8,128)(2,1)} %dynamic-slice_bitcast_fusion.1), channel_id=1, source_target_pairs={{4,8},{8,4},{5,9},{9,5},{6,10},{10,6},{7,11},{11,7},{20,24},{24,20... | collective-permute-start | bytes 1376264 | tf_op jit(solution)/shard_map/ppermute | solution.py:634
  32.3 24.5 %collective-permute-start.11 = (bf16[272,896]{1,0:T(8,128)(2,1)}, bf16[272,896]{1,0:T(8,128)(2,1)S(1)}, u32[]{:S(2)}, u32[]{:S(2)}) collective-permute-start(bf16[272,896]{1,0:T(8,128)(2,1)} %collective-permute-done.10.bz1.bz), channel_id=1, source_target_pairs={{0,16},{16,0},{1,17},{17,1},{2,18},{18,2},{3,19},{19,3},{4,20},{20... | collective-permute-start | bytes 1462280 | tf_op jit(solution)/shard_map/ppermute | solution.py:199
  45.5 18.9 %collective-permute-start.4 = (f32[192,528]{1,0:T(8,128)S(1)}, f32[192,528]{1,0:T(8,128)S(1)}, u32[]{:S(2)}, u32[]{:S(2)}) collective-permute-start(f32[192,528]{1,0:T(8,128)S(1)} %get-tuple-element.42), channel_id=1, source_target_pairs={{0,1},{1,0},{2,3},{3,2},{4,5},{5,4},{6,7},{7,6},{8,9},{9,8},{10,11... | collective-permute-start | bytes 1216520 | tf_op jit(solution)/shard_map/ppermute | solution.py:199
  45.6 27.0 %collective-permute-start.16 = (bf16[256,896]{1,0:T(8,128)(2,1)}, bf16[256,896]{1,0:T(8,128)(2,1)}, u32[]{:S(2)}, u32[]{:S(2)}) collective-permute-start(bf16[256,896]{1,0:T(8,128)(2,1)} %collective-permute-done.15.bz), channel_id=1, source_target_pairs={{0,16},{16,0},{1,17},{17,1},{2,18},{18,2},{3,19},{19,3},{4,20},{20... | collective-permute-start | bytes 1376264 | tf_op jit(solution)/shard_map/ppermute | solution.py:199
  56.7 3.8 %copy-start.2 = (bf16[272,896]{1,0:T(8,128)(2,1)}, bf16[272,896]{1,0:T(8,128)(2,1)S(1)}, u32[]{:S(2)}) copy-start(bf16[272,896]{1,0:T(8,128)(2,1)S(1)} %collective-permute-done.11.by1.by) | copy-start | bytes 1462276
  60.5 6.8 %copy-start.5 = (f32[96,720]{1,0:T(8,128)}, f32[96,720]{1,0:T(8,128)S(1)}, u32[]{:S(2)}) copy-start(f32[96,720]{1,0:T(8,128)S(1)} %get-tuple-element.50.kept.kept_last) | copy-start | bytes 829444
  60.5 8.7 %copy-start.16 = (s32[1,4,8]{2,1,0:T(4,128)S(1)}, s32[1,4,8]{2,1,0:T(4,128)}, u32[]{:S(2)}) copy-start(s32[1,4,8]{2,1,0:T(4,128)} %param.16) | copy-start | bytes 388
  60.5 8.7 %copy-start.17 = (s32[12,2]{0,1:T(2,128)S(1)}, s32[12,2]{0,1:T(2,128)}, u32[]{:S(2)}) copy-start(s32[12,2]{0,1:T(2,128)} %param.15) | copy-start | bytes 292
  60.6 6.8 %collective-permute-start.12 = (f32[96,720]{1,0:T(8,128)S(1)}, f32[96,720]{1,0:T(8,128)S(1)}, u32[]{:S(2)}, u32[]{:S(2)}) collective-permute-start(f32[96,720]{1,0:T(8,128)S(1)} %get-tuple-element.51), channel_id=1, source_target_pairs={{0,1},{1,0},{2,3},{3,2},{4,5},{5,4},{6,7},{7,6},{8,9},{9,8},{10,11... | collective-permute-start | bytes 829448 | tf_op jit(solution)/shard_map/ppermute | solution.py:199
  64.0 4.7 %copy-start.11 = (f32[96,528]{1,0:T(8,128)}, f32[96,528]{1,0:T(8,128)S(1)}, u32[]{:S(2)}) copy-start(f32[96,528]{1,0:T(8,128)S(1)} %get-tuple-element.45.kept) | copy-start | bytes 608260
  64.0 5.5 %collective-permute-start.7 = (f32[96,528]{1,0:T(8,128)}, f32[96,528]{1,0:T(8,128)S(1)}, u32[]{:S(2)}, u32[]{:S(2)}) collective-permute-start(f32[96,528]{1,0:T(8,128)} %get-tuple-element.46), channel_id=1, source_target_pairs={{0,1},{1,0},{2,3},{3,2},{4,5},{5,4},{6,7},{7,6},{8,9},{9,8},{10,11... | collective-permute-start | bytes 608264 | tf_op jit(solution)/shard_map/ppermute | solution.py:199
  65.8 27.5 %collective-permute-start.5 = (f32[192,528]{1,0:T(8,128)}, f32[192,528]{1,0:T(8,128)S(1)}, u32[]{:S(2)}, u32[]{:S(2)}) collective-permute-start(f32[192,528]{1,0:T(8,128)} %get-tuple-element.44), channel_id=1, source_target_pairs={{0,2},{2,0},{1,3},{3,1},{4,6},{6,4},{5,7},{7,5},{8,10},{10,8},{9,1... | collective-permute-start | bytes 1216520 | tf_op jit(solution)/shard_map/ppermute | solution.py:199
  68.7 24.7 %collective-permute-start.13 = (f32[96,720]{1,0:T(8,128)}, f32[96,720]{1,0:T(8,128)S(1)}, u32[]{:S(2)}, u32[]{:S(2)}) collective-permute-start(f32[96,720]{1,0:T(8,128)} %get-tuple-element.53), channel_id=1, source_target_pairs={{0,2},{2,0},{1,3},{3,1},{4,6},{6,4},{5,7},{7,5},{8,10},{10,8},{9,1... | collective-permute-start | bytes 829448 | tf_op jit(solution)/shard_map/ppermute | solution.py:199
  71.0 4.6 %copy-start.3 = (bf16[272,896]{1,0:T(8,128)(2,1)S(1)}, bf16[272,896]{1,0:T(8,128)(2,1)}, u32[]{:S(2)}) copy-start(bf16[272,896]{1,0:T(8,128)(2,1)} %copy-done.2) | copy-start | bytes 1462276
  71.0 19.8 %collective-permute-start.8 = (f32[96,528]{1,0:T(8,128)S(1)}, f32[96,528]{1,0:T(8,128)S(1)}, u32[]{:S(2)}, u32[]{:S(2)}) collective-permute-start(f32[96,528]{1,0:T(8,128)S(1)} %get-tuple-element.48), channel_id=1, source_target_pairs={{0,2},{2,0},{1,3},{3,1},{4,6},{6,4},{5,7},{7,5},{8,10},{10,8},{9,1... | collective-permute-start | bytes 608264 | tf_op jit(solution)/shard_map/ppermute | solution.py:199
  75.5 3.5 %copy-start.18 = (s32[4,1]{0,1:T(1,128)S(1)}, s32[4,1]{0,1:T(1,128)}, u32[]{:S(2)}) copy-start(s32[4,1]{0,1:T(1,128)} %param.17) | copy-start | bytes 52
  75.5 17.8 %copy-start.9 = (f32[384,64]{1,0:T(8,128)S(1)}, f32[384,64]{1,0:T(8,128)}, u32[]{:S(2)}) copy-start(f32[384,64]{1,0:T(8,128)} %get-tuple-element.70.cos) | copy-start | bytes 294916
  75.5 17.8 %copy-start.13 = (f32[512]{0:T(512)S(1)}, f32[512]{0:T(512)}, u32[]{:S(2)}) copy-start(f32[512]{0:T(512)} %param.13) | copy-start | bytes 6148
  75.5 26.8 %collective-permute-start.17 = (f32[192,512]{1,0:T(8,128)S(1)}, f32[192,512]{1,0:T(8,128)S(1)}, u32[]{:S(2)}, u32[]{:S(2)}) collective-permute-start(f32[192,512]{1,0:T(8,128)S(1)} %get-tuple-element.59), channel_id=1, source_target_pairs={{0,1},{1,0},{2,3},{3,2},{4,5},{5,4},{6,7},{7,6},{8,9},{9,8},{10,11... | collective-permute-start | bytes 1179656 | tf_op jit(solution)/shard_map/ppermute | solution.py:199
  78.4 19.4 %copy-start.15 = (bf16[4,576]{1,0:T(4,128)(2,1)S(1)}, bf16[4,576]{1,0:T(4,128)(2,1)}, u32[]{:S(2)}) copy-start(bf16[4,576]{1,0:T(4,128)(2,1)} %param.19) | copy-start | bytes 13828
  78.4 21.3 %copy-start.4 = (bf16[32,32,576]{2,1,0:T(8,128)(2,1)S(1)}, bf16[32,32,576]{2,1,0:T(8,128)(2,1)}, u32[]{:S(2)}) copy-start(bf16[32,32,576]{2,1,0:T(8,128)(2,1)} %param.14) | copy-start | bytes 3538948
  78.5 21.3 %copy-start.10 = (bf16[4,32,576]{2,1,0:T(8,128)(2,1)S(1)}, bf16[4,32,576]{2,1,0:T(8,128)(2,1)}, u32[]{:S(2)}) copy-start(bf16[4,32,576]{2,1,0:T(8,128)(2,1)} %param.18) | copy-start | bytes 442372
  78.5 23.9 %collective-permute-start.14 = (f32[192,480]{1,0:T(8,128)S(1)}, f32[192,480]{1,0:T(8,128)S(1)}, u32[]{:S(2)}, u32[]{:S(2)}) collective-permute-start(f32[192,480]{1,0:T(8,128)S(1)} %get-tuple-element.56), channel_id=1, source_target_pairs={{0,1},{1,0},{2,3},{3,2},{4,5},{5,4},{6,7},{7,6},{8,9},{9,8},{10,11... | collective-permute-start | bytes 1105928 | tf_op jit(solution)/shard_map/ppermute | solution.py:199
  90.8 5.4 %collective-permute-start.27 = (s32[1,60]{1,0:T(1,128)S(1)}, s32[1,60]{1,0:T(1,128)S(1)}, u32[]{:S(2)}, u32[]{:S(2)}) collective-permute-start(s32[1,60]{1,0:T(1,128)S(1)} %add_bitcast_fusion), channel_id=1, source_target_pairs={{12,0},{0,4},{4,8},{8,12},{13,1},{1,5},{5,9},{9,13},{14,2},{2,6},{... | collective-permute-start | bytes 728 | tf_op jit(solution)/shard_map/ppermute | solution.py:624
  93.3 9.0 %copy-start.6 = (f32[96,720]{1,0:T(8,128)S(1)}, f32[96,720]{1,0:T(8,128)}, u32[]{:S(2)}) copy-start(f32[96,720]{1,0:T(8,128)} %copy-done.5) | copy-start | bytes 829444
  93.3 9.0 %copy-start.8 = (f32[96,720]{1,0:T(8,128)S(1)}, f32[96,720]{1,0:T(8,128)}, u32[]{:S(2)}) copy-start(f32[96,720]{1,0:T(8,128)} %copy-done.7) | copy-start | bytes 829444
  94.0 15.8 %collective-permute-start.24 = (bf16[384,576]{1,0:T(8,128)(2,1)S(1)}, bf16[384,576]{1,0:T(8,128)(2,1)S(1)}, u32[]{:S(2)}, u32[]{:S(2)}) collective-permute-start(bf16[384,576]{1,0:T(8,128)(2,1)S(1)} %shard_map.127.k0_ref), channel_id=1, source_target_pairs={{0,1},{1,0},{2,3},{3,2},{4,5},{5,4},{6,7},{7,6},{8,9},{9,8},{10,11... | collective-permute-start | bytes 1327112 | tf_op jit(solution)/shard_map/ppermute | solution.py:199
  94.1 4.5 %collective-permute-start.26 = (s32[1,60]{1,0:T(1,128)S(1)}, s32[1,60]{1,0:T(1,128)S(1)}, u32[]{:S(2)}, u32[]{:S(2)}) collective-permute-start(s32[1,60]{1,0:T(1,128)S(1)} %add_bitcast_fusion), channel_id=1, source_target_pairs={{8,0},{12,4},{0,8},{4,12},{9,1},{13,5},{1,9},{5,13},{10,2},{14,6},... | collective-permute-start | bytes 728 | tf_op jit(solution)/shard_map/ppermute | solution.py:624
  96.2 3.6 %collective-permute-start.25 = (s32[1,60]{1,0:T(1,128)S(1)}, s32[1,60]{1,0:T(1,128)S(1)}, u32[]{:S(2)}, u32[]{:S(2)}) collective-permute-start(s32[1,60]{1,0:T(1,128)S(1)} %add_bitcast_fusion), channel_id=1, source_target_pairs={{4,0},{8,4},{12,8},{0,12},{5,1},{9,5},{13,9},{1,13},{6,2},{10,6},{... | collective-permute-start | bytes 728 | tf_op jit(solution)/shard_map/ppermute | solution.py:624
  101.6 8.2 %collective-permute-start.28 = (f32[128,640]{1,0:T(8,128)S(1)}, f32[128,640]{1,0:T(8,128)S(1)}, u32[]{:S(2)}, u32[]{:S(2)}) collective-permute-start(f32[128,640]{1,0:T(8,128)S(1)} %get-tuple-element.75.old_ref), channel_id=1, source_target_pairs={{0,4},{4,0},{8,12},{12,8},{1,5},{5,1},{9,13},{13,9},{2,6},{6,2},{1... | collective-permute-start | bytes 983048 | tf_op jit(solution)/shard_map/ppermute | solution.py:646
  103.1 13.2 %collective-permute-start.18 = (bf16[192,528]{1,0:T(8,128)(2,1)S(1)}, bf16[192,528]{1,0:T(8,128)(2,1)S(1)}, u32[]{:S(2)}, u32[]{:S(2)}) collective-permute-start(bf16[192,528]{1,0:T(8,128)(2,1)S(1)} %get-tuple-element.61), channel_id=1, source_target_pairs={{0,2},{2,0},{1,3},{3,1},{4,6},{6,4},{5,7},{7,5},{8,10},{10,8},{9,1... | collective-permute-start | bytes 608264 | tf_op jit(solution)/shard_map/ppermute | solution.py:199
  110.6 5.8 %collective-permute-start.29 = (bf16[128,640]{1,0:T(8,128)(2,1)S(1)}, bf16[128,640]{1,0:T(8,128)(2,1)S(1)}, u32[]{:S(2)}, u32[]{:S(2)}) collective-permute-start(bf16[128,640]{1,0:T(8,128)(2,1)S(1)} %get-tuple-element.77), channel_id=1, source_target_pairs={{4,12},{12,4},{5,13},{13,5},{6,14},{14,6},{7,15},{15,7},{20,28},{2... | collective-permute-start | bytes 491528 | tf_op jit(solution)/shard_map/ppermute | solution.py:718
  111.3 10.1 %collective-permute-start.19 = (bf16[96,528]{1,0:T(8,128)(2,1)S(1)}, bf16[96,528]{1,0:T(8,128)(2,1)S(1)}, u32[]{:S(2)}, u32[]{:S(2)}) collective-permute-start(bf16[96,528]{1,0:T(8,128)(2,1)S(1)} %get-tuple-element.63), channel_id=1, source_target_pairs={{0,4},{4,0},{8,12},{12,8},{1,5},{5,1},{9,13},{13,9},{2,6},{6,2},{1... | collective-permute-start | bytes 304136 | tf_op jit(solution)/shard_map/ppermute | solution.py:729
  116.3 5.1 %collective-permute-start.20 = (bf16[96,528]{1,0:T(8,128)(2,1)S(1)}, bf16[96,528]{1,0:T(8,128)(2,1)S(1)}, u32[]{:S(2)}, u32[]{:S(2)}) collective-permute-start(bf16[96,528]{1,0:T(8,128)(2,1)S(1)} %get-tuple-element.64), channel_id=1, source_target_pairs={{0,4},{4,0},{8,12},{12,8},{1,5},{5,1},{9,13},{13,9},{2,6},{6,2},{1... | collective-permute-start | bytes 304136 | tf_op jit(solution)/shard_map/ppermute | solution.py:736
  116.6 13.1 %collective-permute-start.30 = (bf16[128,512]{1,0:T(8,128)(2,1)S(1)}, bf16[128,512]{1,0:T(8,128)(2,1)S(1)}, u32[]{:S(2)}, u32[]{:S(2)}) collective-permute-start(bf16[128,512]{1,0:T(8,128)(2,1)S(1)} %shard_map.130), channel_id=1, source_target_pairs={{0,4},{4,0},{8,12},{12,8},{1,5},{5,1},{9,13},{13,9},{2,6},{6,2},{1... | collective-permute-start | bytes 393224 | tf_op jit(solution)/shard_map/ppermute | solution.py:720
  122.3 1.9 %collective-permute-start.21 = (bf16[96,384]{1,0:T(8,128)(2,1)S(1)}, bf16[96,384]{1,0:T(8,128)(2,1)S(1)}, u32[]{:S(2)}, u32[]{:S(2)}) collective-permute-start(bf16[96,384]{1,0:T(8,128)(2,1)S(1)} %get-tuple-element.67), channel_id=1, source_target_pairs={{0,1},{1,0},{2,3},{3,2},{4,5},{5,4},{6,7},{7,6},{8,9},{9,8},{10,11... | collective-permute-start | bytes 221192 | tf_op jit(solution)/shard_map/ppermute | solution.py:749
  122.4 4.8 %collective-permute-start.22 = (bf16[96,384]{1,0:T(8,128)(2,1)S(1)}, bf16[96,384]{1,0:T(8,128)(2,1)S(1)}, u32[]{:S(2)}, u32[]{:S(2)}) collective-permute-start(bf16[96,384]{1,0:T(8,128)(2,1)S(1)} %get-tuple-element.68), channel_id=1, source_target_pairs={{0,2},{1,3},{2,0},{3,1},{4,6},{5,7},{6,4},{7,5},{8,10},{9,11},{10,... | collective-permute-start | bytes 221192 | tf_op jit(solution)/shard_map/ppermute | solution.py:749
  123.9 4.5 %collective-permute-start.23 = (bf16[96,384]{1,0:T(8,128)(2,1)S(1)}, bf16[96,384]{1,0:T(8,128)(2,1)S(1)}, u32[]{:S(2)}, u32[]{:S(2)}) collective-permute-start(bf16[96,384]{1,0:T(8,128)(2,1)S(1)} %get-tuple-element.69), channel_id=1, source_target_pairs={{0,3},{1,2},{2,1},{3,0},{4,7},{5,6},{6,5},{7,4},{8,11},{9,10},{10,... | collective-permute-start | bytes 221192 | tf_op jit(solution)/shard_map/ppermute | solution.py:749
  (2 other events, 2.3 us)

commit v8 on v7

--- a/solution.py
+++ b/solution.py
@@ -261,8 +261,9 @@
     parts = ((z0, y0), (z1.at[:full, :], y1.at[:full, :]))
     primary(ids, far1, own_ref, parts, send, keep, chunk)
     at, left, own = slice(z1.shape[0] - keys, None), slice(full, None), slice(head + full, None)
-    k_here = chosen(outer, z1[at, :], bz1[at, :])
-    k_there = chosen(outer, y1[at, :], by1[at, :])
+    own_keys = slice(bz1.shape[0] - keys, None)
+    k_here = chosen(outer, z1[at, :], bz1[own_keys, :])
+    k_there = chosen(outer, y1[at, :], by1[own_keys, :])
     w_here = jnp.concatenate([chosen(outer, own_ref[own, here], z1[left, :]), k_here], axis=0)
     w_there = jnp.concatenate([chosen(outer, own_ref[own, there], y1[left, :]), k_there], axis=0)
     out = projected(ids, far1, w_here, w_there)
@@ -274,8 +275,11 @@
     put(ids, projected(ids, far0, k_here, k_there), send, keep, chunk, cols + 2 * keys)
 
 
-def rest_kernel(chunk, used, ids, x_ref, far0, far1, z, y, bz, by, send, keep, rows):
+def rest_kernel(chunk, used, ids, x_ref, far0, far1, z, y, *refs):
+    pieces, (send, keep, rows) = refs[:-3], refs[-3:]
     outer = is_outer(ids)
+    bz = jnp.concatenate([piece[...] for piece in pieces[0::2]], axis=0)
+    by = jnp.concatenate([piece[...] for piece in pieces[1::2]], axis=0)
     w_here = chosen(outer, z[:used, :], bz[:used, :])
     w_there = chosen(outer, y[:used, :], by[:used, :])
     put(ids, projected(ids, x_ref, w_here, w_there), send, keep, chunk, 0)
@@ -613,7 +617,7 @@
         lax.dynamic_slice(weight, (split, group * half), (cols - split, half)),
     ]
     partners = [(0, 1), (1, 0), (2, 3), (3, 2)]
-    a_z, a_y, b_z, b_y = [None] * 2, [None] * 2, [None] * 2, [None] * 2
+    a_z, a_y, b_z, b_y = [None] * 2, [None] * 2, [None] * 3, [None] * 3
     for p in (1, 0):
         a_z[p] = lax.ppermute(pieces[p], DEC, [(0, 2), (3, 1), (1, 0), (2, 3)])
     packed = jnp.concatenate(
@@ -628,12 +632,14 @@
     x_far = []
     for c in range(2):
         x_far.append(lax.ppermute(hidden_x[c * rows : (c + 1) * rows], DEC, partners))
-    held = lax.optimization_barrier((pieces[0], pieces[1], a_z[0]))
+    middle = (cols - split) * 3 // 10 // 16 * 16
+    held = lax.optimization_barrier((pieces[0], pieces[1][middle:], pieces[1][:middle], a_z[0]))
     for p in (1, 0):
         a_y[p] = swap(a_z[p], GRP)
+    for p in (1, 2, 0):
         b_z[p] = lax.ppermute(held[p], DEC, [(1, 2), (2, 1)])
-    for p in (1, 0):
         b_y[p] = swap(b_z[p], GRP)
+
     query = dec_query.reshape(queries, KVW)
     padded_key = jnp.pad(new_key, ((0, 3 * requests), (0, 0)))
     old, bias = call(
@@ -684,13 +690,14 @@
         (ids, hidden_x, *x_far, weight, *a_refs, b_z[1], b_y[1]),
     )
     used = (cols - split - keys, split)
+    b_parts = ((b_z[0], b_y[0]), (b_z[2], b_y[2], b_z[1], b_y[1]))
     rest = []
     for k, p in enumerate((1, 0)):
         send, kept = project(
             functools.partial(rest_kernel, rows, used[k]),
             rows,
             -(-used[k] // 128) * 128 + used[k],
-            (ids, hidden_x, *x_far, a_z[p], a_y[p], b_z[p], b_y[p]),
+            (ids, hidden_x, *x_far, a_z[p], a_y[p], *b_parts[p]),
             scratch=[pltpu.VMEM((tokens, feats), BF16)],
         )
         rest += [kept, swap(send, TP)]

time: 131 us -> 134 us (1.023)
  waiting for transfers between devices: 50.7 us -> 44.8 us
  starting transfers between devices: 44.5 us -> 50.4 us
  local copies, waits for them, and re-layouts: 6.31 us -> 9.02 us
    ppermute x2, waiting for transfers between devices: 9.5 us -> 2.98 us  [pairs_step(): x_far.append(lax.ppermute(hidden_x[c * rows:(c + 1) * rows], DEC, partners))]
    ppermute x14 -> x15, waiting for transfers between devices: 19.9 us -> 24.5 us  [swap(): return lax.ppermute(a, axis, [(0, 1), (1, 0)])]
    ppermute x2, waiting for transfers between devices: 9.58 us -> 5.78 us  [pairs_step(): a_z[p] = lax.ppermute(pieces[p], DEC, [(0, 2), (3, 1), (1, 0), (2, 3)])]
    slice x0 -> x2, local copies, waits for them, and re-layouts: none -> 3.48 us  [the longest x1 1.87 us: pairs_step(): pieces[1][middle:]]
    ppermute x3, starting transfers between devices: 5.72 us -> 7.53 us  [pairs_step(): lax.ppermute(packed, DEC, [((i + s) % n, i) for i in range(n)])]
    ppermute x14 -> x15, starting transfers between devices: 12.6 us -> 14.2 us  [swap(): return lax.ppermute(a, axis, [(0, 1), (1, 0)])]
    ppermute x2 -> x3, starting transfers between devices: 2.88 us -> 4.17 us  [pairs_step(): b_z[p] = lax.ppermute(held[p], DEC, [(1, 2), (2, 1)])]
  transfers between devices with their start and end apart: 31 -> 33, of which waited for: 12 -> 12; matrix products, arithmetic and copies ran while one was open for 4% -> 6% of each run, Pallas kernels for 20% -> 19%
where the time goes in v8:
time: 134 us; the launch traced here: 133 us
  starting transfers between devices  50.4 us (38%)
  waiting for transfers between devices  44.8 us (33%)
  Pallas kernels  25.7 us (19%)
  local copies, waits for them, and re-layouts  9.02 us (7%)
  other arithmetic  2.37 us (2%)
    ppermute x15, waiting for transfers between devices, swap(): return lax.ppermute(a, axis, [(0, 1), (1, 0)])  24.5 us
    pallas_call x5, Pallas kernels, project(): pl.pallas_call(kernel, in_specs=[SMEM] + [VMEM] * (len(args) - 1), out_sp...  15.6 us
    ppermute x15, starting transfers between devices, swap(): return lax.ppermute(a, axis, [(0, 1), (1, 0)])  14.2 us
    pallas_call x13, Pallas kernels, call(): pl.pallas_call(kernel, scratch_shapes=scratch, out_shape=shapes, in_specs...  10.1 us
    ppermute x3, starting transfers between devices, pairs_step(): lax.ppermute(packed, DEC, [((i + s) % n, i) for i in range(n)])  7.53 us
    ppermute x2, waiting for transfers between devices, pairs_step(): a_z[p] = lax.ppermute(pieces[p], DEC, [(0, 2), (3, 1), (1, 0), (2, 3)])  5.78 us
    ppermute x2, starting transfers between devices, pairs_step(): a_z[p] = lax.ppermute(pieces[p], DEC, [(0, 2), (3, 1), (1, 0), (2, 3)])  5.69 us
    ppermute x1, starting transfers between devices, pairs_step(): back0 = lax.ppermute(back0, DEC, partners)  5.64 us
  transfers between devices with their start and end apart: 33, of which 12 were waited for; matrix products, arithmetic and copies ran while one was open for 6% of the time, Pallas kernels for 19%

profile of v8, /device:TPU:0, one launch (start us, length us, event | category | flops | bytes accessed | tf_op | source)
XLA Modules:
  0.0 133.4 jit_solution(6338993770488278207)
XLA Ops:
  0.6 1.2 dynamic-slice_bitcast_fusion.1
  1.8 4.1 %collective-permute-start = (bf16[256,896]{1,0:T(8,128)(2,1)S(1)}, bf16[256,896]{1,0:T(8,128)(2,1)}, u32[]{:S(2)}, u32[]{:S(2)}) collective-permute-start(bf16[256,896]{1,0:T(8,128)(2,1)S(1)} %dynamic-slice_bitcast_fusion.1), channel_id=1, source_target_pairs={{0,8},{12,4},{4,0},{8,12},{1,9},{13,5},{5,1},{9,13},{2,10},{14,6},... | collective-permute-start | bytes 1376264 | tf_op jit(solution)/shard_map/ppermute | solution.py:622
  5.9 1.9 %dynamic-slice_bitcast_fusion = bf16[272,896]{1,0:T(8,128)(2,1)} fusion(bf16[1792,528]{0,1:T(8,128)(2,1)} %param.11, s32[]{:T(128)S(6)} %select_n.42), kind=kLoop, calls=%fused_computation | loop fusion | bytes 974852 | tf_op jit(solution)/shard_map/dynamic_slice | solution.py:617
  7.8 1.6 %collective-permute-start.2 = (bf16[272,896]{1,0:T(8,128)(2,1)}, bf16[272,896]{1,0:T(8,128)(2,1)}, u32[]{:S(2)}, u32[]{:S(2)}) collective-permute-start(bf16[272,896]{1,0:T(8,128)(2,1)} %dynamic-slice_bitcast_fusion), channel_id=1, source_target_pairs={{0,8},{12,4},{4,0},{8,12},{1,9},{13,5},{5,1},{9,13},{2,10},{14,6},... | collective-permute-start | bytes 1462280 | tf_op jit(solution)/shard_map/ppermute | solution.py:622
  9.4 1.6 %slice.17 = bf16[80,896]{1,0:T(8,128)(2,1)} slice(bf16[272,896]{1,0:T(8,128)(2,1)} %dynamic-slice_bitcast_fusion), slice={[0:80], [0:896]} | slice | bytes 286720 | tf_op jit(solution)/shard_map/slice | solution.py:636
  11.0 1.9 %slice.16 = bf16[192,896]{1,0:T(8,128)(2,1)} slice(bf16[272,896]{1,0:T(8,128)(2,1)} %dynamic-slice_bitcast_fusion), slice={[80:272], [0:896]} | slice | bytes 688128 | tf_op jit(solution)/shard_map/slice | solution.py:636
  12.9 4.0 %collective-permute-done.z0.z = bf16[256,896]{1,0:T(8,128)(2,1)} collective-permute-done((bf16[256,896]{1,0:T(8,128)(2,1)S(1)}, bf16[256,896]{1,0:T(8,128)(2,1)}, u32[]{:S(2)}, u32[]{:S(2)}) %collective-permute-start) | collective-permute-done | bytes 458784 | tf_op jit(solution)/shard_map/ppermute | solution.py:622
  16.8 1.4 %collective-permute-start.10 = (bf16[192,896]{1,0:T(8,128)(2,1)}, bf16[192,896]{1,0:T(8,128)(2,1)}, u32[]{:S(2)}, u32[]{:S(2)}) collective-permute-start(bf16[192,896]{1,0:T(8,128)(2,1)} %slice.16), channel_id=1, source_target_pairs={{4,8},{8,4},{5,9},{9,5},{6,10},{10,6},{7,11},{11,7},{20,24},{24,20... | collective-permute-start | bytes 1032200 | tf_op jit(solution)/shard_map/ppermute | solution.py:640
  18.2 1.2 fusion.8
  19.4 4.6 %collective-permute-start.9 = (bf16[192,1792]{1,0:T(8,128)(2,1)}, bf16[192,1792]{1,0:T(8,128)(2,1)}, u32[]{:S(2)}, u32[]{:S(2)}) collective-permute-start(bf16[192,1792]{1,0:T(8,128)(2,1)} %get-tuple-element.80), channel_id=1, source_target_pairs={{0,4},{4,0},{8,12},{12,8},{1,5},{5,1},{9,13},{13,9},{2,6},{6,2},{1... | collective-permute-start | bytes 2064392 | tf_op jit(solution)/shard_map/ppermute | solution.py:634
  24.1 1.6 %collective-permute-start.1 = (bf16[256,896]{1,0:T(8,128)(2,1)}, bf16[256,896]{1,0:T(8,128)(2,1)}, u32[]{:S(2)}, u32[]{:S(2)}) collective-permute-start(bf16[256,896]{1,0:T(8,128)(2,1)} %collective-permute-done.z0.z), channel_id=1, source_target_pairs={{0,16},{16,0},{1,17},{17,1},{2,18},{18,2},{3,19},{19,3},{4,20},{20... | collective-permute-start | bytes 1376264 | tf_op jit(solution)/shard_map/ppermute | solution.py:199
  25.6 1.8 %collective-permute-done.2.z1.z = bf16[272,896]{1,0:T(8,128)(2,1)} collective-permute-done((bf16[272,896]{1,0:T(8,128)(2,1)}, bf16[272,896]{1,0:T(8,128)(2,1)}, u32[]{:S(2)}, u32[]{:S(2)}) %collective-permute-start.2) | collective-permute-done | bytes 487456 | tf_op jit(solution)/shard_map/ppermute | solution.py:622
  27.4 1.5 %collective-permute-start.3 = (bf16[272,896]{1,0:T(8,128)(2,1)}, bf16[272,896]{1,0:T(8,128)(2,1)}, u32[]{:S(2)}, u32[]{:S(2)}) collective-permute-start(bf16[272,896]{1,0:T(8,128)(2,1)} %collective-permute-done.2.z1.z), channel_id=1, source_target_pairs={{0,16},{16,0},{1,17},{17,1},{2,18},{18,2},{3,19},{19,3},{4,20},{20... | collective-permute-start | bytes 1462280 | tf_op jit(solution)/shard_map/ppermute | solution.py:199
  29.1 1.5 %collective-permute-start.17 = (bf16[256,896]{1,0:T(8,128)(2,1)}, bf16[256,896]{1,0:T(8,128)(2,1)}, u32[]{:S(2)}, u32[]{:S(2)}) collective-permute-start(bf16[256,896]{1,0:T(8,128)(2,1)} %copy-done.14), channel_id=1, source_target_pairs={{4,8},{8,4},{5,9},{9,5},{6,10},{10,6},{7,11},{11,7},{20,24},{24,20... | collective-permute-start | bytes 1376264 | tf_op jit(solution)/shard_map/ppermute | solution.py:640
  30.5 1.4 %multiply_sine_fusion = (f32[384,64]{1,0:T(8,128)S(1)}, f32[384,64]{1,0:T(8,128)}) fusion(f32[64]{0:T(128)S(1)} %fusion.6, f32[384]{0:T(512)S(1)} %add_convert_fusion), kind=kLoop, calls=%fused_computation.2 | loop fusion | flops 24576 | bytes 198400 | tf_op jit(solution)/shard_map/sin | solution.py:663
  32.0 5.9 %collective-permute-done.1.y0.y = bf16[256,896]{1,0:T(8,128)(2,1)} collective-permute-done((bf16[256,896]{1,0:T(8,128)(2,1)}, bf16[256,896]{1,0:T(8,128)(2,1)}, u32[]{:S(2)}, u32[]{:S(2)}) %collective-permute-start.1) | collective-permute-done | bytes 458784 | tf_op jit(solution)/shard_map/ppermute | solution.py:199
  37.8 1.5 %collective-permute-start.11 = (bf16[192,896]{1,0:T(8,128)(2,1)}, bf16[192,896]{1,0:T(8,128)(2,1)S(1)}, u32[]{:S(2)}, u32[]{:S(2)}) collective-permute-start(bf16[192,896]{1,0:T(8,128)(2,1)} %collective-permute-done.10.bz1.refs_2_), channel_id=1, source_target_pairs={{0,16},{16,0},{1,17},{17,1},{2,18},{18,2},{3,19},{19,3},{4,20},{20... | collective-permute-start | bytes 1032200 | tf_op jit(solution)/shard_map/ppermute | solution.py:199
  39.4 8.8 %collective-permute-done.3.y1.y = bf16[272,896]{1,0:T(8,128)(2,1)} collective-permute-done((bf16[272,896]{1,0:T(8,128)(2,1)}, bf16[272,896]{1,0:T(8,128)(2,1)}, u32[]{:S(2)}, u32[]{:S(2)}) %collective-permute-start.3) | collective-permute-done | bytes 487456 | tf_op jit(solution)/shard_map/ppermute | solution.py:199
  48.3 2.9 %shard_map.114 = (f32[192,528]{1,0:T(8,128)S(1)}, f32[192,528]{1,0:T(8,128)S(1)}) custom-call(s32[4]{0:T(128)S(1)} %pad_add_fusion.1.ids, bf16[384,1792]{1,0:T(8,128)(2,1)S(1)} %copy-done, bf16[528,1792]{1,0:T(8,128)(2,1)S(1)} %bitcast.16, bf16[256,896]{1,0:T(8,128)(2,1)} %collective-permute-done.z0.z, bf16[256,896]{1,0:T(8,128)(2,1)} %collective-permute-done.1.y0.y, ...), custom_call_target="tpu_custom_call" | custom-call | flops 726663168 | bytes 811008 | tf_op jit(solution)/shard_map/pallas_call | solution.py:295
  51.2 1.6 %collective-permute-start.18 = (bf16[256,896]{1,0:T(8,128)(2,1)}, bf16[256,896]{1,0:T(8,128)(2,1)}, u32[]{:S(2)}, u32[]{:S(2)}) collective-permute-start(bf16[256,896]{1,0:T(8,128)(2,1)} %collective-permute-done.17.refs_0_), channel_id=1, source_target_pairs={{0,16},{16,0},{1,17},{17,1},{2,18},{18,2},{3,19},{19,3},{4,20},{20... | collective-permute-start | bytes 1376264 | tf_op jit(solution)/shard_map/ppermute | solution.py:199
  52.8 3.0 %collective-permute-done.6.x_ref.far0 = bf16[192,1792]{1,0:T(8,128)(2,1)} collective-permute-done((bf16[192,1792]{1,0:T(8,128)(2,1)}, bf16[192,1792]{1,0:T(8,128)(2,1)}, u32[]{:S(2)}, u32[]{:S(2)}) %collective-permute-start.6) | collective-permute-done | bytes 688160 | tf_op jit(solution)/shard_map/ppermute | solution.py:634
  55.8 3.7 %shard_map.118 = (f32[96,720]{1,0:T(8,128)S(1)}, f32[96,720]{1,0:T(8,128)S(1)}) custom-call(s32[4]{0:T(128)S(1)} %pad_add_fusion.1.ids, bf16[384,1792]{1,0:T(8,128)(2,1)S(1)} %copy-done, bf16[192,1792]{1,0:T(8,128)(2,1)} %collective-permute-done.6.x_ref.far0, bf16[192,1792]{1,0:T(8,128)(2,1)} %collective-permute-done.9.far1, bf16[528,1792]{1,0:T(8,128)(2,1)S(1)} %bitcast.17, ...), custom_call_target="tpu_custom_call" | custom-call | flops 495452160 | bytes 552960 | tf_op jit(solution)/shard_map/pallas_call | solution.py:295
  59.6 1.3 collective-permute-start.14
  61.0 3.3 %shard_map.116 = (f32[96,528]{1,0:T(8,128)}, f32[96,528]{1,0:T(8,128)S(1)}) custom-call(s32[4]{0:T(128)S(1)} %pad_add_fusion.1.ids, bf16[192,1792]{1,0:T(8,128)(2,1)} %collective-permute-done.6.x_ref.far0, bf16[528,1792]{1,0:T(8,128)(2,1)S(1)} %bitcast.18, bf16[256,896]{1,0:T(8,128)(2,1)} %collective-permute-done.z0.z, ...), custom_call_target="tpu_custom_call" | custom-call | flops 363331584 | bytes 405504 | tf_op jit(solution)/shard_map/pallas_call | solution.py:295
  64.8 1.4 %shard_map.115 = (f32[192,528]{1,0:T(8,128)}, f32[192,528]{1,0:T(8,128)S(1)}) custom-call(s32[4]{0:T(128)S(1)} %pad_add_fusion.1.ids, f32[192,528]{1,0:T(8,128)S(1)} %get-tuple-element.42.kept, f32[192,528]{1,0:T(8,128)S(1)} %collective-permute-done.4.got), custom_call_target="tpu_custom_call" | custom-call | flops 20000000 | bytes 2000000 | tf_op jit(solution)/shard_map/pallas_call | solution.py:568
  66.2 1.5 %collective-permute-start.5 = (f32[192,528]{1,0:T(8,128)}, f32[192,528]{1,0:T(8,128)S(1)}, u32[]{:S(2)}, u32[]{:S(2)}) collective-permute-start(f32[192,528]{1,0:T(8,128)} %get-tuple-element.45), channel_id=1, source_target_pairs={{0,2},{2,0},{1,3},{3,1},{4,6},{6,4},{5,7},{7,5},{8,10},{10,8},{9,1... | collective-permute-start | bytes 1216520 | tf_op jit(solution)/shard_map/ppermute | solution.py:199
  67.7 1.5 %collective-permute-start.15 = (bf16[80,896]{1,0:T(8,128)(2,1)}, bf16[80,896]{1,0:T(8,128)(2,1)}, u32[]{:S(2)}, u32[]{:S(2)}) collective-permute-start(bf16[80,896]{1,0:T(8,128)(2,1)} %collective-permute-done.14.refs_0_), channel_id=1, source_target_pairs={{0,16},{16,0},{1,17},{17,1},{2,18},{18,2},{3,19},{19,3},{4,20},{20... | collective-permute-start | bytes 430088 | tf_op jit(solution)/shard_map/ppermute | solution.py:199
  69.2 1.3 shard_map.119
  71.3 0.9 copy-done.12
  72.2 1.0 shard_map.117
  73.3 1.6 %collective-permute-start.8 = (f32[96,528]{1,0:T(8,128)S(1)}, f32[96,528]{1,0:T(8,128)S(1)}, u32[]{:S(2)}, u32[]{:S(2)}) collective-permute-start(f32[96,528]{1,0:T(8,128)S(1)} %get-tuple-element.49), channel_id=1, source_target_pairs={{0,2},{2,0},{1,3},{3,1},{4,6},{6,4},{5,7},{7,5},{8,10},{10,8},{9,1... | collective-permute-start | bytes 608264 | tf_op jit(solution)/shard_map/ppermute | solution.py:199
  74.8 2.8 %shard_map.121 = (f32[192,480]{1,0:T(8,128)S(1)}, f32[192,480]{1,0:T(8,128)S(1)}) custom-call(s32[4]{0:T(128)S(1)} %pad_add_fusion.1.ids, bf16[384,1792]{1,0:T(8,128)(2,1)S(1)} %copy-done, bf16[192,1792]{1,0:T(8,128)(2,1)} %collective-permute-done.6.x_ref.far0, bf16[192,1792]{1,0:T(8,128)(2,1)} %collective-permute-done.9.far1, ...), custom_call_target="tpu_custom_call" | custom-call | flops 660602880 | bytes 737280 | tf_op jit(solution)/shard_map/pallas_call | solution.py:295
  77.8 2.9 %shard_map.122 = (f32[192,512]{1,0:T(8,128)S(1)}, f32[192,512]{1,0:T(8,128)S(1)}) custom-call(s32[4]{0:T(128)S(1)} %pad_add_fusion.1.ids, bf16[384,1792]{1,0:T(8,128)(2,1)S(1)} %copy-done, bf16[192,1792]{1,0:T(8,128)(2,1)} %collective-permute-done.6.x_ref.far0, bf16[192,1792]{1,0:T(8,128)(2,1)} %collective-permute-done.9.far1, ...), custom_call_target="tpu_custom_call" | custom-call | flops 704643072 | bytes 786432 | tf_op jit(solution)/shard_map/pallas_call | solution.py:295
  81.4 9.8 %collective-permute-done.8.got1 = f32[96,528]{1,0:T(8,128)S(1)} collective-permute-done((f32[96,528]{1,0:T(8,128)S(1)}, f32[96,528]{1,0:T(8,128)S(1)}, u32[]{:S(2)}, u32[]{:S(2)}) %collective-permute-start.8) | collective-permute-done | bytes 202784 | tf_op jit(solution)/shard_map/ppermute | solution.py:199
  91.1 3.5 %collective-permute-start.29 = (s32[1,60]{1,0:T(1,128)S(1)}, s32[1,60]{1,0:T(1,128)S(1)}, u32[]{:S(2)}, u32[]{:S(2)}) collective-permute-start(s32[1,60]{1,0:T(1,128)S(1)} %add_bitcast_fusion), channel_id=1, source_target_pairs={{12,0},{0,4},{4,8},{8,12},{13,1},{1,5},{5,9},{9,13},{14,2},{2,6},{... | collective-permute-start | bytes 728 | tf_op jit(solution)/shard_map/ppermute | solution.py:628
  95.4 1.1 collective-permute-start.28
  96.5 2.9 %collective-permute-start.27 = (s32[1,60]{1,0:T(1,128)S(1)}, s32[1,60]{1,0:T(1,128)S(1)}, u32[]{:S(2)}, u32[]{:S(2)}) collective-permute-start(s32[1,60]{1,0:T(1,128)S(1)} %add_bitcast_fusion), channel_id=1, source_target_pairs={{4,0},{8,4},{12,8},{0,12},{5,1},{9,5},{13,9},{1,13},{6,2},{10,6},{... | collective-permute-start | bytes 728 | tf_op jit(solution)/shard_map/ppermute | solution.py:628
  100.8 1.8 %shard_map.128 = (f32[128,640]{1,0:T(8,128)S(1)}, f32[8,768]{1,0:T(8,128)S(1)}) custom-call(s32[4]{0:T(128)S(1)} %pad_add_fusion.1.ids, s32[8,128]{1,0:T(8,128)S(1)} %pad.8.tab_ref, bf16[128,576]{1,0:T(8,128)(2,1)S(1)} %bitcast.20, bf16[1024,576]{1,0:T(8,128)(2,1)S(1)} %bitcast.19, bf16[16,576]{1,0:T(8,128)(2,1)S(1)} %pad.9.own_ref), custom_call_target="tpu_custom_call" | custom-call | flops 20000000 | bytes 2000000 | tf_op jit(solution)/shard_map/pallas_call | solution.py:568
  102.6 1.1 collective-permute-start.30
  104.4 1.6 %collective-permute-start.20 = (bf16[192,528]{1,0:T(8,128)(2,1)S(1)}, bf16[192,528]{1,0:T(8,128)(2,1)S(1)}, u32[]{:S(2)}, u32[]{:S(2)}) collective-permute-start(bf16[192,528]{1,0:T(8,128)(2,1)S(1)} %get-tuple-element.63), channel_id=1, source_target_pairs={{0,2},{2,0},{1,3},{3,1},{4,6},{6,4},{5,7},{7,5},{8,10},{10,8},{9,1... | collective-permute-start | bytes 608264 | tf_op jit(solution)/shard_map/ppermute | solution.py:199
  106.0 5.5 %collective-permute-done.30.far_ref = f32[128,640]{1,0:T(8,128)S(1)} collective-permute-done((f32[128,640]{1,0:T(8,128)S(1)}, f32[128,640]{1,0:T(8,128)S(1)}, u32[]{:S(2)}, u32[]{:S(2)}) %collective-permute-start.30) | collective-permute-done | bytes 327712 | tf_op jit(solution)/shard_map/ppermute | solution.py:652
  113.1 5.6 %collective-permute-start.21 = (bf16[96,528]{1,0:T(8,128)(2,1)S(1)}, bf16[96,528]{1,0:T(8,128)(2,1)S(1)}, u32[]{:S(2)}, u32[]{:S(2)}) collective-permute-start(bf16[96,528]{1,0:T(8,128)(2,1)S(1)} %get-tuple-element.65), channel_id=1, source_target_pairs={{0,4},{4,0},{8,12},{12,8},{1,5},{5,1},{9,13},{13,9},{2,6},{6,2},{1... | collective-permute-start | bytes 304136 | tf_op jit(solution)/shard_map/ppermute | solution.py:736
  119.0 4.8 %collective-permute-start.32 = (bf16[128,512]{1,0:T(8,128)(2,1)S(1)}, bf16[128,512]{1,0:T(8,128)(2,1)S(1)}, u32[]{:S(2)}, u32[]{:S(2)}) collective-permute-start(bf16[128,512]{1,0:T(8,128)(2,1)S(1)} %shard_map.130), channel_id=1, source_target_pairs={{0,4},{4,0},{8,12},{12,8},{1,5},{5,1},{9,13},{13,9},{2,6},{6,2},{1... | collective-permute-start | bytes 393224 | tf_op jit(solution)/shard_map/ppermute | solution.py:727
  124.4 0.9 shard_map.125
  125.4 1.6 %collective-permute-start.24 = (bf16[96,384]{1,0:T(8,128)(2,1)S(1)}, bf16[96,384]{1,0:T(8,128)(2,1)S(1)}, u32[]{:S(2)}, u32[]{:S(2)}) collective-permute-start(bf16[96,384]{1,0:T(8,128)(2,1)S(1)} %get-tuple-element.70), channel_id=1, source_target_pairs={{0,2},{1,3},{2,0},{3,1},{4,6},{5,7},{6,4},{7,5},{8,10},{9,11},{10,... | collective-permute-start | bytes 221192 | tf_op jit(solution)/shard_map/ppermute | solution.py:756
  127.2 2.9 %collective-permute-done.24.refs_2_ = bf16[96,384]{1,0:T(8,128)(2,1)S(1)} collective-permute-done((bf16[96,384]{1,0:T(8,128)(2,1)S(1)}, bf16[96,384]{1,0:T(8,128)(2,1)S(1)}, u32[]{:S(2)}, u32[]{:S(2)}) %collective-permute-start.24) | collective-permute-done | bytes 73760 | tf_op jit(solution)/shard_map/ppermute | solution.py:756
  130.1 1.3 collective-permute-done.25.refs_3_
  131.4 1.3 shard_map.126
  (97 shorter events, 8.6 us)
Async XLA Ops:
  0.6 17.6 %copy-start = (bf16[384,1792]{1,0:T(8,128)(2,1)S(1)}, bf16[384,1792]{1,0:T(8,128)(2,1)}, u32[]{:S(2)}) copy-start(bf16[384,1792]{1,0:T(8,128)(2,1)} %x_ref.7) | copy-start | bytes 4128772
  1.8 15.0 %collective-permute-start = (bf16[256,896]{1,0:T(8,128)(2,1)S(1)}, bf16[256,896]{1,0:T(8,128)(2,1)}, u32[]{:S(2)}, u32[]{:S(2)}) collective-permute-start(bf16[256,896]{1,0:T(8,128)(2,1)S(1)} %dynamic-slice_bitcast_fusion.1), channel_id=1, source_target_pairs={{0,8},{12,4},{4,0},{8,12},{1,9},{13,5},{5,1},{9,13},{2,10},{14,6},... | collective-permute-start | bytes 1376264 | tf_op jit(solution)/shard_map/ppermute | solution.py:622
  7.8 19.6 %collective-permute-start.2 = (bf16[272,896]{1,0:T(8,128)(2,1)}, bf16[272,896]{1,0:T(8,128)(2,1)}, u32[]{:S(2)}, u32[]{:S(2)}) collective-permute-start(bf16[272,896]{1,0:T(8,128)(2,1)} %dynamic-slice_bitcast_fusion), channel_id=1, source_target_pairs={{0,8},{12,4},{4,0},{8,12},{1,9},{13,5},{5,1},{9,13},{2,10},{14,6},... | collective-permute-start | bytes 1462280 | tf_op jit(solution)/shard_map/ppermute | solution.py:622
  11.0 20.9 %copy-start.16 = (f32[1536]{0:T(1024)S(1)}, f32[1536]{0:T(1024)}, u32[]{:S(2)}) copy-start(f32[1536]{0:T(1024)} %param.12) | copy-start | bytes 18436
  11.0 37.3 %copy-start.1 = (bf16[1792,528]{0,1:T(8,128)(2,1)S(1)}, bf16[1792,528]{0,1:T(8,128)(2,1)}, u32[]{:S(2)}) copy-start(bf16[1792,528]{0,1:T(8,128)(2,1)} %param.11) | copy-start | bytes 5677060
  16.8 12.2 %collective-permute-start.10 = (bf16[192,896]{1,0:T(8,128)(2,1)}, bf16[192,896]{1,0:T(8,128)(2,1)}, u32[]{:S(2)}, u32[]{:S(2)}) collective-permute-start(bf16[192,896]{1,0:T(8,128)(2,1)} %slice.16), channel_id=1, source_target_pairs={{4,8},{8,4},{5,9},{9,5},{6,10},{10,6},{7,11},{11,7},{20,24},{24,20... | collective-permute-start | bytes 1032200 | tf_op jit(solution)/shard_map/ppermute | solution.py:640
  19.4 33.4 %collective-permute-start.9 = (bf16[192,1792]{1,0:T(8,128)(2,1)}, bf16[192,1792]{1,0:T(8,128)(2,1)}, u32[]{:S(2)}, u32[]{:S(2)}) collective-permute-start(bf16[192,1792]{1,0:T(8,128)(2,1)} %get-tuple-element.80), channel_id=1, source_target_pairs={{0,4},{4,0},{8,12},{12,8},{1,5},{5,1},{9,13},{13,9},{2,6},{6,2},{1... | collective-permute-start | bytes 2064392 | tf_op jit(solution)/shard_map/ppermute | solution.py:634
  24.0 31.8 %collective-permute-start.6 = (bf16[192,1792]{1,0:T(8,128)(2,1)}, bf16[192,1792]{1,0:T(8,128)(2,1)}, u32[]{:S(2)}, u32[]{:S(2)}) collective-permute-start(bf16[192,1792]{1,0:T(8,128)(2,1)} %get-tuple-element.81), channel_id=1, source_target_pairs={{0,4},{4,0},{8,12},{12,8},{1,5},{5,1},{9,13},{13,9},{2,6},{6,2},{1... | collective-permute-start | bytes 2064392 | tf_op jit(solution)/shard_map/ppermute | solution.py:634
  24.1 13.8 %collective-permute-start.1 = (bf16[256,896]{1,0:T(8,128)(2,1)}, bf16[256,896]{1,0:T(8,128)(2,1)}, u32[]{:S(2)}, u32[]{:S(2)}) collective-permute-start(bf16[256,896]{1,0:T(8,128)(2,1)} %collective-permute-done.z0.z), channel_id=1, source_target_pairs={{0,16},{16,0},{1,17},{17,1},{2,18},{18,2},{3,19},{19,3},{4,20},{20... | collective-permute-start | bytes 1376264 | tf_op jit(solution)/shard_map/ppermute | solution.py:199
  27.4 20.8 %collective-permute-start.3 = (bf16[272,896]{1,0:T(8,128)(2,1)}, bf16[272,896]{1,0:T(8,128)(2,1)}, u32[]{:S(2)}, u32[]{:S(2)}) collective-permute-start(bf16[272,896]{1,0:T(8,128)(2,1)} %collective-permute-done.2.z1.z), channel_id=1, source_target_pairs={{0,16},{16,0},{1,17},{17,1},{2,18},{18,2},{3,19},{19,3},{4,20},{20... | collective-permute-start | bytes 1462280 | tf_op jit(solution)/shard_map/ppermute | solution.py:199
  29.1 22.2 %collective-permute-start.17 = (bf16[256,896]{1,0:T(8,128)(2,1)}, bf16[256,896]{1,0:T(8,128)(2,1)}, u32[]{:S(2)}, u32[]{:S(2)}) collective-permute-start(bf16[256,896]{1,0:T(8,128)(2,1)} %copy-done.14), channel_id=1, source_target_pairs={{4,8},{8,4},{5,9},{9,5},{6,10},{10,6},{7,11},{11,7},{20,24},{24,20... | collective-permute-start | bytes 1376264 | tf_op jit(solution)/shard_map/ppermute | solution.py:640
  37.8 18.0 %collective-permute-start.11 = (bf16[192,896]{1,0:T(8,128)(2,1)}, bf16[192,896]{1,0:T(8,128)(2,1)S(1)}, u32[]{:S(2)}, u32[]{:S(2)}) collective-permute-start(bf16[192,896]{1,0:T(8,128)(2,1)} %collective-permute-done.10.bz1.refs_2_), channel_id=1, source_target_pairs={{0,16},{16,0},{1,17},{17,1},{2,18},{18,2},{3,19},{19,3},{4,20},{20... | collective-permute-start | bytes 1032200 | tf_op jit(solution)/shard_map/ppermute | solution.py:199
  51.1 8.5 %copy-start.15 = (bf16[80,896]{1,0:T(8,128)(2,1)S(1)}, bf16[80,896]{1,0:T(8,128)(2,1)}, u32[]{:S(2)}) copy-start(bf16[80,896]{1,0:T(8,128)(2,1)} %slice.17) | copy-start | bytes 430084
  51.2 13.6 %collective-permute-start.4 = (f32[192,528]{1,0:T(8,128)S(1)}, f32[192,528]{1,0:T(8,128)S(1)}, u32[]{:S(2)}, u32[]{:S(2)}) collective-permute-start(f32[192,528]{1,0:T(8,128)S(1)} %get-tuple-element.43), channel_id=1, source_target_pairs={{0,1},{1,0},{2,3},{3,2},{4,5},{5,4},{6,7},{7,6},{8,9},{9,8},{10,11... | collective-permute-start | bytes 1216520 | tf_op jit(solution)/shard_map/ppermute | solution.py:199
  51.2 26.5 %collective-permute-start.18 = (bf16[256,896]{1,0:T(8,128)(2,1)}, bf16[256,896]{1,0:T(8,128)(2,1)}, u32[]{:S(2)}, u32[]{:S(2)}) collective-permute-start(bf16[256,896]{1,0:T(8,128)(2,1)} %collective-permute-done.17.refs_0_), channel_id=1, source_target_pairs={{0,16},{16,0},{1,17},{17,1},{2,18},{18,2},{3,19},{19,3},{4,20},{20... | collective-permute-start | bytes 1376264 | tf_op jit(solution)/shard_map/ppermute | solution.py:199
  59.5 9.7 %copy-start.5 = (f32[96,720]{1,0:T(8,128)}, f32[96,720]{1,0:T(8,128)S(1)}, u32[]{:S(2)}) copy-start(f32[96,720]{1,0:T(8,128)S(1)} %get-tuple-element.51.kept.kept_last) | copy-start | bytes 829444
  59.5 11.5 %copy-start.18 = (s32[1,4,8]{2,1,0:T(4,128)S(1)}, s32[1,4,8]{2,1,0:T(4,128)}, u32[]{:S(2)}) copy-start(s32[1,4,8]{2,1,0:T(4,128)} %param.16) | copy-start | bytes 388
  59.5 11.6 %copy-start.19 = (s32[12,2]{0,1:T(2,128)S(1)}, s32[12,2]{0,1:T(2,128)}, u32[]{:S(2)}) copy-start(s32[12,2]{0,1:T(2,128)} %param.15) | copy-start | bytes 292
  59.6 9.6 %collective-permute-start.12 = (f32[96,720]{1,0:T(8,128)S(1)}, f32[96,720]{1,0:T(8,128)S(1)}, u32[]{:S(2)}, u32[]{:S(2)}) collective-permute-start(f32[96,720]{1,0:T(8,128)S(1)} %get-tuple-element.52), channel_id=1, source_target_pairs={{0,1},{1,0},{2,3},{3,2},{4,5},{5,4},{6,7},{7,6},{8,9},{9,8},{10,11... | collective-permute-start | bytes 829448 | tf_op jit(solution)/shard_map/ppermute | solution.py:199
  59.6 8.0 %collective-permute-start.14 = (bf16[80,896]{1,0:T(8,128)(2,1)S(1)}, bf16[80,896]{1,0:T(8,128)(2,1)}, u32[]{:S(2)}, u32[]{:S(2)}) collective-permute-start(bf16[80,896]{1,0:T(8,128)(2,1)S(1)} %copy-done.15), channel_id=1, source_target_pairs={{4,8},{8,4},{5,9},{9,5},{6,10},{10,6},{7,11},{11,7},{20,24},{24,20... | collective-permute-start | bytes 430088 | tf_op jit(solution)/shard_map/ppermute | solution.py:640
  64.3 10.5 %copy-start.3 = (bf16[192,896]{1,0:T(8,128)(2,1)S(1)}, bf16[192,896]{1,0:T(8,128)(2,1)}, u32[]{:S(2)}) copy-start(bf16[192,896]{1,0:T(8,128)(2,1)} %copy-done.2) | copy-start | bytes 1032196
  64.3 7.0 %collective-permute-start.7 = (f32[96,528]{1,0:T(8,128)}, f32[96,528]{1,0:T(8,128)}, u32[]{:S(2)}, u32[]{:S(2)}) collective-permute-start(f32[96,528]{1,0:T(8,128)} %get-tuple-element.47), channel_id=1, source_target_pairs={{0,1},{1,0},{2,3},{3,2},{4,5},{5,4},{6,7},{7,6},{8,9},{9,8},{10,11... | collective-permute-start | bytes 608264 | tf_op jit(solution)/shard_map/ppermute | solution.py:199
  66.2 28.5 %collective-permute-start.5 = (f32[192,528]{1,0:T(8,128)}, f32[192,528]{1,0:T(8,128)S(1)}, u32[]{:S(2)}, u32[]{:S(2)}) collective-permute-start(f32[192,528]{1,0:T(8,128)} %get-tuple-element.45), channel_id=1, source_target_pairs={{0,2},{2,0},{1,3},{3,1},{4,6},{6,4},{5,7},{7,5},{8,10},{10,8},{9,1... | collective-permute-start | bytes 1216520 | tf_op jit(solution)/shard_map/ppermute | solution.py:199
  67.7 7.2 %collective-permute-start.15 = (bf16[80,896]{1,0:T(8,128)(2,1)}, bf16[80,896]{1,0:T(8,128)(2,1)}, u32[]{:S(2)}, u32[]{:S(2)}) collective-permute-start(bf16[80,896]{1,0:T(8,128)(2,1)} %collective-permute-done.14.refs_0_), channel_id=1, source_target_pairs={{0,16},{16,0},{1,17},{17,1},{2,18},{18,2},{3,19},{19,3},{4,20},{20... | collective-permute-start | bytes 430088 | tf_op jit(solution)/shard_map/ppermute | solution.py:199
  70.5 24.2 %collective-permute-start.13 = (f32[96,720]{1,0:T(8,128)}, f32[96,720]{1,0:T(8,128)S(1)}, u32[]{:S(2)}, u32[]{:S(2)}) collective-permute-start(f32[96,720]{1,0:T(8,128)} %get-tuple-element.54), channel_id=1, source_target_pairs={{0,2},{2,0},{1,3},{3,1},{4,6},{6,4},{5,7},{7,5},{8,10},{10,8},{9,1... | collective-permute-start | bytes 829448 | tf_op jit(solution)/shard_map/ppermute | solution.py:199
  73.3 17.9 %collective-permute-start.8 = (f32[96,528]{1,0:T(8,128)S(1)}, f32[96,528]{1,0:T(8,128)S(1)}, u32[]{:S(2)}, u32[]{:S(2)}) collective-permute-start(f32[96,528]{1,0:T(8,128)S(1)} %get-tuple-element.49), channel_id=1, source_target_pairs={{0,2},{2,0},{1,3},{3,1},{4,6},{6,4},{5,7},{7,5},{8,10},{10,8},{9,1... | collective-permute-start | bytes 608264 | tf_op jit(solution)/shard_map/ppermute | solution.py:199
  77.7 17.0 %copy-start.9 = (f32[384,64]{1,0:T(8,128)S(1)}, f32[384,64]{1,0:T(8,128)}, u32[]{:S(2)}) copy-start(f32[384,64]{1,0:T(8,128)} %get-tuple-element.72.cos) | copy-start | bytes 294916
  77.7 17.0 %copy-start.13 = (f32[512]{0:T(512)S(1)}, f32[512]{0:T(512)}, u32[]{:S(2)}) copy-start(f32[512]{0:T(512)} %param.13) | copy-start | bytes 6148
  77.7 26.0 %collective-permute-start.16 = (f32[192,480]{1,0:T(8,128)S(1)}, f32[192,480]{1,0:T(8,128)S(1)}, u32[]{:S(2)}, u32[]{:S(2)}) collective-permute-start(f32[192,480]{1,0:T(8,128)S(1)} %get-tuple-element.58), channel_id=1, source_target_pairs={{0,1},{1,0},{2,3},{3,2},{4,5},{5,4},{6,7},{7,6},{8,9},{9,8},{10,11... | collective-permute-start | bytes 1105928 | tf_op jit(solution)/shard_map/ppermute | solution.py:199
  80.7 18.7 %copy-start.17 = (bf16[4,576]{1,0:T(4,128)(2,1)S(1)}, bf16[4,576]{1,0:T(4,128)(2,1)}, u32[]{:S(2)}) copy-start(bf16[4,576]{1,0:T(4,128)(2,1)} %param.19) | copy-start | bytes 13828
  80.7 20.1 %copy-start.4 = (bf16[32,32,576]{2,1,0:T(8,128)(2,1)S(1)}, bf16[32,32,576]{2,1,0:T(8,128)(2,1)}, u32[]{:S(2)}) copy-start(bf16[32,32,576]{2,1,0:T(8,128)(2,1)} %param.14) | copy-start | bytes 3538948
  80.7 20.0 %copy-start.10 = (bf16[4,32,576]{2,1,0:T(8,128)(2,1)S(1)}, bf16[4,32,576]{2,1,0:T(8,128)(2,1)}, u32[]{:S(2)}) copy-start(bf16[4,32,576]{2,1,0:T(8,128)(2,1)} %param.18) | copy-start | bytes 442372
  80.7 22.9 %collective-permute-start.19 = (f32[192,512]{1,0:T(8,128)S(1)}, f32[192,512]{1,0:T(8,128)S(1)}, u32[]{:S(2)}, u32[]{:S(2)}) collective-permute-start(f32[192,512]{1,0:T(8,128)S(1)} %get-tuple-element.61), channel_id=1, source_target_pairs={{0,1},{1,0},{2,3},{3,2},{4,5},{5,4},{6,7},{7,6},{8,9},{9,8},{10,11... | collective-permute-start | bytes 1179656 | tf_op jit(solution)/shard_map/ppermute | solution.py:199
  91.1 5.4 %collective-permute-start.29 = (s32[1,60]{1,0:T(1,128)S(1)}, s32[1,60]{1,0:T(1,128)S(1)}, u32[]{:S(2)}, u32[]{:S(2)}) collective-permute-start(s32[1,60]{1,0:T(1,128)S(1)} %add_bitcast_fusion), channel_id=1, source_target_pairs={{12,0},{0,4},{4,8},{8,12},{13,1},{1,5},{5,9},{9,13},{14,2},{2,6},{... | collective-permute-start | bytes 728 | tf_op jit(solution)/shard_map/ppermute | solution.py:628
  94.7 9.0 %copy-start.6 = (f32[96,720]{1,0:T(8,128)S(1)}, f32[96,720]{1,0:T(8,128)}, u32[]{:S(2)}) copy-start(f32[96,720]{1,0:T(8,128)} %copy-done.5) | copy-start | bytes 829444
  94.7 9.0 %copy-start.8 = (f32[96,720]{1,0:T(8,128)S(1)}, f32[96,720]{1,0:T(8,128)}, u32[]{:S(2)}) copy-start(f32[96,720]{1,0:T(8,128)} %copy-done.7) | copy-start | bytes 829444
  95.3 16.2 %collective-permute-start.26 = (bf16[384,576]{1,0:T(8,128)(2,1)S(1)}, bf16[384,576]{1,0:T(8,128)(2,1)S(1)}, u32[]{:S(2)}, u32[]{:S(2)}) collective-permute-start(bf16[384,576]{1,0:T(8,128)(2,1)S(1)} %shard_map.127.k0_ref), channel_id=1, source_target_pairs={{0,1},{1,0},{2,3},{3,2},{4,5},{5,4},{6,7},{7,6},{8,9},{9,8},{10,11... | collective-permute-start | bytes 1327112 | tf_op jit(solution)/shard_map/ppermute | solution.py:199
  95.4 4.5 %collective-permute-start.28 = (s32[1,60]{1,0:T(1,128)S(1)}, s32[1,60]{1,0:T(1,128)S(1)}, u32[]{:S(2)}, u32[]{:S(2)}) collective-permute-start(s32[1,60]{1,0:T(1,128)S(1)} %add_bitcast_fusion), channel_id=1, source_target_pairs={{8,0},{12,4},{0,8},{4,12},{9,1},{13,5},{1,9},{5,13},{10,2},{14,6},... | collective-permute-start | bytes 728 | tf_op jit(solution)/shard_map/ppermute | solution.py:628
  96.5 4.2 %collective-permute-start.27 = (s32[1,60]{1,0:T(1,128)S(1)}, s32[1,60]{1,0:T(1,128)S(1)}, u32[]{:S(2)}, u32[]{:S(2)}) collective-permute-start(s32[1,60]{1,0:T(1,128)S(1)} %add_bitcast_fusion), channel_id=1, source_target_pairs={{4,0},{8,4},{12,8},{0,12},{5,1},{9,5},{13,9},{1,13},{6,2},{10,6},{... | collective-permute-start | bytes 728 | tf_op jit(solution)/shard_map/ppermute | solution.py:628
  102.6 9.0 %collective-permute-start.30 = (f32[128,640]{1,0:T(8,128)S(1)}, f32[128,640]{1,0:T(8,128)S(1)}, u32[]{:S(2)}, u32[]{:S(2)}) collective-permute-start(f32[128,640]{1,0:T(8,128)S(1)} %get-tuple-element.77.old_ref), channel_id=1, source_target_pairs={{0,4},{4,0},{8,12},{12,8},{1,5},{5,1},{9,13},{13,9},{2,6},{6,2},{1... | collective-permute-start | bytes 983048 | tf_op jit(solution)/shard_map/ppermute | solution.py:652
  104.4 14.3 %collective-permute-start.20 = (bf16[192,528]{1,0:T(8,128)(2,1)S(1)}, bf16[192,528]{1,0:T(8,128)(2,1)S(1)}, u32[]{:S(2)}, u32[]{:S(2)}) collective-permute-start(bf16[192,528]{1,0:T(8,128)(2,1)S(1)} %get-tuple-element.63), channel_id=1, source_target_pairs={{0,2},{2,0},{1,3},{3,1},{4,6},{6,4},{5,7},{7,5},{8,10},{10,8},{9,1... | collective-permute-start | bytes 608264 | tf_op jit(solution)/shard_map/ppermute | solution.py:199
  112.4 6.5 %collective-permute-start.31 = (bf16[128,640]{1,0:T(8,128)(2,1)S(1)}, bf16[128,640]{1,0:T(8,128)(2,1)S(1)}, u32[]{:S(2)}, u32[]{:S(2)}) collective-permute-start(bf16[128,640]{1,0:T(8,128)(2,1)S(1)} %get-tuple-element.79), channel_id=1, source_target_pairs={{4,12},{12,4},{5,13},{13,5},{6,14},{14,6},{7,15},{15,7},{20,28},{2... | collective-permute-start | bytes 491528 | tf_op jit(solution)/shard_map/ppermute | solution.py:725
  113.1 10.8 %collective-permute-start.21 = (bf16[96,528]{1,0:T(8,128)(2,1)S(1)}, bf16[96,528]{1,0:T(8,128)(2,1)S(1)}, u32[]{:S(2)}, u32[]{:S(2)}) collective-permute-start(bf16[96,528]{1,0:T(8,128)(2,1)S(1)} %get-tuple-element.65), channel_id=1, source_target_pairs={{0,4},{4,0},{8,12},{12,8},{1,5},{5,1},{9,13},{13,9},{2,6},{6,2},{1... | collective-permute-start | bytes 304136 | tf_op jit(solution)/shard_map/ppermute | solution.py:736
  118.8 5.6 %collective-permute-start.22 = (bf16[96,528]{1,0:T(8,128)(2,1)S(1)}, bf16[96,528]{1,0:T(8,128)(2,1)S(1)}, u32[]{:S(2)}, u32[]{:S(2)}) collective-permute-start(bf16[96,528]{1,0:T(8,128)(2,1)S(1)} %get-tuple-element.66), channel_id=1, source_target_pairs={{0,4},{4,0},{8,12},{12,8},{1,5},{5,1},{9,13},{13,9},{2,6},{6,2},{1... | collective-permute-start | bytes 304136 | tf_op jit(solution)/shard_map/ppermute | solution.py:743
  119.0 13.7 %collective-permute-start.32 = (bf16[128,512]{1,0:T(8,128)(2,1)S(1)}, bf16[128,512]{1,0:T(8,128)(2,1)S(1)}, u32[]{:S(2)}, u32[]{:S(2)}) collective-permute-start(bf16[128,512]{1,0:T(8,128)(2,1)S(1)} %shard_map.130), channel_id=1, source_target_pairs={{0,4},{4,0},{8,12},{12,8},{1,5},{5,1},{9,13},{13,9},{2,6},{6,2},{1... | collective-permute-start | bytes 393224 | tf_op jit(solution)/shard_map/ppermute | solution.py:727
  125.3 1.9 %collective-permute-start.23 = (bf16[96,384]{1,0:T(8,128)(2,1)S(1)}, bf16[96,384]{1,0:T(8,128)(2,1)S(1)}, u32[]{:S(2)}, u32[]{:S(2)}) collective-permute-start(bf16[96,384]{1,0:T(8,128)(2,1)S(1)} %get-tuple-element.69), channel_id=1, source_target_pairs={{0,1},{1,0},{2,3},{3,2},{4,5},{5,4},{6,7},{7,6},{8,9},{9,8},{10,11... | collective-permute-start | bytes 221192 | tf_op jit(solution)/shard_map/ppermute | solution.py:756
  125.4 4.8 %collective-permute-start.24 = (bf16[96,384]{1,0:T(8,128)(2,1)S(1)}, bf16[96,384]{1,0:T(8,128)(2,1)S(1)}, u32[]{:S(2)}, u32[]{:S(2)}) collective-permute-start(bf16[96,384]{1,0:T(8,128)(2,1)S(1)} %get-tuple-element.70), channel_id=1, source_target_pairs={{0,2},{1,3},{2,0},{3,1},{4,6},{5,7},{6,4},{7,5},{8,10},{9,11},{10,... | collective-permute-start | bytes 221192 | tf_op jit(solution)/shard_map/ppermute | solution.py:756
  126.9 4.5 %collective-permute-start.25 = (bf16[96,384]{1,0:T(8,128)(2,1)S(1)}, bf16[96,384]{1,0:T(8,128)(2,1)S(1)}, u32[]{:S(2)}, u32[]{:S(2)}) collective-permute-start(bf16[96,384]{1,0:T(8,128)(2,1)S(1)} %get-tuple-element.71), channel_id=1, source_target_pairs={{0,3},{1,2},{2,1},{3,0},{4,7},{5,6},{6,5},{7,4},{8,11},{9,10},{10,... | collective-permute-start | bytes 221192 | tf_op jit(solution)/shard_map/ppermute | solution.py:756
  (6 other events, 23.4 us)
